TPU v7x, 32 devices: a whole 2x2x4 slice. The times are simulated.
32 devices in a mesh: seq: 8 (over z, x), head: 4 (over y, core).
Axes of the slice: x: 2, y: 2, z: 4, core: 2. Of those that a mesh axis runs over, the one named last changes fastest.
Arguments:
- queries: bfloat16 [8192, 2048], P('seq', 'head'), may hold values from -64 to 64
- keys: bfloat16 [8192, 2048], P('seq', 'head'), may hold values from -16 to 16
- values: bfloat16 [8192, 2048], P('seq', 'head'), may hold values from -6 to 6
- span_bounds: int32 [16, 2], replicated, may hold values from 0 to 8192, as said below
- mem_decay: float32 [8, 16], P(None, 'head'), may hold values from 0.01 to 1
- mem_gate: float32 [16], P('head'), may hold values from -2 to 2
- out_weight: bfloat16 [2048, 4096], P('head'), may hold values from -0.125 to 0.125
Outputs:
- mixed: bfloat16 [8192, 4096], P('seq', 'head')
Inputs may be any that keep to these rules, and one draw needn't show every extreme that they name: `span_bounds`: slot k lies in segment k // 2, inside the k % 2-th of 2 equal parts of it; start <= end, an empty slot has start == end; some slot covers a whole part.
All inputs are finite; a program needn't handle non-finite values.
Results may differ from a plain program's by a relative error of at most 0.0052.
The roundings to bfloat16 on the way count: a program that leaves them out, or rounds other values in their place, can miss the bound.
Values may be sent and summed in bfloat16 or wider, within the bound.
No kernel may reach another device: no remote copies, remote signals or barrier semaphores. Data moves between devices by JAX's collectives and lax.ppermute only.
A program may use at most 128 MiB of HBM per device.

v0:
```python
import math

import jax
import jax.numpy as jnp
from jax import lax
from jax.sharding import PartitionSpec as P

BAND = 512
SPAN_DEV = 2


HIGHEST_PRECISION = lax.Precision.HIGHEST


def from_behind(block, axis, distance):
    devices = range(lax.axis_size(axis))
    route = [(i - distance, i) for i in devices if i - distance in devices]
    return lax.ppermute(block, axis, route)


def feature_map(values_in):
    return jnp.where(values_in > 0, values_in + 1.0, jnp.exp(jnp.minimum(values_in, 0.0)))


def local_attention(
    queries_3d, band_keys, band_values, query_labels, key_labels, shard_index, band_width
):
    seg_rows, head_count, head_width = queries_3d.shape
    block_rows = min(seg_rows, 512)
    key_count = band_keys.shape[0]
    key_pos = jnp.arange(key_count) - band_width
    key_valid = (key_pos >= 0) | (shard_index > 0)
    score_scale = 1.0 / math.sqrt(head_width)

    def attend_block(block_index):
        row_start = block_index * block_rows
        query_block = lax.dynamic_slice_in_dim(queries_3d, row_start, block_rows, 0)
        label_block = lax.dynamic_slice_in_dim(query_labels, row_start, block_rows, 0)
        query_pos = row_start + jnp.arange(block_rows)
        scores = (
            jnp.einsum("qhd,khd->hqk", query_block, band_keys, preferred_element_type=jnp.float32)
            * score_scale
        )
        nearby = (
            (key_pos[None, :] <= query_pos[:, None])
            & (key_pos[None, :] > query_pos[:, None] - band_width)
            & key_valid[None, :]
        )
        same_span = (label_block[:, None] > 0) & (label_block[:, None] == key_labels[None, :])
        visible = nearby | same_span
        scores = jnp.where(visible[None], scores, -1e30)
        top_score = jnp.max(scores, axis=-1, keepdims=True)
        weights = jnp.exp(scores - top_score)
        totals = jnp.sum(weights, axis=-1)
        mixed_out = jnp.einsum(
            "hqk,khd->qhd",
            weights.astype(jnp.bfloat16),
            band_values,
            preferred_element_type=jnp.float32,
        )
        return mixed_out / jnp.transpose(totals)[:, :, None]

    blocks = lax.map(attend_block, jnp.arange(seg_rows // block_rows))
    return blocks.reshape(seg_rows, head_count, head_width)


def body(queries, keys, values, span_bounds, mem_decay, mem_gate, out_weight):
    seg_rows = queries.shape[0]
    head_count = mem_gate.shape[0]
    head_width = queries.shape[1] // head_count
    band_width = BAND
    shard_index = lax.axis_index("seq")
    prev_keys, prev_values = from_behind(
        (keys[seg_rows - band_width :], values[seg_rows - band_width :]), "seq", 1
    )
    key_feats = feature_map(keys.astype(jnp.float32)).reshape(seg_rows, head_count, head_width)
    value_rows = values.astype(jnp.float32).reshape(seg_rows, head_count, head_width)
    state = jnp.einsum("thd,the->hde", key_feats, value_rows, precision=HIGHEST_PRECISION)
    feat_sum = jnp.sum(key_feats, axis=0)
    cumulative = jnp.cumsum(jnp.log(mem_decay), axis=0)
    before = lax.dynamic_index_in_dim(
        cumulative, jnp.maximum(shard_index - 1, 0), 0, keepdims=False
    )
    part_state = lax.all_gather(state[None], "seq", axis=0, tiled=True)
    part_sum = lax.all_gather(feat_sum[None], "seq", axis=0, tiled=True)
    piece_count = part_state.shape[0]
    piece_index = jnp.arange(piece_count)
    factor = jnp.where(
        (piece_index < shard_index)[:, None],
        jnp.exp(jnp.minimum(before[None, :] - cumulative, 0.0)),
        0.0,
    )
    memory = jnp.einsum("nh,nhde->hde", factor, part_state, precision=HIGHEST_PRECISION)
    feat_total = jnp.einsum("nh,nhd->hd", factor, part_sum, precision=HIGHEST_PRECISION)
    query_feats = feature_map(queries.astype(jnp.float32)).reshape(seg_rows, head_count, head_width)
    numer = jnp.einsum("thd,hde->the", query_feats, memory, precision=HIGHEST_PRECISION)
    denom = jnp.einsum("thd,hd->th", query_feats, feat_total, precision=HIGHEST_PRECISION) + 1.0
    readout = numer / denom[:, :, None]
    own_spans = lax.dynamic_slice_in_dim(span_bounds, shard_index * SPAN_DEV, SPAN_DEV, 0)
    positions = shard_index * seg_rows + jnp.arange(seg_rows)
    inside = (positions[:, None] >= own_spans[None, :, 0]) & (
        positions[:, None] < own_spans[None, :, 1]
    )
    slot_ids = (jnp.arange(SPAN_DEV) + 1)[None, :]
    query_labels = jnp.sum(inside.astype(jnp.int32) * slot_ids, axis=1)
    key_labels = jnp.concatenate([jnp.zeros((band_width,), jnp.int32), query_labels])
    band_keys = jnp.concatenate([prev_keys, keys], axis=0).reshape(
        band_width + seg_rows, head_count, head_width
    )
    band_values = jnp.concatenate([prev_values, values], axis=0).reshape(
        band_width + seg_rows, head_count, head_width
    )
    queries_3d = queries.reshape(seg_rows, head_count, head_width)
    local = local_attention(
        queries_3d, band_keys, band_values, query_labels, key_labels, shard_index, band_width
    )
    gate = jax.nn.sigmoid(mem_gate)[None, :, None]
    attended = (
        (gate * readout + (1.0 - gate) * local)
        .astype(jnp.bfloat16)
        .reshape(seg_rows, head_count * head_width)
    )
    gathered = lax.all_gather(attended, "head", axis=1, tiled=True)
    columns = lax.all_to_all(out_weight, "head", split_axis=1, concat_axis=0, tiled=True)
    mixed = jnp.dot(gathered, columns, preferred_element_type=jnp.float32)
    return mixed.astype(jnp.bfloat16)


def solution(mesh):
    return jax.shard_map(
        body,
        mesh=mesh,
        in_specs=(
            P("seq", "head"),
            P("seq", "head"),
            P("seq", "head"),
            P(),
            P(None, "head"),
            P("head"),
            P("head", None),
        ),
        out_specs=P("seq", "head"),
        check_vma=False,
    )
```

profile of v0, /device:TPU:0, one launch (start us, length us, event | category | flops | bytes accessed | tf_op | source)
XLA Modules:
  0.0 270.6 jit_solution(7278276117064473592)
XLA Ops:
  6.5 1.6 copy.56
  9.0 5.7 %collective-permute-start = (bf16[512,512]{0,1:T(8,128)(2,1)}, bf16[512,512]{0,1:T(8,128)(2,1)}, u32[]{:S(2)}, u32[]{:S(2)}) collective-permute-start(bf16[512,512]{0,1:T(8,128)(2,1)} %slice.16), channel_id=1, source_target_pairs={{0,4},{4,8},{8,12},{12,16},{16,20},{20,24},{24,28},{1,5},{5,9},{9,... | collective-permute-start | bytes 1572872 | tf_op jit(solution)/shard_map/ppermute | solution.py:18
  16.1 3.5 %collective-permute-start.1 = (bf16[512,512]{0,1:T(8,128)(2,1)}, bf16[512,512]{0,1:T(8,128)(2,1)}, u32[]{:S(2)}, u32[]{:S(2)}) collective-permute-start(bf16[512,512]{0,1:T(8,128)(2,1)} %slice.17), channel_id=1, source_target_pairs={{0,4},{4,8},{8,12},{12,16},{16,20},{20,24},{24,28},{1,5},{5,9},{9,... | collective-permute-start | bytes 1572872 | tf_op jit(solution)/shard_map/ppermute | solution.py:18
  19.6 1.8 fusion.35
  21.4 1.8 copy.75
  23.2 3.8 %fusion.29 = f32[4,128,128]{2,1,0:T(8,128)} fusion(f32[1024,4,128]{0,2,1:T(8,128)} %bitcast.87, bf16[1024,512]{1,0:T(8,128)(2,1)} %param.11), kind=kOutput, calls=%fused_computation.42 | convolution fusion | flops 805306368 | bytes 3407872 | tf_op jit(solution)/shard_map/thd,the->hde/dot_general | solution.py:78
  27.1 37.5 %all_gather.10 = f32[8,4,128]{2,1,0:T(4,128)S(1)} all-gather(f32[1,4,128]{2,1,0:T(4,128)S(1)} %bitcast.97), channel_id=1, replica_groups=mesh['seq'=8,'head'=4] {'seq'}, dimensions={0}, use_global_device_ids=true | all-gather | bytes 18432 | tf_op jit(solution)/shard_map/all_gather | solution.py:85
  64.7 1.8 fusion.22
  66.5 1.9 copy.81
  70.3 2.3 copy.55
  72.6 2.6 pad_maximum_fusion
  75.2 1.9 copy.61
  77.2 2.3 pad_maximum_fusion.1
  79.5 2.6 copy.62
  82.1 77.2 %while.14 = (s32[]{:T(128)}, f32[2,512,4,128]{1,0,3,2:T(2,128)}, s32[2]{0:T(128)S(1)}, s32[1024]{0:T(1024)S(1)}, s32[1536]{0:T(1024)S(1)}, /*index=5*/bf16[1024,...) while((s32[]{:T(128)}, f32[2,512,4,128]{1,0,3,2:T(2,128)}, ...), condition=%wide.region_6.7_spmd.clone.clone, body=%wide.region_3.6_spmd.clone.clone.sunk | while | flops 1650986496 | bytes 49885384 | solution.py:63
  84.9 4.1 %fusion.57 = (f32[4,512]{1,0:T(4,128)S(1)}, f32[4,512,1536]{2,1,0:T(8,128)S(1)}) fusion(pred[512,1536]{1,0:T(8,128)(4,1)S(1)} %and_or_fusion.2, bf16[1536,4,128]{2,0,1:T(8,128)(2,1)S(1)} %get-tuple-element.345, bf16[1024,4,128]{0,2,1:T(8,128)(2,1)} %get-tuple-element.344, s32[]{:T(128)S(6)} %select_n.64), kind=kOutput, calls=%fused_computation.4.clone.1 | convolution fusion | flops 814741504 | bytes 15474692 | tf_op jit(solution)/shard_map/while/body/eval_jaxpr/qhd,khd->hqk/dot_general | solution.py:41
  89.0 3.6 %fusion.58 = f32[4,512]{1,0:T(4,128)S(1)} fusion(f32[4,512,1536]{2,1,0:T(8,128)S(1)} %get-tuple-element.311, f32[4,512]{1,0:T(4,128)S(1)} %get-tuple-element.312, pred[512,1536]{1,0:T(8,128)(4,1)S(1)} %and_or_fusion.2), kind=kLoop, calls=%fused_computation.5.clone.1 | loop fusion | flops 12580864 | bytes 13385728 | tf_op jit(solution)/shard_map/while/body/eval_jaxpr/reduce_sum | solution.py:54
  92.7 6.0 %divide_bitcast_fusion.2 = f32[1,512,4,128]{3,1,2,0:T(8,128)} fusion(bf16[1536,4,128]{2,0,1:T(8,128)(2,1)} %get-tuple-element.346, f32[4,512,1536]{2,1,0:T(8,128)S(1)} %get-tuple-element.311, f32[4,512]{1,0:T(4,128)S(1)} %get-tuple-element.312, pred[512,1536]{1,0:T(8,128)(4,1)S(1)} %and_or_fusion.2, f32[512,4]{0,1:T(4,128)S(1)} %bitcast.94), kind=kOutput, calls=%fused_computation.11.clone.1 | convolution fusion | flops 818151424 | bytes 16007168 | tf_op jit(solution)/shard_map/while/body/eval_jaxpr/hqk,khd->qhd/dot_general | solution.py:55
  98.7 2.4 copy.93
  101.1 19.6 %dynamic_update_slice.10 = f32[2,512,4,128]{1,0,3,2:T(2,128)} dynamic-update-slice(f32[2,512,4,128]{1,0,3,2:T(2,128)} %get-tuple-element.327, f32[1,512,4,128]{1,0,3,2:T(1,128)S(1)} %copy.93, s32[]{:T(128)} %get-tuple-element.326, s32[]{:T(128)} %constant.90.clone.1..sunk, s32[]{:T(128)} %constant.90.clone.1..sunk, s32[]{:T(128)} %constant.90.clone.1..sunk) | dynamic-update-slice | bytes 2097156 | tf_op jit(solution)/shard_map/while/body/jit(dynamic_update_index_in_dim)/dynamic_update_slice | solution.py:63
  123.5 4.1 %fusion.57 = (f32[4,512]{1,0:T(4,128)S(1)}, f32[4,512,1536]{2,1,0:T(8,128)S(1)}) fusion(pred[512,1536]{1,0:T(8,128)(4,1)S(1)} %and_or_fusion.2, bf16[1536,4,128]{2,0,1:T(8,128)(2,1)S(1)} %get-tuple-element.345, bf16[1024,4,128]{0,2,1:T(8,128)(2,1)} %get-tuple-element.344, s32[]{:T(128)S(6)} %select_n.64), kind=kOutput, calls=%fused_computation.4.clone.1 | convolution fusion | flops 814741504 | bytes 15474692 | tf_op jit(solution)/shard_map/while/body/eval_jaxpr/qhd,khd->hqk/dot_general | solution.py:41
  127.6 3.6 %fusion.58 = f32[4,512]{1,0:T(4,128)S(1)} fusion(f32[4,512,1536]{2,1,0:T(8,128)S(1)} %get-tuple-element.311, f32[4,512]{1,0:T(4,128)S(1)} %get-tuple-element.312, pred[512,1536]{1,0:T(8,128)(4,1)S(1)} %and_or_fusion.2), kind=kLoop, calls=%fused_computation.5.clone.1 | loop fusion | flops 12580864 | bytes 13385728 | tf_op jit(solution)/shard_map/while/body/eval_jaxpr/reduce_sum | solution.py:54
  131.3 6.0 %divide_bitcast_fusion.2 = f32[1,512,4,128]{3,1,2,0:T(8,128)} fusion(bf16[1536,4,128]{2,0,1:T(8,128)(2,1)} %get-tuple-element.346, f32[4,512,1536]{2,1,0:T(8,128)S(1)} %get-tuple-element.311, f32[4,512]{1,0:T(4,128)S(1)} %get-tuple-element.312, pred[512,1536]{1,0:T(8,128)(4,1)S(1)} %and_or_fusion.2, f32[512,4]{0,1:T(4,128)S(1)} %bitcast.94), kind=kOutput, calls=%fused_computation.11.clone.1 | convolution fusion | flops 818151424 | bytes 16007168 | tf_op jit(solution)/shard_map/while/body/eval_jaxpr/hqk,khd->qhd/dot_general | solution.py:55
  137.3 2.4 copy.93
  139.7 19.6 %dynamic_update_slice.10 = f32[2,512,4,128]{1,0,3,2:T(2,128)} dynamic-update-slice(f32[2,512,4,128]{1,0,3,2:T(2,128)} %get-tuple-element.327, f32[1,512,4,128]{1,0,3,2:T(1,128)S(1)} %copy.93, s32[]{:T(128)} %get-tuple-element.326, s32[]{:T(128)} %constant.90.clone.1..sunk, s32[]{:T(128)} %constant.90.clone.1..sunk, s32[]{:T(128)} %constant.90.clone.1..sunk) | dynamic-update-slice | bytes 2097156 | tf_op jit(solution)/shard_map/while/body/jit(dynamic_update_index_in_dim)/dynamic_update_slice | solution.py:63
  159.3 4.0 %reshape.179 = f32[1024,4,128]{0,2,1:T(8,128)} reshape(f32[2,512,4,128]{1,0,3,2:T(2,128)} %get-tuple-element.133) | data formatting | bytes 4194304 | tf_op jit(solution)/shard_map/reshape | solution.py:64
  163.3 4.6 %fusion.27 = f32[4,1,128,128]{3,1,2,0:T(1,128)S(1)} fusion(f32[8,4,1,1]{0,2,3,1:T(1,128)S(1)} %bitcast.96, f32[8,4,128,128]{3,2,1,0:T(8,128)} %bitcast.91), kind=kOutput, calls=%fused_computation.36 | convolution fusion | flops 6291456 | bytes 2359424 | tf_op jit(solution)/shard_map/nh,nhde->hde/dot_general | solution.py:93
  167.9 4.8 %fusion.26 = bf16[1024,4,128]{0,2,1:T(8,128)(2,1)} fusion(f32[1024,4,128]{0,2,1:T(8,128)} %reshape.179, f32[4,128,128]{2,1,0:T(8,128)S(1)} %bitcast.93, f32[1024,4,128]{0,2,1:T(8,128)S(1)} %bitcast.86, f32[4]{0:T(128)S(1)} %get-tuple-element.236, f32[1024,4]{0,1:T(4,128)S(1)} %fusion.32, f32[4]{0:T(128)S(1)} %get-tuple-element.237), kind=kOutput, calls=%fused_computation.35 | convolution fusion | flops 807927808 | bytes 5521440 | tf_op jit(solution)/shard_map/thd,hde->the/dot_general | solution.py:96
  172.7 6.6 %copy.64 = bf16[512,4096]{0,1:T(8,128)(2,1)} copy(bf16[512,4096]{1,0:T(8,128)(2,1)} %param.15) | data formatting | bytes 8388608 | tf_op args[6]
  179.3 68.7 %all_to_all.19 = bf16[512,4,1024]{0,2,1:T(8,128)(2,1)} all-to-all(bf16[512,4,1024]{0,2,1:T(8,128)(2,1)} %bitcast.84), channel_id=1, replica_groups=mesh['seq'=8,'head'=4] {'head'}, dimensions={1} | all-to-all | bytes 8388608 | tf_op jit(solution)/shard_map/all_to_all | solution.py:124
  248.0 6.3 %copy.65 = bf16[4,512,1024]{2,1,0:T(8,128)(2,1)} copy(bf16[4,512,1024]{1,2,0:T(8,128)(2,1)} %bitcast.83) | data formatting | bytes 8388608 | tf_op jit(solution)/shard_map/all_to_all | solution.py:124
  254.3 9.4 %convolution_convert_fusion = bf16[1024,1024]{1,0:T(8,128)(2,1)} fusion(bf16[1024,2048]{0,1:T(8,128)(2,1)} %all-gather.4.cloned.1.call-done, bf16[2048,1024]{1,0:T(8,128)(2,1)} %bitcast.90), kind=kOutput, calls=%fused_computation.38 | convolution fusion | flops 4296015872 | bytes 10485760 | tf_op jit(solution)/shard_map/dot_general | solution.py:125
  (58 shorter events, 8.6 us)
Async XLA Ops:
  6.5 20.5 %copy-start = (s32[16,2]{0,1:T(2,128)S(1)}, s32[16,2]{0,1:T(2,128)}, u32[]{:S(2)}) copy-start(s32[16,2]{0,1:T(2,128)} %param.12) | copy-start | bytes 388
  6.5 8.2 %copy-start.6 = (bf16[1024,512]{1,0:T(8,128)(2,1)S(1)}, bf16[1024,512]{1,0:T(8,128)(2,1)}, u32[]{:S(2)}) copy-start(bf16[1024,512]{1,0:T(8,128)(2,1)} %param.11) | copy-start | bytes 3145732
  6.5 156.8 %all-gather.6.cloned.1.call-start = ((), (), s32[]{:S(2)}) async-start(), calls=%async_computation.2 | async-start | bytes 2359296 | tf_op jit(solution)/shard_map/all_gather | solution.py:84
  8.1 8.0 %copy-start.4 = (bf16[1024,512]{0,1:T(8,128)(2,1)}, bf16[1024,512]{0,1:T(8,128)(2,1)S(1)}, u32[]{:S(2)}) copy-start(bf16[1024,512]{0,1:T(8,128)(2,1)S(1)} %copy.56) | copy-start | bytes 3145732
  9.0 63.6 %collective-permute-start = (bf16[512,512]{0,1:T(8,128)(2,1)}, bf16[512,512]{0,1:T(8,128)(2,1)}, u32[]{:S(2)}, u32[]{:S(2)}) collective-permute-start(bf16[512,512]{0,1:T(8,128)(2,1)} %slice.16), channel_id=1, source_target_pairs={{0,4},{4,8},{8,12},{12,16},{16,20},{20,24},{24,28},{1,5},{5,9},{9,... | collective-permute-start | bytes 1572872 | tf_op jit(solution)/shard_map/ppermute | solution.py:18
  16.1 61.0 %collective-permute-start.1 = (bf16[512,512]{0,1:T(8,128)(2,1)}, bf16[512,512]{0,1:T(8,128)(2,1)}, u32[]{:S(2)}, u32[]{:S(2)}) collective-permute-start(bf16[512,512]{0,1:T(8,128)(2,1)} %slice.17), channel_id=1, source_target_pairs={{0,4},{4,8},{8,12},{12,16},{16,20},{20,24},{24,28},{1,5},{5,9},{9,... | collective-permute-start | bytes 1572872 | tf_op jit(solution)/shard_map/ppermute | solution.py:18
  23.2 4.0 %copy-start.7 = (f32[8,4]{0,1:T(4,128)S(1)}, f32[8,4]{0,1:T(4,128)}, u32[]{:S(2)}) copy-start(f32[8,4]{0,1:T(4,128)} %param.13) | copy-start | bytes 388
  23.2 41.5 %copy-start.5 = (bf16[1024,512]{1,0:T(8,128)(2,1)S(1)}, bf16[1024,512]{1,0:T(8,128)(2,1)}, u32[]{:S(2)}) copy-start(bf16[1024,512]{1,0:T(8,128)(2,1)} %param.9) | copy-start | bytes 3145732
  27.0 227.4 %all-gather.4.cloned.1.call-start = ((), (), s32[]{:S(2)}) async-start(), calls=%async_computation.1 | async-start | bytes 5242880 | tf_op jit(solution)/shard_map/all_gather | solution.py:123
  68.4 4.2 %copy-start.2 = (f32[1024,512]{0,1:T(8,128)}, f32[1024,512]{0,1:T(8,128)S(1)}, u32[]{:S(2)}) copy-start(f32[1024,512]{0,1:T(8,128)S(1)} %copy.81) | copy-start | bytes 6291460
  68.4 1.7 copy-start.8
  163.3 4.6 %copy-start.3 = (f32[1024,512]{0,1:T(8,128)S(1)}, f32[1024,512]{0,1:T(8,128)}, u32[]{:S(2)}) copy-start(f32[1024,512]{0,1:T(8,128)} %copy-done.2) | copy-start | bytes 6291460
  254.3 9.4 %copy-start.1 = (s32[16,2]{0,1:T(2,128)S(1)}, s32[16,2]{0,1:T(2,128)}, u32[]{:S(2)}) copy-start(s32[16,2]{0,1:T(2,128)} %param.12) | copy-start | bytes 388
Sparse Core Ops, SparseCore 0:
  27.1 49.7 all-gather.5
  172.8 46.6 all-gather.3
where the time goes:
time: 274 us; the launch traced here: 271 us
  blocking collectives  106 us (39%)
  local copies, waits for them, and re-layouts  76.8 us (28%)
  matrix products  44 us (16%)
  other arithmetic  19.3 us (7%)
  between operations  13.6 us (5%)
  starting transfers between devices  9.21 us (3%)
    all_to_all x1, blocking collectives, body(): lax.all_to_all(out_weight, 'head', split_axis=1, concat_axis=0, tiled=True)  68.7 us
    dynamic_update_slice x4, local copies, waits for them, and re-layouts, local_attention(): blocks = lax.map(attend_block, jnp.arange(seg_rows // block_rows))  44 us
    all_gather x1, blocking collectives, body(): part_sum = lax.all_gather(feat_sum[None], 'seq', axis=0, tiled=True)  37.5 us
    unnamed x24, local copies, waits for them, and re-layouts  15.5 us
    dot_general x2, matrix products, attend_block(): jnp.einsum('hqk,khd->qhd', weights.astype(jnp.bfloat16), band_values, pre...  12 us
    dot_general x1, matrix products, body(): mixed = jnp.dot(gathered, columns, preferred_element_type=jnp.float32)  9.37 us
    ppermute x2, starting transfers between devices, from_behind(): return lax.ppermute(block, axis, route)  9.17 us
    dot_general x2, matrix products, attend_block(): jnp.einsum('qhd,khd->hqk', query_block, band_keys, preferred_element_type...  8.27 us
  transfers between devices with their start and end apart: 4, of which 0 were waited for; matrix products, arithmetic and copies ran while one was open for 44% of the time, Pallas kernels for 0%

commit v1 on v0

v1 whole, which is shorter than its diff:
```python
import functools
import math

import jax
import jax.numpy as jnp
from jax import lax
from jax.experimental import pallas as pl
from jax.experimental.pallas import tpu as pltpu
from jax.sharding import PartitionSpec as P

BAND = 512
SPAN_DEV = 2
PAD = 8
SEND_PAD = 16
MASKED = -1e30
BLOCK = 256


SMEM = pl.BlockSpec(memory_space=pltpu.SMEM)
VMEM = pl.BlockSpec(memory_space=pltpu.VMEM)
HBM = pl.BlockSpec(memory_space=pltpu.HBM)
F32, BF16 = jnp.float32, jnp.bfloat16


def phi(x):
    return jnp.where(x > 0, x + 1.0, jnp.exp(jnp.minimum(x, 0.0)))


def split(x):
    high = x.astype(BF16)
    return high, (x - high.astype(F32)).astype(BF16)


def params(limit_mib):
    return pltpu.CompilerParams(vmem_limit_bytes=limit_mib << 20)


def cost(flops, moved):
    return pl.CostEstimate(flops=int(flops), bytes_accessed=int(moved), transcendentals=0)


def pack(ref, head, memory, total):
    width = memory.shape[0]
    ref[head, :width, :] = memory.astype(BF16)
    high, low = split(total)
    row = lax.broadcasted_iota(jnp.int32, (SEND_PAD, total.shape[1]), 0)
    both = jnp.where(row == 0, high.astype(F32), jnp.where(row == 1, low.astype(F32), 0.0))
    ref[head, width:, :] = both.astype(BF16)


def unpack(ref, head):
    width = ref.shape[2]
    memory = ref[head, :width, :].astype(F32)
    total = jnp.sum(ref[head, width:, :].astype(F32), axis=0, keepdims=True)
    return memory, total


def store(ref, head, memory, total):
    width = memory.shape[0]
    ref[head, :width, :] = memory
    ref[head, width:, :] = jnp.broadcast_to(total, (PAD, total.shape[1]))


def load(ref, head):
    width = ref.shape[2]
    return ref[head, :width, :], ref[head, width : width + 1, :]


def state_kernel(k_hbm, v_hbm, state_ref, send_ref, *refs):
    *tails, k_buf, v_buf, sems = refs
    heads, width = state_ref.shape[0], state_ref.shape[2]
    rows = k_buf.shape[0]
    steps = rows // BLOCK
    copies = []
    for step in range(steps):
        at = pl.ds(step * BLOCK, BLOCK)
        pair = [
            pltpu.make_async_copy(src.at[at], buf.at[at], sems.at[which, step])
            for which, (src, buf) in enumerate(((k_hbm, k_buf), (v_hbm, v_buf)))
        ]
        for copy in pair:
            copy.start()
        copies.append(pair)
    for step in range(steps):
        for copy in copies[step]:
            copy.wait()
        at = slice(step * BLOCK, (step + 1) * BLOCK)
        for head in range(heads):
            cols = slice(head * width, (head + 1) * width)
            feats = phi(k_buf[at, cols].astype(F32))
            high, low = split(feats)
            vals = v_buf[at, cols]
            dims = (((0,), (0,)), ((), ()))
            memory = lax.dot_general(high, vals, dims, preferred_element_type=F32)
            memory += lax.dot_general(low, vals, dims, preferred_element_type=F32)
            total = jnp.sum(feats, axis=0, keepdims=True)
            if step:
                had, had_total = load(state_ref, head)
                memory, total = memory + had, total + had_total
            store(state_ref, head, memory, total)
            if step == steps - 1:
                pack(send_ref, head, memory, total)
    half = BAND // 2
    tails[0][...] = k_buf[rows - BAND : rows - half, :]
    tails[1][...] = k_buf[rows - half :, :]
    tails[2][...] = v_buf[rows - BAND :, :]


def make_state(keys, values, heads, width):
    rows, cols = keys.shape
    steps = rows // BLOCK
    half = jax.ShapeDtypeStruct((BAND // 2, cols), BF16)
    return pl.pallas_call(
        state_kernel,
        in_specs=[HBM, HBM],
        out_specs=[VMEM] * 5,
        out_shape=[
            jax.ShapeDtypeStruct((heads, width + PAD, width), F32),
            jax.ShapeDtypeStruct((heads, width + SEND_PAD, width), BF16),
            half,
            half,
            jax.ShapeDtypeStruct((BAND, cols), BF16),
        ],
        scratch_shapes=[
            pltpu.VMEM((rows, cols), BF16),
            pltpu.VMEM((rows, cols), BF16),
            pltpu.SemaphoreType.DMA((2, steps)),
        ],
        compiler_params=params(24),
        cost_estimate=cost(1e10, 4 * keys.size * 2),
        name="state",
    )(keys, values)


def fold(distance, me, decay_ref, head, memory, group, got):
    upper = (me & distance) != 0
    base = me & ~(distance - 1)
    above = base | distance
    through, before = 1.0, 1.0
    for step in range(distance):
        through = through * decay_ref[above + step, head]
        if step < distance - 1:
            factor = decay_ref[base + step, head]
            before = before * jnp.where(base + step < me, factor, 1.0)
    before = jnp.where(upper, before, 0.0)
    low, high = jnp.where(upper, 1.0, through), jnp.where(upper, through, 1.0)
    both = [low * mine + high * theirs for mine, theirs in zip(group, got)]
    if memory is None:
        memory = [before * theirs for theirs in got]
    else:
        memory = [mine + before * theirs for mine, theirs in zip(memory, got)]
    return memory, both


def fold_kernel(distance, me_ref, decay_ref, *refs):
    *inner, got_ref, group_ref, memory_ref, total_ref, send_ref = refs
    me = me_ref[0]
    for head in range(group_ref.shape[0]):
        memory = load(inner[0], head) if inner else None
        memory, both = fold(
            distance, me, decay_ref, head, memory, load(group_ref, head), unpack(got_ref, head)
        )
        store(memory_ref, head, *memory)
        store(total_ref, head, *both)
        pack(send_ref, head, *both)


def local_kernel(half, me_ref, spans_ref, q_hbm, k_hbm, v_hbm, *refs):
    *halo, out_ref, q_buf, k_buf, v_buf, kp_buf, vp_buf, sems = refs
    me = me_ref[0]
    heads, rows, width = q_buf.shape
    here, before = pl.ds(half * rows, rows), pl.ds((half - 1) * rows, rows)

    def copies(head):
        cols = pl.ds(head * width, width)
        table = [(q_hbm, here, q_buf), (k_hbm, here, k_buf), (v_hbm, here, v_buf)]
        if half:
            table += [(k_hbm, before, kp_buf), (v_hbm, before, vp_buf)]
        return [
            pltpu.make_async_copy(src.at[at, cols], buf.at[head], sems.at[which, head])
            for which, (src, at, buf) in enumerate(table)
        ]

    for head in range(heads):
        for copy in copies(head):
            copy.start()
    if not half:
        for head in range(heads):
            cols = slice(head * width, (head + 1) * width)
            kp_buf[head, : rows // 2, :] = halo[0][:, cols]
            kp_buf[head, rows // 2 :, :] = halo[1][:, cols]
            vp_buf[head] = halo[2][:, cols]

    factor = math.log2(math.e) / math.sqrt(width)
    origin = (me * SPAN_DEV + half) * rows
    first = spans_ref[me * SPAN_DEV + half, 0] - origin
    end = spans_ref[me * SPAN_DEV + half, 1] - origin
    shift = 0 if half else jnp.where(me > 0, 0, rows + 1)
    for head in range(heads):
        for copy in copies(head):
            copy.wait()
        for start in range(0, rows, BLOCK):
            query = q_buf[head, start : start + BLOCK, :]
            dims = (((1,), (1,)), ((), ()))
            prev = lax.dot_general(query, kp_buf[head, start:, :], dims, preferred_element_type=F32)
            own = lax.dot_general(query, k_buf[head], dims, preferred_element_type=F32)
            row = start + lax.broadcasted_iota(jnp.int32, (BLOCK, 1), 0)
            limit = jnp.where((row >= first) & (row < end), end - 1, row)
            col = lax.broadcasted_iota(jnp.int32, prev.shape, 1) + start
            prev = jnp.where(col > row + shift, prev, MASKED)
            col = lax.broadcasted_iota(jnp.int32, own.shape, 1)
            own = jnp.where(col <= limit, own, MASKED)
            top = jnp.maximum(
                jnp.max(prev, axis=1, keepdims=True), jnp.max(own, axis=1, keepdims=True)
            )
            prev = jnp.exp2((prev - top) * factor)
            own = jnp.exp2((own - top) * factor)
            total = jnp.sum(prev, axis=1, keepdims=True) + jnp.sum(own, axis=1, keepdims=True)
            mixed = jnp.dot(prev.astype(BF16), vp_buf[head, start:, :], preferred_element_type=F32)
            mixed += jnp.dot(own.astype(BF16), v_buf[head], preferred_element_type=F32)
            out_ref[start : start + BLOCK, head * width : (head + 1) * width] = mixed / total


def local_half(half, queries, keys, values, halo, spans, me, heads, width):
    rows = queries.shape[0] // SPAN_DEV
    buf = pltpu.VMEM((heads, rows, width), BF16)
    halo = list(halo)
    return pl.pallas_call(
        functools.partial(local_kernel, half),
        in_specs=[SMEM, SMEM, HBM, HBM, HBM] + [VMEM] * len(halo),
        out_specs=VMEM,
        out_shape=jax.ShapeDtypeStruct((rows, heads * width), F32),
        scratch_shapes=[buf] * 5 + [pltpu.SemaphoreType.DMA((5, heads))],
        compiler_params=params(32),
        cost_estimate=cost(1.5e10, 6 * rows * heads * width * 2),
    )(me, spans, queries, keys, values, *halo)


def readout_kernel(distance, me_ref, decay_ref, gate_ref, q_ref, local_ref, *refs):
    *inner, got_ref, group_ref, out_ref = refs
    me = me_ref[0]
    heads, width = group_ref.shape[0], group_ref.shape[2]
    for head in range(heads):
        memory = load(inner[0], head) if inner else None
        (memory, norm), unused = fold(
            distance, me, decay_ref, head, memory, load(group_ref, head), unpack(got_ref, head)
        )
        cols = slice(head * width, (head + 1) * width)
        feats = phi(q_ref[:, cols].astype(F32))
        q_high, q_low = split(feats)
        m_high, m_low = split(memory)
        left = jnp.concatenate([q_high, q_low], axis=1)
        right = jnp.concatenate(
            [
                jnp.concatenate([m_high, m_low], axis=1),
                jnp.concatenate([m_high, jnp.zeros_like(m_low)], axis=1),
            ],
            axis=0,
        )
        both = jnp.dot(left, right, preferred_element_type=F32)
        numer = both[:, :width] + both[:, width:]
        denom = jnp.sum(feats * norm, axis=1, keepdims=True) + 1.0
        gate = 1.0 / (1.0 + jnp.exp(jnp.full((1, width), -gate_ref[head], F32)))
        out = gate * (numer / denom) + (1.0 - gate) * local_ref[:, cols]
        out_ref[:, cols] = out.astype(BF16)


def readout(distance, start, rows, queries, local, memory, me, decay, gate):
    cols = queries.shape[1]
    chunk = lambda at: pl.BlockSpec((rows, cols), lambda i: (at // rows, 0))
    whole = [pl.BlockSpec(m.shape, lambda i: (0, 0, 0)) for m in memory]
    return pl.pallas_call(
        functools.partial(readout_kernel, distance),
        grid=(1,),
        in_specs=[SMEM, SMEM, SMEM, chunk(start), chunk(start % BAND), *whole],
        out_specs=chunk(0),
        out_shape=jax.ShapeDtypeStruct((rows, cols), BF16),
        compiler_params=params(16),
        cost_estimate=cost(2e9, rows * cols * 8),
    )(me, decay, gate, queries, local, *memory)


def project_kernel(shared, odd_ref, *refs):
    xs, ws, out_ref = refs[: len(shared)], list(refs[len(shared) :]), refs[-1]
    columns = out_ref.shape[1]
    odd = odd_ref[0]
    lefts, rights = [], []
    for x_ref, is_shared in zip(xs, shared):
        if is_shared:
            unit = x_ref.shape[1] // 4
            most = x_ref[:, pl.ds(pl.multiple_of(odd * unit, unit), 3 * unit)]
            rest = x_ref[:, pl.ds(pl.multiple_of((1 - odd) * 3 * unit, unit), unit)]
            lefts.append(jnp.concatenate([most, rest], axis=1))
            rights.append((ws.pop(0), ws.pop(0)))
        else:
            lefts.append(x_ref[...])
            rights.append((ws.pop(0),))
    tile = 256
    for start in range(0, columns, tile):
        at = slice(start, start + tile)
        acc = None
        for left, right in zip(lefts, rights):
            block = [w_ref[:, at] for w_ref in right]
            block = jnp.concatenate(block, axis=0) if len(block) > 1 else block[0]
            term = jnp.dot(left, block, preferred_element_type=F32)
            acc = term if acc is None else acc + term
        out_ref[:, at] = acc.astype(out_ref.dtype)


def project(start, total_rows, xs, weights, odd, out):
    rows = xs[0].shape[0]
    flat = [w for ws in weights for w in ws]
    columns = flat[0].shape[1]
    whole = lambda a: pl.BlockSpec(a.shape, lambda i: (0, 0))
    operands = [odd, *xs, *flat]
    in_specs = [SMEM] + [whole(a) for a in operands[1:]]
    aliases = {}
    if out is not None:
        in_specs.append(pl.BlockSpec(memory_space=pl.ANY))
        aliases = {len(operands): 0}
        operands.append(out)
    depth = sum(w.shape[0] for w in flat)
    return pl.pallas_call(
        functools.partial(project_kernel, [len(ws) > 1 for ws in weights]),
        grid=(1,),
        in_specs=in_specs,
        out_specs=pl.BlockSpec((rows, columns), lambda i: (start // rows, 0)),
        out_shape=jax.ShapeDtypeStruct((total_rows, columns), BF16),
        input_output_aliases=aliases,
        compiler_params=params(24),
        cost_estimate=cost(2 * rows * depth * columns, depth * columns * 2),
    )(*operands)


def swap(x, axis, mask):
    size = lax.axis_size(axis)
    return lax.ppermute(x, axis, [(i, i ^ mask) for i in range(size)])


CHUNKS = ((512, 512), (0, 256), (256, 256))


def body(queries, keys, values, span_bounds, mem_decay, mem_gate, out_weight):
    seg_rows = queries.shape[0]
    heads = mem_gate.shape[0]
    width = queries.shape[1] // heads
    seq_size, head_size = lax.axis_size("seq"), lax.axis_size("head")
    assert head_size & (head_size - 1) == 0 and seg_rows == BAND * SPAN_DEV
    assert seq_size & (seq_size - 1) == 0 and seq_size > 1
    seq_index, head_index = lax.axis_index("seq"), lax.axis_index("head")
    me = seq_index.astype(jnp.int32).reshape(1)
    odd = me & 1
    depth = out_weight.shape[0]
    unit = depth // 4
    columns = out_weight.shape[1] // head_size

    weights = {}
    last = out_weight
    for mask in sorted(range(1, head_size), reverse=True):
        shared = mask > 1
        row, rows = (odd[0] * unit, 3 * unit) if shared else (0, depth)
        source, _ = lax.optimization_barrier((out_weight, last))
        block = lax.dynamic_slice(source, (row, (head_index ^ mask) * columns), (rows, columns))
        last = block[:8, :128]
        weights[mask] = (swap(block, "head", mask),)
    for mask in weights:
        if mask > 1:
            most = weights[mask][0]
            part = lax.dynamic_slice_in_dim(most, odd[0] * 2 * unit, unit, 0)
            weights[mask] = (most, swap(part, "seq", 1))
    weights[0] = (lax.dynamic_slice_in_dim(out_weight, head_index * columns, columns, 1),)

    state, send, *tails = make_state(keys, values, heads, width)
    halo = []
    for tail in tails:
        halo.append(lax.ppermute(tail, "seq", [(i, i + 1) for i in range(seq_size - 1)]))

    inner, group, distance = [], state, 1
    while True:
        got = swap(send, "seq", distance)
        if 2 * distance >= seq_size:
            break
        shape = jax.ShapeDtypeStruct(state.shape, F32)
        operands = [me, mem_decay, *inner, got, group]
        memory, group, send = pl.pallas_call(
            functools.partial(fold_kernel, distance),
            in_specs=[SMEM, SMEM] + [VMEM] * (len(operands) - 2),
            out_specs=[VMEM] * 3,
            out_shape=[shape, shape, jax.ShapeDtypeStruct(send.shape, BF16)],
            compiler_params=params(16),
            cost_estimate=cost(1e9, 5 * state.size * 4),
        )(*operands)
        inner, distance = [memory], 2 * distance
    memory = [*inner, got, group]

    locals_ = {}
    for half in (1, 0):
        locals_[half] = local_half(
            half, queries, keys, values, () if half else halo,
            span_bounds, me, heads, width,
        )

    out = None
    for start, rows in CHUNKS:
        own = readout(
            distance, start, rows, queries,
            locals_[start // BAND], memory, me, mem_decay, mem_gate,
        )
        xs = {0: own}
        mask = head_size // 2
        while mask:
            for at, x in list(xs.items()):
                xs[at ^ mask] = swap(x, "head", mask)
            mask //= 2
        order = range(head_size)
        out = project(
            start, seg_rows,
            [xs[i] for i in order], [weights[i] for i in order], odd, out,
        )
    return out


def solution(mesh):
    return jax.shard_map(
        body,
        mesh=mesh,
        in_specs=(
            P("seq", "head"),
            P("seq", "head"),
            P("seq", "head"),
            P(),
            P(None, "head"),
            P("head"),
            P("head", None),
        ),
        out_specs=P("seq", "head"),
        check_vma=False,
    )
```

time: 274 us -> 117 us (0.43)
  blocking collectives: 106 us -> 0 us
  local copies, waits for them, and re-layouts: 76.8 us -> 29.5 us
  matrix products: 44 us -> 0 us
  waiting for transfers between devices: 0.04 us -> 31.8 us
  Pallas kernels: 0 us -> 30.2 us
  other arithmetic: 19.3 us -> 0 us
  starting transfers between devices: 9.21 us -> 24.2 us
  between operations: 13.6 us -> 0.25 us
    all_to_all x1 -> x0, blocking collectives: 68.7 us -> none  [body(): lax.all_to_all(out_weight, 'head', split_axis=1, concat_axis=0, tiled=True)]
    dot_general x10 -> x0, matrix products: 44 us -> none  [the longest x2 12 us: attend_block(): jnp.einsum('hqk,khd->qhd', weights.astype(jnp.bfloat16), band_values, pre...]
    dynamic_update_slice x4 -> x0, local copies, waits for them, and re-layouts: 44 us -> none  [local_attention(): blocks = lax.map(attend_block, jnp.arange(seg_rows // block_rows))]
    all_gather x1 -> x0, blocking collectives: 37.5 us -> none  [body(): part_sum = lax.all_gather(feat_sum[None], 'seq', axis=0, tiled=True)]
    ppermute x2 -> x20, waiting for transfers between devices: 0.01 us -> 31.8 us  [the longest x17 31.8 us: swap(): return lax.ppermute(x, axis, [(i, i ^ mask) for i in range(size)])]
    pallas_call x0 -> x11, Pallas kernels: none -> 30.2 us  [the longest x2 12 us: local_half(): pl.pallas_call(functools.partial(local_kernel, half), in_specs=[SMEM, SME...]
    ppermute x2 -> x20, starting transfers between devices: 9.17 us -> 24.2 us  [the longest x17 14.3 us: swap(): return lax.ppermute(x, axis, [(i, i ^ mask) for i in range(size)])]
    reduce_sum x4 -> x0, other arithmetic: 9.17 us -> none  [the longest x2 7.29 us: attend_block(): totals = jnp.sum(weights, axis=-1)]
  transfers between devices with their start and end apart: 4 -> 20, of which waited for: 0 -> 5; matrix products, arithmetic and copies ran while one was open for 44% -> 8% of each run, Pallas kernels for 0% -> 21%
where the time goes in v1:
time: 117 us; the launch traced here: 116 us
  waiting for transfers between devices  31.8 us (27%)
  Pallas kernels  30.2 us (26%)
  local copies, waits for them, and re-layouts  29.5 us (25%)
  starting transfers between devices  24.2 us (21%)
    ppermute x17, waiting for transfers between devices, swap(): return lax.ppermute(x, axis, [(i, i ^ mask) for i in range(size)])  31.8 us
    unnamed x70, local copies, waits for them, and re-layouts  20.2 us
    ppermute x17, starting transfers between devices, swap(): return lax.ppermute(x, axis, [(i, i ^ mask) for i in range(size)])  14.3 us
    pallas_call x2, Pallas kernels, local_half(): pl.pallas_call(functools.partial(local_kernel, half), in_specs=[SMEM, SME...  12 us
    pallas_call x3, Pallas kernels, project(): pl.pallas_call(functools.partial(project_kernel, [len(ws) > 1 for ws in w...  9.99 us
    ppermute x3, starting transfers between devices, body(): lax.ppermute(tail, 'seq', [(i, i + 1) for i in range(seq_size - 1)])  9.93 us
    dynamic_slice x3, local copies, waits for them, and re-layouts, body(): lax.dynamic_slice(source, (row, (head_index ^ mask) * columns), (rows, co...  6.51 us
    pallas_call x3, Pallas kernels, readout(): pl.pallas_call(functools.partial(readout_kernel, distance), grid=(1,), in...  4.19 us
  transfers between devices with their start and end apart: 20, of which 5 were waited for; matrix products, arithmetic and copies ran while one was open for 8% of the time, Pallas kernels for 21%

profile of v1, /device:TPU:0, one launch (start us, length us, event | category | flops | bytes accessed | tf_op | source)
XLA Modules:
  0.0 115.9 jit_solution(5592068314264973192)
XLA Ops:
  0.0 1.2 %copy-done.4 = bf16[1024,512]{1,0:T(8,128)(2,1)S(1)} copy-done((bf16[1024,512]{1,0:T(8,128)(2,1)S(1)}, bf16[1024,512]{1,0:T(8,128)(2,1)}, u32[]{:S(2)}) %copy-start.4) | copy-done | bytes 1048600
  1.2 1.2 %copy-done.7 = bf16[1024,512]{1,0:T(8,128)(2,1)S(1)} copy-done((bf16[1024,512]{1,0:T(8,128)(2,1)S(1)}, bf16[1024,512]{1,0:T(8,128)(2,1)}, u32[]{:S(2)}) %copy-start.7) | copy-done | bytes 1048600
  2.5 2.7 %state.1 = (f32[4,136,128]{2,1,0:T(8,128)S(1)}, bf16[4,144,128]{2,1,0:T(8,128)(2,1)S(1)}, bf16[256,512]{1,0:T(8,128)(2,1)S(1)}, bf16[256,512]{1,0:T(8,128)(2,1)}, bf16[512,512]{1,0:T(8,128)(2,1)S(1)}) custom-call(bf16[1024,512]{1,0:T(8,128)(2,1)S(1)} %copy-done.4, bf16[1024,512]{1,0:T(8,128)(2,1)S(1)} %copy-done.7), custom_call_target="tpu_custom_call" | custom-call | flops 10000000000 | bytes 4194304 | tf_op jit(solution)/shard_map/state/pallas_call | solution.py:113
  5.8 3.0 %collective-permute-start.3 = (bf16[4,144,128]{2,1,0:T(8,128)(2,1)S(1)}, bf16[4,144,128]{2,1,0:T(8,128)(2,1)S(1)}, u32[]{:S(2)}, u32[]{:S(2)}) collective-permute-start(bf16[4,144,128]{2,1,0:T(8,128)(2,1)S(1)} %get-tuple-element.20), channel_id=1, source_target_pairs={{0,4},{4,0},{8,12},{12,8},{16,20},{20,16},{24,28},{28,24},{1,5},{5... | collective-permute-start | bytes 442376 | tf_op jit(solution)/shard_map/ppermute | solution.py:337
  8.9 3.8 %collective-permute-done.3.refs_0_ = bf16[4,144,128]{2,1,0:T(8,128)(2,1)S(1)} collective-permute-done((bf16[4,144,128]{2,1,0:T(8,128)(2,1)S(1)}, bf16[4,144,128]{2,1,0:T(8,128)(2,1)S(1)}, u32[]{:S(2)}, u32[]{:S(2)}) %collective-permute-start.3) | collective-permute-done | bytes 147488 | tf_op jit(solution)/shard_map/ppermute | solution.py:337
  15.7 1.8 %collective-permute-start.4 = (bf16[4,144,128]{2,1,0:T(8,128)(2,1)S(1)}, bf16[4,144,128]{2,1,0:T(8,128)(2,1)S(1)}, u32[]{:S(2)}, u32[]{:S(2)}) collective-permute-start(bf16[4,144,128]{2,1,0:T(8,128)(2,1)S(1)} %get-tuple-element.23), channel_id=1, source_target_pairs={{0,8},{4,12},{8,0},{12,4},{16,24},{20,28},{24,16},{28,20},{1,9},{5... | collective-permute-start | bytes 442376 | tf_op jit(solution)/shard_map/ppermute | solution.py:337
  17.5 2.1 %dynamic_slice.20 = bf16[384,1024]{1,0:T(8,128)(2,1)} dynamic-slice(bf16[512,4096]{1,0:T(8,128)(2,1)} %param.13, s32[]{:T(128)S(6)} %select_n.22, s32[]{:T(128)S(6)} %select_n.23), dynamic_slice_sizes={384,1024} | dynamic-slice | bytes 1572868 | tf_op jit(solution)/shard_map/dynamic_slice | solution.py:363
  19.6 1.5 %collective-permute-start.10 = (bf16[384,1024]{1,0:T(8,128)(2,1)}, bf16[384,1024]{1,0:T(8,128)(2,1)S(1)}, u32[]{:S(2)}, u32[]{:S(2)}) collective-permute-start(bf16[384,1024]{1,0:T(8,128)(2,1)} %dynamic_slice.20), channel_id=1, source_target_pairs={{0,2},{1,3},{2,0},{3,1},{4,6},{5,7},{6,4},{7,5},{8,10},{9,11},{10,... | collective-permute-start | bytes 2359304 | tf_op jit(solution)/shard_map/ppermute | solution.py:337
  21.1 3.4 %collective-permute-start = (bf16[256,512]{1,0:T(8,128)(2,1)S(1)}, bf16[256,512]{1,0:T(8,128)(2,1)S(1)}, u32[]{:S(2)}, u32[]{:S(2)}) collective-permute-start(bf16[256,512]{1,0:T(8,128)(2,1)S(1)} %get-tuple-element.17), channel_id=1, source_target_pairs={{0,4},{4,8},{8,12},{12,16},{16,20},{20,24},{24,28},{1,5},{5,9},{9,... | collective-permute-start | bytes 786440 | tf_op jit(solution)/shard_map/ppermute | solution.py:376
  24.5 3.0 %collective-permute-start.1 = (bf16[256,512]{1,0:T(8,128)(2,1)}, bf16[256,512]{1,0:T(8,128)(2,1)}, u32[]{:S(2)}, u32[]{:S(2)}) collective-permute-start(bf16[256,512]{1,0:T(8,128)(2,1)} %get-tuple-element.18), channel_id=1, source_target_pairs={{0,4},{4,8},{8,12},{12,16},{16,20},{20,24},{24,28},{1,5},{5,9},{9,... | collective-permute-start | bytes 786440 | tf_op jit(solution)/shard_map/ppermute | solution.py:376
  27.6 3.5 %collective-permute-start.2 = (bf16[512,512]{1,0:T(8,128)(2,1)S(1)}, bf16[512,512]{1,0:T(8,128)(2,1)}, u32[]{:S(2)}, u32[]{:S(2)}) collective-permute-start(bf16[512,512]{1,0:T(8,128)(2,1)S(1)} %get-tuple-element.19), channel_id=1, source_target_pairs={{0,4},{4,8},{8,12},{12,16},{16,20},{20,24},{24,28},{1,5},{5,9},{9,... | collective-permute-start | bytes 1572872 | tf_op jit(solution)/shard_map/ppermute | solution.py:376
  35.2 2.0 %collective-permute-start.5 = (bf16[4,144,128]{2,1,0:T(8,128)(2,1)S(1)}, bf16[4,144,128]{2,1,0:T(8,128)(2,1)S(1)}, u32[]{:S(2)}, u32[]{:S(2)}) collective-permute-start(bf16[4,144,128]{2,1,0:T(8,128)(2,1)S(1)} %get-tuple-element.26), channel_id=1, source_target_pairs={{0,16},{4,20},{8,24},{12,28},{16,0},{20,4},{24,8},{28,12},{1,17},{... | collective-permute-start | bytes 442376 | tf_op jit(solution)/shard_map/ppermute | solution.py:337
  37.1 1.2 %copy-done.8 = bf16[1024,512]{1,0:T(8,128)(2,1)S(1)} copy-done((bf16[1024,512]{1,0:T(8,128)(2,1)S(1)}, bf16[1024,512]{1,0:T(8,128)(2,1)}, u32[]{:S(2)}) %copy-start.8) | copy-done | bytes 1048600
  38.4 1.2 %copy-done.10 = bf16[1024,512]{1,0:T(8,128)(2,1)S(1)} copy-done((bf16[1024,512]{1,0:T(8,128)(2,1)S(1)}, bf16[1024,512]{1,0:T(8,128)(2,1)}, u32[]{:S(2)}) %copy-start.10) | copy-done | bytes 1048600
  39.6 5.7 %shard_map.78.local_ref = f32[512,512]{1,0:T(8,128)S(1)} custom-call(s32[1]{0:T(128)} %bitcast.me_ref, s32[16,2]{1,0:T(8,128)S(1)} %copy.10.spans_ref, bf16[1024,512]{1,0:T(8,128)(2,1)S(1)} %copy-done.10, bf16[1024,512]{1,0:T(8,128)(2,1)S(1)} %copy-done.5, bf16[1024,512]{1,0:T(8,128)(2,1)S(1)} %copy-done.8), custom_call_target="tpu_custom_call" | custom-call | flops 15000000512 | bytes 3145728 | tf_op jit(solution)/shard_map/pallas_call | solution.py:228
  46.3 2.1 %dynamic_slice.22 = bf16[384,1024]{1,0:T(8,128)(2,1)} dynamic-slice(bf16[512,4096]{1,0:T(8,128)(2,1)} %param.13, s32[]{:T(128)S(6)} %select_n.22, s32[]{:T(128)S(6)} %select_n.25), dynamic_slice_sizes={384,1024} | dynamic-slice | bytes 1572868 | tf_op jit(solution)/shard_map/dynamic_slice | solution.py:363
  48.4 2.4 %constant_dynamic-slice_fusion.2 = bf16[512,1024]{1,0:T(8,128)(2,1)} fusion(bf16[512,4096]{1,0:T(8,128)(2,1)} %param.13, s32[]{:T(128)S(6)} %select_n.21), kind=kLoop, calls=%fused_computation.2 | loop fusion | bytes 2097156 | tf_op jit(solution)/shard_map/dynamic_slice | solution.py:363
  50.8 1.4 %copy-done.11 = bf16[1024,512]{1,0:T(8,128)(2,1)S(1)} copy-done((bf16[1024,512]{1,0:T(8,128)(2,1)S(1)}, bf16[1024,512]{1,0:T(8,128)(2,1)}, u32[]{:S(2)}) %copy-start.11) | copy-done | bytes 1048600
  52.2 1.2 %copy-done.19 = f32[512,512]{1,0:T(8,128)S(1)} copy-done((f32[512,512]{1,0:T(8,128)S(1)}, f32[512,512]{1,0:T(8,128)}, u32[]{:S(2)}) %copy-start.19) | copy-done | bytes 1048600
  55.3 2.2 %shard_map.79.refs_0_ = bf16[512,512]{1,0:T(8,128)(2,1)} custom-call(s32[1]{0:T(128)} %bitcast.me_ref, f32[8,4]{1,0:T(8,128)S(1)} %copy.13.decay_ref, f32[4]{0:T(128)S(1)} %copy-done.17, bf16[1024,512]{1,0:T(8,128)(2,1)S(1)} %copy-done.11, f32[512,512]{1,0:T(8,128)S(1)} %copy-done.19, f32[4,136,128]{2,1,0:T(8,128)S(1)} %copy-done.21, ...), custom_call_target="tpu_custom_call" | custom-call | flops 2000000000 | bytes 2097152 | tf_op jit(solution)/shard_map/pallas_call | solution.py:272
  58.7 1.5 %collective-permute-start.18 = (bf16[512,512]{1,0:T(8,128)(2,1)}, bf16[512,512]{1,0:T(8,128)(2,1)}, u32[]{:S(2)}, u32[]{:S(2)}) collective-permute-start(bf16[512,512]{1,0:T(8,128)(2,1)} %shard_map.79.refs_0_), channel_id=1, source_target_pairs={{0,2},{1,3},{2,0},{3,1},{4,6},{5,7},{6,4},{7,5},{8,10},{9,11},{10,... | collective-permute-start | bytes 1572872 | tf_op jit(solution)/shard_map/ppermute | solution.py:337
  61.2 6.3 %shard_map.73.local_ref = f32[512,512]{1,0:T(8,128)S(1)} custom-call(s32[1]{0:T(128)} %bitcast.me_ref, s32[16,2]{1,0:T(8,128)S(1)} %copy.10.spans_ref, bf16[1024,512]{1,0:T(8,128)(2,1)S(1)} %copy-done.12, bf16[1024,512]{1,0:T(8,128)(2,1)S(1)} %copy-done.6, bf16[1024,512]{1,0:T(8,128)(2,1)S(1)} %copy-done.9, bf16[256,512]{1,0:T(8,128)(2,1)S(1)} %copy-done.14, ...), custom_call_target="tpu_custom_call" | custom-call | flops 15000000512 | bytes 3145728 | tf_op jit(solution)/shard_map/pallas_call | solution.py:228
  70.0 15.8 %collective-permute-done.7.refs_2_ = bf16[256,512]{1,0:T(8,128)(2,1)S(1)} collective-permute-done((bf16[256,512]{1,0:T(8,128)(2,1)S(1)}, bf16[256,512]{1,0:T(8,128)(2,1)S(1)}, u32[]{:S(2)}, u32[]{:S(2)}) %collective-permute-start.7) | collective-permute-done | bytes 262176 | tf_op jit(solution)/shard_map/ppermute | solution.py:337
  87.3 1.0 shard_map.77.refs_0_
  88.3 1.7 %collective-permute-start.15 = (bf16[256,512]{1,0:T(8,128)(2,1)S(1)}, bf16[256,512]{1,0:T(8,128)(2,1)}, u32[]{:S(2)}, u32[]{:S(2)}) collective-permute-start(bf16[256,512]{1,0:T(8,128)(2,1)S(1)} %shard_map.77.refs_0_), channel_id=1, source_target_pairs={{0,2},{1,3},{2,0},{3,1},{4,6},{5,7},{6,4},{7,5},{8,10},{9,11},{10,... | collective-permute-start | bytes 786440 | tf_op jit(solution)/shard_map/ppermute | solution.py:337
  91.8 5.3 %collective-permute-done.15.refs_2_ = bf16[256,512]{1,0:T(8,128)(2,1)} collective-permute-done((bf16[256,512]{1,0:T(8,128)(2,1)S(1)}, bf16[256,512]{1,0:T(8,128)(2,1)}, u32[]{:S(2)}, u32[]{:S(2)}) %collective-permute-start.15) | collective-permute-done | bytes 262176 | tf_op jit(solution)/shard_map/ppermute | solution.py:337
  97.2 2.8 %collective-permute-done.11.refs_7_ = bf16[128,1024]{1,0:T(8,128)(2,1)S(1)} collective-permute-done((bf16[128,1024]{1,0:T(8,128)(2,1)}, bf16[128,1024]{1,0:T(8,128)(2,1)S(1)}, u32[]{:S(2)}, u32[]{:S(2)}) %collective-permute-start.11) | collective-permute-done | bytes 262176 | tf_op jit(solution)/shard_map/ppermute | solution.py:337
  100.0 1.3 %constant_dynamic-slice_fusion.3.refs_4_ = bf16[512,1024]{1,0:T(8,128)(2,1)S(1)} fusion(bf16[512,4096]{1,0:T(8,128)(2,1)} %param.13, s32[]{:T(128)S(6)} %select_n.20), kind=kLoop, calls=%fused_computation.3 | loop fusion | bytes 2097156 | tf_op jit(solution)/shard_map/dynamic_slice | solution.py:371
  101.3 4.0 %collective-permute-done.13.refs_9_ = bf16[128,1024]{1,0:T(8,128)(2,1)S(1)} collective-permute-done((bf16[128,1024]{1,0:T(8,128)(2,1)}, bf16[128,1024]{1,0:T(8,128)(2,1)S(1)}, u32[]{:S(2)}, u32[]{:S(2)}) %collective-permute-start.13) | collective-permute-done | bytes 262176 | tf_op jit(solution)/shard_map/ppermute | solution.py:337
  105.9 4.8 %shard_map.80.refs_10_ = bf16[1024,1024]{1,0:T(8,128)(2,1)} custom-call(s32[1]{0:T(128)S(6)} %and.5.odd_ref, bf16[512,512]{1,0:T(8,128)(2,1)} %shard_map.79.refs_0_, bf16[512,512]{1,0:T(8,128)(2,1)} %collective-permute-done.17.refs_1_, bf16[512,512]{1,0:T(8,128)(2,1)} %collective-permute-done.18.refs_2_, bf16[512,512]{1,0:T(8,128)(2,1)} %collective-permute-done.19.refs_3_, ...), custom_call_target="tpu_custom_call" | custom-call | flops 2147483648 | bytes 4194304 | tf_op jit(solution)/shard_map/pallas_call | solution.py:323
  110.7 3.1 %shard_map.81.refs_10_ = bf16[1024,1024]{1,0:T(8,128)(2,1)} custom-call(s32[1]{0:T(128)S(6)} %and.5.odd_ref, bf16[256,512]{1,0:T(8,128)(2,1)S(1)} %copy-done.3, bf16[256,512]{1,0:T(8,128)(2,1)S(1)} %collective-permute-done.14.refs_1_, bf16[256,512]{1,0:T(8,128)(2,1)} %collective-permute-done.15.refs_2_, ...), custom_call_target="tpu_custom_call", output_to_operand_aliasing={{}: (11, {})} | custom-call | flops 1073741824 | bytes 4194304 | tf_op jit(solution)/shard_map/pallas_call | solution.py:323
  113.8 2.1 %shard_map.82 = bf16[1024,1024]{1,0:T(8,128)(2,1)} custom-call(s32[1]{0:T(128)S(6)} %and.5.odd_ref, bf16[256,512]{1,0:T(8,128)(2,1)S(1)} %shard_map.76.refs_0_, bf16[256,512]{1,0:T(8,128)(2,1)S(1)} %collective-permute-done.6.refs_1_, bf16[256,512]{1,0:T(8,128)(2,1)S(1)} %copy-done.1, ...), custom_call_target="tpu_custom_call", output_to_operand_aliasing={{}: (11, {})} | custom-call | flops 1073741824 | bytes 4194304 | tf_op jit(solution)/shard_map/pallas_call | solution.py:323
  (95 shorter events, 19.4 us)
Async XLA Ops:
  2.5 6.3 %copy-start.32 = (f32[8,4]{0,1:T(4,128)S(1)}, f32[8,4]{0,1:T(4,128)}, u32[]{:S(2)}) copy-start(f32[8,4]{0,1:T(4,128)} %param.11) | copy-start | bytes 388
  5.8 25.2 %copy-start.33 = (s32[16,2]{0,1:T(2,128)S(1)}, s32[16,2]{0,1:T(2,128)}, u32[]{:S(2)}) copy-start(s32[16,2]{0,1:T(2,128)} %param.10) | copy-start | bytes 388
  5.8 6.8 %collective-permute-start.3 = (bf16[4,144,128]{2,1,0:T(8,128)(2,1)S(1)}, bf16[4,144,128]{2,1,0:T(8,128)(2,1)S(1)}, u32[]{:S(2)}, u32[]{:S(2)}) collective-permute-start(bf16[4,144,128]{2,1,0:T(8,128)(2,1)S(1)} %get-tuple-element.20), channel_id=1, source_target_pairs={{0,4},{4,0},{8,12},{12,8},{16,20},{20,16},{24,28},{28,24},{1,5},{5... | collective-permute-start | bytes 442376 | tf_op jit(solution)/shard_map/ppermute | solution.py:337
  13.6 23.5 %copy-start.5 = (bf16[1024,512]{1,0:T(8,128)(2,1)S(1)}, bf16[1024,512]{1,0:T(8,128)(2,1)}, u32[]{:S(2)}) copy-start(bf16[1024,512]{1,0:T(8,128)(2,1)} %k_hbm.5) | copy-start | bytes 3145732
  15.7 15.4 %collective-permute-start.4 = (bf16[4,144,128]{2,1,0:T(8,128)(2,1)S(1)}, bf16[4,144,128]{2,1,0:T(8,128)(2,1)S(1)}, u32[]{:S(2)}, u32[]{:S(2)}) collective-permute-start(bf16[4,144,128]{2,1,0:T(8,128)(2,1)S(1)} %get-tuple-element.23), channel_id=1, source_target_pairs={{0,8},{4,12},{8,0},{12,4},{16,24},{20,28},{24,16},{28,20},{1,9},{5... | collective-permute-start | bytes 442376 | tf_op jit(solution)/shard_map/ppermute | solution.py:337
  19.6 68.7 %collective-permute-start.10 = (bf16[384,1024]{1,0:T(8,128)(2,1)}, bf16[384,1024]{1,0:T(8,128)(2,1)S(1)}, u32[]{:S(2)}, u32[]{:S(2)}) collective-permute-start(bf16[384,1024]{1,0:T(8,128)(2,1)} %dynamic_slice.20), channel_id=1, source_target_pairs={{0,2},{1,3},{2,0},{3,1},{4,6},{5,7},{6,4},{7,5},{8,10},{9,11},{10,... | collective-permute-start | bytes 2359304 | tf_op jit(solution)/shard_map/ppermute | solution.py:337
  21.1 36.4 %collective-permute-start = (bf16[256,512]{1,0:T(8,128)(2,1)S(1)}, bf16[256,512]{1,0:T(8,128)(2,1)S(1)}, u32[]{:S(2)}, u32[]{:S(2)}) collective-permute-start(bf16[256,512]{1,0:T(8,128)(2,1)S(1)} %get-tuple-element.17), channel_id=1, source_target_pairs={{0,4},{4,8},{8,12},{12,16},{16,20},{20,24},{24,28},{1,5},{5,9},{9,... | collective-permute-start | bytes 786440 | tf_op jit(solution)/shard_map/ppermute | solution.py:376
  24.5 34.1 %collective-permute-start.1 = (bf16[256,512]{1,0:T(8,128)(2,1)}, bf16[256,512]{1,0:T(8,128)(2,1)}, u32[]{:S(2)}, u32[]{:S(2)}) collective-permute-start(bf16[256,512]{1,0:T(8,128)(2,1)} %get-tuple-element.18), channel_id=1, source_target_pairs={{0,4},{4,8},{8,12},{12,16},{16,20},{20,24},{24,28},{1,5},{5,9},{9,... | collective-permute-start | bytes 786440 | tf_op jit(solution)/shard_map/ppermute | solution.py:376
  27.6 32.6 %collective-permute-start.2 = (bf16[512,512]{1,0:T(8,128)(2,1)S(1)}, bf16[512,512]{1,0:T(8,128)(2,1)}, u32[]{:S(2)}, u32[]{:S(2)}) collective-permute-start(bf16[512,512]{1,0:T(8,128)(2,1)S(1)} %get-tuple-element.19), channel_id=1, source_target_pairs={{0,4},{4,8},{8,12},{12,16},{16,20},{20,24},{24,28},{1,5},{5,9},{9,... | collective-permute-start | bytes 1572872 | tf_op jit(solution)/shard_map/ppermute | solution.py:376
  35.2 15.6 %collective-permute-start.5 = (bf16[4,144,128]{2,1,0:T(8,128)(2,1)S(1)}, bf16[4,144,128]{2,1,0:T(8,128)(2,1)S(1)}, u32[]{:S(2)}, u32[]{:S(2)}) collective-permute-start(bf16[4,144,128]{2,1,0:T(8,128)(2,1)S(1)} %get-tuple-element.26), channel_id=1, source_target_pairs={{0,16},{4,20},{8,24},{12,28},{16,0},{20,4},{24,8},{28,12},{1,17},{... | collective-permute-start | bytes 442376 | tf_op jit(solution)/shard_map/ppermute | solution.py:337
  39.6 11.2 %copy-start.17 = (f32[4]{0:T(128)S(1)}, f32[4]{0:T(128)}, u32[]{:S(2)}) copy-start(f32[4]{0:T(128)} %gate_ref.5) | copy-start | bytes 52
  48.4 11.8 %copy-start.12 = (bf16[1024,512]{1,0:T(8,128)(2,1)S(1)}, bf16[1024,512]{1,0:T(8,128)(2,1)}, u32[]{:S(2)}) copy-start(bf16[1024,512]{1,0:T(8,128)(2,1)} %q_ref.5) | copy-start | bytes 3145732
  50.7 9.5 %copy-start.6 = (bf16[1024,512]{1,0:T(8,128)(2,1)S(1)}, bf16[1024,512]{1,0:T(8,128)(2,1)}, u32[]{:S(2)}) copy-start(bf16[1024,512]{1,0:T(8,128)(2,1)} %k_hbm.5) | copy-start | bytes 3145732
  50.7 9.5 %copy-start.9 = (bf16[1024,512]{1,0:T(8,128)(2,1)S(1)}, bf16[1024,512]{1,0:T(8,128)(2,1)}, u32[]{:S(2)}) copy-start(bf16[1024,512]{1,0:T(8,128)(2,1)} %v_hbm.5) | copy-start | bytes 3145732
  50.7 9.5 %copy-start.15 = (bf16[4,144,128]{2,1,0:T(8,128)(2,1)}, bf16[4,144,128]{2,1,0:T(8,128)(2,1)S(1)}, u32[]{:S(2)}) copy-start(bf16[4,144,128]{2,1,0:T(8,128)(2,1)S(1)} %collective-permute-done.5.refs_1_) | copy-start | bytes 442372
  50.7 40.3 %collective-permute-start.12 = (bf16[384,1024]{1,0:T(8,128)(2,1)}, bf16[384,1024]{1,0:T(8,128)(2,1)S(1)}, u32[]{:S(2)}, u32[]{:S(2)}) collective-permute-start(bf16[384,1024]{1,0:T(8,128)(2,1)} %dynamic_slice.22), channel_id=1, source_target_pairs={{0,3},{1,2},{2,1},{3,0},{4,7},{5,6},{6,5},{7,4},{8,11},{9,10},{10,... | collective-permute-start | bytes 2359304 | tf_op jit(solution)/shard_map/ppermute | solution.py:337
  55.3 12.2 %copy-start.22 = (f32[4,136,128]{2,1,0:T(8,128)S(1)}, f32[4,136,128]{2,1,0:T(8,128)}, u32[]{:S(2)}) copy-start(f32[4,136,128]{2,1,0:T(8,128)} %copy-done.20) | copy-start | bytes 835588
  55.3 12.2 %copy-start.25 = (f32[4,136,128]{2,1,0:T(8,128)S(1)}, f32[4,136,128]{2,1,0:T(8,128)}, u32[]{:S(2)}) copy-start(f32[4,136,128]{2,1,0:T(8,128)} %copy-done.23) | copy-start | bytes 835588
  58.2 47.2 %collective-permute-start.9 = (bf16[512,1024]{1,0:T(8,128)(2,1)}, bf16[512,1024]{1,0:T(8,128)(2,1)S(1)}, u32[]{:S(2)}, u32[]{:S(2)}) collective-permute-start(bf16[512,1024]{1,0:T(8,128)(2,1)} %constant_dynamic-slice_fusion.2), channel_id=1, source_target_pairs={{0,1},{1,0},{2,3},{3,2},{4,5},{5,4},{6,7},{7,6},{8,9},{9,8},{10,11... | collective-permute-start | bytes 3145736 | tf_op jit(solution)/shard_map/ppermute | solution.py:337
  58.7 31.4 %collective-permute-start.18 = (bf16[512,512]{1,0:T(8,128)(2,1)}, bf16[512,512]{1,0:T(8,128)(2,1)}, u32[]{:S(2)}, u32[]{:S(2)}) collective-permute-start(bf16[512,512]{1,0:T(8,128)(2,1)} %shard_map.79.refs_0_), channel_id=1, source_target_pairs={{0,2},{1,3},{2,0},{3,1},{4,6},{5,7},{6,4},{7,5},{8,10},{9,11},{10,... | collective-permute-start | bytes 1572872 | tf_op jit(solution)/shard_map/ppermute | solution.py:337
  69.4 16.4 %collective-permute-start.7 = (bf16[256,512]{1,0:T(8,128)(2,1)S(1)}, bf16[256,512]{1,0:T(8,128)(2,1)S(1)}, u32[]{:S(2)}, u32[]{:S(2)}) collective-permute-start(bf16[256,512]{1,0:T(8,128)(2,1)S(1)} %shard_map.76.refs_0_), channel_id=1, source_target_pairs={{0,2},{1,3},{2,0},{3,1},{4,6},{5,7},{6,4},{7,5},{8,10},{9,11},{10,... | collective-permute-start | bytes 786440 | tf_op jit(solution)/shard_map/ppermute | solution.py:337
  86.5 10.7 %collective-permute-start.17 = (bf16[512,512]{1,0:T(8,128)(2,1)}, bf16[512,512]{1,0:T(8,128)(2,1)}, u32[]{:S(2)}, u32[]{:S(2)}) collective-permute-start(bf16[512,512]{1,0:T(8,128)(2,1)} %shard_map.79.refs_0_), channel_id=1, source_target_pairs={{0,1},{1,0},{2,3},{3,2},{4,5},{5,4},{6,7},{7,6},{8,9},{9,8},{10,11... | collective-permute-start | bytes 1572872 | tf_op jit(solution)/shard_map/ppermute | solution.py:337
  88.3 3.5 %copy-start.2 = (bf16[256,512]{1,0:T(8,128)(2,1)}, bf16[256,512]{1,0:T(8,128)(2,1)S(1)}, u32[]{:S(2)}) copy-start(bf16[256,512]{1,0:T(8,128)(2,1)S(1)} %shard_map.77.refs_0_) | copy-start | bytes 786436
  88.3 8.8 %collective-permute-start.15 = (bf16[256,512]{1,0:T(8,128)(2,1)S(1)}, bf16[256,512]{1,0:T(8,128)(2,1)}, u32[]{:S(2)}, u32[]{:S(2)}) collective-permute-start(bf16[256,512]{1,0:T(8,128)(2,1)S(1)} %shard_map.77.refs_0_), channel_id=1, source_target_pairs={{0,2},{1,3},{2,0},{3,1},{4,6},{5,7},{6,4},{7,5},{8,10},{9,11},{10,... | collective-permute-start | bytes 786440 | tf_op jit(solution)/shard_map/ppermute | solution.py:337
  90.1 15.8 %collective-permute-start.19 = (bf16[512,512]{1,0:T(8,128)(2,1)}, bf16[512,512]{1,0:T(8,128)(2,1)}, u32[]{:S(2)}, u32[]{:S(2)}) collective-permute-start(bf16[512,512]{1,0:T(8,128)(2,1)} %collective-permute-done.18.refs_2_), channel_id=1, source_target_pairs={{0,1},{1,0},{2,3},{3,2},{4,5},{5,4},{6,7},{7,6},{8,9},{9,8},{10,11... | collective-permute-start | bytes 1572872 | tf_op jit(solution)/shard_map/ppermute | solution.py:337
  91.0 9.0 %collective-permute-start.11 = (bf16[128,1024]{1,0:T(8,128)(2,1)}, bf16[128,1024]{1,0:T(8,128)(2,1)S(1)}, u32[]{:S(2)}, u32[]{:S(2)}) collective-permute-start(bf16[128,1024]{1,0:T(8,128)(2,1)} %constant_dynamic-slice_fusion.1), channel_id=1, source_target_pairs={{0,4},{4,0},{8,12},{12,8},{16,20},{20,16},{24,28},{28,24},{1,5},{5... | collective-permute-start | bytes 786440 | tf_op jit(solution)/shard_map/ppermute | solution.py:337
  97.1 8.2 %collective-permute-start.13 = (bf16[128,1024]{1,0:T(8,128)(2,1)}, bf16[128,1024]{1,0:T(8,128)(2,1)S(1)}, u32[]{:S(2)}, u32[]{:S(2)}) collective-permute-start(bf16[128,1024]{1,0:T(8,128)(2,1)} %constant_dynamic-slice_fusion), channel_id=1, source_target_pairs={{0,4},{4,0},{8,12},{12,8},{16,20},{20,16},{24,28},{28,24},{1,5},{5... | collective-permute-start | bytes 786440 | tf_op jit(solution)/shard_map/ppermute | solution.py:337
  97.2 13.5 %collective-permute-start.14 = (bf16[256,512]{1,0:T(8,128)(2,1)}, bf16[256,512]{1,0:T(8,128)(2,1)S(1)}, u32[]{:S(2)}, u32[]{:S(2)}) collective-permute-start(bf16[256,512]{1,0:T(8,128)(2,1)} %copy-done.2), channel_id=1, source_target_pairs={{0,1},{1,0},{2,3},{3,2},{4,5},{5,4},{6,7},{7,6},{8,9},{9,8},{10,11... | collective-permute-start | bytes 786440 | tf_op jit(solution)/shard_map/ppermute | solution.py:337
  100.0 10.7 %collective-permute-start.16 = (bf16[256,512]{1,0:T(8,128)(2,1)}, bf16[256,512]{1,0:T(8,128)(2,1)S(1)}, u32[]{:S(2)}, u32[]{:S(2)}) collective-permute-start(bf16[256,512]{1,0:T(8,128)(2,1)} %collective-permute-done.15.refs_2_), channel_id=1, source_target_pairs={{0,1},{1,0},{2,3},{3,2},{4,5},{5,4},{6,7},{7,6},{8,9},{9,8},{10,11... | collective-permute-start | bytes 786440 | tf_op jit(solution)/shard_map/ppermute | solution.py:337
  101.3 9.4 %copy-start.3 = (bf16[256,512]{1,0:T(8,128)(2,1)S(1)}, bf16[256,512]{1,0:T(8,128)(2,1)}, u32[]{:S(2)}) copy-start(bf16[256,512]{1,0:T(8,128)(2,1)} %copy-done.2) | copy-start | bytes 786436
  105.4 8.4 %collective-permute-start.6 = (bf16[256,512]{1,0:T(8,128)(2,1)S(1)}, bf16[256,512]{1,0:T(8,128)(2,1)S(1)}, u32[]{:S(2)}, u32[]{:S(2)}) collective-permute-start(bf16[256,512]{1,0:T(8,128)(2,1)S(1)} %shard_map.76.refs_0_), channel_id=1, source_target_pairs={{0,1},{1,0},{2,3},{3,2},{4,5},{5,4},{6,7},{7,6},{8,9},{9,8},{10,11... | collective-permute-start | bytes 786440 | tf_op jit(solution)/shard_map/ppermute | solution.py:337
  105.4 8.4 %collective-permute-start.8 = (bf16[256,512]{1,0:T(8,128)(2,1)}, bf16[256,512]{1,0:T(8,128)(2,1)S(1)}, u32[]{:S(2)}, u32[]{:S(2)}) collective-permute-start(bf16[256,512]{1,0:T(8,128)(2,1)} %copy-done), channel_id=1, source_target_pairs={{0,1},{1,0},{2,3},{3,2},{4,5},{5,4},{6,7},{7,6},{8,9},{9,8},{10,11... | collective-permute-start | bytes 786440 | tf_op jit(solution)/shard_map/ppermute | solution.py:337
  (22 other events, 23.2 us)

commit v2 on v1

--- a/solution.py
+++ b/solution.py
@@ -14,6 +14,7 @@
 SEND_PAD = 16
 MASKED = -1e30
 BLOCK = 256
+TILE = 256
 
 
 SMEM = pl.BlockSpec(memory_space=pltpu.SMEM)
@@ -33,6 +34,14 @@
 
 def params(limit_mib):
     return pltpu.CompilerParams(vmem_limit_bytes=limit_mib << 20)
+
+
+def in_hbm(x):
+    return pltpu.with_memory_space_constraint(x, pltpu.HBM)
+
+
+def in_vmem(x):
+    return pltpu.with_memory_space_constraint(x, pltpu.VMEM)
 
 
 def cost(flops, moved):
@@ -66,8 +75,61 @@
     return ref[head, :width, :], ref[head, width : width + 1, :]
 
 
-def state_kernel(k_hbm, v_hbm, state_ref, send_ref, *refs):
-    *tails, k_buf, v_buf, sems = refs
+def slice_copies(slices, at_ref, w_hbm, blocks, sems):
+    odd, head_index = at_ref[0], at_ref[1]
+    copies = []
+    for number, (mask, rows) in enumerate(slices):
+        columns = blocks[number].shape[1]
+        unit = w_hbm.shape[0] // 4
+        row = pl.multiple_of(odd * unit, unit) if rows < w_hbm.shape[0] else 0
+        col = pl.multiple_of((head_index ^ mask) * columns, columns)
+        source = w_hbm.at[pl.ds(row, rows), pl.ds(col, columns)]
+        copies.append(pltpu.make_async_copy(source, blocks[number], sems.at[number]))
+    return copies
+
+
+def slice_kernel(slices, at_ref, w_hbm, *refs):
+    *blocks, sems = refs
+    copies = slice_copies(slices, at_ref, w_hbm, blocks, sems)
+    for copy in copies:
+        copy.start()
+    for copy in copies:
+        copy.wait()
+
+
+def make_slices(out_weight, slices, at, columns):
+    return pl.pallas_call(
+        functools.partial(slice_kernel, slices),
+        in_specs=[SMEM, HBM],
+        out_specs=[VMEM] * len(slices),
+        out_shape=[pltpu.VMEM((rows, columns), BF16) for _, rows in slices],
+        scratch_shapes=[pltpu.SemaphoreType.DMA((len(slices),))],
+        compiler_params=params(8),
+        cost_estimate=cost(1e9, 2 * columns * sum(rows for _, rows in slices) * 2),
+        name="slices",
+    )(at, in_hbm(out_weight))
+
+
+def part_kernel(odd_ref, most_ref, part_ref):
+    unit = part_ref.shape[0]
+    part_ref[...] = most_ref[pl.ds(pl.multiple_of(odd_ref[0] * 2 * unit, unit), unit), :]
+
+
+def make_part(most, odd, unit):
+    return pl.pallas_call(
+        part_kernel,
+        in_specs=[SMEM, VMEM],
+        out_specs=VMEM,
+        out_shape=pltpu.VMEM((unit, most.shape[1]), BF16),
+        compiler_params=params(4),
+        cost_estimate=cost(1e8, 4 * unit * most.shape[1]),
+        name="part",
+    )(odd, in_vmem(most))
+
+
+def state_kernel(slices, at_ref, k_hbm, v_hbm, w_hbm, state_ref, send_ref, *refs):
+    *outs, k_buf, v_buf, sems, w_sems = refs
+    tails, blocks = outs[:3], outs[3:]
     heads, width = state_ref.shape[0], state_ref.shape[2]
     rows = k_buf.shape[0]
     steps = rows // BLOCK
@@ -81,6 +143,9 @@
         for copy in pair:
             copy.start()
         copies.append(pair)
+    moves = slice_copies(slices, at_ref, w_hbm, blocks, w_sems)
+    for copy in moves:
+        copy.start()
     for step in range(steps):
         for copy in copies[step]:
             copy.wait()
@@ -104,32 +169,36 @@
     tails[0][...] = k_buf[rows - BAND : rows - half, :]
     tails[1][...] = k_buf[rows - half :, :]
     tails[2][...] = v_buf[rows - BAND :, :]
-
-
-def make_state(keys, values, heads, width):
+    for copy in moves:
+        copy.wait()
+
+
+def make_state(keys, values, out_weight, slices, at, heads, width, columns):
     rows, cols = keys.shape
     steps = rows // BLOCK
-    half = jax.ShapeDtypeStruct((BAND // 2, cols), BF16)
+    half = pltpu.VMEM((BAND // 2, cols), BF16)
     return pl.pallas_call(
-        state_kernel,
-        in_specs=[HBM, HBM],
-        out_specs=[VMEM] * 5,
+        functools.partial(state_kernel, slices),
+        in_specs=[SMEM, HBM, HBM, HBM],
+        out_specs=[VMEM] * (5 + len(slices)),
         out_shape=[
-            jax.ShapeDtypeStruct((heads, width + PAD, width), F32),
-            jax.ShapeDtypeStruct((heads, width + SEND_PAD, width), BF16),
+            pltpu.VMEM((heads, width + PAD, width), F32),
+            pltpu.VMEM((heads, width + SEND_PAD, width), BF16),
             half,
             half,
-            jax.ShapeDtypeStruct((BAND, cols), BF16),
+            pltpu.VMEM((BAND, cols), BF16),
+            *(pltpu.VMEM((rows_, columns), BF16) for _, rows_ in slices),
         ],
         scratch_shapes=[
             pltpu.VMEM((rows, cols), BF16),
             pltpu.VMEM((rows, cols), BF16),
             pltpu.SemaphoreType.DMA((2, steps)),
+            pltpu.SemaphoreType.DMA((len(slices),)),
         ],
         compiler_params=params(24),
         cost_estimate=cost(1e10, 4 * keys.size * 2),
         name="state",
-    )(keys, values)
+    )(at, in_hbm(keys), in_hbm(values), in_hbm(out_weight))
 
 
 def fold(distance, me, decay_ref, head, memory, group, got):
@@ -138,9 +207,9 @@
     above = base | distance
     through, before = 1.0, 1.0
     for step in range(distance):
-        through = through * decay_ref[above + step, head]
+        through = through * decay_ref[head, above + step]
         if step < distance - 1:
-            factor = decay_ref[base + step, head]
+            factor = decay_ref[head, base + step]
             before = before * jnp.where(base + step < me, factor, 1.0)
     before = jnp.where(upper, before, 0.0)
     low, high = jnp.where(upper, 1.0, through), jnp.where(upper, through, 1.0)
@@ -193,8 +262,8 @@
 
     factor = math.log2(math.e) / math.sqrt(width)
     origin = (me * SPAN_DEV + half) * rows
-    first = spans_ref[me * SPAN_DEV + half, 0] - origin
-    end = spans_ref[me * SPAN_DEV + half, 1] - origin
+    first = spans_ref[0, me * SPAN_DEV + half] - origin
+    end = spans_ref[1, me * SPAN_DEV + half] - origin
     shift = 0 if half else jnp.where(me > 0, 0, rows + 1)
     for head in range(heads):
         for copy in copies(head):
@@ -229,16 +298,21 @@
         functools.partial(local_kernel, half),
         in_specs=[SMEM, SMEM, HBM, HBM, HBM] + [VMEM] * len(halo),
         out_specs=VMEM,
-        out_shape=jax.ShapeDtypeStruct((rows, heads * width), F32),
+        out_shape=pltpu.VMEM((rows, heads * width), F32),
         scratch_shapes=[buf] * 5 + [pltpu.SemaphoreType.DMA((5, heads))],
         compiler_params=params(32),
         cost_estimate=cost(1.5e10, 6 * rows * heads * width * 2),
-    )(me, spans, queries, keys, values, *halo)
-
-
-def readout_kernel(distance, me_ref, decay_ref, gate_ref, q_ref, local_ref, *refs):
-    *inner, got_ref, group_ref, out_ref = refs
+    )(me, spans, in_hbm(queries), in_hbm(keys), in_hbm(values), *halo)
+
+
+def readout_kernel(distance, start, me_ref, decay_ref, gate_ref, q_hbm, local_ref, *refs):
+    *inner, got_ref, group_ref, out_ref, q_ref, sem = refs
     me = me_ref[0]
+    rows = out_ref.shape[0]
+    fetch = pltpu.make_async_copy(q_hbm.at[pl.ds(start, rows)], q_ref, sem)
+    fetch.start()
+    local_rows = slice(start % BAND, start % BAND + rows)
+    fetch.wait()
     heads, width = group_ref.shape[0], group_ref.shape[2]
     for head in range(heads):
         memory = load(inner[0], head) if inner else None
@@ -261,28 +335,27 @@
         numer = both[:, :width] + both[:, width:]
         denom = jnp.sum(feats * norm, axis=1, keepdims=True) + 1.0
         gate = 1.0 / (1.0 + jnp.exp(jnp.full((1, width), -gate_ref[head], F32)))
-        out = gate * (numer / denom) + (1.0 - gate) * local_ref[:, cols]
+        out = gate * (numer / denom) + (1.0 - gate) * local_ref[local_rows, cols]
         out_ref[:, cols] = out.astype(BF16)
 
 
 def readout(distance, start, rows, queries, local, memory, me, decay, gate):
     cols = queries.shape[1]
-    chunk = lambda at: pl.BlockSpec((rows, cols), lambda i: (at // rows, 0))
-    whole = [pl.BlockSpec(m.shape, lambda i: (0, 0, 0)) for m in memory]
     return pl.pallas_call(
-        functools.partial(readout_kernel, distance),
-        grid=(1,),
-        in_specs=[SMEM, SMEM, SMEM, chunk(start), chunk(start % BAND), *whole],
-        out_specs=chunk(0),
-        out_shape=jax.ShapeDtypeStruct((rows, cols), BF16),
+        functools.partial(readout_kernel, distance, start),
+        in_specs=[SMEM, SMEM, SMEM, HBM, VMEM] + [VMEM] * len(memory),
+        out_specs=VMEM,
+        out_shape=pltpu.VMEM((rows, cols), BF16),
+        scratch_shapes=[pltpu.VMEM((rows, cols), BF16), pltpu.SemaphoreType.DMA],
         compiler_params=params(16),
         cost_estimate=cost(2e9, rows * cols * 8),
-    )(me, decay, gate, queries, local, *memory)
-
-
-def project_kernel(shared, odd_ref, *refs):
-    xs, ws, out_ref = refs[: len(shared)], list(refs[len(shared) :]), refs[-1]
-    columns = out_ref.shape[1]
+    )(me, decay, gate, in_hbm(queries), local, *memory)
+
+
+def project_kernel(shared, first_row, odd_ref, *refs):
+    *refs, out_hbm, out_ref, sems = refs
+    xs, ws = refs[: len(shared)], list(refs[len(shared) :])
+    rows, columns = out_ref.shape
     odd = odd_ref[0]
     lefts, rights = [], []
     for x_ref, is_shared in zip(xs, shared):
@@ -295,9 +368,9 @@
         else:
             lefts.append(x_ref[...])
             rights.append((ws.pop(0),))
-    tile = 256
-    for start in range(0, columns, tile):
-        at = slice(start, start + tile)
+    copies = []
+    for number, start in enumerate(range(0, columns, TILE)):
+        at = slice(start, start + TILE)
         acc = None
         for left, right in zip(lefts, rights):
             block = [w_ref[:, at] for w_ref in right]
@@ -305,27 +378,35 @@
             term = jnp.dot(left, block, preferred_element_type=F32)
             acc = term if acc is None else acc + term
         out_ref[:, at] = acc.astype(out_ref.dtype)
+        target = out_hbm.at[pl.ds(first_row, rows), pl.ds(start, TILE)]
+        copy = pltpu.make_async_copy(out_ref.at[:, pl.ds(start, TILE)], target, sems.at[number])
+        copy.start()
+        copies.append(copy)
+    for copy in copies:
+        copy.wait()
 
 
 def project(start, total_rows, xs, weights, odd, out):
     rows = xs[0].shape[0]
     flat = [w for ws in weights for w in ws]
     columns = flat[0].shape[1]
-    whole = lambda a: pl.BlockSpec(a.shape, lambda i: (0, 0))
-    operands = [odd, *xs, *flat]
-    in_specs = [SMEM] + [whole(a) for a in operands[1:]]
+    operands = [odd, *map(in_vmem, xs), *map(in_vmem, flat)]
+    in_specs = [SMEM] + [VMEM] * (len(operands) - 1)
     aliases = {}
     if out is not None:
-        in_specs.append(pl.BlockSpec(memory_space=pl.ANY))
+        in_specs.append(HBM)
         aliases = {len(operands): 0}
         operands.append(out)
     depth = sum(w.shape[0] for w in flat)
     return pl.pallas_call(
-        functools.partial(project_kernel, [len(ws) > 1 for ws in weights]),
-        grid=(1,),
+        functools.partial(project_kernel, [len(ws) > 1 for ws in weights], start),
         in_specs=in_specs,
-        out_specs=pl.BlockSpec((rows, columns), lambda i: (start // rows, 0)),
-        out_shape=jax.ShapeDtypeStruct((total_rows, columns), BF16),
+        out_specs=HBM,
+        out_shape=pltpu.HBM((total_rows, columns), BF16),
+        scratch_shapes=[
+            pltpu.VMEM((rows, columns), BF16),
+            pltpu.SemaphoreType.DMA((columns // TILE,)),
+        ],
         input_output_aliases=aliases,
         compiler_params=params(24),
         cost_estimate=cost(2 * rows * depth * columns, depth * columns * 2),
@@ -341,6 +422,7 @@
 
 
 def body(queries, keys, values, span_bounds, mem_decay, mem_gate, out_weight):
+    mem_decay, span_bounds = mem_decay.T, span_bounds.T
     seg_rows = queries.shape[0]
     heads = mem_gate.shape[0]
     width = queries.shape[1] // heads
@@ -354,23 +436,20 @@
     unit = depth // 4
     columns = out_weight.shape[1] // head_size
 
+    masks = sorted(range(1, head_size), reverse=True)
+    slices = [(mask, depth if mask == 1 else 3 * unit) for mask in masks] + [(0, depth)]
+    at = jnp.concatenate([odd, head_index.astype(jnp.int32).reshape(1)])
+    first = make_slices(out_weight, slices[:1], at, columns)
+    state, send, *more = make_state(keys, values, out_weight, slices[1:], at, heads, width, columns)
+    tails, blocks = more[:3], [*first, *more[3:]]
     weights = {}
-    last = out_weight
-    for mask in sorted(range(1, head_size), reverse=True):
-        shared = mask > 1
-        row, rows = (odd[0] * unit, 3 * unit) if shared else (0, depth)
-        source, _ = lax.optimization_barrier((out_weight, last))
-        block = lax.dynamic_slice(source, (row, (head_index ^ mask) * columns), (rows, columns))
-        last = block[:8, :128]
-        weights[mask] = (swap(block, "head", mask),)
-    for mask in weights:
+    for mask, block in zip([*masks, 0], blocks):
+        weights[mask] = (swap(block, "head", mask) if mask else block,)
         if mask > 1:
             most = weights[mask][0]
-            part = lax.dynamic_slice_in_dim(most, odd[0] * 2 * unit, unit, 0)
+            part = make_part(most, odd, unit)
             weights[mask] = (most, swap(part, "seq", 1))
-    weights[0] = (lax.dynamic_slice_in_dim(out_weight, head_index * columns, columns, 1),)
-
-    state, send, *tails = make_state(keys, values, heads, width)
+
     halo = []
     for tail in tails:
         halo.append(lax.ppermute(tail, "seq", [(i, i + 1) for i in range(seq_size - 1)]))
@@ -380,13 +459,13 @@
         got = swap(send, "seq", distance)
         if 2 * distance >= seq_size:
             break
-        shape = jax.ShapeDtypeStruct(state.shape, F32)
+        shape = pltpu.VMEM(state.shape, F32)
         operands = [me, mem_decay, *inner, got, group]
         memory, group, send = pl.pallas_call(
             functools.partial(fold_kernel, distance),
             in_specs=[SMEM, SMEM] + [VMEM] * (len(operands) - 2),
             out_specs=[VMEM] * 3,
-            out_shape=[shape, shape, jax.ShapeDtypeStruct(send.shape, BF16)],
+            out_shape=[shape, shape, pltpu.VMEM(send.shape, BF16)],
             compiler_params=params(16),
             cost_estimate=cost(1e9, 5 * state.size * 4),
         )(*operands)

time: 117 us -> 111 us (0.949)
  the two profiles are of different devices: /device:TPU:0 before, /device:TPU:27 now
where the time goes in v2:
time: 111 us; the launch traced here: 110 us
  waiting for transfers between devices  54.7 us (49%)
  Pallas kernels  32.7 us (29%)
  starting transfers between devices  22.5 us (20%)
    ppermute x17, waiting for transfers between devices, swap(): return lax.ppermute(x, axis, [(i, i ^ mask) for i in range(size)])  54.7 us
    ppermute x17, starting transfers between devices, swap(): return lax.ppermute(x, axis, [(i, i ^ mask) for i in range(size)])  18.5 us
    pallas_call x2, Pallas kernels, local_half(): pl.pallas_call(functools.partial(local_kernel, half), in_specs=[SMEM, SME...  12.6 us
    pallas_call x3, Pallas kernels, project(): pl.pallas_call(functools.partial(project_kernel, [len(ws) > 1 for ws in w...  7.34 us
    pallas_call x3, Pallas kernels, readout(): pl.pallas_call(functools.partial(readout_kernel, distance, start), in_spe...  6.29 us
    ppermute x3, starting transfers between devices, body(): lax.ppermute(tail, 'seq', [(i, i + 1) for i in range(seq_size - 1)])  4.04 us
    pallas_call x1, Pallas kernels, make_state(): pl.pallas_call(functools.partial(state_kernel, slices), in_specs=[SMEM, H...  3.48 us
  transfers between devices with their start and end apart: 20, of which 6 were waited for; matrix products, arithmetic and copies ran while one was open for 0% of the time, Pallas kernels for 24%

profile of v2, /device:TPU:27, one launch (start us, length us, event | category | flops | bytes accessed | tf_op | source)
XLA Modules:
  0.0 110.4 jit_solution(16455740766596576022)
XLA Ops:
  0.1 3.5 %state.1 = (f32[4,136,128]{2,1,0:T(8,128)S(1)}, bf16[4,144,128]{2,1,0:T(8,128)(2,1)S(1)}, bf16[256,512]{1,0:T(8,128)(2,1)S(1)}, bf16[256,512]{1,0:T(8,128)(2,1)S...) custom-call(s32[2]{0:T(128)S(1)} %pad_add_fusion.at_ref, ...), custom_call_target="tpu_custom_call" | custom-call | flops 10000000000 | bytes 4194304 | tf_op jit(solution)/shard_map/state/pallas_call | solution.py:180
  3.6 0.3 collective-permute-start.3
  3.9 4.5 %collective-permute-done.3.refs_0_ = bf16[4,144,128]{2,1,0:T(8,128)(2,1)S(1)} collective-permute-done((bf16[4,144,128]{2,1,0:T(8,128)(2,1)S(1)}, bf16[4,144,128]{2,1,0:T(8,128)(2,1)S(1)}, u32[]{:S(2)}, u32[]{:S(2)}) %collective-permute-start.3) | collective-permute-done | bytes 147488 | tf_op jit(solution)/shard_map/ppermute | solution.py:418
  8.4 0.6 shard_map.74
  9.2 1.7 %slices.1 = bf16[384,1024]{1,0:T(8,128)(2,1)S(1)} custom-call(s32[2]{0:T(128)S(1)} %pad_add_fusion.at_ref, bf16[512,4096]{1,0:T(8,128)(2,1)} %w_hbm.3), custom_call_target="tpu_custom_call" | custom-call | flops 1000000000 | bytes 1572864 | tf_op jit(solution)/shard_map/slices/pallas_call | solution.py:101
  10.9 3.0 %collective-permute-start.12 = (bf16[384,1024]{1,0:T(8,128)(2,1)S(1)}, bf16[384,1024]{1,0:T(8,128)(2,1)S(1)}, u32[]{:S(2)}, u32[]{:S(2)}) collective-permute-start(bf16[384,1024]{1,0:T(8,128)(2,1)S(1)} %slices.1), channel_id=1, source_target_pairs={{0,3},{1,2},{2,1},{3,0},{4,7},{5,6},{6,5},{7,4},{8,11},{9,10},{10,... | collective-permute-start | bytes 2359304 | tf_op jit(solution)/shard_map/ppermute | solution.py:418
  14.0 1.3 %collective-permute-start = (bf16[256,512]{1,0:T(8,128)(2,1)S(1)}, bf16[256,512]{1,0:T(8,128)(2,1)S(1)}, u32[]{:S(2)}, u32[]{:S(2)}) collective-permute-start(bf16[256,512]{1,0:T(8,128)(2,1)S(1)} %get-tuple-element.19), channel_id=1, source_target_pairs={{0,4},{4,8},{8,12},{12,16},{16,20},{20,24},{24,28},{1,5},{5,9},{9,... | collective-permute-start | bytes 786440 | tf_op jit(solution)/shard_map/ppermute | solution.py:455
  15.2 1.3 %collective-permute-start.1 = (bf16[256,512]{1,0:T(8,128)(2,1)S(1)}, bf16[256,512]{1,0:T(8,128)(2,1)S(1)}, u32[]{:S(2)}, u32[]{:S(2)}) collective-permute-start(bf16[256,512]{1,0:T(8,128)(2,1)S(1)} %get-tuple-element.20), channel_id=1, source_target_pairs={{0,4},{4,8},{8,12},{12,16},{16,20},{20,24},{24,28},{1,5},{5,9},{9,... | collective-permute-start | bytes 786440 | tf_op jit(solution)/shard_map/ppermute | solution.py:455
  16.5 1.5 %collective-permute-start.2 = (bf16[512,512]{1,0:T(8,128)(2,1)S(1)}, bf16[512,512]{1,0:T(8,128)(2,1)S(1)}, u32[]{:S(2)}, u32[]{:S(2)}) collective-permute-start(bf16[512,512]{1,0:T(8,128)(2,1)S(1)} %get-tuple-element.21), channel_id=1, source_target_pairs={{0,4},{4,8},{8,12},{12,16},{16,20},{20,24},{24,28},{1,5},{5,9},{9,... | collective-permute-start | bytes 1572872 | tf_op jit(solution)/shard_map/ppermute | solution.py:455
  18.0 0.7 shard_map.75
  18.7 5.7 %collective-permute-start.5 = (bf16[4,144,128]{2,1,0:T(8,128)(2,1)S(1)}, bf16[4,144,128]{2,1,0:T(8,128)(2,1)S(1)}, u32[]{:S(2)}, u32[]{:S(2)}) collective-permute-start(bf16[4,144,128]{2,1,0:T(8,128)(2,1)S(1)} %get-tuple-element.28), channel_id=1, source_target_pairs={{0,16},{4,20},{8,24},{12,28},{16,0},{20,4},{24,8},{28,12},{1,17},{... | collective-permute-start | bytes 442376 | tf_op jit(solution)/shard_map/ppermute | solution.py:418
  24.4 6.3 %shard_map.78.local_ref = f32[512,512]{1,0:T(8,128)S(1)} custom-call(s32[1]{0:T(128)} %bitcast.me_ref, s32[2,16]{1,0:T(2,128)S(1)} %bitcast.9, bf16[1024,512]{1,0:T(8,128)(2,1)} %q_hbm.9, bf16[1024,512]{1,0:T(8,128)(2,1)} %k_hbm.5, bf16[1024,512]{1,0:T(8,128)(2,1)} %v_hbm.5), custom_call_target="tpu_custom_call" | custom-call | flops 15000000512 | bytes 3145728 | tf_op jit(solution)/shard_map/pallas_call | solution.py:297
  30.7 16.7 %collective-permute-done.5.refs_1_ = bf16[4,144,128]{2,1,0:T(8,128)(2,1)S(1)} collective-permute-done((bf16[4,144,128]{2,1,0:T(8,128)(2,1)S(1)}, bf16[4,144,128]{2,1,0:T(8,128)(2,1)S(1)}, u32[]{:S(2)}, u32[]{:S(2)}) %collective-permute-start.5) | collective-permute-done | bytes 147488 | tf_op jit(solution)/shard_map/ppermute | solution.py:418
  47.4 0.8 collective-permute-start.10
  48.2 2.4 %shard_map.79.refs_0_ = bf16[512,512]{1,0:T(8,128)(2,1)S(1)} custom-call(s32[1]{0:T(128)} %bitcast.me_ref, f32[4,8]{1,0:T(4,128)S(1)} %bitcast.6, f32[4]{0:T(128)S(1)} %copy-done.2, bf16[1024,512]{1,0:T(8,128)(2,1)} %q_hbm.9, f32[512,512]{1,0:T(8,128)S(1)} %shard_map.78.local_ref, f32[4,136,128]{2,1,0:T(8,128)S(1)} %get-tuple-element.27.refs_0_, ...), custom_call_target="tpu_custom_call" | custom-call | flops 2000000000 | bytes 2097152 | tf_op jit(solution)/shard_map/pallas_call | solution.py:344
  50.6 1.1 %collective-permute-start.9 = (bf16[512,1024]{1,0:T(8,128)(2,1)S(1)}, bf16[512,1024]{1,0:T(8,128)(2,1)S(1)}, u32[]{:S(2)}, u32[]{:S(2)}) collective-permute-start(bf16[512,1024]{1,0:T(8,128)(2,1)S(1)} %get-tuple-element.31), channel_id=1, source_target_pairs={{0,1},{1,0},{2,3},{3,2},{4,5},{5,4},{6,7},{7,6},{8,9},{9,8},{10,11... | collective-permute-start | bytes 3145736 | tf_op jit(solution)/shard_map/ppermute | solution.py:418
  51.7 6.3 %shard_map.73.local_ref = f32[512,512]{1,0:T(8,128)S(1)} custom-call(s32[1]{0:T(128)} %bitcast.me_ref, s32[2,16]{1,0:T(2,128)S(1)} %bitcast.10, bf16[1024,512]{1,0:T(8,128)(2,1)} %q_hbm.9, bf16[1024,512]{1,0:T(8,128)(2,1)} %k_hbm.5, bf16[1024,512]{1,0:T(8,128)(2,1)} %v_hbm.5, bf16[256,512]{1,0:T(8,128)(2,1)S(1)} %collective-permute-done.refs_0_, ...), custom_call_target="tpu_custom_call" | custom-call | flops 15000000512 | bytes 3145728 | tf_op jit(solution)/shard_map/pallas_call | solution.py:297
  58.0 2.0 %shard_map.76.refs_0_ = bf16[256,512]{1,0:T(8,128)(2,1)S(1)} custom-call(s32[1]{0:T(128)} %bitcast.me_ref, f32[4,8]{1,0:T(4,128)S(1)} %bitcast.7, f32[4]{0:T(128)S(1)} %copy-done.2, bf16[1024,512]{1,0:T(8,128)(2,1)} %q_hbm.9, f32[512,512]{1,0:T(8,128)S(1)} %shard_map.73.local_ref, f32[4,136,128]{2,1,0:T(8,128)S(1)} %get-tuple-element.27.refs_0_, ...), custom_call_target="tpu_custom_call" | custom-call | flops 2000000000 | bytes 1048576 | tf_op jit(solution)/shard_map/pallas_call | solution.py:344
  60.0 1.5 %collective-permute-start.7 = (bf16[256,512]{1,0:T(8,128)(2,1)S(1)}, bf16[256,512]{1,0:T(8,128)(2,1)S(1)}, u32[]{:S(2)}, u32[]{:S(2)}) collective-permute-start(bf16[256,512]{1,0:T(8,128)(2,1)S(1)} %shard_map.76.refs_0_), channel_id=1, source_target_pairs={{0,2},{1,3},{2,0},{3,1},{4,6},{5,7},{6,4},{7,5},{8,10},{9,11},{10,... | collective-permute-start | bytes 786440 | tf_op jit(solution)/shard_map/ppermute | solution.py:418
  61.5 21.8 %collective-permute-done.7.refs_2_ = bf16[256,512]{1,0:T(8,128)(2,1)S(1)} collective-permute-done((bf16[256,512]{1,0:T(8,128)(2,1)S(1)}, bf16[256,512]{1,0:T(8,128)(2,1)S(1)}, u32[]{:S(2)}, u32[]{:S(2)}) %collective-permute-start.7) | collective-permute-done | bytes 262176 | tf_op jit(solution)/shard_map/ppermute | solution.py:418
  83.3 0.9 collective-permute-start.17
  84.2 2.0 %shard_map.77.refs_0_ = bf16[256,512]{1,0:T(8,128)(2,1)S(1)} custom-call(s32[1]{0:T(128)} %bitcast.me_ref, f32[4,8]{1,0:T(4,128)S(1)} %bitcast.8, f32[4]{0:T(128)S(1)} %copy-done.2, bf16[1024,512]{1,0:T(8,128)(2,1)} %q_hbm.9, f32[512,512]{1,0:T(8,128)S(1)} %shard_map.73.local_ref, f32[4,136,128]{2,1,0:T(8,128)S(1)} %get-tuple-element.27.refs_0_, ...), custom_call_target="tpu_custom_call" | custom-call | flops 2000000000 | bytes 1048576 | tf_op jit(solution)/shard_map/pallas_call | solution.py:344
  86.2 0.9 collective-permute-start.15
  87.0 0.3 collective-permute-start.19
  87.5 6.6 %collective-permute-done.15.refs_2_ = bf16[256,512]{1,0:T(8,128)(2,1)S(1)} collective-permute-done((bf16[256,512]{1,0:T(8,128)(2,1)S(1)}, bf16[256,512]{1,0:T(8,128)(2,1)S(1)}, u32[]{:S(2)}, u32[]{:S(2)}) %collective-permute-start.15) | collective-permute-done | bytes 262176 | tf_op jit(solution)/shard_map/ppermute | solution.py:418
  94.1 0.9 collective-permute-start.14
  95.0 1.1 collective-permute-start.16
  96.1 5.0 %collective-permute-done.11.refs_7_ = bf16[128,1024]{1,0:T(8,128)(2,1)S(1)} collective-permute-done((bf16[128,1024]{1,0:T(8,128)(2,1)S(1)}, bf16[128,1024]{1,0:T(8,128)(2,1)S(1)}, u32[]{:S(2)}, u32[]{:S(2)}) %collective-permute-start.11) | collective-permute-done | bytes 262176 | tf_op jit(solution)/shard_map/ppermute | solution.py:418
  101.1 1.7 %collective-permute-start.6 = (bf16[256,512]{1,0:T(8,128)(2,1)S(1)}, bf16[256,512]{1,0:T(8,128)(2,1)S(1)}, u32[]{:S(2)}, u32[]{:S(2)}) collective-permute-start(bf16[256,512]{1,0:T(8,128)(2,1)S(1)} %shard_map.76.refs_0_), channel_id=1, source_target_pairs={{0,1},{1,0},{2,3},{3,2},{4,5},{5,4},{6,7},{7,6},{8,9},{9,8},{10,11... | collective-permute-start | bytes 786440 | tf_op jit(solution)/shard_map/ppermute | solution.py:418
  102.8 3.2 %shard_map.80.refs_10_ = bf16[1024,1024]{1,0:T(8,128)(2,1)} custom-call(s32[1]{0:T(128)S(6)} %and.5.odd_ref, bf16[512,512]{1,0:T(8,128)(2,1)S(1)} %shard_map.79.refs_0_, bf16[512,512]{1,0:T(8,128)(2,1)S(1)} %collective-permute-done.17.refs_1_, bf16[512,512]{1,0:T(8,128)(2,1)S(1)} %collective-permute-done.18.refs_2_, ...), custom_call_target="tpu_custom_call" | custom-call | flops 2147483648 | bytes 4194304 | tf_op jit(solution)/shard_map/pallas_call | solution.py:401
  106.1 2.1 %shard_map.81.refs_10_ = bf16[1024,1024]{1,0:T(8,128)(2,1)} custom-call(s32[1]{0:T(128)S(6)} %and.5.odd_ref, bf16[256,512]{1,0:T(8,128)(2,1)S(1)} %shard_map.77.refs_0_, bf16[256,512]{1,0:T(8,128)(2,1)S(1)} %collective-permute-done.14.refs_1_, bf16[256,512]{1,0:T(8,128)(2,1)S(1)} %collective-permute-done.15.refs_2_, ...), custom_call_target="tpu_custom_call", output_to_operand_aliasing={{}: (11, {})} | custom-call | flops 1073741824 | bytes 4194304 | tf_op jit(solution)/shard_map/pallas_call | solution.py:401
  108.2 2.1 %shard_map.82 = bf16[1024,1024]{1,0:T(8,128)(2,1)} custom-call(s32[1]{0:T(128)S(6)} %and.5.odd_ref, bf16[256,512]{1,0:T(8,128)(2,1)S(1)} %shard_map.76.refs_0_, bf16[256,512]{1,0:T(8,128)(2,1)S(1)} %collective-permute-done.6.refs_1_, bf16[256,512]{1,0:T(8,128)(2,1)S(1)} %collective-permute-done.7.refs_2_, ...), custom_call_target="tpu_custom_call", output_to_operand_aliasing={{}: (11, {})} | custom-call | flops 1073741824 | bytes 4194304 | tf_op jit(solution)/shard_map/pallas_call | solution.py:401
  (29 shorter events, 0.5 us)
Async XLA Ops:
  0.1 8.3 %copy-start = (f32[8,4]{0,1:T(4,128)S(1)}, f32[8,4]{0,1:T(4,128)}, u32[]{:S(2)}) copy-start(f32[8,4]{0,1:T(4,128)} %param.11) | copy-start | bytes 388
  3.6 4.8 %collective-permute-start.3 = (bf16[4,144,128]{2,1,0:T(8,128)(2,1)S(1)}, bf16[4,144,128]{2,1,0:T(8,128)(2,1)S(1)}, u32[]{:S(2)}, u32[]{:S(2)}) collective-permute-start(bf16[4,144,128]{2,1,0:T(8,128)(2,1)S(1)} %get-tuple-element.22), channel_id=1, source_target_pairs={{0,4},{4,0},{8,12},{12,8},{16,20},{20,16},{24,28},{28,24},{1,5},{5... | collective-permute-start | bytes 442376 | tf_op jit(solution)/shard_map/ppermute | solution.py:418
  9.0 9.0 %collective-permute-start.4 = (bf16[4,144,128]{2,1,0:T(8,128)(2,1)S(1)}, bf16[4,144,128]{2,1,0:T(8,128)(2,1)S(1)}, u32[]{:S(2)}, u32[]{:S(2)}) collective-permute-start(bf16[4,144,128]{2,1,0:T(8,128)(2,1)S(1)} %get-tuple-element.25), channel_id=1, source_target_pairs={{0,8},{4,12},{8,0},{12,4},{16,24},{20,28},{24,16},{28,20},{1,9},{5... | collective-permute-start | bytes 442376 | tf_op jit(solution)/shard_map/ppermute | solution.py:418
  10.9 13.5 %copy-start.1 = (s32[16,2]{0,1:T(2,128)S(1)}, s32[16,2]{0,1:T(2,128)}, u32[]{:S(2)}) copy-start(s32[16,2]{0,1:T(2,128)} %param.10) | copy-start | bytes 388
  10.9 75.2 %collective-permute-start.12 = (bf16[384,1024]{1,0:T(8,128)(2,1)S(1)}, bf16[384,1024]{1,0:T(8,128)(2,1)S(1)}, u32[]{:S(2)}, u32[]{:S(2)}) collective-permute-start(bf16[384,1024]{1,0:T(8,128)(2,1)S(1)} %slices.1), channel_id=1, source_target_pairs={{0,3},{1,2},{2,1},{3,0},{4,7},{5,6},{6,5},{7,4},{8,11},{9,10},{10,... | collective-permute-start | bytes 2359304 | tf_op jit(solution)/shard_map/ppermute | solution.py:418
  14.0 36.6 %collective-permute-start = (bf16[256,512]{1,0:T(8,128)(2,1)S(1)}, bf16[256,512]{1,0:T(8,128)(2,1)S(1)}, u32[]{:S(2)}, u32[]{:S(2)}) collective-permute-start(bf16[256,512]{1,0:T(8,128)(2,1)S(1)} %get-tuple-element.19), channel_id=1, source_target_pairs={{0,4},{4,8},{8,12},{12,16},{16,20},{20,24},{24,28},{1,5},{5,9},{9,... | collective-permute-start | bytes 786440 | tf_op jit(solution)/shard_map/ppermute | solution.py:455
  15.2 36.4 %collective-permute-start.1 = (bf16[256,512]{1,0:T(8,128)(2,1)S(1)}, bf16[256,512]{1,0:T(8,128)(2,1)S(1)}, u32[]{:S(2)}, u32[]{:S(2)}) collective-permute-start(bf16[256,512]{1,0:T(8,128)(2,1)S(1)} %get-tuple-element.20), channel_id=1, source_target_pairs={{0,4},{4,8},{8,12},{12,16},{16,20},{20,24},{24,28},{1,5},{5,9},{9,... | collective-permute-start | bytes 786440 | tf_op jit(solution)/shard_map/ppermute | solution.py:455
  16.5 35.1 %collective-permute-start.2 = (bf16[512,512]{1,0:T(8,128)(2,1)S(1)}, bf16[512,512]{1,0:T(8,128)(2,1)S(1)}, u32[]{:S(2)}, u32[]{:S(2)}) collective-permute-start(bf16[512,512]{1,0:T(8,128)(2,1)S(1)} %get-tuple-element.21), channel_id=1, source_target_pairs={{0,4},{4,8},{8,12},{12,16},{16,20},{20,24},{24,28},{1,5},{5,9},{9,... | collective-permute-start | bytes 1572872 | tf_op jit(solution)/shard_map/ppermute | solution.py:455
  18.7 28.7 %collective-permute-start.5 = (bf16[4,144,128]{2,1,0:T(8,128)(2,1)S(1)}, bf16[4,144,128]{2,1,0:T(8,128)(2,1)S(1)}, u32[]{:S(2)}, u32[]{:S(2)}) collective-permute-start(bf16[4,144,128]{2,1,0:T(8,128)(2,1)S(1)} %get-tuple-element.28), channel_id=1, source_target_pairs={{0,16},{4,20},{8,24},{12,28},{16,0},{20,4},{24,8},{28,12},{1,17},{... | collective-permute-start | bytes 442376 | tf_op jit(solution)/shard_map/ppermute | solution.py:418
  24.4 23.8 %copy-start.2 = (f32[4]{0:T(128)S(1)}, f32[4]{0:T(128)}, u32[]{:S(2)}) copy-start(f32[4]{0:T(128)} %gate_ref.5) | copy-start | bytes 52
  47.4 39.9 %collective-permute-start.10 = (bf16[384,1024]{1,0:T(8,128)(2,1)S(1)}, bf16[384,1024]{1,0:T(8,128)(2,1)S(1)}, u32[]{:S(2)}, u32[]{:S(2)}) collective-permute-start(bf16[384,1024]{1,0:T(8,128)(2,1)S(1)} %get-tuple-element.32), channel_id=1, source_target_pairs={{0,2},{1,3},{2,0},{3,1},{4,6},{5,7},{6,4},{7,5},{8,10},{9,11},{10,... | collective-permute-start | bytes 2359304 | tf_op jit(solution)/shard_map/ppermute | solution.py:418
  50.6 52.3 %collective-permute-start.9 = (bf16[512,1024]{1,0:T(8,128)(2,1)S(1)}, bf16[512,1024]{1,0:T(8,128)(2,1)S(1)}, u32[]{:S(2)}, u32[]{:S(2)}) collective-permute-start(bf16[512,1024]{1,0:T(8,128)(2,1)S(1)} %get-tuple-element.31), channel_id=1, source_target_pairs={{0,1},{1,0},{2,3},{3,2},{4,5},{5,4},{6,7},{7,6},{8,9},{9,8},{10,11... | collective-permute-start | bytes 3145736 | tf_op jit(solution)/shard_map/ppermute | solution.py:418
  51.7 35.3 %collective-permute-start.18 = (bf16[512,512]{1,0:T(8,128)(2,1)S(1)}, bf16[512,512]{1,0:T(8,128)(2,1)S(1)}, u32[]{:S(2)}, u32[]{:S(2)}) collective-permute-start(bf16[512,512]{1,0:T(8,128)(2,1)S(1)} %shard_map.79.refs_0_), channel_id=1, source_target_pairs={{0,2},{1,3},{2,0},{3,1},{4,6},{5,7},{6,4},{7,5},{8,10},{9,11},{10,... | collective-permute-start | bytes 1572872 | tf_op jit(solution)/shard_map/ppermute | solution.py:418
  60.0 23.3 %collective-permute-start.7 = (bf16[256,512]{1,0:T(8,128)(2,1)S(1)}, bf16[256,512]{1,0:T(8,128)(2,1)S(1)}, u32[]{:S(2)}, u32[]{:S(2)}) collective-permute-start(bf16[256,512]{1,0:T(8,128)(2,1)S(1)} %shard_map.76.refs_0_), channel_id=1, source_target_pairs={{0,2},{1,3},{2,0},{3,1},{4,6},{5,7},{6,4},{7,5},{8,10},{9,11},{10,... | collective-permute-start | bytes 786440 | tf_op jit(solution)/shard_map/ppermute | solution.py:418
  83.3 10.8 %collective-permute-start.17 = (bf16[512,512]{1,0:T(8,128)(2,1)S(1)}, bf16[512,512]{1,0:T(8,128)(2,1)S(1)}, u32[]{:S(2)}, u32[]{:S(2)}) collective-permute-start(bf16[512,512]{1,0:T(8,128)(2,1)S(1)} %shard_map.79.refs_0_), channel_id=1, source_target_pairs={{0,1},{1,0},{2,3},{3,2},{4,5},{5,4},{6,7},{7,6},{8,9},{9,8},{10,11... | collective-permute-start | bytes 1572872 | tf_op jit(solution)/shard_map/ppermute | solution.py:418
  86.2 7.9 %collective-permute-start.15 = (bf16[256,512]{1,0:T(8,128)(2,1)S(1)}, bf16[256,512]{1,0:T(8,128)(2,1)S(1)}, u32[]{:S(2)}, u32[]{:S(2)}) collective-permute-start(bf16[256,512]{1,0:T(8,128)(2,1)S(1)} %shard_map.77.refs_0_), channel_id=1, source_target_pairs={{0,2},{1,3},{2,0},{3,1},{4,6},{5,7},{6,4},{7,5},{8,10},{9,11},{10,... | collective-permute-start | bytes 786440 | tf_op jit(solution)/shard_map/ppermute | solution.py:418
  87.0 15.8 %collective-permute-start.19 = (bf16[512,512]{1,0:T(8,128)(2,1)S(1)}, bf16[512,512]{1,0:T(8,128)(2,1)S(1)}, u32[]{:S(2)}, u32[]{:S(2)}) collective-permute-start(bf16[512,512]{1,0:T(8,128)(2,1)S(1)} %collective-permute-done.18.refs_2_), channel_id=1, source_target_pairs={{0,1},{1,0},{2,3},{3,2},{4,5},{5,4},{6,7},{7,6},{8,9},{9,8},{10,11... | collective-permute-start | bytes 1572872 | tf_op jit(solution)/shard_map/ppermute | solution.py:418
  87.3 7.7 %collective-permute-start.13 = (bf16[128,1024]{1,0:T(8,128)(2,1)S(1)}, bf16[128,1024]{1,0:T(8,128)(2,1)S(1)}, u32[]{:S(2)}, u32[]{:S(2)}) collective-permute-start(bf16[128,1024]{1,0:T(8,128)(2,1)S(1)} %part.3), channel_id=1, source_target_pairs={{0,4},{4,0},{8,12},{12,8},{16,20},{20,16},{24,28},{28,24},{1,5},{5... | collective-permute-start | bytes 786440 | tf_op jit(solution)/shard_map/ppermute | solution.py:418
  94.1 7.0 %collective-permute-start.11 = (bf16[128,1024]{1,0:T(8,128)(2,1)S(1)}, bf16[128,1024]{1,0:T(8,128)(2,1)S(1)}, u32[]{:S(2)}, u32[]{:S(2)}) collective-permute-start(bf16[128,1024]{1,0:T(8,128)(2,1)S(1)} %part.2), channel_id=1, source_target_pairs={{0,4},{4,0},{8,12},{12,8},{16,20},{20,16},{24,28},{28,24},{1,5},{5... | collective-permute-start | bytes 786440 | tf_op jit(solution)/shard_map/ppermute | solution.py:418
  94.1 12.0 %collective-permute-start.14 = (bf16[256,512]{1,0:T(8,128)(2,1)S(1)}, bf16[256,512]{1,0:T(8,128)(2,1)S(1)}, u32[]{:S(2)}, u32[]{:S(2)}) collective-permute-start(bf16[256,512]{1,0:T(8,128)(2,1)S(1)} %shard_map.77.refs_0_), channel_id=1, source_target_pairs={{0,1},{1,0},{2,3},{3,2},{4,5},{5,4},{6,7},{7,6},{8,9},{9,8},{10,11... | collective-permute-start | bytes 786440 | tf_op jit(solution)/shard_map/ppermute | solution.py:418
  95.0 11.0 %collective-permute-start.16 = (bf16[256,512]{1,0:T(8,128)(2,1)S(1)}, bf16[256,512]{1,0:T(8,128)(2,1)S(1)}, u32[]{:S(2)}, u32[]{:S(2)}) collective-permute-start(bf16[256,512]{1,0:T(8,128)(2,1)S(1)} %collective-permute-done.15.refs_2_), channel_id=1, source_target_pairs={{0,1},{1,0},{2,3},{3,2},{4,5},{5,4},{6,7},{7,6},{8,9},{9,8},{10,11... | collective-permute-start | bytes 786440 | tf_op jit(solution)/shard_map/ppermute | solution.py:418
  101.1 7.1 %collective-permute-start.6 = (bf16[256,512]{1,0:T(8,128)(2,1)S(1)}, bf16[256,512]{1,0:T(8,128)(2,1)S(1)}, u32[]{:S(2)}, u32[]{:S(2)}) collective-permute-start(bf16[256,512]{1,0:T(8,128)(2,1)S(1)} %shard_map.76.refs_0_), channel_id=1, source_target_pairs={{0,1},{1,0},{2,3},{3,2},{4,5},{5,4},{6,7},{7,6},{8,9},{9,8},{10,11... | collective-permute-start | bytes 786440 | tf_op jit(solution)/shard_map/ppermute | solution.py:418
  102.8 5.3 %collective-permute-start.8 = (bf16[256,512]{1,0:T(8,128)(2,1)S(1)}, bf16[256,512]{1,0:T(8,128)(2,1)S(1)}, u32[]{:S(2)}, u32[]{:S(2)}) collective-permute-start(bf16[256,512]{1,0:T(8,128)(2,1)S(1)} %collective-permute-done.7.refs_2_), channel_id=1, source_target_pairs={{0,1},{1,0},{2,3},{3,2},{4,5},{5,4},{6,7},{7,6},{8,9},{9,8},{10,11... | collective-permute-start | bytes 786440 | tf_op jit(solution)/shard_map/ppermute | solution.py:418

commit v3 on v2

--- a/solution.py
+++ b/solution.py
@@ -15,6 +15,7 @@
 MASKED = -1e30
 BLOCK = 256
 TILE = 256
+HALO = (128, 256)
 
 
 SMEM = pl.BlockSpec(memory_space=pltpu.SMEM)
@@ -127,9 +128,9 @@
     )(odd, in_vmem(most))
 
 
-def state_kernel(slices, at_ref, k_hbm, v_hbm, w_hbm, state_ref, send_ref, *refs):
-    *outs, k_buf, v_buf, sems, w_sems = refs
-    tails, blocks = outs[:3], outs[3:]
+def state_kernel(slices, at_ref, q_hbm, k_hbm, v_hbm, w_hbm, state_ref, send_ref, *refs):
+    *outs, sems, w_sems = refs
+    (q_buf, k_buf, v_buf), tails, blocks = outs[:3], outs[3:6], outs[6:]
     heads, width = state_ref.shape[0], state_ref.shape[2]
     rows = k_buf.shape[0]
     steps = rows // BLOCK
@@ -144,6 +145,7 @@
             copy.start()
         copies.append(pair)
     moves = slice_copies(slices, at_ref, w_hbm, blocks, w_sems)
+    moves.append(pltpu.make_async_copy(q_hbm, q_buf, w_sems.at[len(slices)]))
     for copy in moves:
         copy.start()
     for step in range(steps):
@@ -165,40 +167,38 @@
             store(state_ref, head, memory, total)
             if step == steps - 1:
                 pack(send_ref, head, memory, total)
-    half = BAND // 2
-    tails[0][...] = k_buf[rows - BAND : rows - half, :]
-    tails[1][...] = k_buf[rows - half :, :]
-    tails[2][...] = v_buf[rows - BAND :, :]
+    near, far = rows - BAND + HALO[0], rows - BAND + HALO[0] + HALO[1]
+    tails[0][...] = k_buf[rows - BAND : near, :]
+    tails[1][...] = k_buf[near:far, :]
+    tails[2][: rows - far, :] = k_buf[far:, :]
+    tails[2][rows - far :, :] = v_buf[rows - BAND :, :]
     for copy in moves:
         copy.wait()
 
 
-def make_state(keys, values, out_weight, slices, at, heads, width, columns):
+def make_state(queries, keys, values, out_weight, slices, at, heads, width, columns):
     rows, cols = keys.shape
     steps = rows // BLOCK
-    half = pltpu.VMEM((BAND // 2, cols), BF16)
+    tails = (*HALO, 2 * BAND - sum(HALO))
     return pl.pallas_call(
         functools.partial(state_kernel, slices),
-        in_specs=[SMEM, HBM, HBM, HBM],
-        out_specs=[VMEM] * (5 + len(slices)),
+        in_specs=[SMEM, HBM, HBM, HBM, HBM],
+        out_specs=[VMEM] * (8 + len(slices)),
         out_shape=[
             pltpu.VMEM((heads, width + PAD, width), F32),
             pltpu.VMEM((heads, width + SEND_PAD, width), BF16),
-            half,
-            half,
-            pltpu.VMEM((BAND, cols), BF16),
+            *[pltpu.VMEM((rows, cols), BF16)] * 3,
+            *(pltpu.VMEM((tail, cols), BF16) for tail in tails),
             *(pltpu.VMEM((rows_, columns), BF16) for _, rows_ in slices),
         ],
         scratch_shapes=[
-            pltpu.VMEM((rows, cols), BF16),
-            pltpu.VMEM((rows, cols), BF16),
             pltpu.SemaphoreType.DMA((2, steps)),
-            pltpu.SemaphoreType.DMA((len(slices),)),
+            pltpu.SemaphoreType.DMA((len(slices) + 1,)),
         ],
         compiler_params=params(24),
         cost_estimate=cost(1e10, 4 * keys.size * 2),
         name="state",
-    )(at, in_hbm(keys), in_hbm(values), in_hbm(out_weight))
+    )(at, in_hbm(queries), in_hbm(keys), in_hbm(values), in_hbm(out_weight))
 
 
 def fold(distance, me, decay_ref, head, memory, group, got):
@@ -234,122 +234,139 @@
         pack(send_ref, head, *both)
 
 
-def local_kernel(half, me_ref, spans_ref, q_hbm, k_hbm, v_hbm, *refs):
-    *halo, out_ref, q_buf, k_buf, v_buf, kp_buf, vp_buf, sems = refs
+def local_block(half, start, me_ref, spans_ref, query, keys_before, values_before, keys, values):
     me = me_ref[0]
-    heads, rows, width = q_buf.shape
-    here, before = pl.ds(half * rows, rows), pl.ds((half - 1) * rows, rows)
-
-    def copies(head):
-        cols = pl.ds(head * width, width)
-        table = [(q_hbm, here, q_buf), (k_hbm, here, k_buf), (v_hbm, here, v_buf)]
-        if half:
-            table += [(k_hbm, before, kp_buf), (v_hbm, before, vp_buf)]
-        return [
-            pltpu.make_async_copy(src.at[at, cols], buf.at[head], sems.at[which, head])
-            for which, (src, at, buf) in enumerate(table)
-        ]
-
-    for head in range(heads):
-        for copy in copies(head):
-            copy.start()
-    if not half:
-        for head in range(heads):
-            cols = slice(head * width, (head + 1) * width)
-            kp_buf[head, : rows // 2, :] = halo[0][:, cols]
-            kp_buf[head, rows // 2 :, :] = halo[1][:, cols]
-            vp_buf[head] = halo[2][:, cols]
-
+    rows, width = keys.shape
     factor = math.log2(math.e) / math.sqrt(width)
     origin = (me * SPAN_DEV + half) * rows
     first = spans_ref[0, me * SPAN_DEV + half] - origin
     end = spans_ref[1, me * SPAN_DEV + half] - origin
     shift = 0 if half else jnp.where(me > 0, 0, rows + 1)
+    dims = (((1,), (1,)), ((), ()))
+    prev = lax.dot_general(query, keys_before, dims, preferred_element_type=F32)
+    own = lax.dot_general(query, keys, dims, preferred_element_type=F32)
+    row = start + lax.broadcasted_iota(jnp.int32, (query.shape[0], 1), 0)
+    limit = jnp.where((row >= first) & (row < end), end - 1, row)
+    col = lax.broadcasted_iota(jnp.int32, prev.shape, 1) + start
+    prev = jnp.where(col > row + shift, prev, MASKED)
+    col = lax.broadcasted_iota(jnp.int32, own.shape, 1)
+    own = jnp.where(col <= limit, own, MASKED)
+    top = jnp.maximum(jnp.max(prev, axis=1, keepdims=True), jnp.max(own, axis=1, keepdims=True))
+    prev = jnp.exp2((prev - top) * factor)
+    own = jnp.exp2((own - top) * factor)
+    total = jnp.sum(prev, axis=1, keepdims=True) + jnp.sum(own, axis=1, keepdims=True)
+    mixed = jnp.dot(prev.astype(BF16), values_before, preferred_element_type=F32)
+    mixed += jnp.dot(own.astype(BF16), values, preferred_element_type=F32)
+    return mixed / total
+
+
+def read_block(query, memory, norm, gate, local):
+    width = query.shape[1]
+    feats = phi(query.astype(F32))
+    left = jnp.concatenate(split(feats), axis=1)
+    both = jnp.dot(left, memory, preferred_element_type=F32)
+    numer = both[:, :width] + both[:, width:]
+    denom = jnp.sum(feats * norm, axis=1, keepdims=True) + 1.0
+    gate = 1.0 / (1.0 + jnp.exp(jnp.full((1, width), -gate, F32)))
+    return (gate * (numer / denom) + (1.0 - gate) * local).astype(BF16)
+
+
+def local_kernel(width, me_ref, spans_ref, q_ref, k_ref, v_ref, out_ref):
+    rows, cols = out_ref.shape
+    for head in range(cols // width):
+        at = slice(head * width, (head + 1) * width)
+        for start in range(0, rows, BLOCK):
+            out_ref[start : start + BLOCK, at] = local_block(
+                1, start, me_ref, spans_ref, q_ref[rows + start : rows + start + BLOCK, at],
+                k_ref[start:rows, at], v_ref[start:rows, at], k_ref[rows:, at], v_ref[rows:, at],
+            )
+
+
+def make_local(queries, keys, values, spans, me, width):
+    rows, cols = queries.shape[0] // SPAN_DEV, queries.shape[1]
+    return pl.pallas_call(
+        functools.partial(local_kernel, width),
+        in_specs=[SMEM, SMEM, VMEM, VMEM, VMEM],
+        out_specs=VMEM,
+        out_shape=pltpu.VMEM((rows, cols), F32),
+        compiler_params=params(24),
+        cost_estimate=cost(1.5e10, 6 * rows * cols * 2),
+        name="local",
+    )(me, spans, *map(in_vmem, (queries, keys, values)))
+
+
+def readout_kernel(distance, me_ref, decay_ref, gate_ref, q_ref, local_ref, *refs):
+    *inner, got_ref, group_ref, out_ref, memory_ref, norm_ref = refs
+    me = me_ref[0]
+    heads, width = group_ref.shape[0], group_ref.shape[2]
+    rows = out_ref.shape[0]
     for head in range(heads):
-        for copy in copies(head):
-            copy.wait()
-        for start in range(0, rows, BLOCK):
-            query = q_buf[head, start : start + BLOCK, :]
-            dims = (((1,), (1,)), ((), ()))
-            prev = lax.dot_general(query, kp_buf[head, start:, :], dims, preferred_element_type=F32)
-            own = lax.dot_general(query, k_buf[head], dims, preferred_element_type=F32)
-            row = start + lax.broadcasted_iota(jnp.int32, (BLOCK, 1), 0)
-            limit = jnp.where((row >= first) & (row < end), end - 1, row)
-            col = lax.broadcasted_iota(jnp.int32, prev.shape, 1) + start
-            prev = jnp.where(col > row + shift, prev, MASKED)
-            col = lax.broadcasted_iota(jnp.int32, own.shape, 1)
-            own = jnp.where(col <= limit, own, MASKED)
-            top = jnp.maximum(
-                jnp.max(prev, axis=1, keepdims=True), jnp.max(own, axis=1, keepdims=True)
-            )
-            prev = jnp.exp2((prev - top) * factor)
-            own = jnp.exp2((own - top) * factor)
-            total = jnp.sum(prev, axis=1, keepdims=True) + jnp.sum(own, axis=1, keepdims=True)
-            mixed = jnp.dot(prev.astype(BF16), vp_buf[head, start:, :], preferred_element_type=F32)
-            mixed += jnp.dot(own.astype(BF16), v_buf[head], preferred_element_type=F32)
-            out_ref[start : start + BLOCK, head * width : (head + 1) * width] = mixed / total
-
-
-def local_half(half, queries, keys, values, halo, spans, me, heads, width):
-    rows = queries.shape[0] // SPAN_DEV
-    buf = pltpu.VMEM((heads, rows, width), BF16)
-    halo = list(halo)
-    return pl.pallas_call(
-        functools.partial(local_kernel, half),
-        in_specs=[SMEM, SMEM, HBM, HBM, HBM] + [VMEM] * len(halo),
-        out_specs=VMEM,
-        out_shape=pltpu.VMEM((rows, heads * width), F32),
-        scratch_shapes=[buf] * 5 + [pltpu.SemaphoreType.DMA((5, heads))],
-        compiler_params=params(32),
-        cost_estimate=cost(1.5e10, 6 * rows * heads * width * 2),
-    )(me, spans, in_hbm(queries), in_hbm(keys), in_hbm(values), *halo)
-
-
-def readout_kernel(distance, start, me_ref, decay_ref, gate_ref, q_hbm, local_ref, *refs):
-    *inner, got_ref, group_ref, out_ref, q_ref, sem = refs
-    me = me_ref[0]
-    rows = out_ref.shape[0]
-    fetch = pltpu.make_async_copy(q_hbm.at[pl.ds(start, rows)], q_ref, sem)
-    fetch.start()
-    local_rows = slice(start % BAND, start % BAND + rows)
-    fetch.wait()
-    heads, width = group_ref.shape[0], group_ref.shape[2]
-    for head in range(heads):
-        memory = load(inner[0], head) if inner else None
+        had = load(inner[0], head) if inner else None
         (memory, norm), unused = fold(
-            distance, me, decay_ref, head, memory, load(group_ref, head), unpack(got_ref, head)
-        )
-        cols = slice(head * width, (head + 1) * width)
-        feats = phi(q_ref[:, cols].astype(F32))
-        q_high, q_low = split(feats)
-        m_high, m_low = split(memory)
-        left = jnp.concatenate([q_high, q_low], axis=1)
-        right = jnp.concatenate(
-            [
-                jnp.concatenate([m_high, m_low], axis=1),
-                jnp.concatenate([m_high, jnp.zeros_like(m_low)], axis=1),
-            ],
-            axis=0,
-        )
-        both = jnp.dot(left, right, preferred_element_type=F32)
-        numer = both[:, :width] + both[:, width:]
-        denom = jnp.sum(feats * norm, axis=1, keepdims=True) + 1.0
-        gate = 1.0 / (1.0 + jnp.exp(jnp.full((1, width), -gate_ref[head], F32)))
-        out = gate * (numer / denom) + (1.0 - gate) * local_ref[local_rows, cols]
-        out_ref[:, cols] = out.astype(BF16)
-
-
-def readout(distance, start, rows, queries, local, memory, me, decay, gate):
-    cols = queries.shape[1]
-    return pl.pallas_call(
-        functools.partial(readout_kernel, distance, start),
-        in_specs=[SMEM, SMEM, SMEM, HBM, VMEM] + [VMEM] * len(memory),
-        out_specs=VMEM,
-        out_shape=pltpu.VMEM((rows, cols), BF16),
-        scratch_shapes=[pltpu.VMEM((rows, cols), BF16), pltpu.SemaphoreType.DMA],
+            distance, me, decay_ref, head, had, load(group_ref, head), unpack(got_ref, head)
+        )
+        high, low = split(memory)
+        memory_ref[head, :width, :width] = high
+        memory_ref[head, :width, width:] = low
+        memory_ref[head, width:, :width] = high
+        memory_ref[head, width:, width:] = jnp.zeros_like(low)
+        norm_ref[head] = jnp.broadcast_to(norm, (PAD, width))
+        at = slice(head * width, (head + 1) * width)
+        out_ref[:, at] = read_block(
+            q_ref[-rows:, at], memory_ref[head], norm, gate_ref[head], local_ref[:, at]
+        )
+
+
+def make_readout(distance, queries, local, memory, me, decay, gate):
+    rows, cols = local.shape
+    heads, _, width = memory[-1].shape
+    return pl.pallas_call(
+        functools.partial(readout_kernel, distance),
+        in_specs=[SMEM, SMEM, SMEM] + [VMEM] * (2 + len(memory)),
+        out_specs=[VMEM] * 3,
+        out_shape=[
+            pltpu.VMEM((rows, cols), BF16),
+            pltpu.VMEM((heads, 2 * width, 2 * width), BF16),
+            pltpu.VMEM((heads, PAD, width), F32),
+        ],
         compiler_params=params(16),
         cost_estimate=cost(2e9, rows * cols * 8),
-    )(me, decay, gate, in_hbm(queries), local, *memory)
+        name="readout",
+    )(me, decay, gate, *map(in_vmem, (queries, local)), *memory)
+
+
+def attend_kernel(start, me_ref, spans_ref, gate_ref, q_ref, k_ref, v_ref, *refs):
+    *halo, memory_ref, norm_ref, out_ref, before_ref = refs
+    heads, width = norm_ref.shape[0], norm_ref.shape[2]
+    rows = before_ref.shape[0]
+    near, far = HALO[0], sum(HALO)
+    before_ref[:near, :] = halo[0][...]
+    before_ref[near:far, :] = halo[1][...]
+    before_ref[far:, :] = halo[2][: rows - far, :]
+    for head in range(heads):
+        at = slice(head * width, (head + 1) * width)
+        query = q_ref[start : start + BLOCK, at]
+        local = local_block(
+            0, start, me_ref, spans_ref, query, before_ref[start:, at],
+            halo[2][rows - far + start :, at], k_ref[:rows, at], v_ref[:rows, at],
+        )
+        out_ref[:, at] = read_block(
+            query, memory_ref[head], norm_ref[head, :1, :], gate_ref[head], local
+        )
+
+
+def make_attend(start, queries, keys, values, halo, memory, norm, spans, me, gate):
+    rows, cols = queries.shape[0] // SPAN_DEV, queries.shape[1]
+    operands = [*map(in_vmem, (queries, keys, values, *halo)), memory, norm]
+    return pl.pallas_call(
+        functools.partial(attend_kernel, start),
+        in_specs=[SMEM] * 3 + [VMEM] * len(operands),
+        out_specs=VMEM,
+        out_shape=pltpu.VMEM((BLOCK, cols), BF16),
+        scratch_shapes=[pltpu.VMEM((rows, cols), BF16)],
+        compiler_params=params(24),
+        cost_estimate=cost(8e9, 6 * rows * cols * 2),
+    )(me, spans, gate, *operands)
 
 
 def project_kernel(shared, first_row, odd_ref, *refs):
@@ -418,9 +435,6 @@
     return lax.ppermute(x, axis, [(i, i ^ mask) for i in range(size)])
 
 
-CHUNKS = ((512, 512), (0, 256), (256, 256))
-
-
 def body(queries, keys, values, span_bounds, mem_decay, mem_gate, out_weight):
     mem_decay, span_bounds = mem_decay.T, span_bounds.T
     seg_rows = queries.shape[0]
@@ -440,8 +454,12 @@
     slices = [(mask, depth if mask == 1 else 3 * unit) for mask in masks] + [(0, depth)]
     at = jnp.concatenate([odd, head_index.astype(jnp.int32).reshape(1)])
     first = make_slices(out_weight, slices[:1], at, columns)
-    state, send, *more = make_state(keys, values, out_weight, slices[1:], at, heads, width, columns)
-    tails, blocks = more[:3], [*first, *more[3:]]
+    state, send, *more = make_state(
+        queries, keys, values, out_weight, slices[1:], at, heads, width,
+        columns,
+    )
+    queries, keys, values = more[:3]
+    tails, blocks = more[3:6], [*first, *more[6:]]
     weights = {}
     for mask, block in zip([*masks, 0], blocks):
         weights[mask] = (swap(block, "head", mask) if mask else block,)
@@ -472,19 +490,18 @@
         inner, distance = [memory], 2 * distance
     memory = [*inner, got, group]
 
-    locals_ = {}
-    for half in (1, 0):
-        locals_[half] = local_half(
-            half, queries, keys, values, () if half else halo,
-            span_bounds, me, heads, width,
-        )
+    local = make_local(queries, keys, values, span_bounds, me, width)
+    own, total, norm = make_readout(distance, queries, local, memory, me, mem_decay, mem_gate)
+    chunks = [(BAND, own)]
+    for start in range(0, BAND, BLOCK):
+        own = make_attend(
+            start, queries, keys,
+            values, halo, total, norm, span_bounds, me, mem_gate,
+        )
+        chunks.append((start, own))
 
     out = None
-    for start, rows in CHUNKS:
-        own = readout(
-            distance, start, rows, queries,
-            locals_[start // BAND], memory, me, mem_decay, mem_gate,
-        )
+    for start, own in chunks:
         xs = {0: own}
         mask = head_size // 2
         while mask:

time: 111 us -> 117 us (1.054)
  starting transfers between devices: 22.5 us -> 39.3 us
  Pallas kernels: 32.7 us -> 25.8 us
  waiting for transfers between devices: 54.7 us -> 51.5 us
    ppermute x17, starting transfers between devices: 18.5 us -> 35.5 us  [swap(): return lax.ppermute(x, axis, [(i, i ^ mask) for i in range(size)])]
    pallas_call x5 -> x4, Pallas kernels: 18.9 us -> 11.9 us  [the longest x2 5.96 us: make_attend(): pl.pallas_call(functools.partial(attend_kernel, start), in_specs=[SMEM] *...]
    ppermute x17, waiting for transfers between devices: 54.7 us -> 51.5 us  [swap(): return lax.ppermute(x, axis, [(i, i ^ mask) for i in range(size)])]
  transfers between devices with their start and end apart: 20 -> 20, of which waited for: 6 -> 6; matrix products, arithmetic and copies ran while one was open for 0% -> 0% of each run, Pallas kernels for 24% -> 17%
where the time goes in v3:
time: 117 us
  waiting for transfers between devices  51.5 us (44%)
  starting transfers between devices  39.3 us (34%)
  Pallas kernels  25.8 us (22%)
    ppermute x17, waiting for transfers between devices, swap(): return lax.ppermute(x, axis, [(i, i ^ mask) for i in range(size)])  51.5 us
    ppermute x17, starting transfers between devices, swap(): return lax.ppermute(x, axis, [(i, i ^ mask) for i in range(size)])  35.5 us
    pallas_call x3, Pallas kernels, project(): pl.pallas_call(functools.partial(project_kernel, [len(ws) > 1 for ws in w...  7.3 us
    pallas_call x2, Pallas kernels, make_attend(): pl.pallas_call(functools.partial(attend_kernel, start), in_specs=[SMEM] *...  5.96 us
    pallas_call x1, Pallas kernels, make_local(): pl.pallas_call(functools.partial(local_kernel, width), in_specs=[SMEM, SM...  4.59 us
    ppermute x3, starting transfers between devices, body(): lax.ppermute(tail, 'seq', [(i, i + 1) for i in range(seq_size - 1)])  3.86 us
    pallas_call x1, Pallas kernels, make_state(): pl.pallas_call(functools.partial(state_kernel, slices), in_specs=[SMEM, H...  3.54 us
  transfers between devices with their start and end apart: 20, of which 6 were waited for; matrix products, arithmetic and copies ran while one was open for 0% of the time, Pallas kernels for 17%

profile of v3, /device:TPU:27, one launch (start us, length us, event | category | flops | bytes accessed | tf_op | source)
XLA Modules:
  0.0 116.9 jit_solution(2240033213170925137)
XLA Ops:
  0.1 3.5 %state.1 = (f32[4,136,128]{2,1,0:T(8,128)S(1)}, bf16[4,144,128]{2,1,0:T(8,128)(2,1)S(1)}, bf16[1024,512]{1,0:T(8,128)(2,1)S(1)}, bf16[1024,512]{1,0:T(8,128)(2,1...) custom-call(s32[2]{0:T(128)S(1)} %pad_add_fusion.at_ref, ...), custom_call_target="tpu_custom_call" | custom-call | flops 10000000000 | bytes 4194304 | tf_op jit(solution)/shard_map/state/pallas_call | solution.py:183
  3.6 0.3 collective-permute-start.3
  3.9 4.5 %collective-permute-done.3.refs_0_ = bf16[4,144,128]{2,1,0:T(8,128)(2,1)S(1)} collective-permute-done((bf16[4,144,128]{2,1,0:T(8,128)(2,1)S(1)}, bf16[4,144,128]{2,1,0:T(8,128)(2,1)S(1)}, u32[]{:S(2)}, u32[]{:S(2)}) %collective-permute-start.3) | collective-permute-done | bytes 147488 | tf_op jit(solution)/shard_map/ppermute | solution.py:435
  8.4 0.6 shard_map.73
  9.3 1.3 %collective-permute-start = (bf16[128,512]{1,0:T(8,128)(2,1)S(1)}, bf16[128,512]{1,0:T(8,128)(2,1)S(1)}, u32[]{:S(2)}, u32[]{:S(2)}) collective-permute-start(bf16[128,512]{1,0:T(8,128)(2,1)S(1)} %get-tuple-element.28), channel_id=1, source_target_pairs={{0,4},{4,8},{8,12},{12,16},{16,20},{20,24},{24,28},{1,5},{5,9},{9,... | collective-permute-start | bytes 393224 | tf_op jit(solution)/shard_map/ppermute | solution.py:473
  10.6 1.3 %collective-permute-start.1 = (bf16[256,512]{1,0:T(8,128)(2,1)S(1)}, bf16[256,512]{1,0:T(8,128)(2,1)S(1)}, u32[]{:S(2)}, u32[]{:S(2)}) collective-permute-start(bf16[256,512]{1,0:T(8,128)(2,1)S(1)} %get-tuple-element.29), channel_id=1, source_target_pairs={{0,4},{4,8},{8,12},{12,16},{16,20},{20,24},{24,28},{1,5},{5,9},{9,... | collective-permute-start | bytes 786440 | tf_op jit(solution)/shard_map/ppermute | solution.py:473
  11.9 1.3 %collective-permute-start.2 = (bf16[640,512]{1,0:T(8,128)(2,1)S(1)}, bf16[640,512]{1,0:T(8,128)(2,1)S(1)}, u32[]{:S(2)}, u32[]{:S(2)}) collective-permute-start(bf16[640,512]{1,0:T(8,128)(2,1)S(1)} %get-tuple-element.30), channel_id=1, source_target_pairs={{0,4},{4,8},{8,12},{12,16},{16,20},{20,24},{24,28},{1,5},{5,9},{9,... | collective-permute-start | bytes 1966088 | tf_op jit(solution)/shard_map/ppermute | solution.py:473
  13.2 1.9 %collective-permute-start.9 = (bf16[512,1024]{1,0:T(8,128)(2,1)S(1)}, bf16[512,1024]{1,0:T(8,128)(2,1)S(1)}, u32[]{:S(2)}, u32[]{:S(2)}) collective-permute-start(bf16[512,1024]{1,0:T(8,128)(2,1)S(1)} %get-tuple-element.42), channel_id=1, source_target_pairs={{0,1},{1,0},{2,3},{3,2},{4,5},{5,4},{6,7},{7,6},{8,9},{9,8},{10,11... | collective-permute-start | bytes 3145736 | tf_op jit(solution)/shard_map/ppermute | solution.py:435
  15.1 0.7 shard_map.74
  15.7 6.6 %collective-permute-start.5 = (bf16[4,144,128]{2,1,0:T(8,128)(2,1)S(1)}, bf16[4,144,128]{2,1,0:T(8,128)(2,1)S(1)}, u32[]{:S(2)}, u32[]{:S(2)}) collective-permute-start(bf16[4,144,128]{2,1,0:T(8,128)(2,1)S(1)} %get-tuple-element.37), channel_id=1, source_target_pairs={{0,16},{4,20},{8,24},{12,28},{16,0},{20,4},{24,8},{28,12},{1,17},{... | collective-permute-start | bytes 442376 | tf_op jit(solution)/shard_map/ppermute | solution.py:435
  22.3 4.6 %local.1.local_ref = f32[512,512]{1,0:T(8,128)S(1)} custom-call(s32[1]{0:T(128)} %bitcast.me_ref, s32[2,16]{1,0:T(2,128)S(1)} %bitcast.7, bf16[1024,512]{1,0:T(8,128)(2,1)S(1)} %get-tuple-element.25.q_ref, bf16[1024,512]{1,0:T(8,128)(2,1)S(1)} %get-tuple-element.26.k_ref, bf16[1024,512]{1,0:T(8,128)(2,1)S(1)} %get-tuple-element.27.v_ref), custom_call_target="tpu_custom_call" | custom-call | flops 15000000512 | bytes 3145728 | tf_op jit(solution)/shard_map/local/pallas_call | solution.py:287
  26.9 1.7 %slices.1 = bf16[384,1024]{1,0:T(8,128)(2,1)S(1)} custom-call(s32[2]{0:T(128)S(1)} %pad_add_fusion.at_ref, bf16[512,4096]{1,0:T(8,128)(2,1)} %w_hbm.3), custom_call_target="tpu_custom_call" | custom-call | flops 1000000000 | bytes 1572864 | tf_op jit(solution)/shard_map/slices/pallas_call | solution.py:102
  28.6 13.6 %collective-permute-done.5.refs_1_ = bf16[4,144,128]{2,1,0:T(8,128)(2,1)S(1)} collective-permute-done((bf16[4,144,128]{2,1,0:T(8,128)(2,1)S(1)}, bf16[4,144,128]{2,1,0:T(8,128)(2,1)S(1)}, u32[]{:S(2)}, u32[]{:S(2)}) %collective-permute-start.5) | collective-permute-done | bytes 147488 | tf_op jit(solution)/shard_map/ppermute | solution.py:435
  42.2 1.2 %collective-permute-start.10 = (bf16[384,1024]{1,0:T(8,128)(2,1)S(1)}, bf16[384,1024]{1,0:T(8,128)(2,1)S(1)}, u32[]{:S(2)}, u32[]{:S(2)}) collective-permute-start(bf16[384,1024]{1,0:T(8,128)(2,1)S(1)} %get-tuple-element.43), channel_id=1, source_target_pairs={{0,2},{1,3},{2,0},{3,1},{4,6},{5,7},{6,4},{7,5},{8,10},{9,11},{10,... | collective-permute-start | bytes 2359304 | tf_op jit(solution)/shard_map/ppermute | solution.py:435
  43.5 1.4 %readout.1 = (bf16[512,512]{1,0:T(8,128)(2,1)S(1)}, bf16[4,256,256]{2,1,0:T(8,128)(2,1)S(1)}, f32[4,8,128]{2,1,0:T(8,128)S(1)}) custom-call(s32[1]{0:T(128)} %bitcast.me_ref, f32[4,8]{1,0:T(4,128)S(1)} %bitcast.6, f32[4]{0:T(128)S(1)} %copy-done.2, bf16[1024,512]{1,0:T(8,128)(2,1)S(1)} %get-tuple-element.25.q_ref, f32[512,512]{1,0:T(8,128)S(1)} %local.1.local_ref, ...), custom_call_target="tpu_custom_call" | custom-call | flops 2000000000 | bytes 2097152 | tf_op jit(solution)/shard_map/readout/pallas_call | solution.py:323
  44.9 3.2 %collective-permute-start.12 = (bf16[384,1024]{1,0:T(8,128)(2,1)S(1)}, bf16[384,1024]{1,0:T(8,128)(2,1)S(1)}, u32[]{:S(2)}, u32[]{:S(2)}) collective-permute-start(bf16[384,1024]{1,0:T(8,128)(2,1)S(1)} %slices.1), channel_id=1, source_target_pairs={{0,3},{1,2},{2,1},{3,0},{4,7},{5,6},{6,5},{7,4},{8,11},{9,10},{10,... | collective-permute-start | bytes 2359304 | tf_op jit(solution)/shard_map/ppermute | solution.py:435
  48.0 1.3 %collective-permute-start.18 = (bf16[512,512]{1,0:T(8,128)(2,1)S(1)}, bf16[512,512]{1,0:T(8,128)(2,1)S(1)}, u32[]{:S(2)}, u32[]{:S(2)}) collective-permute-start(bf16[512,512]{1,0:T(8,128)(2,1)S(1)} %get-tuple-element.44.refs_0_), channel_id=1, source_target_pairs={{0,2},{1,3},{2,0},{3,1},{4,6},{5,7},{6,4},{7,5},{8,10},{9,11},{10,... | collective-permute-start | bytes 1572872 | tf_op jit(solution)/shard_map/ppermute | solution.py:435
  49.3 2.7 %shard_map.75.refs_0_ = bf16[256,512]{1,0:T(8,128)(2,1)S(1)} custom-call(s32[1]{0:T(128)} %bitcast.me_ref, s32[2,16]{1,0:T(2,128)S(1)} %bitcast.8, f32[4]{0:T(128)S(1)} %copy-done.2, bf16[1024,512]{1,0:T(8,128)(2,1)S(1)} %get-tuple-element.25.q_ref, bf16[1024,512]{1,0:T(8,128)(2,1)S(1)} %get-tuple-element.26.k_ref, ...), custom_call_target="tpu_custom_call" | custom-call | flops 8000000000 | bytes 3145728 | tf_op jit(solution)/shard_map/pallas_call | solution.py:361
  52.1 3.2 %shard_map.76.refs_0_ = bf16[256,512]{1,0:T(8,128)(2,1)S(1)} custom-call(s32[1]{0:T(128)} %bitcast.me_ref, s32[2,16]{1,0:T(2,128)S(1)} %bitcast.9, f32[4]{0:T(128)S(1)} %copy-done.2, bf16[1024,512]{1,0:T(8,128)(2,1)S(1)} %get-tuple-element.25.q_ref, bf16[1024,512]{1,0:T(8,128)(2,1)S(1)} %get-tuple-element.26.k_ref, ...), custom_call_target="tpu_custom_call" | custom-call | flops 8000000000 | bytes 3145728 | tf_op jit(solution)/shard_map/pallas_call | solution.py:361
  55.3 3.3 %collective-permute-done.10.most_ref.refs_6_ = bf16[384,1024]{1,0:T(8,128)(2,1)S(1)} collective-permute-done((bf16[384,1024]{1,0:T(8,128)(2,1)S(1)}, bf16[384,1024]{1,0:T(8,128)(2,1)S(1)}, u32[]{:S(2)}, u32[]{:S(2)}) %collective-permute-start.10) | collective-permute-done | bytes 786464 | tf_op jit(solution)/shard_map/ppermute | solution.py:435
  58.6 1.2 %collective-permute-start.7 = (bf16[256,512]{1,0:T(8,128)(2,1)S(1)}, bf16[256,512]{1,0:T(8,128)(2,1)S(1)}, u32[]{:S(2)}, u32[]{:S(2)}) collective-permute-start(bf16[256,512]{1,0:T(8,128)(2,1)S(1)} %shard_map.75.refs_0_), channel_id=1, source_target_pairs={{0,2},{1,3},{2,0},{3,1},{4,6},{5,7},{6,4},{7,5},{8,10},{9,11},{10,... | collective-permute-start | bytes 786440 | tf_op jit(solution)/shard_map/ppermute | solution.py:435
  59.9 21.6 %collective-permute-done.12.most_ref.refs_8_ = bf16[384,1024]{1,0:T(8,128)(2,1)S(1)} collective-permute-done((bf16[384,1024]{1,0:T(8,128)(2,1)S(1)}, bf16[384,1024]{1,0:T(8,128)(2,1)S(1)}, u32[]{:S(2)}, u32[]{:S(2)}) %collective-permute-start.12) | collective-permute-done | bytes 786464 | tf_op jit(solution)/shard_map/ppermute | solution.py:435
  81.5 1.2 %collective-permute-start.15 = (bf16[256,512]{1,0:T(8,128)(2,1)S(1)}, bf16[256,512]{1,0:T(8,128)(2,1)S(1)}, u32[]{:S(2)}, u32[]{:S(2)}) collective-permute-start(bf16[256,512]{1,0:T(8,128)(2,1)S(1)} %shard_map.76.refs_0_), channel_id=1, source_target_pairs={{0,2},{1,3},{2,0},{3,1},{4,6},{5,7},{6,4},{7,5},{8,10},{9,11},{10,... | collective-permute-start | bytes 786440 | tf_op jit(solution)/shard_map/ppermute | solution.py:435
  82.8 4.0 %collective-permute-done.18.refs_2_ = bf16[512,512]{1,0:T(8,128)(2,1)S(1)} collective-permute-done((bf16[512,512]{1,0:T(8,128)(2,1)S(1)}, bf16[512,512]{1,0:T(8,128)(2,1)S(1)}, u32[]{:S(2)}, u32[]{:S(2)}) %collective-permute-start.18) | collective-permute-done | bytes 524320 | tf_op jit(solution)/shard_map/ppermute | solution.py:435
  86.7 6.7 %collective-permute-start.19 = (bf16[512,512]{1,0:T(8,128)(2,1)S(1)}, bf16[512,512]{1,0:T(8,128)(2,1)S(1)}, u32[]{:S(2)}, u32[]{:S(2)}) collective-permute-start(bf16[512,512]{1,0:T(8,128)(2,1)S(1)} %collective-permute-done.18.refs_2_), channel_id=1, source_target_pairs={{0,1},{1,0},{2,3},{3,2},{4,5},{5,4},{6,7},{7,6},{8,9},{9,8},{10,11... | collective-permute-start | bytes 1572872 | tf_op jit(solution)/shard_map/ppermute | solution.py:435
  93.6 4.4 %collective-permute-done.15.refs_2_ = bf16[256,512]{1,0:T(8,128)(2,1)S(1)} collective-permute-done((bf16[256,512]{1,0:T(8,128)(2,1)S(1)}, bf16[256,512]{1,0:T(8,128)(2,1)S(1)}, u32[]{:S(2)}, u32[]{:S(2)}) %collective-permute-start.15) | collective-permute-done | bytes 262176 | tf_op jit(solution)/shard_map/ppermute | solution.py:435
  98.0 3.6 %collective-permute-start.14 = (bf16[256,512]{1,0:T(8,128)(2,1)S(1)}, bf16[256,512]{1,0:T(8,128)(2,1)S(1)}, u32[]{:S(2)}, u32[]{:S(2)}) collective-permute-start(bf16[256,512]{1,0:T(8,128)(2,1)S(1)} %shard_map.76.refs_0_), channel_id=1, source_target_pairs={{0,1},{1,0},{2,3},{3,2},{4,5},{5,4},{6,7},{7,6},{8,9},{9,8},{10,11... | collective-permute-start | bytes 786440 | tf_op jit(solution)/shard_map/ppermute | solution.py:435
  101.6 5.1 %collective-permute-start.6 = (bf16[256,512]{1,0:T(8,128)(2,1)S(1)}, bf16[256,512]{1,0:T(8,128)(2,1)S(1)}, u32[]{:S(2)}, u32[]{:S(2)}) collective-permute-start(bf16[256,512]{1,0:T(8,128)(2,1)S(1)} %shard_map.75.refs_0_), channel_id=1, source_target_pairs={{0,1},{1,0},{2,3},{3,2},{4,5},{5,4},{6,7},{7,6},{8,9},{9,8},{10,11... | collective-permute-start | bytes 786440 | tf_op jit(solution)/shard_map/ppermute | solution.py:435
  106.7 2.8 %collective-permute-start.8 = (bf16[256,512]{1,0:T(8,128)(2,1)S(1)}, bf16[256,512]{1,0:T(8,128)(2,1)S(1)}, u32[]{:S(2)}, u32[]{:S(2)}) collective-permute-start(bf16[256,512]{1,0:T(8,128)(2,1)S(1)} %collective-permute-done.7.refs_2_), channel_id=1, source_target_pairs={{0,1},{1,0},{2,3},{3,2},{4,5},{5,4},{6,7},{7,6},{8,9},{9,8},{10,11... | collective-permute-start | bytes 786440 | tf_op jit(solution)/shard_map/ppermute | solution.py:435
  109.5 3.2 %shard_map.77.refs_10_ = bf16[1024,1024]{1,0:T(8,128)(2,1)} custom-call(s32[1]{0:T(128)S(6)} %and.5.odd_ref, bf16[512,512]{1,0:T(8,128)(2,1)S(1)} %get-tuple-element.44.refs_0_, bf16[512,512]{1,0:T(8,128)(2,1)S(1)} %collective-permute-done.17.refs_1_, bf16[512,512]{1,0:T(8,128)(2,1)S(1)} %collective-permute-done.18.refs_2_, ...), custom_call_target="tpu_custom_call" | custom-call | flops 2147483648 | bytes 4194304 | tf_op jit(solution)/shard_map/pallas_call | solution.py:418
  112.7 2.0 %shard_map.78.refs_10_ = bf16[1024,1024]{1,0:T(8,128)(2,1)} custom-call(s32[1]{0:T(128)S(6)} %and.5.odd_ref, bf16[256,512]{1,0:T(8,128)(2,1)S(1)} %shard_map.76.refs_0_, bf16[256,512]{1,0:T(8,128)(2,1)S(1)} %collective-permute-done.14.refs_1_, bf16[256,512]{1,0:T(8,128)(2,1)S(1)} %collective-permute-done.15.refs_2_, ...), custom_call_target="tpu_custom_call", output_to_operand_aliasing={{}: (11, {})} | custom-call | flops 1073741824 | bytes 4194304 | tf_op jit(solution)/shard_map/pallas_call | solution.py:418
  114.8 2.1 %shard_map.79 = bf16[1024,1024]{1,0:T(8,128)(2,1)} custom-call(s32[1]{0:T(128)S(6)} %and.5.odd_ref, bf16[256,512]{1,0:T(8,128)(2,1)S(1)} %shard_map.75.refs_0_, bf16[256,512]{1,0:T(8,128)(2,1)S(1)} %collective-permute-done.6.refs_1_, bf16[256,512]{1,0:T(8,128)(2,1)S(1)} %collective-permute-done.7.refs_2_, ...), custom_call_target="tpu_custom_call", output_to_operand_aliasing={{}: (11, {})} | custom-call | flops 1073741824 | bytes 4194304 | tf_op jit(solution)/shard_map/pallas_call | solution.py:418
  (28 shorter events, 0.6 us)
Async XLA Ops:
  0.1 8.3 %copy-start = (f32[8,4]{0,1:T(4,128)S(1)}, f32[8,4]{0,1:T(4,128)}, u32[]{:S(2)}) copy-start(f32[8,4]{0,1:T(4,128)} %param.11) | copy-start | bytes 388
  3.6 4.8 %collective-permute-start.3 = (bf16[4,144,128]{2,1,0:T(8,128)(2,1)S(1)}, bf16[4,144,128]{2,1,0:T(8,128)(2,1)S(1)}, u32[]{:S(2)}, u32[]{:S(2)}) collective-permute-start(bf16[4,144,128]{2,1,0:T(8,128)(2,1)S(1)} %get-tuple-element.31), channel_id=1, source_target_pairs={{0,4},{4,0},{8,12},{12,8},{16,20},{20,16},{24,28},{28,24},{1,5},{5... | collective-permute-start | bytes 442376 | tf_op jit(solution)/shard_map/ppermute | solution.py:435
  9.1 13.2 %copy-start.1 = (s32[16,2]{0,1:T(2,128)S(1)}, s32[16,2]{0,1:T(2,128)}, u32[]{:S(2)}) copy-start(s32[16,2]{0,1:T(2,128)} %param.10) | copy-start | bytes 388
  9.1 6.0 %collective-permute-start.4 = (bf16[4,144,128]{2,1,0:T(8,128)(2,1)S(1)}, bf16[4,144,128]{2,1,0:T(8,128)(2,1)S(1)}, u32[]{:S(2)}, u32[]{:S(2)}) collective-permute-start(bf16[4,144,128]{2,1,0:T(8,128)(2,1)S(1)} %get-tuple-element.34), channel_id=1, source_target_pairs={{0,8},{4,12},{8,0},{12,4},{16,24},{20,28},{24,16},{28,20},{1,9},{5... | collective-permute-start | bytes 442376 | tf_op jit(solution)/shard_map/ppermute | solution.py:435
  9.3 35.5 %collective-permute-start = (bf16[128,512]{1,0:T(8,128)(2,1)S(1)}, bf16[128,512]{1,0:T(8,128)(2,1)S(1)}, u32[]{:S(2)}, u32[]{:S(2)}) collective-permute-start(bf16[128,512]{1,0:T(8,128)(2,1)S(1)} %get-tuple-element.28), channel_id=1, source_target_pairs={{0,4},{4,8},{8,12},{12,16},{16,20},{20,24},{24,28},{1,5},{5,9},{9,... | collective-permute-start | bytes 393224 | tf_op jit(solution)/shard_map/ppermute | solution.py:473
  10.6 37.4 %collective-permute-start.1 = (bf16[256,512]{1,0:T(8,128)(2,1)S(1)}, bf16[256,512]{1,0:T(8,128)(2,1)S(1)}, u32[]{:S(2)}, u32[]{:S(2)}) collective-permute-start(bf16[256,512]{1,0:T(8,128)(2,1)S(1)} %get-tuple-element.29), channel_id=1, source_target_pairs={{0,4},{4,8},{8,12},{12,16},{16,20},{20,24},{24,28},{1,5},{5,9},{9,... | collective-permute-start | bytes 786440 | tf_op jit(solution)/shard_map/ppermute | solution.py:473
  11.9 36.1 %collective-permute-start.2 = (bf16[640,512]{1,0:T(8,128)(2,1)S(1)}, bf16[640,512]{1,0:T(8,128)(2,1)S(1)}, u32[]{:S(2)}, u32[]{:S(2)}) collective-permute-start(bf16[640,512]{1,0:T(8,128)(2,1)S(1)} %get-tuple-element.30), channel_id=1, source_target_pairs={{0,4},{4,8},{8,12},{12,16},{16,20},{20,24},{24,28},{1,5},{5,9},{9,... | collective-permute-start | bytes 1966088 | tf_op jit(solution)/shard_map/ppermute | solution.py:473
  13.2 88.3 %collective-permute-start.9 = (bf16[512,1024]{1,0:T(8,128)(2,1)S(1)}, bf16[512,1024]{1,0:T(8,128)(2,1)S(1)}, u32[]{:S(2)}, u32[]{:S(2)}) collective-permute-start(bf16[512,1024]{1,0:T(8,128)(2,1)S(1)} %get-tuple-element.42), channel_id=1, source_target_pairs={{0,1},{1,0},{2,3},{3,2},{4,5},{5,4},{6,7},{7,6},{8,9},{9,8},{10,11... | collective-permute-start | bytes 3145736 | tf_op jit(solution)/shard_map/ppermute | solution.py:435
  15.7 26.5 %collective-permute-start.5 = (bf16[4,144,128]{2,1,0:T(8,128)(2,1)S(1)}, bf16[4,144,128]{2,1,0:T(8,128)(2,1)S(1)}, u32[]{:S(2)}, u32[]{:S(2)}) collective-permute-start(bf16[4,144,128]{2,1,0:T(8,128)(2,1)S(1)} %get-tuple-element.37), channel_id=1, source_target_pairs={{0,16},{4,20},{8,24},{12,28},{16,0},{20,4},{24,8},{28,12},{1,17},{... | collective-permute-start | bytes 442376 | tf_op jit(solution)/shard_map/ppermute | solution.py:435
  26.9 16.6 %copy-start.2 = (f32[4]{0:T(128)S(1)}, f32[4]{0:T(128)}, u32[]{:S(2)}) copy-start(f32[4]{0:T(128)} %gate_ref.5) | copy-start | bytes 52
  42.2 16.4 %collective-permute-start.10 = (bf16[384,1024]{1,0:T(8,128)(2,1)S(1)}, bf16[384,1024]{1,0:T(8,128)(2,1)S(1)}, u32[]{:S(2)}, u32[]{:S(2)}) collective-permute-start(bf16[384,1024]{1,0:T(8,128)(2,1)S(1)} %get-tuple-element.43), channel_id=1, source_target_pairs={{0,2},{1,3},{2,0},{3,1},{4,6},{5,7},{6,4},{7,5},{8,10},{9,11},{10,... | collective-permute-start | bytes 2359304 | tf_op jit(solution)/shard_map/ppermute | solution.py:435
  44.9 36.6 %collective-permute-start.12 = (bf16[384,1024]{1,0:T(8,128)(2,1)S(1)}, bf16[384,1024]{1,0:T(8,128)(2,1)S(1)}, u32[]{:S(2)}, u32[]{:S(2)}) collective-permute-start(bf16[384,1024]{1,0:T(8,128)(2,1)S(1)} %slices.1), channel_id=1, source_target_pairs={{0,3},{1,2},{2,1},{3,0},{4,7},{5,6},{6,5},{7,4},{8,11},{9,10},{10,... | collective-permute-start | bytes 2359304 | tf_op jit(solution)/shard_map/ppermute | solution.py:435
  48.0 49.9 %collective-permute-start.17 = (bf16[512,512]{1,0:T(8,128)(2,1)S(1)}, bf16[512,512]{1,0:T(8,128)(2,1)S(1)}, u32[]{:S(2)}, u32[]{:S(2)}) collective-permute-start(bf16[512,512]{1,0:T(8,128)(2,1)S(1)} %get-tuple-element.44.refs_0_), channel_id=1, source_target_pairs={{0,1},{1,0},{2,3},{3,2},{4,5},{5,4},{6,7},{7,6},{8,9},{9,8},{10,11... | collective-permute-start | bytes 1572872 | tf_op jit(solution)/shard_map/ppermute | solution.py:435
  48.0 38.7 %collective-permute-start.18 = (bf16[512,512]{1,0:T(8,128)(2,1)S(1)}, bf16[512,512]{1,0:T(8,128)(2,1)S(1)}, u32[]{:S(2)}, u32[]{:S(2)}) collective-permute-start(bf16[512,512]{1,0:T(8,128)(2,1)S(1)} %get-tuple-element.44.refs_0_), channel_id=1, source_target_pairs={{0,2},{1,3},{2,0},{3,1},{4,6},{5,7},{6,4},{7,5},{8,10},{9,11},{10,... | collective-permute-start | bytes 1572872 | tf_op jit(solution)/shard_map/ppermute | solution.py:435
  58.6 34.9 %collective-permute-start.7 = (bf16[256,512]{1,0:T(8,128)(2,1)S(1)}, bf16[256,512]{1,0:T(8,128)(2,1)S(1)}, u32[]{:S(2)}, u32[]{:S(2)}) collective-permute-start(bf16[256,512]{1,0:T(8,128)(2,1)S(1)} %shard_map.75.refs_0_), channel_id=1, source_target_pairs={{0,2},{1,3},{2,0},{3,1},{4,6},{5,7},{6,4},{7,5},{8,10},{9,11},{10,... | collective-permute-start | bytes 786440 | tf_op jit(solution)/shard_map/ppermute | solution.py:435
  81.5 16.5 %collective-permute-start.15 = (bf16[256,512]{1,0:T(8,128)(2,1)S(1)}, bf16[256,512]{1,0:T(8,128)(2,1)S(1)}, u32[]{:S(2)}, u32[]{:S(2)}) collective-permute-start(bf16[256,512]{1,0:T(8,128)(2,1)S(1)} %shard_map.76.refs_0_), channel_id=1, source_target_pairs={{0,2},{1,3},{2,0},{3,1},{4,6},{5,7},{6,4},{7,5},{8,10},{9,11},{10,... | collective-permute-start | bytes 786440 | tf_op jit(solution)/shard_map/ppermute | solution.py:435
  86.7 22.8 %collective-permute-start.19 = (bf16[512,512]{1,0:T(8,128)(2,1)S(1)}, bf16[512,512]{1,0:T(8,128)(2,1)S(1)}, u32[]{:S(2)}, u32[]{:S(2)}) collective-permute-start(bf16[512,512]{1,0:T(8,128)(2,1)S(1)} %collective-permute-done.18.refs_2_), channel_id=1, source_target_pairs={{0,1},{1,0},{2,3},{3,2},{4,5},{5,4},{6,7},{7,6},{8,9},{9,8},{10,11... | collective-permute-start | bytes 1572872 | tf_op jit(solution)/shard_map/ppermute | solution.py:435
  93.5 8.1 %collective-permute-start.11 = (bf16[128,1024]{1,0:T(8,128)(2,1)S(1)}, bf16[128,1024]{1,0:T(8,128)(2,1)S(1)}, u32[]{:S(2)}, u32[]{:S(2)}) collective-permute-start(bf16[128,1024]{1,0:T(8,128)(2,1)S(1)} %part.2), channel_id=1, source_target_pairs={{0,4},{4,0},{8,12},{12,8},{16,20},{20,16},{24,28},{28,24},{1,5},{5... | collective-permute-start | bytes 786440 | tf_op jit(solution)/shard_map/ppermute | solution.py:435
  98.0 8.7 %collective-permute-start.13 = (bf16[128,1024]{1,0:T(8,128)(2,1)S(1)}, bf16[128,1024]{1,0:T(8,128)(2,1)S(1)}, u32[]{:S(2)}, u32[]{:S(2)}) collective-permute-start(bf16[128,1024]{1,0:T(8,128)(2,1)S(1)} %part.3), channel_id=1, source_target_pairs={{0,4},{4,0},{8,12},{12,8},{16,20},{20,16},{24,28},{28,24},{1,5},{5... | collective-permute-start | bytes 786440 | tf_op jit(solution)/shard_map/ppermute | solution.py:435
  98.0 14.8 %collective-permute-start.14 = (bf16[256,512]{1,0:T(8,128)(2,1)S(1)}, bf16[256,512]{1,0:T(8,128)(2,1)S(1)}, u32[]{:S(2)}, u32[]{:S(2)}) collective-permute-start(bf16[256,512]{1,0:T(8,128)(2,1)S(1)} %shard_map.76.refs_0_), channel_id=1, source_target_pairs={{0,1},{1,0},{2,3},{3,2},{4,5},{5,4},{6,7},{7,6},{8,9},{9,8},{10,11... | collective-permute-start | bytes 786440 | tf_op jit(solution)/shard_map/ppermute | solution.py:435
  101.5 11.2 %collective-permute-start.16 = (bf16[256,512]{1,0:T(8,128)(2,1)S(1)}, bf16[256,512]{1,0:T(8,128)(2,1)S(1)}, u32[]{:S(2)}, u32[]{:S(2)}) collective-permute-start(bf16[256,512]{1,0:T(8,128)(2,1)S(1)} %collective-permute-done.15.refs_2_), channel_id=1, source_target_pairs={{0,1},{1,0},{2,3},{3,2},{4,5},{5,4},{6,7},{7,6},{8,9},{9,8},{10,11... | collective-permute-start | bytes 786440 | tf_op jit(solution)/shard_map/ppermute | solution.py:435
  101.6 13.2 %collective-permute-start.6 = (bf16[256,512]{1,0:T(8,128)(2,1)S(1)}, bf16[256,512]{1,0:T(8,128)(2,1)S(1)}, u32[]{:S(2)}, u32[]{:S(2)}) collective-permute-start(bf16[256,512]{1,0:T(8,128)(2,1)S(1)} %shard_map.75.refs_0_), channel_id=1, source_target_pairs={{0,1},{1,0},{2,3},{3,2},{4,5},{5,4},{6,7},{7,6},{8,9},{9,8},{10,11... | collective-permute-start | bytes 786440 | tf_op jit(solution)/shard_map/ppermute | solution.py:435
  106.7 8.1 %collective-permute-start.8 = (bf16[256,512]{1,0:T(8,128)(2,1)S(1)}, bf16[256,512]{1,0:T(8,128)(2,1)S(1)}, u32[]{:S(2)}, u32[]{:S(2)}) collective-permute-start(bf16[256,512]{1,0:T(8,128)(2,1)S(1)} %collective-permute-done.7.refs_2_), channel_id=1, source_target_pairs={{0,1},{1,0},{2,3},{3,2},{4,5},{5,4},{6,7},{7,6},{8,9},{9,8},{10,11... | collective-permute-start | bytes 786440 | tf_op jit(solution)/shard_map/ppermute | solution.py:435

commit v4 on v3

--- a/solution.py
+++ b/solution.py
@@ -77,55 +77,15 @@
 
 
 def slice_copies(slices, at_ref, w_hbm, blocks, sems):
-    odd, head_index = at_ref[0], at_ref[1]
+    me, head_index = at_ref[0], at_ref[1]
     copies = []
-    for number, (mask, rows) in enumerate(slices):
-        columns = blocks[number].shape[1]
-        unit = w_hbm.shape[0] // 4
-        row = pl.multiple_of(odd * unit, unit) if rows < w_hbm.shape[0] else 0
+    for number, (mask, partner) in enumerate(slices):
+        rows, columns = blocks[number].shape
+        row = jnp.where((me & partner) != 0, rows, 0) if partner else 0
         col = pl.multiple_of((head_index ^ mask) * columns, columns)
-        source = w_hbm.at[pl.ds(row, rows), pl.ds(col, columns)]
+        source = w_hbm.at[pl.ds(pl.multiple_of(row, rows), rows), pl.ds(col, columns)]
         copies.append(pltpu.make_async_copy(source, blocks[number], sems.at[number]))
     return copies
-
-
-def slice_kernel(slices, at_ref, w_hbm, *refs):
-    *blocks, sems = refs
-    copies = slice_copies(slices, at_ref, w_hbm, blocks, sems)
-    for copy in copies:
-        copy.start()
-    for copy in copies:
-        copy.wait()
-
-
-def make_slices(out_weight, slices, at, columns):
-    return pl.pallas_call(
-        functools.partial(slice_kernel, slices),
-        in_specs=[SMEM, HBM],
-        out_specs=[VMEM] * len(slices),
-        out_shape=[pltpu.VMEM((rows, columns), BF16) for _, rows in slices],
-        scratch_shapes=[pltpu.SemaphoreType.DMA((len(slices),))],
-        compiler_params=params(8),
-        cost_estimate=cost(1e9, 2 * columns * sum(rows for _, rows in slices) * 2),
-        name="slices",
-    )(at, in_hbm(out_weight))
-
-
-def part_kernel(odd_ref, most_ref, part_ref):
-    unit = part_ref.shape[0]
-    part_ref[...] = most_ref[pl.ds(pl.multiple_of(odd_ref[0] * 2 * unit, unit), unit), :]
-
-
-def make_part(most, odd, unit):
-    return pl.pallas_call(
-        part_kernel,
-        in_specs=[SMEM, VMEM],
-        out_specs=VMEM,
-        out_shape=pltpu.VMEM((unit, most.shape[1]), BF16),
-        compiler_params=params(4),
-        cost_estimate=cost(1e8, 4 * unit * most.shape[1]),
-        name="part",
-    )(odd, in_vmem(most))
 
 
 def state_kernel(slices, at_ref, q_hbm, k_hbm, v_hbm, w_hbm, state_ref, send_ref, *refs):
@@ -178,6 +138,7 @@
 
 def make_state(queries, keys, values, out_weight, slices, at, heads, width, columns):
     rows, cols = keys.shape
+    depth = out_weight.shape[0]
     steps = rows // BLOCK
     tails = (*HALO, 2 * BAND - sum(HALO))
     return pl.pallas_call(
@@ -189,7 +150,7 @@
             pltpu.VMEM((heads, width + SEND_PAD, width), BF16),
             *[pltpu.VMEM((rows, cols), BF16)] * 3,
             *(pltpu.VMEM((tail, cols), BF16) for tail in tails),
-            *(pltpu.VMEM((rows_, columns), BF16) for _, rows_ in slices),
+            *(pltpu.VMEM((depth // (2 if by else 1), columns), BF16) for _, by in slices),
         ],
         scratch_shapes=[
             pltpu.SemaphoreType.DMA((2, steps)),
@@ -369,18 +330,18 @@
     )(me, spans, gate, *operands)
 
 
-def project_kernel(shared, first_row, odd_ref, *refs):
+def project_kernel(partners, first_row, me_ref, *refs):
     *refs, out_hbm, out_ref, sems = refs
-    xs, ws = refs[: len(shared)], list(refs[len(shared) :])
+    xs, ws = refs[: len(partners)], list(refs[len(partners) :])
     rows, columns = out_ref.shape
-    odd = odd_ref[0]
+    me = me_ref[0]
     lefts, rights = [], []
-    for x_ref, is_shared in zip(xs, shared):
-        if is_shared:
-            unit = x_ref.shape[1] // 4
-            most = x_ref[:, pl.ds(pl.multiple_of(odd * unit, unit), 3 * unit)]
-            rest = x_ref[:, pl.ds(pl.multiple_of((1 - odd) * 3 * unit, unit), unit)]
-            lefts.append(jnp.concatenate([most, rest], axis=1))
+    for x_ref, partner in zip(xs, partners):
+        if partner:
+            half = x_ref.shape[1] // 2
+            mine = jnp.where((me & partner) != 0, half, 0)
+            parts = [x_ref[:, pl.ds(pl.multiple_of(at, half), half)] for at in (mine, half - mine)]
+            lefts.append(jnp.concatenate(parts, axis=1))
             rights.append((ws.pop(0), ws.pop(0)))
         else:
             lefts.append(x_ref[...])
@@ -403,11 +364,11 @@
         copy.wait()
 
 
-def project(start, total_rows, xs, weights, odd, out):
+def project(start, total_rows, xs, weights, partners, me, out):
     rows = xs[0].shape[0]
     flat = [w for ws in weights for w in ws]
     columns = flat[0].shape[1]
-    operands = [odd, *map(in_vmem, xs), *map(in_vmem, flat)]
+    operands = [me, *map(in_vmem, xs), *map(in_vmem, flat)]
     in_specs = [SMEM] + [VMEM] * (len(operands) - 1)
     aliases = {}
     if out is not None:
@@ -416,7 +377,7 @@
         operands.append(out)
     depth = sum(w.shape[0] for w in flat)
     return pl.pallas_call(
-        functools.partial(project_kernel, [len(ws) > 1 for ws in weights], start),
+        functools.partial(project_kernel, partners, start),
         in_specs=in_specs,
         out_specs=HBM,
         out_shape=pltpu.HBM((total_rows, columns), BF16),
@@ -445,28 +406,21 @@
     assert seq_size & (seq_size - 1) == 0 and seq_size > 1
     seq_index, head_index = lax.axis_index("seq"), lax.axis_index("head")
     me = seq_index.astype(jnp.int32).reshape(1)
-    odd = me & 1
-    depth = out_weight.shape[0]
-    unit = depth // 4
     columns = out_weight.shape[1] // head_size
 
     masks = sorted(range(1, head_size), reverse=True)
-    slices = [(mask, depth if mask == 1 else 3 * unit) for mask in masks] + [(0, depth)]
-    at = jnp.concatenate([odd, head_index.astype(jnp.int32).reshape(1)])
-    first = make_slices(out_weight, slices[:1], at, columns)
+    partners = {mask: 1 << (mask % 2 == 0 and seq_size > 2) for mask in masks if mask > 1}
+    slices = [(mask, partners.get(mask, 0)) for mask in (*masks, 0)]
+    at = jnp.concatenate([me, head_index.astype(jnp.int32).reshape(1)])
     state, send, *more = make_state(
-        queries, keys, values, out_weight, slices[1:], at, heads, width,
-        columns,
+        queries, keys, values, out_weight, slices, at, heads, width, columns
     )
     queries, keys, values = more[:3]
-    tails, blocks = more[3:6], [*first, *more[6:]]
+    tails, blocks = more[3:6], more[6:]
     weights = {}
-    for mask, block in zip([*masks, 0], blocks):
-        weights[mask] = (swap(block, "head", mask) if mask else block,)
-        if mask > 1:
-            most = weights[mask][0]
-            part = make_part(most, odd, unit)
-            weights[mask] = (most, swap(part, "seq", 1))
+    for (mask, partner), block in zip(slices, blocks):
+        block = swap(block, "head", mask) if mask else block
+        weights[mask] = (block, swap(block, "seq", partner)) if partner else (block,)
 
     halo = []
     for tail in tails:
@@ -511,7 +465,7 @@
         order = range(head_size)
         out = project(
             start, seg_rows,
-            [xs[i] for i in order], [weights[i] for i in order], odd, out,
+            [xs[i] for i in order], [weights[i] for i in order], [partners.get(i, 0) for i in order], me, out,
         )
     return out
 

time: 117 us -> 109 us (0.932)
  the two profiles are of different devices: /device:TPU:27 before, /device:TPU:0 now
where the time goes in v4:
time: 109 us; the launch traced here: 107 us
  waiting for transfers between devices  47.6 us (44%)
  starting transfers between devices  34.6 us (32%)
  Pallas kernels  24.1 us (22%)
    ppermute x17, waiting for transfers between devices, swap(): return lax.ppermute(x, axis, [(i, i ^ mask) for i in range(size)])  46.5 us
    ppermute x17, starting transfers between devices, swap(): return lax.ppermute(x, axis, [(i, i ^ mask) for i in range(size)])  25.4 us
    ppermute x3, starting transfers between devices, body(): lax.ppermute(tail, 'seq', [(i, i + 1) for i in range(seq_size - 1)])  9.15 us
    pallas_call x3, Pallas kernels, project(): pl.pallas_call(functools.partial(project_kernel, partners, start), in_spe...  7.29 us
    pallas_call x2, Pallas kernels, make_attend(): pl.pallas_call(functools.partial(attend_kernel, start), in_specs=[SMEM] *...  5.95 us
    pallas_call x1, Pallas kernels, make_local(): pl.pallas_call(functools.partial(local_kernel, width), in_specs=[SMEM, SM...  4.59 us
    pallas_call x1, Pallas kernels, make_state(): pl.pallas_call(functools.partial(state_kernel, slices), in_specs=[SMEM, H...  3.63 us
  transfers between devices with their start and end apart: 20, of which 8 were waited for; matrix products, arithmetic and copies ran while one was open for 0% of the time, Pallas kernels for 17%

profile of v4, /device:TPU:0, one launch (start us, length us, event | category | flops | bytes accessed | tf_op | source)
XLA Modules:
  0.0 106.6 jit_solution(16504278979272625007)
XLA Ops:
  0.1 3.6 %state.1 = (f32[4,136,128]{2,1,0:T(8,128)S(1)}, bf16[4,144,128]{2,1,0:T(8,128)(2,1)S(1)}, bf16[1024,512]{1,0:T(8,128)(2,1)S(1)}, bf16[1024,512]{1,0:T(8,128)(2,1...) custom-call(s32[2]{0:T(128)S(1)} %pad_add_fusion.at_ref, ...), custom_call_target="tpu_custom_call" | custom-call | flops 10000000000 | bytes 4194304 | tf_op jit(solution)/shard_map/state/pallas_call | solution.py:144
  3.7 3.0 %collective-permute-start.3 = (bf16[4,144,128]{2,1,0:T(8,128)(2,1)S(1)}, bf16[4,144,128]{2,1,0:T(8,128)(2,1)S(1)}, u32[]{:S(2)}, u32[]{:S(2)}) collective-permute-start(bf16[4,144,128]{2,1,0:T(8,128)(2,1)S(1)} %get-tuple-element.32), channel_id=1, source_target_pairs={{0,4},{4,0},{8,12},{12,8},{16,20},{20,16},{24,28},{28,24},{1,5},{5... | collective-permute-start | bytes 442376 | tf_op jit(solution)/shard_map/ppermute | solution.py:396
  6.7 3.8 %collective-permute-done.3.refs_0_ = bf16[4,144,128]{2,1,0:T(8,128)(2,1)S(1)} collective-permute-done((bf16[4,144,128]{2,1,0:T(8,128)(2,1)S(1)}, bf16[4,144,128]{2,1,0:T(8,128)(2,1)S(1)}, u32[]{:S(2)}, u32[]{:S(2)}) %collective-permute-start.3) | collective-permute-done | bytes 147488 | tf_op jit(solution)/shard_map/ppermute | solution.py:396
  10.6 0.6 shard_map.73
  11.2 1.9 %collective-permute-start.4 = (bf16[4,144,128]{2,1,0:T(8,128)(2,1)S(1)}, bf16[4,144,128]{2,1,0:T(8,128)(2,1)S(1)}, u32[]{:S(2)}, u32[]{:S(2)}) collective-permute-start(bf16[4,144,128]{2,1,0:T(8,128)(2,1)S(1)} %get-tuple-element.35), channel_id=1, source_target_pairs={{0,8},{4,12},{8,0},{12,4},{16,24},{20,28},{24,16},{28,20},{1,9},{5... | collective-permute-start | bytes 442376 | tf_op jit(solution)/shard_map/ppermute | solution.py:396
  13.1 3.4 %collective-permute-start = (bf16[128,512]{1,0:T(8,128)(2,1)S(1)}, bf16[128,512]{1,0:T(8,128)(2,1)S(1)}, u32[]{:S(2)}, u32[]{:S(2)}) collective-permute-start(bf16[128,512]{1,0:T(8,128)(2,1)S(1)} %get-tuple-element.29), channel_id=1, source_target_pairs={{0,4},{4,8},{8,12},{12,16},{16,20},{20,24},{24,28},{1,5},{5,9},{9,... | collective-permute-start | bytes 393224 | tf_op jit(solution)/shard_map/ppermute | solution.py:427
  16.5 2.1 %collective-permute-start.1 = (bf16[256,512]{1,0:T(8,128)(2,1)S(1)}, bf16[256,512]{1,0:T(8,128)(2,1)S(1)}, u32[]{:S(2)}, u32[]{:S(2)}) collective-permute-start(bf16[256,512]{1,0:T(8,128)(2,1)S(1)} %get-tuple-element.30), channel_id=1, source_target_pairs={{0,4},{4,8},{8,12},{12,16},{16,20},{20,24},{24,28},{1,5},{5,9},{9,... | collective-permute-start | bytes 786440 | tf_op jit(solution)/shard_map/ppermute | solution.py:427
  18.6 3.7 %collective-permute-start.2 = (bf16[640,512]{1,0:T(8,128)(2,1)S(1)}, bf16[640,512]{1,0:T(8,128)(2,1)S(1)}, u32[]{:S(2)}, u32[]{:S(2)}) collective-permute-start(bf16[640,512]{1,0:T(8,128)(2,1)S(1)} %get-tuple-element.31), channel_id=1, source_target_pairs={{0,4},{4,8},{8,12},{12,16},{16,20},{20,24},{24,28},{1,5},{5,9},{9,... | collective-permute-start | bytes 1966088 | tf_op jit(solution)/shard_map/ppermute | solution.py:427
  22.4 0.7 shard_map.74
  23.1 2.6 %collective-permute-start.5 = (bf16[4,144,128]{2,1,0:T(8,128)(2,1)S(1)}, bf16[4,144,128]{2,1,0:T(8,128)(2,1)S(1)}, u32[]{:S(2)}, u32[]{:S(2)}) collective-permute-start(bf16[4,144,128]{2,1,0:T(8,128)(2,1)S(1)} %get-tuple-element.38), channel_id=1, source_target_pairs={{0,16},{4,20},{8,24},{12,28},{16,0},{20,4},{24,8},{28,12},{1,17},{... | collective-permute-start | bytes 442376 | tf_op jit(solution)/shard_map/ppermute | solution.py:396
  25.7 4.6 %local.1.local_ref = f32[512,512]{1,0:T(8,128)S(1)} custom-call(s32[1]{0:T(128)} %bitcast.me_ref, s32[2,16]{1,0:T(2,128)S(1)} %bitcast.7, bf16[1024,512]{1,0:T(8,128)(2,1)S(1)} %get-tuple-element.26.q_ref, bf16[1024,512]{1,0:T(8,128)(2,1)S(1)} %get-tuple-element.27.k_ref, bf16[1024,512]{1,0:T(8,128)(2,1)S(1)} %get-tuple-element.28.v_ref), custom_call_target="tpu_custom_call" | custom-call | flops 15000000512 | bytes 3145728 | tf_op jit(solution)/shard_map/local/pallas_call | solution.py:248
  30.3 3.1 %collective-permute-done.5.refs_1_ = bf16[4,144,128]{2,1,0:T(8,128)(2,1)S(1)} collective-permute-done((bf16[4,144,128]{2,1,0:T(8,128)(2,1)S(1)}, bf16[4,144,128]{2,1,0:T(8,128)(2,1)S(1)}, u32[]{:S(2)}, u32[]{:S(2)}) %collective-permute-start.5) | collective-permute-done | bytes 147488 | tf_op jit(solution)/shard_map/ppermute | solution.py:396
  33.4 1.5 %collective-permute-start.10 = (bf16[256,1024]{1,0:T(8,128)(2,1)S(1)}, bf16[256,1024]{1,0:T(8,128)(2,1)S(1)}, u32[]{:S(2)}, u32[]{:S(2)}) collective-permute-start(bf16[256,1024]{1,0:T(8,128)(2,1)S(1)} %get-tuple-element.44), channel_id=1, source_target_pairs={{0,2},{1,3},{2,0},{3,1},{4,6},{5,7},{6,4},{7,5},{8,10},{9,11},{10,... | collective-permute-start | bytes 1572872 | tf_op jit(solution)/shard_map/ppermute | solution.py:396
  35.0 1.4 %readout.1 = (bf16[512,512]{1,0:T(8,128)(2,1)S(1)}, bf16[4,256,256]{2,1,0:T(8,128)(2,1)S(1)}, f32[4,8,128]{2,1,0:T(8,128)S(1)}) custom-call(s32[1]{0:T(128)} %bitcast.me_ref, f32[4,8]{1,0:T(4,128)S(1)} %bitcast.6, f32[4]{0:T(128)S(1)} %copy-done.2, bf16[1024,512]{1,0:T(8,128)(2,1)S(1)} %get-tuple-element.26.q_ref, f32[512,512]{1,0:T(8,128)S(1)} %local.1.local_ref, ...), custom_call_target="tpu_custom_call" | custom-call | flops 2000000000 | bytes 2097152 | tf_op jit(solution)/shard_map/readout/pallas_call | solution.py:284
  36.4 1.0 collective-permute-start.18
  37.4 1.1 %collective-permute-done.2.refs_2_ = bf16[640,512]{1,0:T(8,128)(2,1)S(1)} collective-permute-done((bf16[640,512]{1,0:T(8,128)(2,1)S(1)}, bf16[640,512]{1,0:T(8,128)(2,1)S(1)}, u32[]{:S(2)}, u32[]{:S(2)}) %collective-permute-start.2) | collective-permute-done | bytes 655392 | tf_op jit(solution)/shard_map/ppermute | solution.py:427
  38.5 2.7 %shard_map.75.refs_0_ = bf16[256,512]{1,0:T(8,128)(2,1)S(1)} custom-call(s32[1]{0:T(128)} %bitcast.me_ref, s32[2,16]{1,0:T(2,128)S(1)} %bitcast.8, f32[4]{0:T(128)S(1)} %copy-done.2, bf16[1024,512]{1,0:T(8,128)(2,1)S(1)} %get-tuple-element.26.q_ref, bf16[1024,512]{1,0:T(8,128)(2,1)S(1)} %get-tuple-element.27.k_ref, ...), custom_call_target="tpu_custom_call" | custom-call | flops 8000000000 | bytes 3145728 | tf_op jit(solution)/shard_map/pallas_call | solution.py:322
  41.2 1.6 %collective-permute-start.7 = (bf16[256,512]{1,0:T(8,128)(2,1)S(1)}, bf16[256,512]{1,0:T(8,128)(2,1)S(1)}, u32[]{:S(2)}, u32[]{:S(2)}) collective-permute-start(bf16[256,512]{1,0:T(8,128)(2,1)S(1)} %shard_map.75.refs_0_), channel_id=1, source_target_pairs={{0,2},{1,3},{2,0},{3,1},{4,6},{5,7},{6,4},{7,5},{8,10},{9,11},{10,... | collective-permute-start | bytes 786440 | tf_op jit(solution)/shard_map/ppermute | solution.py:396
  42.8 3.2 %shard_map.76.refs_0_ = bf16[256,512]{1,0:T(8,128)(2,1)S(1)} custom-call(s32[1]{0:T(128)} %bitcast.me_ref, s32[2,16]{1,0:T(2,128)S(1)} %bitcast.9, f32[4]{0:T(128)S(1)} %copy-done.2, bf16[1024,512]{1,0:T(8,128)(2,1)S(1)} %get-tuple-element.26.q_ref, bf16[1024,512]{1,0:T(8,128)(2,1)S(1)} %get-tuple-element.27.k_ref, ...), custom_call_target="tpu_custom_call" | custom-call | flops 8000000000 | bytes 3145728 | tf_op jit(solution)/shard_map/pallas_call | solution.py:322
  46.0 2.2 %collective-permute-done.10.refs_6_ = bf16[256,1024]{1,0:T(8,128)(2,1)S(1)} collective-permute-done((bf16[256,1024]{1,0:T(8,128)(2,1)S(1)}, bf16[256,1024]{1,0:T(8,128)(2,1)S(1)}, u32[]{:S(2)}, u32[]{:S(2)}) %collective-permute-start.10) | collective-permute-done | bytes 524320 | tf_op jit(solution)/shard_map/ppermute | solution.py:396
  48.2 1.5 %collective-permute-start.15 = (bf16[256,512]{1,0:T(8,128)(2,1)S(1)}, bf16[256,512]{1,0:T(8,128)(2,1)S(1)}, u32[]{:S(2)}, u32[]{:S(2)}) collective-permute-start(bf16[256,512]{1,0:T(8,128)(2,1)S(1)} %shard_map.76.refs_0_), channel_id=1, source_target_pairs={{0,2},{1,3},{2,0},{3,1},{4,6},{5,7},{6,4},{7,5},{8,10},{9,11},{10,... | collective-permute-start | bytes 786440 | tf_op jit(solution)/shard_map/ppermute | solution.py:396
  49.7 8.8 %collective-permute-done.12.refs_8_ = bf16[256,1024]{1,0:T(8,128)(2,1)S(1)} collective-permute-done((bf16[256,1024]{1,0:T(8,128)(2,1)S(1)}, bf16[256,1024]{1,0:T(8,128)(2,1)S(1)}, u32[]{:S(2)}, u32[]{:S(2)}) %collective-permute-start.12) | collective-permute-done | bytes 524320 | tf_op jit(solution)/shard_map/ppermute | solution.py:396
  58.5 0.8 collective-permute-start.17
  59.3 17.0 %collective-permute-done.7.refs_2_ = bf16[256,512]{1,0:T(8,128)(2,1)S(1)} collective-permute-done((bf16[256,512]{1,0:T(8,128)(2,1)S(1)}, bf16[256,512]{1,0:T(8,128)(2,1)S(1)}, u32[]{:S(2)}, u32[]{:S(2)}) %collective-permute-start.7) | collective-permute-done | bytes 262176 | tf_op jit(solution)/shard_map/ppermute | solution.py:396
  76.3 4.3 %collective-permute-done.15.refs_2_ = bf16[256,512]{1,0:T(8,128)(2,1)S(1)} collective-permute-done((bf16[256,512]{1,0:T(8,128)(2,1)S(1)}, bf16[256,512]{1,0:T(8,128)(2,1)S(1)}, u32[]{:S(2)}, u32[]{:S(2)}) %collective-permute-start.15) | collective-permute-done | bytes 262176 | tf_op jit(solution)/shard_map/ppermute | solution.py:396
  80.6 10.4 %collective-permute-start.13 = (bf16[256,1024]{1,0:T(8,128)(2,1)S(1)}, bf16[256,1024]{1,0:T(8,128)(2,1)S(1)}, u32[]{:S(2)}, u32[]{:S(2)}) collective-permute-start(bf16[256,1024]{1,0:T(8,128)(2,1)S(1)} %collective-permute-done.12.refs_8_), channel_id=1, source_target_pairs={{0,4},{4,0},{8,12},{12,8},{16,20},{20,16},{24,28},{28,24},{1,5},{5... | collective-permute-start | bytes 1572872 | tf_op jit(solution)/shard_map/ppermute | solution.py:396
  91.0 0.5 collective-permute-start.14
  91.6 0.4 collective-permute-start.6
  92.0 7.3 %collective-permute-done.13.refs_9_ = bf16[256,1024]{1,0:T(8,128)(2,1)S(1)} collective-permute-done((bf16[256,1024]{1,0:T(8,128)(2,1)S(1)}, bf16[256,1024]{1,0:T(8,128)(2,1)S(1)}, u32[]{:S(2)}, u32[]{:S(2)}) %collective-permute-start.13) | collective-permute-done | bytes 524320 | tf_op jit(solution)/shard_map/ppermute | solution.py:396
  99.3 3.2 %shard_map.77.refs_10_ = bf16[1024,1024]{1,0:T(8,128)(2,1)} custom-call(s32[1]{0:T(128)} %bitcast.me_ref, bf16[512,512]{1,0:T(8,128)(2,1)S(1)} %get-tuple-element.46.refs_0_, bf16[512,512]{1,0:T(8,128)(2,1)S(1)} %collective-permute-done.17.refs_1_, bf16[512,512]{1,0:T(8,128)(2,1)S(1)} %collective-permute-done.18.refs_2_, ...), custom_call_target="tpu_custom_call" | custom-call | flops 2147483648 | bytes 4194304 | tf_op jit(solution)/shard_map/pallas_call | solution.py:379
  102.5 2.0 %shard_map.78.refs_10_ = bf16[1024,1024]{1,0:T(8,128)(2,1)} custom-call(s32[1]{0:T(128)} %bitcast.me_ref, bf16[256,512]{1,0:T(8,128)(2,1)S(1)} %shard_map.76.refs_0_, bf16[256,512]{1,0:T(8,128)(2,1)S(1)} %collective-permute-done.14.refs_1_, bf16[256,512]{1,0:T(8,128)(2,1)S(1)} %collective-permute-done.15.refs_2_, ...), custom_call_target="tpu_custom_call", output_to_operand_aliasing={{}: (11, {})} | custom-call | flops 1073741824 | bytes 4194304 | tf_op jit(solution)/shard_map/pallas_call | solution.py:379
  104.6 2.0 %shard_map.79 = bf16[1024,1024]{1,0:T(8,128)(2,1)} custom-call(s32[1]{0:T(128)} %bitcast.me_ref, bf16[256,512]{1,0:T(8,128)(2,1)S(1)} %shard_map.75.refs_0_, bf16[256,512]{1,0:T(8,128)(2,1)S(1)} %collective-permute-done.6.refs_1_, bf16[256,512]{1,0:T(8,128)(2,1)S(1)} %collective-permute-done.7.refs_2_, ...), custom_call_target="tpu_custom_call", output_to_operand_aliasing={{}: (11, {})} | custom-call | flops 1073741824 | bytes 4194304 | tf_op jit(solution)/shard_map/pallas_call | solution.py:379
  (25 shorter events, 0.3 us)
Async XLA Ops:
  0.1 10.5 %copy-start = (f32[8,4]{0,1:T(4,128)S(1)}, f32[8,4]{0,1:T(4,128)}, u32[]{:S(2)}) copy-start(f32[8,4]{0,1:T(4,128)} %param.11) | copy-start | bytes 388
  3.7 6.9 %collective-permute-start.3 = (bf16[4,144,128]{2,1,0:T(8,128)(2,1)S(1)}, bf16[4,144,128]{2,1,0:T(8,128)(2,1)S(1)}, u32[]{:S(2)}, u32[]{:S(2)}) collective-permute-start(bf16[4,144,128]{2,1,0:T(8,128)(2,1)S(1)} %get-tuple-element.32), channel_id=1, source_target_pairs={{0,4},{4,0},{8,12},{12,8},{16,20},{20,16},{24,28},{28,24},{1,5},{5... | collective-permute-start | bytes 442376 | tf_op jit(solution)/shard_map/ppermute | solution.py:396
  11.2 14.5 %copy-start.1 = (s32[16,2]{0,1:T(2,128)S(1)}, s32[16,2]{0,1:T(2,128)}, u32[]{:S(2)}) copy-start(s32[16,2]{0,1:T(2,128)} %param.10) | copy-start | bytes 388
  11.2 11.1 %collective-permute-start.4 = (bf16[4,144,128]{2,1,0:T(8,128)(2,1)S(1)}, bf16[4,144,128]{2,1,0:T(8,128)(2,1)S(1)}, u32[]{:S(2)}, u32[]{:S(2)}) collective-permute-start(bf16[4,144,128]{2,1,0:T(8,128)(2,1)S(1)} %get-tuple-element.35), channel_id=1, source_target_pairs={{0,8},{4,12},{8,0},{12,4},{16,24},{20,28},{24,16},{28,20},{1,9},{5... | collective-permute-start | bytes 442376 | tf_op jit(solution)/shard_map/ppermute | solution.py:396
  13.1 23.2 %collective-permute-start = (bf16[128,512]{1,0:T(8,128)(2,1)S(1)}, bf16[128,512]{1,0:T(8,128)(2,1)S(1)}, u32[]{:S(2)}, u32[]{:S(2)}) collective-permute-start(bf16[128,512]{1,0:T(8,128)(2,1)S(1)} %get-tuple-element.29), channel_id=1, source_target_pairs={{0,4},{4,8},{8,12},{12,16},{16,20},{20,24},{24,28},{1,5},{5,9},{9,... | collective-permute-start | bytes 393224 | tf_op jit(solution)/shard_map/ppermute | solution.py:427
  16.5 19.9 %collective-permute-start.1 = (bf16[256,512]{1,0:T(8,128)(2,1)S(1)}, bf16[256,512]{1,0:T(8,128)(2,1)S(1)}, u32[]{:S(2)}, u32[]{:S(2)}) collective-permute-start(bf16[256,512]{1,0:T(8,128)(2,1)S(1)} %get-tuple-element.30), channel_id=1, source_target_pairs={{0,4},{4,8},{8,12},{12,16},{16,20},{20,24},{24,28},{1,5},{5,9},{9,... | collective-permute-start | bytes 786440 | tf_op jit(solution)/shard_map/ppermute | solution.py:427
  18.6 19.8 %collective-permute-start.2 = (bf16[640,512]{1,0:T(8,128)(2,1)S(1)}, bf16[640,512]{1,0:T(8,128)(2,1)S(1)}, u32[]{:S(2)}, u32[]{:S(2)}) collective-permute-start(bf16[640,512]{1,0:T(8,128)(2,1)S(1)} %get-tuple-element.31), channel_id=1, source_target_pairs={{0,4},{4,8},{8,12},{12,16},{16,20},{20,24},{24,28},{1,5},{5,9},{9,... | collective-permute-start | bytes 1966088 | tf_op jit(solution)/shard_map/ppermute | solution.py:427
  22.3 69.2 %collective-permute-start.9 = (bf16[512,1024]{1,0:T(8,128)(2,1)S(1)}, bf16[512,1024]{1,0:T(8,128)(2,1)S(1)}, u32[]{:S(2)}, u32[]{:S(2)}) collective-permute-start(bf16[512,1024]{1,0:T(8,128)(2,1)S(1)} %get-tuple-element.43), channel_id=1, source_target_pairs={{0,1},{1,0},{2,3},{3,2},{4,5},{5,4},{6,7},{7,6},{8,9},{9,8},{10,11... | collective-permute-start | bytes 3145736 | tf_op jit(solution)/shard_map/ppermute | solution.py:396
  23.1 10.4 %collective-permute-start.5 = (bf16[4,144,128]{2,1,0:T(8,128)(2,1)S(1)}, bf16[4,144,128]{2,1,0:T(8,128)(2,1)S(1)}, u32[]{:S(2)}, u32[]{:S(2)}) collective-permute-start(bf16[4,144,128]{2,1,0:T(8,128)(2,1)S(1)} %get-tuple-element.38), channel_id=1, source_target_pairs={{0,16},{4,20},{8,24},{12,28},{16,0},{20,4},{24,8},{28,12},{1,17},{... | collective-permute-start | bytes 442376 | tf_op jit(solution)/shard_map/ppermute | solution.py:396
  25.7 9.3 %copy-start.2 = (f32[4]{0:T(128)S(1)}, f32[4]{0:T(128)}, u32[]{:S(2)}) copy-start(f32[4]{0:T(128)} %gate_ref.5) | copy-start | bytes 52
  33.4 14.8 %collective-permute-start.10 = (bf16[256,1024]{1,0:T(8,128)(2,1)S(1)}, bf16[256,1024]{1,0:T(8,128)(2,1)S(1)}, u32[]{:S(2)}, u32[]{:S(2)}) collective-permute-start(bf16[256,1024]{1,0:T(8,128)(2,1)S(1)} %get-tuple-element.44), channel_id=1, source_target_pairs={{0,2},{1,3},{2,0},{3,1},{4,6},{5,7},{6,4},{7,5},{8,10},{9,11},{10,... | collective-permute-start | bytes 1572872 | tf_op jit(solution)/shard_map/ppermute | solution.py:396
  36.3 22.2 %collective-permute-start.12 = (bf16[256,1024]{1,0:T(8,128)(2,1)S(1)}, bf16[256,1024]{1,0:T(8,128)(2,1)S(1)}, u32[]{:S(2)}, u32[]{:S(2)}) collective-permute-start(bf16[256,1024]{1,0:T(8,128)(2,1)S(1)} %get-tuple-element.45), channel_id=1, source_target_pairs={{0,3},{1,2},{2,1},{3,0},{4,7},{5,6},{6,5},{7,4},{8,11},{9,10},{10,... | collective-permute-start | bytes 1572872 | tf_op jit(solution)/shard_map/ppermute | solution.py:396
  36.4 54.5 %collective-permute-start.18 = (bf16[512,512]{1,0:T(8,128)(2,1)S(1)}, bf16[512,512]{1,0:T(8,128)(2,1)S(1)}, u32[]{:S(2)}, u32[]{:S(2)}) collective-permute-start(bf16[512,512]{1,0:T(8,128)(2,1)S(1)} %get-tuple-element.46.refs_0_), channel_id=1, source_target_pairs={{0,2},{1,3},{2,0},{3,1},{4,6},{5,7},{6,4},{7,5},{8,10},{9,11},{10,... | collective-permute-start | bytes 1572872 | tf_op jit(solution)/shard_map/ppermute | solution.py:396
  41.2 35.1 %collective-permute-start.7 = (bf16[256,512]{1,0:T(8,128)(2,1)S(1)}, bf16[256,512]{1,0:T(8,128)(2,1)S(1)}, u32[]{:S(2)}, u32[]{:S(2)}) collective-permute-start(bf16[256,512]{1,0:T(8,128)(2,1)S(1)} %shard_map.75.refs_0_), channel_id=1, source_target_pairs={{0,2},{1,3},{2,0},{3,1},{4,6},{5,7},{6,4},{7,5},{8,10},{9,11},{10,... | collective-permute-start | bytes 786440 | tf_op jit(solution)/shard_map/ppermute | solution.py:396
  48.2 32.4 %collective-permute-start.15 = (bf16[256,512]{1,0:T(8,128)(2,1)S(1)}, bf16[256,512]{1,0:T(8,128)(2,1)S(1)}, u32[]{:S(2)}, u32[]{:S(2)}) collective-permute-start(bf16[256,512]{1,0:T(8,128)(2,1)S(1)} %shard_map.76.refs_0_), channel_id=1, source_target_pairs={{0,2},{1,3},{2,0},{3,1},{4,6},{5,7},{6,4},{7,5},{8,10},{9,11},{10,... | collective-permute-start | bytes 786440 | tf_op jit(solution)/shard_map/ppermute | solution.py:396
  58.5 32.5 %collective-permute-start.17 = (bf16[512,512]{1,0:T(8,128)(2,1)S(1)}, bf16[512,512]{1,0:T(8,128)(2,1)S(1)}, u32[]{:S(2)}, u32[]{:S(2)}) collective-permute-start(bf16[512,512]{1,0:T(8,128)(2,1)S(1)} %get-tuple-element.46.refs_0_), channel_id=1, source_target_pairs={{0,1},{1,0},{2,3},{3,2},{4,5},{5,4},{6,7},{7,6},{8,9},{9,8},{10,11... | collective-permute-start | bytes 1572872 | tf_op jit(solution)/shard_map/ppermute | solution.py:396
  76.3 15.2 %collective-permute-start.11 = (bf16[256,1024]{1,0:T(8,128)(2,1)S(1)}, bf16[256,1024]{1,0:T(8,128)(2,1)S(1)}, u32[]{:S(2)}, u32[]{:S(2)}) collective-permute-start(bf16[256,1024]{1,0:T(8,128)(2,1)S(1)} %collective-permute-done.10.refs_6_), channel_id=1, source_target_pairs={{0,8},{4,12},{8,0},{12,4},{16,24},{20,28},{24,16},{28,20},{1,9},{5... | collective-permute-start | bytes 1572872 | tf_op jit(solution)/shard_map/ppermute | solution.py:396
  80.6 18.7 %collective-permute-start.13 = (bf16[256,1024]{1,0:T(8,128)(2,1)S(1)}, bf16[256,1024]{1,0:T(8,128)(2,1)S(1)}, u32[]{:S(2)}, u32[]{:S(2)}) collective-permute-start(bf16[256,1024]{1,0:T(8,128)(2,1)S(1)} %collective-permute-done.12.refs_8_), channel_id=1, source_target_pairs={{0,4},{4,0},{8,12},{12,8},{16,20},{20,16},{24,28},{28,24},{1,5},{5... | collective-permute-start | bytes 1572872 | tf_op jit(solution)/shard_map/ppermute | solution.py:396
  91.0 8.3 %collective-permute-start.19 = (bf16[512,512]{1,0:T(8,128)(2,1)S(1)}, bf16[512,512]{1,0:T(8,128)(2,1)S(1)}, u32[]{:S(2)}, u32[]{:S(2)}) collective-permute-start(bf16[512,512]{1,0:T(8,128)(2,1)S(1)} %collective-permute-done.18.refs_2_), channel_id=1, source_target_pairs={{0,1},{1,0},{2,3},{3,2},{4,5},{5,4},{6,7},{7,6},{8,9},{9,8},{10,11... | collective-permute-start | bytes 1572872 | tf_op jit(solution)/shard_map/ppermute | solution.py:396
  91.0 11.5 %collective-permute-start.14 = (bf16[256,512]{1,0:T(8,128)(2,1)S(1)}, bf16[256,512]{1,0:T(8,128)(2,1)S(1)}, u32[]{:S(2)}, u32[]{:S(2)}) collective-permute-start(bf16[256,512]{1,0:T(8,128)(2,1)S(1)} %shard_map.76.refs_0_), channel_id=1, source_target_pairs={{0,1},{1,0},{2,3},{3,2},{4,5},{5,4},{6,7},{7,6},{8,9},{9,8},{10,11... | collective-permute-start | bytes 786440 | tf_op jit(solution)/shard_map/ppermute | solution.py:396
  91.5 11.0 %collective-permute-start.16 = (bf16[256,512]{1,0:T(8,128)(2,1)S(1)}, bf16[256,512]{1,0:T(8,128)(2,1)S(1)}, u32[]{:S(2)}, u32[]{:S(2)}) collective-permute-start(bf16[256,512]{1,0:T(8,128)(2,1)S(1)} %collective-permute-done.15.refs_2_), channel_id=1, source_target_pairs={{0,1},{1,0},{2,3},{3,2},{4,5},{5,4},{6,7},{7,6},{8,9},{9,8},{10,11... | collective-permute-start | bytes 786440 | tf_op jit(solution)/shard_map/ppermute | solution.py:396
  91.6 13.0 %collective-permute-start.6 = (bf16[256,512]{1,0:T(8,128)(2,1)S(1)}, bf16[256,512]{1,0:T(8,128)(2,1)S(1)}, u32[]{:S(2)}, u32[]{:S(2)}) collective-permute-start(bf16[256,512]{1,0:T(8,128)(2,1)S(1)} %shard_map.75.refs_0_), channel_id=1, source_target_pairs={{0,1},{1,0},{2,3},{3,2},{4,5},{5,4},{6,7},{7,6},{8,9},{9,8},{10,11... | collective-permute-start | bytes 786440 | tf_op jit(solution)/shard_map/ppermute | solution.py:396
  99.2 5.3 %collective-permute-start.8 = (bf16[256,512]{1,0:T(8,128)(2,1)S(1)}, bf16[256,512]{1,0:T(8,128)(2,1)S(1)}, u32[]{:S(2)}, u32[]{:S(2)}) collective-permute-start(bf16[256,512]{1,0:T(8,128)(2,1)S(1)} %collective-permute-done.7.refs_2_), channel_id=1, source_target_pairs={{0,1},{1,0},{2,3},{3,2},{4,5},{5,4},{6,7},{7,6},{8,9},{9,8},{10,11... | collective-permute-start | bytes 786440 | tf_op jit(solution)/shard_map/ppermute | solution.py:396

commit v5 on v4

--- a/solution.py
+++ b/solution.py
@@ -15,7 +15,7 @@
 MASKED = -1e30
 BLOCK = 256
 TILE = 256
-HALO = (128, 256)
+LATE = 384
 
 
 SMEM = pl.BlockSpec(memory_space=pltpu.SMEM)
@@ -127,11 +127,12 @@
             store(state_ref, head, memory, total)
             if step == steps - 1:
                 pack(send_ref, head, memory, total)
-    near, far = rows - BAND + HALO[0], rows - BAND + HALO[0] + HALO[1]
-    tails[0][...] = k_buf[rows - BAND : near, :]
-    tails[1][...] = k_buf[near:far, :]
-    tails[2][: rows - far, :] = k_buf[far:, :]
-    tails[2][rows - far :, :] = v_buf[rows - BAND :, :]
+    base = rows - BAND
+    tails[0][...] = k_buf[base + LATE :, :]
+    tails[1][: LATE - BLOCK, :] = k_buf[base + BLOCK : base + LATE, :]
+    tails[1][LATE - BLOCK :, :] = v_buf[base + BLOCK :, :]
+    tails[2][:BLOCK, :] = k_buf[base : base + BLOCK, :]
+    tails[2][BLOCK:, :] = v_buf[base : base + BLOCK, :]
     for copy in moves:
         copy.wait()
 
@@ -140,7 +141,7 @@
     rows, cols = keys.shape
     depth = out_weight.shape[0]
     steps = rows // BLOCK
-    tails = (*HALO, 2 * BAND - sum(HALO))
+    tails = (BAND - LATE, LATE - BLOCK + BAND - BLOCK, 2 * BLOCK)
     return pl.pallas_call(
         functools.partial(state_kernel, slices),
         in_specs=[SMEM, HBM, HBM, HBM, HBM],
@@ -297,19 +298,22 @@
 
 
 def attend_kernel(start, me_ref, spans_ref, gate_ref, q_ref, k_ref, v_ref, *refs):
-    *halo, memory_ref, norm_ref, out_ref, before_ref = refs
+    *halo, memory_ref, norm_ref, out_ref, keys_ref, values_ref = refs
     heads, width = norm_ref.shape[0], norm_ref.shape[2]
-    rows = before_ref.shape[0]
-    near, far = HALO[0], sum(HALO)
-    before_ref[:near, :] = halo[0][...]
-    before_ref[near:far, :] = halo[1][...]
-    before_ref[far:, :] = halo[2][: rows - far, :]
+    rows = q_ref.shape[0] // SPAN_DEV
+    middle = LATE - BLOCK
+    if start == 0:
+        keys_ref[:BLOCK, :] = halo[2][:BLOCK, :]
+        values_ref[:BLOCK, :] = halo[2][BLOCK:, :]
+    keys_ref[BLOCK - start : LATE - start, :] = halo[1][:middle, :]
+    keys_ref[LATE - start :, :] = halo[0][...]
+    values_ref[BLOCK - start :, :] = halo[1][middle:, :]
     for head in range(heads):
         at = slice(head * width, (head + 1) * width)
         query = q_ref[start : start + BLOCK, at]
         local = local_block(
-            0, start, me_ref, spans_ref, query, before_ref[start:, at],
-            halo[2][rows - far + start :, at], k_ref[:rows, at], v_ref[:rows, at],
+            0, start, me_ref, spans_ref, query, keys_ref[:, at], values_ref[:, at],
+            k_ref[:rows, at], v_ref[:rows, at],
         )
         out_ref[:, at] = read_block(
             query, memory_ref[head], norm_ref[head, :1, :], gate_ref[head], local
@@ -318,13 +322,15 @@
 
 def make_attend(start, queries, keys, values, halo, memory, norm, spans, me, gate):
     rows, cols = queries.shape[0] // SPAN_DEV, queries.shape[1]
+    halo = halo if start == 0 else halo[:2]
+    before = pltpu.VMEM((BAND - start, cols), BF16)
     operands = [*map(in_vmem, (queries, keys, values, *halo)), memory, norm]
     return pl.pallas_call(
         functools.partial(attend_kernel, start),
         in_specs=[SMEM] * 3 + [VMEM] * len(operands),
         out_specs=VMEM,
         out_shape=pltpu.VMEM((BLOCK, cols), BF16),
-        scratch_shapes=[pltpu.VMEM((rows, cols), BF16)],
+        scratch_shapes=[before, before],
         compiler_params=params(24),
         cost_estimate=cost(8e9, 6 * rows * cols * 2),
     )(me, spans, gate, *operands)
@@ -402,7 +408,7 @@
     heads = mem_gate.shape[0]
     width = queries.shape[1] // heads
     seq_size, head_size = lax.axis_size("seq"), lax.axis_size("head")
-    assert head_size & (head_size - 1) == 0 and seg_rows == BAND * SPAN_DEV
+    assert head_size & (head_size - 1) == 0 and seg_rows == BAND * SPAN_DEV == 4 * BLOCK
     assert seq_size & (seq_size - 1) == 0 and seq_size > 1
     seq_index, head_index = lax.axis_index("seq"), lax.axis_index("head")
     me = seq_index.astype(jnp.int32).reshape(1)
@@ -447,7 +453,7 @@
     local = make_local(queries, keys, values, span_bounds, me, width)
     own, total, norm = make_readout(distance, queries, local, memory, me, mem_decay, mem_gate)
     chunks = [(BAND, own)]
-    for start in range(0, BAND, BLOCK):
+    for start in (BLOCK, 0):
         own = make_attend(
             start, queries, keys,
             values, halo, total, norm, span_bounds, me, mem_gate,
@@ -465,7 +471,8 @@
         order = range(head_size)
         out = project(
             start, seg_rows,
-            [xs[i] for i in order], [weights[i] for i in order], [partners.get(i, 0) for i in order], me, out,
+            [xs[i] for i in order], [weights[i] for i in order],
+            [partners.get(i, 0) for i in order], me, out,
         )
     return out
 

time: 109 us -> 109 us (level)
  starting transfers between devices: 34.6 us -> 32.5 us
  waiting for transfers between devices: 47.6 us -> 49.7 us
    ppermute x17, waiting for transfers between devices: 46.5 us -> 49.7 us  [swap(): return lax.ppermute(x, axis, [(i, i ^ mask) for i in range(size)])]
    ppermute x17, starting transfers between devices: 25.4 us -> 23.3 us  [swap(): return lax.ppermute(x, axis, [(i, i ^ mask) for i in range(size)])]
  transfers between devices with their start and end apart: 20 -> 20, of which waited for: 8 -> 7; matrix products, arithmetic and copies ran while one was open for 0% -> 0% of each run, Pallas kernels for 17% -> 17%
where the time goes in v5:
time: 109 us; the launch traced here: 107 us
  waiting for transfers between devices  49.7 us (46%)
  starting transfers between devices  32.5 us (30%)
  Pallas kernels  24.2 us (22%)
    ppermute x17, waiting for transfers between devices, swap(): return lax.ppermute(x, axis, [(i, i ^ mask) for i in range(size)])  49.7 us
    ppermute x17, starting transfers between devices, swap(): return lax.ppermute(x, axis, [(i, i ^ mask) for i in range(size)])  23.3 us
    ppermute x3, starting transfers between devices, body(): lax.ppermute(tail, 'seq', [(i, i + 1) for i in range(seq_size - 1)])  9.14 us
    pallas_call x3, Pallas kernels, project(): pl.pallas_call(functools.partial(project_kernel, partners, start), in_spe...  7.29 us
    pallas_call x2, Pallas kernels, make_attend(): pl.pallas_call(functools.partial(attend_kernel, start), in_specs=[SMEM] *...  6.01 us
    pallas_call x1, Pallas kernels, make_local(): pl.pallas_call(functools.partial(local_kernel, width), in_specs=[SMEM, SM...  4.59 us
    pallas_call x1, Pallas kernels, make_state(): pl.pallas_call(functools.partial(state_kernel, slices), in_specs=[SMEM, H...  3.64 us
  transfers between devices with their start and end apart: 20, of which 7 were waited for; matrix products, arithmetic and copies ran while one was open for 0% of the time, Pallas kernels for 17%

profile of v5, /device:TPU:0, one launch (start us, length us, event | category | flops | bytes accessed | tf_op | source)
XLA Modules:
  0.0 106.6 jit_solution(9121091837836754623)
XLA Ops:
  0.0 0.1 pad_add_fusion.at_ref
  0.1 3.6 %state.1 = (f32[4,136,128]{2,1,0:T(8,128)S(1)}, bf16[4,144,128]{2,1,0:T(8,128)(2,1)S(1)}, bf16[1024,512]{1,0:T(8,128)(2,1)S(1)}, bf16[1024,512]{1,0:T(8,128)(2,1...) custom-call(s32[2]{0:T(128)S(1)} %pad_add_fusion.at_ref, ...), custom_call_target="tpu_custom_call" | custom-call | flops 10000000000 | bytes 4194304 | tf_op jit(solution)/shard_map/state/pallas_call | solution.py:145
  3.7 3.0 %collective-permute-start.3 = (bf16[4,144,128]{2,1,0:T(8,128)(2,1)S(1)}, bf16[4,144,128]{2,1,0:T(8,128)(2,1)S(1)}, u32[]{:S(2)}, u32[]{:S(2)}) collective-permute-start(bf16[4,144,128]{2,1,0:T(8,128)(2,1)S(1)} %get-tuple-element.32), channel_id=1, source_target_pairs={{0,4},{4,0},{8,12},{12,8},{16,20},{20,16},{24,28},{28,24},{1,5},{5... | collective-permute-start | bytes 442376 | tf_op jit(solution)/shard_map/ppermute | solution.py:402
  6.7 3.8 %collective-permute-done.3.refs_0_ = bf16[4,144,128]{2,1,0:T(8,128)(2,1)S(1)} collective-permute-done((bf16[4,144,128]{2,1,0:T(8,128)(2,1)S(1)}, bf16[4,144,128]{2,1,0:T(8,128)(2,1)S(1)}, u32[]{:S(2)}, u32[]{:S(2)}) %collective-permute-start.3) | collective-permute-done | bytes 147488 | tf_op jit(solution)/shard_map/ppermute | solution.py:402
  10.6 0.6 shard_map.73
  11.2 1.9 %collective-permute-start.4 = (bf16[4,144,128]{2,1,0:T(8,128)(2,1)S(1)}, bf16[4,144,128]{2,1,0:T(8,128)(2,1)S(1)}, u32[]{:S(2)}, u32[]{:S(2)}) collective-permute-start(bf16[4,144,128]{2,1,0:T(8,128)(2,1)S(1)} %get-tuple-element.35), channel_id=1, source_target_pairs={{0,8},{4,12},{8,0},{12,4},{16,24},{20,28},{24,16},{28,20},{1,9},{5... | collective-permute-start | bytes 442376 | tf_op jit(solution)/shard_map/ppermute | solution.py:402
  13.1 3.4 %collective-permute-start = (bf16[128,512]{1,0:T(8,128)(2,1)S(1)}, bf16[128,512]{1,0:T(8,128)(2,1)S(1)}, u32[]{:S(2)}, u32[]{:S(2)}) collective-permute-start(bf16[128,512]{1,0:T(8,128)(2,1)S(1)} %get-tuple-element.29), channel_id=1, source_target_pairs={{0,4},{4,8},{8,12},{12,16},{16,20},{20,24},{24,28},{1,5},{5,9},{9,... | collective-permute-start | bytes 393224 | tf_op jit(solution)/shard_map/ppermute | solution.py:433
  16.5 2.1 %collective-permute-start.1 = (bf16[384,512]{1,0:T(8,128)(2,1)S(1)}, bf16[384,512]{1,0:T(8,128)(2,1)S(1)}, u32[]{:S(2)}, u32[]{:S(2)}) collective-permute-start(bf16[384,512]{1,0:T(8,128)(2,1)S(1)} %get-tuple-element.30), channel_id=1, source_target_pairs={{0,4},{4,8},{8,12},{12,16},{16,20},{20,24},{24,28},{1,5},{5,9},{9,... | collective-permute-start | bytes 1179656 | tf_op jit(solution)/shard_map/ppermute | solution.py:433
  18.6 3.7 %collective-permute-start.2 = (bf16[512,512]{1,0:T(8,128)(2,1)S(1)}, bf16[512,512]{1,0:T(8,128)(2,1)S(1)}, u32[]{:S(2)}, u32[]{:S(2)}) collective-permute-start(bf16[512,512]{1,0:T(8,128)(2,1)S(1)} %get-tuple-element.31), channel_id=1, source_target_pairs={{0,4},{4,8},{8,12},{12,16},{16,20},{20,24},{24,28},{1,5},{5,9},{9,... | collective-permute-start | bytes 1572872 | tf_op jit(solution)/shard_map/ppermute | solution.py:433
  22.4 0.7 shard_map.74
  23.1 2.6 %collective-permute-start.5 = (bf16[4,144,128]{2,1,0:T(8,128)(2,1)S(1)}, bf16[4,144,128]{2,1,0:T(8,128)(2,1)S(1)}, u32[]{:S(2)}, u32[]{:S(2)}) collective-permute-start(bf16[4,144,128]{2,1,0:T(8,128)(2,1)S(1)} %get-tuple-element.38), channel_id=1, source_target_pairs={{0,16},{4,20},{8,24},{12,28},{16,0},{20,4},{24,8},{28,12},{1,17},{... | collective-permute-start | bytes 442376 | tf_op jit(solution)/shard_map/ppermute | solution.py:402
  25.7 4.6 %local.1.local_ref = f32[512,512]{1,0:T(8,128)S(1)} custom-call(s32[1]{0:T(128)} %bitcast.me_ref, s32[2,16]{1,0:T(2,128)S(1)} %bitcast.7, bf16[1024,512]{1,0:T(8,128)(2,1)S(1)} %get-tuple-element.26.q_ref, bf16[1024,512]{1,0:T(8,128)(2,1)S(1)} %get-tuple-element.27.k_ref, bf16[1024,512]{1,0:T(8,128)(2,1)S(1)} %get-tuple-element.28.v_ref), custom_call_target="tpu_custom_call" | custom-call | flops 15000000512 | bytes 3145728 | tf_op jit(solution)/shard_map/local/pallas_call | solution.py:249
  30.3 3.1 %collective-permute-done.5.refs_1_ = bf16[4,144,128]{2,1,0:T(8,128)(2,1)S(1)} collective-permute-done((bf16[4,144,128]{2,1,0:T(8,128)(2,1)S(1)}, bf16[4,144,128]{2,1,0:T(8,128)(2,1)S(1)}, u32[]{:S(2)}, u32[]{:S(2)}) %collective-permute-start.5) | collective-permute-done | bytes 147488 | tf_op jit(solution)/shard_map/ppermute | solution.py:402
  33.4 1.5 %collective-permute-start.10 = (bf16[256,1024]{1,0:T(8,128)(2,1)S(1)}, bf16[256,1024]{1,0:T(8,128)(2,1)S(1)}, u32[]{:S(2)}, u32[]{:S(2)}) collective-permute-start(bf16[256,1024]{1,0:T(8,128)(2,1)S(1)} %get-tuple-element.44), channel_id=1, source_target_pairs={{0,2},{1,3},{2,0},{3,1},{4,6},{5,7},{6,4},{7,5},{8,10},{9,11},{10,... | collective-permute-start | bytes 1572872 | tf_op jit(solution)/shard_map/ppermute | solution.py:402
  34.9 1.4 %readout.1 = (bf16[512,512]{1,0:T(8,128)(2,1)S(1)}, bf16[4,256,256]{2,1,0:T(8,128)(2,1)S(1)}, f32[4,8,128]{2,1,0:T(8,128)S(1)}) custom-call(s32[1]{0:T(128)} %bitcast.me_ref, f32[4,8]{1,0:T(4,128)S(1)} %bitcast.6, f32[4]{0:T(128)S(1)} %copy-done.2, bf16[1024,512]{1,0:T(8,128)(2,1)S(1)} %get-tuple-element.26.q_ref, f32[512,512]{1,0:T(8,128)S(1)} %local.1.local_ref, ...), custom_call_target="tpu_custom_call" | custom-call | flops 2000000000 | bytes 2097152 | tf_op jit(solution)/shard_map/readout/pallas_call | solution.py:285
  36.4 2.7 %shard_map.76.refs_0_ = bf16[256,512]{1,0:T(8,128)(2,1)S(1)} custom-call(s32[1]{0:T(128)} %bitcast.me_ref, s32[2,16]{1,0:T(2,128)S(1)} %bitcast.8, f32[4]{0:T(128)S(1)} %copy-done.2, bf16[1024,512]{1,0:T(8,128)(2,1)S(1)} %get-tuple-element.26.q_ref, bf16[1024,512]{1,0:T(8,128)(2,1)S(1)} %get-tuple-element.27.k_ref, ...), custom_call_target="tpu_custom_call" | custom-call | flops 8000000000 | bytes 3145728 | tf_op jit(solution)/shard_map/pallas_call | solution.py:328
  39.1 1.0 collective-permute-start.15
  40.2 1.1 %collective-permute-start.18 = (bf16[512,512]{1,0:T(8,128)(2,1)S(1)}, bf16[512,512]{1,0:T(8,128)(2,1)S(1)}, u32[]{:S(2)}, u32[]{:S(2)}) collective-permute-start(bf16[512,512]{1,0:T(8,128)(2,1)S(1)} %get-tuple-element.46.refs_0_), channel_id=1, source_target_pairs={{0,2},{1,3},{2,0},{3,1},{4,6},{5,7},{6,4},{7,5},{8,10},{9,11},{10,... | collective-permute-start | bytes 1572872 | tf_op jit(solution)/shard_map/ppermute | solution.py:402
  41.2 3.3 %shard_map.75.refs_0_ = bf16[256,512]{1,0:T(8,128)(2,1)S(1)} custom-call(s32[1]{0:T(128)} %bitcast.me_ref, s32[2,16]{1,0:T(2,128)S(1)} %bitcast.9, f32[4]{0:T(128)S(1)} %copy-done.2, bf16[1024,512]{1,0:T(8,128)(2,1)S(1)} %get-tuple-element.26.q_ref, bf16[1024,512]{1,0:T(8,128)(2,1)S(1)} %get-tuple-element.27.k_ref, ...), custom_call_target="tpu_custom_call" | custom-call | flops 8000000000 | bytes 3145728 | tf_op jit(solution)/shard_map/pallas_call | solution.py:328
  44.5 3.7 %collective-permute-done.10.refs_6_ = bf16[256,1024]{1,0:T(8,128)(2,1)S(1)} collective-permute-done((bf16[256,1024]{1,0:T(8,128)(2,1)S(1)}, bf16[256,1024]{1,0:T(8,128)(2,1)S(1)}, u32[]{:S(2)}, u32[]{:S(2)}) %collective-permute-start.10) | collective-permute-done | bytes 524320 | tf_op jit(solution)/shard_map/ppermute | solution.py:402
  48.2 1.5 %collective-permute-start.7 = (bf16[256,512]{1,0:T(8,128)(2,1)S(1)}, bf16[256,512]{1,0:T(8,128)(2,1)S(1)}, u32[]{:S(2)}, u32[]{:S(2)}) collective-permute-start(bf16[256,512]{1,0:T(8,128)(2,1)S(1)} %shard_map.75.refs_0_), channel_id=1, source_target_pairs={{0,2},{1,3},{2,0},{3,1},{4,6},{5,7},{6,4},{7,5},{8,10},{9,11},{10,... | collective-permute-start | bytes 786440 | tf_op jit(solution)/shard_map/ppermute | solution.py:402
  49.7 8.8 %collective-permute-done.12.refs_8_ = bf16[256,1024]{1,0:T(8,128)(2,1)S(1)} collective-permute-done((bf16[256,1024]{1,0:T(8,128)(2,1)S(1)}, bf16[256,1024]{1,0:T(8,128)(2,1)S(1)}, u32[]{:S(2)}, u32[]{:S(2)}) %collective-permute-start.12) | collective-permute-done | bytes 524320 | tf_op jit(solution)/shard_map/ppermute | solution.py:402
  58.5 0.8 collective-permute-start.17
  59.3 5.8 %collective-permute-done.15.refs_2_ = bf16[256,512]{1,0:T(8,128)(2,1)S(1)} collective-permute-done((bf16[256,512]{1,0:T(8,128)(2,1)S(1)}, bf16[256,512]{1,0:T(8,128)(2,1)S(1)}, u32[]{:S(2)}, u32[]{:S(2)}) %collective-permute-start.15) | collective-permute-done | bytes 262176 | tf_op jit(solution)/shard_map/ppermute | solution.py:402
  65.1 15.5 %collective-permute-done.7.refs_2_ = bf16[256,512]{1,0:T(8,128)(2,1)S(1)} collective-permute-done((bf16[256,512]{1,0:T(8,128)(2,1)S(1)}, bf16[256,512]{1,0:T(8,128)(2,1)S(1)}, u32[]{:S(2)}, u32[]{:S(2)}) %collective-permute-start.7) | collective-permute-done | bytes 262176 | tf_op jit(solution)/shard_map/ppermute | solution.py:402
  80.6 8.7 %collective-permute-start.13 = (bf16[256,1024]{1,0:T(8,128)(2,1)S(1)}, bf16[256,1024]{1,0:T(8,128)(2,1)S(1)}, u32[]{:S(2)}, u32[]{:S(2)}) collective-permute-start(bf16[256,1024]{1,0:T(8,128)(2,1)S(1)} %collective-permute-done.12.refs_8_), channel_id=1, source_target_pairs={{0,4},{4,0},{8,12},{12,8},{16,20},{20,16},{24,28},{28,24},{1,5},{5... | collective-permute-start | bytes 1572872 | tf_op jit(solution)/shard_map/ppermute | solution.py:402
  89.3 0.5 collective-permute-start.14
  89.9 0.4 collective-permute-start.6
  90.3 8.9 %collective-permute-done.13.refs_9_ = bf16[256,1024]{1,0:T(8,128)(2,1)S(1)} collective-permute-done((bf16[256,1024]{1,0:T(8,128)(2,1)S(1)}, bf16[256,1024]{1,0:T(8,128)(2,1)S(1)}, u32[]{:S(2)}, u32[]{:S(2)}) %collective-permute-start.13) | collective-permute-done | bytes 524320 | tf_op jit(solution)/shard_map/ppermute | solution.py:402
  99.3 3.2 %shard_map.77.refs_10_ = bf16[1024,1024]{1,0:T(8,128)(2,1)} custom-call(s32[1]{0:T(128)} %bitcast.me_ref, bf16[512,512]{1,0:T(8,128)(2,1)S(1)} %get-tuple-element.46.refs_0_, bf16[512,512]{1,0:T(8,128)(2,1)S(1)} %collective-permute-done.17.refs_1_, bf16[512,512]{1,0:T(8,128)(2,1)S(1)} %collective-permute-done.18.refs_2_, ...), custom_call_target="tpu_custom_call" | custom-call | flops 2147483648 | bytes 4194304 | tf_op jit(solution)/shard_map/pallas_call | solution.py:385
  102.5 2.0 %shard_map.78.refs_10_ = bf16[1024,1024]{1,0:T(8,128)(2,1)} custom-call(s32[1]{0:T(128)} %bitcast.me_ref, bf16[256,512]{1,0:T(8,128)(2,1)S(1)} %shard_map.76.refs_0_, bf16[256,512]{1,0:T(8,128)(2,1)S(1)} %collective-permute-done.14.refs_1_, bf16[256,512]{1,0:T(8,128)(2,1)S(1)} %collective-permute-done.15.refs_2_, ...), custom_call_target="tpu_custom_call", output_to_operand_aliasing={{}: (11, {})} | custom-call | flops 1073741824 | bytes 4194304 | tf_op jit(solution)/shard_map/pallas_call | solution.py:385
  104.6 2.0 %shard_map.79 = bf16[1024,1024]{1,0:T(8,128)(2,1)} custom-call(s32[1]{0:T(128)} %bitcast.me_ref, bf16[256,512]{1,0:T(8,128)(2,1)S(1)} %shard_map.75.refs_0_, bf16[256,512]{1,0:T(8,128)(2,1)S(1)} %collective-permute-done.6.refs_1_, bf16[256,512]{1,0:T(8,128)(2,1)S(1)} %collective-permute-done.7.refs_2_, ...), custom_call_target="tpu_custom_call", output_to_operand_aliasing={{}: (11, {})} | custom-call | flops 1073741824 | bytes 4194304 | tf_op jit(solution)/shard_map/pallas_call | solution.py:385
  (25 shorter events, 0.3 us)
Async XLA Ops:
  0.1 10.5 %copy-start = (f32[8,4]{0,1:T(4,128)S(1)}, f32[8,4]{0,1:T(4,128)}, u32[]{:S(2)}) copy-start(f32[8,4]{0,1:T(4,128)} %param.11) | copy-start | bytes 388
  3.7 6.9 %collective-permute-start.3 = (bf16[4,144,128]{2,1,0:T(8,128)(2,1)S(1)}, bf16[4,144,128]{2,1,0:T(8,128)(2,1)S(1)}, u32[]{:S(2)}, u32[]{:S(2)}) collective-permute-start(bf16[4,144,128]{2,1,0:T(8,128)(2,1)S(1)} %get-tuple-element.32), channel_id=1, source_target_pairs={{0,4},{4,0},{8,12},{12,8},{16,20},{20,16},{24,28},{28,24},{1,5},{5... | collective-permute-start | bytes 442376 | tf_op jit(solution)/shard_map/ppermute | solution.py:402
  11.2 14.4 %copy-start.1 = (s32[16,2]{0,1:T(2,128)S(1)}, s32[16,2]{0,1:T(2,128)}, u32[]{:S(2)}) copy-start(s32[16,2]{0,1:T(2,128)} %param.10) | copy-start | bytes 388
  11.2 11.1 %collective-permute-start.4 = (bf16[4,144,128]{2,1,0:T(8,128)(2,1)S(1)}, bf16[4,144,128]{2,1,0:T(8,128)(2,1)S(1)}, u32[]{:S(2)}, u32[]{:S(2)}) collective-permute-start(bf16[4,144,128]{2,1,0:T(8,128)(2,1)S(1)} %get-tuple-element.35), channel_id=1, source_target_pairs={{0,8},{4,12},{8,0},{12,4},{16,24},{20,28},{24,16},{28,20},{1,9},{5... | collective-permute-start | bytes 442376 | tf_op jit(solution)/shard_map/ppermute | solution.py:402
  13.1 23.2 %collective-permute-start = (bf16[128,512]{1,0:T(8,128)(2,1)S(1)}, bf16[128,512]{1,0:T(8,128)(2,1)S(1)}, u32[]{:S(2)}, u32[]{:S(2)}) collective-permute-start(bf16[128,512]{1,0:T(8,128)(2,1)S(1)} %get-tuple-element.29), channel_id=1, source_target_pairs={{0,4},{4,8},{8,12},{12,16},{16,20},{20,24},{24,28},{1,5},{5,9},{9,... | collective-permute-start | bytes 393224 | tf_op jit(solution)/shard_map/ppermute | solution.py:433
  16.5 19.9 %collective-permute-start.1 = (bf16[384,512]{1,0:T(8,128)(2,1)S(1)}, bf16[384,512]{1,0:T(8,128)(2,1)S(1)}, u32[]{:S(2)}, u32[]{:S(2)}) collective-permute-start(bf16[384,512]{1,0:T(8,128)(2,1)S(1)} %get-tuple-element.30), channel_id=1, source_target_pairs={{0,4},{4,8},{8,12},{12,16},{16,20},{20,24},{24,28},{1,5},{5,9},{9,... | collective-permute-start | bytes 1179656 | tf_op jit(solution)/shard_map/ppermute | solution.py:433
  18.6 21.5 %collective-permute-start.2 = (bf16[512,512]{1,0:T(8,128)(2,1)S(1)}, bf16[512,512]{1,0:T(8,128)(2,1)S(1)}, u32[]{:S(2)}, u32[]{:S(2)}) collective-permute-start(bf16[512,512]{1,0:T(8,128)(2,1)S(1)} %get-tuple-element.31), channel_id=1, source_target_pairs={{0,4},{4,8},{8,12},{12,16},{16,20},{20,24},{24,28},{1,5},{5,9},{9,... | collective-permute-start | bytes 1572872 | tf_op jit(solution)/shard_map/ppermute | solution.py:433
  22.3 67.5 %collective-permute-start.9 = (bf16[512,1024]{1,0:T(8,128)(2,1)S(1)}, bf16[512,1024]{1,0:T(8,128)(2,1)S(1)}, u32[]{:S(2)}, u32[]{:S(2)}) collective-permute-start(bf16[512,1024]{1,0:T(8,128)(2,1)S(1)} %get-tuple-element.43), channel_id=1, source_target_pairs={{0,1},{1,0},{2,3},{3,2},{4,5},{5,4},{6,7},{7,6},{8,9},{9,8},{10,11... | collective-permute-start | bytes 3145736 | tf_op jit(solution)/shard_map/ppermute | solution.py:402
  23.1 10.4 %collective-permute-start.5 = (bf16[4,144,128]{2,1,0:T(8,128)(2,1)S(1)}, bf16[4,144,128]{2,1,0:T(8,128)(2,1)S(1)}, u32[]{:S(2)}, u32[]{:S(2)}) collective-permute-start(bf16[4,144,128]{2,1,0:T(8,128)(2,1)S(1)} %get-tuple-element.38), channel_id=1, source_target_pairs={{0,16},{4,20},{8,24},{12,28},{16,0},{20,4},{24,8},{28,12},{1,17},{... | collective-permute-start | bytes 442376 | tf_op jit(solution)/shard_map/ppermute | solution.py:402
  25.7 9.3 %copy-start.2 = (f32[4]{0:T(128)S(1)}, f32[4]{0:T(128)}, u32[]{:S(2)}) copy-start(f32[4]{0:T(128)} %gate_ref.5) | copy-start | bytes 52
  33.4 14.8 %collective-permute-start.10 = (bf16[256,1024]{1,0:T(8,128)(2,1)S(1)}, bf16[256,1024]{1,0:T(8,128)(2,1)S(1)}, u32[]{:S(2)}, u32[]{:S(2)}) collective-permute-start(bf16[256,1024]{1,0:T(8,128)(2,1)S(1)} %get-tuple-element.44), channel_id=1, source_target_pairs={{0,2},{1,3},{2,0},{3,1},{4,6},{5,7},{6,4},{7,5},{8,10},{9,11},{10,... | collective-permute-start | bytes 1572872 | tf_op jit(solution)/shard_map/ppermute | solution.py:402
  36.3 22.2 %collective-permute-start.12 = (bf16[256,1024]{1,0:T(8,128)(2,1)S(1)}, bf16[256,1024]{1,0:T(8,128)(2,1)S(1)}, u32[]{:S(2)}, u32[]{:S(2)}) collective-permute-start(bf16[256,1024]{1,0:T(8,128)(2,1)S(1)} %get-tuple-element.45), channel_id=1, source_target_pairs={{0,3},{1,2},{2,1},{3,0},{4,7},{5,6},{6,5},{7,4},{8,11},{9,10},{10,... | collective-permute-start | bytes 1572872 | tf_op jit(solution)/shard_map/ppermute | solution.py:402
  39.1 25.9 %collective-permute-start.15 = (bf16[256,512]{1,0:T(8,128)(2,1)S(1)}, bf16[256,512]{1,0:T(8,128)(2,1)S(1)}, u32[]{:S(2)}, u32[]{:S(2)}) collective-permute-start(bf16[256,512]{1,0:T(8,128)(2,1)S(1)} %shard_map.76.refs_0_), channel_id=1, source_target_pairs={{0,2},{1,3},{2,0},{3,1},{4,6},{5,7},{6,4},{7,5},{8,10},{9,11},{10,... | collective-permute-start | bytes 786440 | tf_op jit(solution)/shard_map/ppermute | solution.py:402
  40.2 49.1 %collective-permute-start.18 = (bf16[512,512]{1,0:T(8,128)(2,1)S(1)}, bf16[512,512]{1,0:T(8,128)(2,1)S(1)}, u32[]{:S(2)}, u32[]{:S(2)}) collective-permute-start(bf16[512,512]{1,0:T(8,128)(2,1)S(1)} %get-tuple-element.46.refs_0_), channel_id=1, source_target_pairs={{0,2},{1,3},{2,0},{3,1},{4,6},{5,7},{6,4},{7,5},{8,10},{9,11},{10,... | collective-permute-start | bytes 1572872 | tf_op jit(solution)/shard_map/ppermute | solution.py:402
  48.2 32.4 %collective-permute-start.7 = (bf16[256,512]{1,0:T(8,128)(2,1)S(1)}, bf16[256,512]{1,0:T(8,128)(2,1)S(1)}, u32[]{:S(2)}, u32[]{:S(2)}) collective-permute-start(bf16[256,512]{1,0:T(8,128)(2,1)S(1)} %shard_map.75.refs_0_), channel_id=1, source_target_pairs={{0,2},{1,3},{2,0},{3,1},{4,6},{5,7},{6,4},{7,5},{8,10},{9,11},{10,... | collective-permute-start | bytes 786440 | tf_op jit(solution)/shard_map/ppermute | solution.py:402
  58.5 30.8 %collective-permute-start.17 = (bf16[512,512]{1,0:T(8,128)(2,1)S(1)}, bf16[512,512]{1,0:T(8,128)(2,1)S(1)}, u32[]{:S(2)}, u32[]{:S(2)}) collective-permute-start(bf16[512,512]{1,0:T(8,128)(2,1)S(1)} %get-tuple-element.46.refs_0_), channel_id=1, source_target_pairs={{0,1},{1,0},{2,3},{3,2},{4,5},{5,4},{6,7},{7,6},{8,9},{9,8},{10,11... | collective-permute-start | bytes 1572872 | tf_op jit(solution)/shard_map/ppermute | solution.py:402
  65.1 24.8 %collective-permute-start.11 = (bf16[256,1024]{1,0:T(8,128)(2,1)S(1)}, bf16[256,1024]{1,0:T(8,128)(2,1)S(1)}, u32[]{:S(2)}, u32[]{:S(2)}) collective-permute-start(bf16[256,1024]{1,0:T(8,128)(2,1)S(1)} %collective-permute-done.10.refs_6_), channel_id=1, source_target_pairs={{0,8},{4,12},{8,0},{12,4},{16,24},{20,28},{24,16},{28,20},{1,9},{5... | collective-permute-start | bytes 1572872 | tf_op jit(solution)/shard_map/ppermute | solution.py:402
  80.6 18.7 %collective-permute-start.13 = (bf16[256,1024]{1,0:T(8,128)(2,1)S(1)}, bf16[256,1024]{1,0:T(8,128)(2,1)S(1)}, u32[]{:S(2)}, u32[]{:S(2)}) collective-permute-start(bf16[256,1024]{1,0:T(8,128)(2,1)S(1)} %collective-permute-done.12.refs_8_), channel_id=1, source_target_pairs={{0,4},{4,0},{8,12},{12,8},{16,20},{20,16},{24,28},{28,24},{1,5},{5... | collective-permute-start | bytes 1572872 | tf_op jit(solution)/shard_map/ppermute | solution.py:402
  89.3 10.0 %collective-permute-start.19 = (bf16[512,512]{1,0:T(8,128)(2,1)S(1)}, bf16[512,512]{1,0:T(8,128)(2,1)S(1)}, u32[]{:S(2)}, u32[]{:S(2)}) collective-permute-start(bf16[512,512]{1,0:T(8,128)(2,1)S(1)} %collective-permute-done.18.refs_2_), channel_id=1, source_target_pairs={{0,1},{1,0},{2,3},{3,2},{4,5},{5,4},{6,7},{7,6},{8,9},{9,8},{10,11... | collective-permute-start | bytes 1572872 | tf_op jit(solution)/shard_map/ppermute | solution.py:402
  89.3 13.2 %collective-permute-start.14 = (bf16[256,512]{1,0:T(8,128)(2,1)S(1)}, bf16[256,512]{1,0:T(8,128)(2,1)S(1)}, u32[]{:S(2)}, u32[]{:S(2)}) collective-permute-start(bf16[256,512]{1,0:T(8,128)(2,1)S(1)} %shard_map.76.refs_0_), channel_id=1, source_target_pairs={{0,1},{1,0},{2,3},{3,2},{4,5},{5,4},{6,7},{7,6},{8,9},{9,8},{10,11... | collective-permute-start | bytes 786440 | tf_op jit(solution)/shard_map/ppermute | solution.py:402
  89.8 12.7 %collective-permute-start.16 = (bf16[256,512]{1,0:T(8,128)(2,1)S(1)}, bf16[256,512]{1,0:T(8,128)(2,1)S(1)}, u32[]{:S(2)}, u32[]{:S(2)}) collective-permute-start(bf16[256,512]{1,0:T(8,128)(2,1)S(1)} %collective-permute-done.15.refs_2_), channel_id=1, source_target_pairs={{0,1},{1,0},{2,3},{3,2},{4,5},{5,4},{6,7},{7,6},{8,9},{9,8},{10,11... | collective-permute-start | bytes 786440 | tf_op jit(solution)/shard_map/ppermute | solution.py:402
  89.9 14.7 %collective-permute-start.6 = (bf16[256,512]{1,0:T(8,128)(2,1)S(1)}, bf16[256,512]{1,0:T(8,128)(2,1)S(1)}, u32[]{:S(2)}, u32[]{:S(2)}) collective-permute-start(bf16[256,512]{1,0:T(8,128)(2,1)S(1)} %shard_map.75.refs_0_), channel_id=1, source_target_pairs={{0,1},{1,0},{2,3},{3,2},{4,5},{5,4},{6,7},{7,6},{8,9},{9,8},{10,11... | collective-permute-start | bytes 786440 | tf_op jit(solution)/shard_map/ppermute | solution.py:402
  99.3 5.3 %collective-permute-start.8 = (bf16[256,512]{1,0:T(8,128)(2,1)S(1)}, bf16[256,512]{1,0:T(8,128)(2,1)S(1)}, u32[]{:S(2)}, u32[]{:S(2)}) collective-permute-start(bf16[256,512]{1,0:T(8,128)(2,1)S(1)} %collective-permute-done.7.refs_2_), channel_id=1, source_target_pairs={{0,1},{1,0},{2,3},{3,2},{4,5},{5,4},{6,7},{7,6},{8,9},{9,8},{10,11... | collective-permute-start | bytes 786440 | tf_op jit(solution)/shard_map/ppermute | solution.py:402

commit v6 on v5

--- a/solution.py
+++ b/solution.py
@@ -79,9 +79,10 @@
 def slice_copies(slices, at_ref, w_hbm, blocks, sems):
     me, head_index = at_ref[0], at_ref[1]
     copies = []
-    for number, (mask, partner) in enumerate(slices):
+    for number, (mask, partner, part) in enumerate(slices):
         rows, columns = blocks[number].shape
-        row = jnp.where((me & partner) != 0, rows, 0) if partner else 0
+        half = w_hbm.shape[0] // 2
+        row = part * rows + (jnp.where((me & partner) != 0, half, 0) if partner else 0)
         col = pl.multiple_of((head_index ^ mask) * columns, columns)
         source = w_hbm.at[pl.ds(pl.multiple_of(row, rows), rows), pl.ds(col, columns)]
         copies.append(pltpu.make_async_copy(source, blocks[number], sems.at[number]))
@@ -128,9 +129,10 @@
             if step == steps - 1:
                 pack(send_ref, head, memory, total)
     base = rows - BAND
+    middle = LATE - BLOCK
     tails[0][...] = k_buf[base + LATE :, :]
-    tails[1][: LATE - BLOCK, :] = k_buf[base + BLOCK : base + LATE, :]
-    tails[1][LATE - BLOCK :, :] = v_buf[base + BLOCK :, :]
+    tails[1][:middle, :] = k_buf[base + BLOCK : base + LATE, :]
+    tails[1][middle:, :] = v_buf[base + BLOCK :, :]
     tails[2][:BLOCK, :] = k_buf[base : base + BLOCK, :]
     tails[2][BLOCK:, :] = v_buf[base : base + BLOCK, :]
     for copy in moves:
@@ -140,6 +142,8 @@
 def make_state(queries, keys, values, out_weight, slices, at, heads, width, columns):
     rows, cols = keys.shape
     depth = out_weight.shape[0]
+    split_in = [sum(other[0] == mask for other in slices) for mask, _, _ in slices]
+    sizes = [depth // (2 * n if by else n) for n, (_, by, _) in zip(split_in, slices)]
     steps = rows // BLOCK
     tails = (BAND - LATE, LATE - BLOCK + BAND - BLOCK, 2 * BLOCK)
     return pl.pallas_call(
@@ -151,7 +155,7 @@
             pltpu.VMEM((heads, width + SEND_PAD, width), BF16),
             *[pltpu.VMEM((rows, cols), BF16)] * 3,
             *(pltpu.VMEM((tail, cols), BF16) for tail in tails),
-            *(pltpu.VMEM((depth // (2 if by else 1), columns), BF16) for _, by in slices),
+            *(pltpu.VMEM((rows_, columns), BF16) for rows_ in sizes),
         ],
         scratch_shapes=[
             pltpu.SemaphoreType.DMA((2, steps)),
@@ -322,8 +326,8 @@
 
 def make_attend(start, queries, keys, values, halo, memory, norm, spans, me, gate):
     rows, cols = queries.shape[0] // SPAN_DEV, queries.shape[1]
+    before = pltpu.VMEM((BAND - start, cols), BF16)
     halo = halo if start == 0 else halo[:2]
-    before = pltpu.VMEM((BAND - start, cols), BF16)
     operands = [*map(in_vmem, (queries, keys, values, *halo)), memory, norm]
     return pl.pallas_call(
         functools.partial(attend_kernel, start),
@@ -336,65 +340,73 @@
     )(me, spans, gate, *operands)
 
 
-def project_kernel(partners, first_row, me_ref, *refs):
-    *refs, out_hbm, out_ref, sems = refs
-    xs, ws = refs[: len(partners)], list(refs[len(partners) :])
-    rows, columns = out_ref.shape
+def project_kernel(plan, first_row, adds, done, me_ref, *refs):
+    if done:
+        *refs, out_hbm, out_ref, sems = refs
+    else:
+        *refs, out_ref = refs
+    refs = list(refs)
+    copies = []
+    for number, row in enumerate(done):
+        ready = refs.pop()
+        target = out_hbm.at[pl.ds(row, ready.shape[0])]
+        copies.append(pltpu.make_async_copy(ready, target, sems.at[number]))
+        copies[-1].start()
     me = me_ref[0]
     lefts, rights = [], []
-    for x_ref, partner in zip(xs, partners):
-        if partner:
+    for pieces in plan:
+        x_ref = refs.pop(0)
+        parts = []
+        for piece in pieces:
+            if piece is None:
+                parts.append(x_ref[...])
+                continue
+            partner, count, part, own = piece
             half = x_ref.shape[1] // 2
+            size = half // count
             mine = jnp.where((me & partner) != 0, half, 0)
-            parts = [x_ref[:, pl.ds(pl.multiple_of(at, half), half)] for at in (mine, half - mine)]
-            lefts.append(jnp.concatenate(parts, axis=1))
-            rights.append((ws.pop(0), ws.pop(0)))
-        else:
-            lefts.append(x_ref[...])
-            rights.append((ws.pop(0),))
-    copies = []
-    for number, start in enumerate(range(0, columns, TILE)):
+            at = (mine if own else half - mine) + part * size
+            parts.append(x_ref[:, pl.ds(pl.multiple_of(at, size), size)])
+        lefts.append(jnp.concatenate(parts, axis=1) if len(parts) > 1 else parts[0])
+    for pieces in plan:
+        rights.append([refs.pop(0) for _ in pieces])
+    sums_ref = refs.pop(0) if adds else None
+    rows, columns = out_ref.shape
+    for number, start in enumerate(range(0, columns, TILE), len(done)):
         at = slice(start, start + TILE)
-        acc = None
+        acc = sums_ref[:, at] if adds else None
         for left, right in zip(lefts, rights):
             block = [w_ref[:, at] for w_ref in right]
             block = jnp.concatenate(block, axis=0) if len(block) > 1 else block[0]
             term = jnp.dot(left, block, preferred_element_type=F32)
             acc = term if acc is None else acc + term
         out_ref[:, at] = acc.astype(out_ref.dtype)
-        target = out_hbm.at[pl.ds(first_row, rows), pl.ds(start, TILE)]
-        copy = pltpu.make_async_copy(out_ref.at[:, pl.ds(start, TILE)], target, sems.at[number])
-        copy.start()
-        copies.append(copy)
+        if done:
+            target = out_hbm.at[pl.ds(first_row, rows), pl.ds(start, TILE)]
+            source = out_ref.at[:, pl.ds(start, TILE)]
+            copies.append(pltpu.make_async_copy(source, target, sems.at[number]))
+            copies[-1].start()
     for copy in copies:
         copy.wait()
 
 
-def project(start, total_rows, xs, weights, partners, me, out):
-    rows = xs[0].shape[0]
-    flat = [w for ws in weights for w in ws]
-    columns = flat[0].shape[1]
-    operands = [me, *map(in_vmem, xs), *map(in_vmem, flat)]
-    in_specs = [SMEM] + [VMEM] * (len(operands) - 1)
-    aliases = {}
-    if out is not None:
-        in_specs.append(HBM)
-        aliases = {len(operands): 0}
-        operands.append(out)
+def project(start, total_rows, dtype, terms, me, sums=None, done=()):
+    xs = [x for x, _ in terms]
+    flat = [w for _, pieces in terms for _, w in pieces]
+    plan = [[kind for kind, _ in pieces] for _, pieces in terms]
+    rows, columns = xs[0].shape[0], flat[0].shape[1]
     depth = sum(w.shape[0] for w in flat)
+    operands = [*xs, *flat, *([] if sums is None else [sums]), *(x for _, x in reversed(done))]
+    copies = pltpu.SemaphoreType.DMA((len(done) + columns // TILE,))
     return pl.pallas_call(
-        functools.partial(project_kernel, partners, start),
-        in_specs=in_specs,
-        out_specs=HBM,
-        out_shape=pltpu.HBM((total_rows, columns), BF16),
-        scratch_shapes=[
-            pltpu.VMEM((rows, columns), BF16),
-            pltpu.SemaphoreType.DMA((columns // TILE,)),
-        ],
-        input_output_aliases=aliases,
+        functools.partial(project_kernel, plan, start, sums is not None, [row for row, _ in done]),
+        in_specs=[SMEM] + [VMEM] * len(operands),
+        out_specs=HBM if done else VMEM,
+        out_shape=pltpu.HBM((total_rows, columns), BF16) if done else pltpu.VMEM((rows, columns), dtype),
+        scratch_shapes=[pltpu.VMEM((rows, columns), BF16), copies] if done else [],
         compiler_params=params(24),
         cost_estimate=cost(2 * rows * depth * columns, depth * columns * 2),
-    )(*operands)
+    )(me, *map(in_vmem, operands))
 
 
 def swap(x, axis, mask):
@@ -415,18 +427,29 @@
     columns = out_weight.shape[1] // head_size
 
     masks = sorted(range(1, head_size), reverse=True)
-    partners = {mask: 1 << (mask % 2 == 0 and seq_size > 2) for mask in masks if mask > 1}
-    slices = [(mask, partners.get(mask, 0)) for mask in (*masks, 0)]
+    partners = {
+        mask: (2, 1) if mask % 2 == 0 and seq_size > 2 else (1, 1) for mask in masks if mask > 1
+    }
+    slices = []
+    for mask in (*masks, 0):
+        partner, parts = partners.get(mask, (0, 1))
+        slices += [(mask, partner, part) for part in range(parts)]
     at = jnp.concatenate([me, head_index.astype(jnp.int32).reshape(1)])
     state, send, *more = make_state(
         queries, keys, values, out_weight, slices, at, heads, width, columns
     )
     queries, keys, values = more[:3]
     tails, blocks = more[3:6], more[6:]
-    weights = {}
-    for (mask, partner), block in zip(slices, blocks):
+    weights = {mask: [] for mask in (*masks, 0)}
+    for (mask, partner, part), block in zip(slices, blocks):
         block = swap(block, "head", mask) if mask else block
-        weights[mask] = (block, swap(block, "seq", partner)) if partner else (block,)
+        if partner:
+            count = partners[mask][1]
+            other = swap(block, "seq", partner)
+            weights[mask].append(((partner, count, part, True), block))
+            weights[mask].append(((partner, count, part, False), other))
+        else:
+            weights[mask].append((None, block))
 
     halo = []
     for tail in tails:
@@ -460,20 +483,27 @@
         )
         chunks.append((start, own))
 
-    out = None
-    for start, own in chunks:
+    done = []
+    for number, (start, own) in enumerate(chunks):
         xs = {0: own}
         mask = head_size // 2
         while mask:
             for at, x in list(xs.items()):
                 xs[at ^ mask] = swap(x, "head", mask)
             mask //= 2
-        order = range(head_size)
+        terms = [(xs[i], weights[i]) for i in range(head_size)]
+        sums = None
+        if number == 0 and partners:
+            late = lambda kind: kind is not None and not kind[3]
+            early = [(x, [w for w in ws if not late(w[0])]) for x, ws in terms]
+            sums = project(start, seg_rows, F32, early, me)
+            terms = [(xs[i], [w for w in weights[i] if late(w[0])]) for i in partners]
+        ready = done if number == len(chunks) - 1 else ()
         out = project(
-            start, seg_rows,
-            [xs[i] for i in order], [weights[i] for i in order],
-            [partners.get(i, 0) for i in order], me, out,
-        )
+            start, seg_rows, BF16, terms, me, sums,
+            ready,
+        )
+        done.append((start, out))
     return out
 
 

time: 109 us -> 107 us (0.982)
  starting transfers between devices: 32.5 us -> 30.6 us
  waiting for transfers between devices: 49.7 us -> 51.5 us
  Pallas kernels: 24.2 us -> 22.7 us
    ppermute x17, starting transfers between devices: 23.3 us -> 21.5 us  [swap(): return lax.ppermute(x, axis, [(i, i ^ mask) for i in range(size)])]
    ppermute x17, waiting for transfers between devices: 49.7 us -> 51.5 us  [swap(): return lax.ppermute(x, axis, [(i, i ^ mask) for i in range(size)])]
    pallas_call x3 -> x4, Pallas kernels: 7.29 us -> 5.81 us  [project(): pl.pallas_call(functools.partial(project_kernel, plan, start, sums is not...]
  transfers between devices with their start and end apart: 20 -> 20, of which waited for: 7 -> 7; matrix products, arithmetic and copies ran while one was open for 0% -> 0% of each run, Pallas kernels for 17% -> 16%
where the time goes in v6:
time: 107 us; the launch traced here: 105 us
  waiting for transfers between devices  51.5 us (48%)
  starting transfers between devices  30.6 us (29%)
  Pallas kernels  22.7 us (21%)
    ppermute x17, waiting for transfers between devices, swap(): return lax.ppermute(x, axis, [(i, i ^ mask) for i in range(size)])  51.5 us
    ppermute x17, starting transfers between devices, swap(): return lax.ppermute(x, axis, [(i, i ^ mask) for i in range(size)])  21.5 us
    ppermute x3, starting transfers between devices, body(): lax.ppermute(tail, 'seq', [(i, i + 1) for i in range(seq_size - 1)])  9.15 us
    pallas_call x2, Pallas kernels, make_attend(): pl.pallas_call(functools.partial(attend_kernel, start), in_specs=[SMEM] *...  6.04 us
    pallas_call x4, Pallas kernels, project(): pl.pallas_call(functools.partial(project_kernel, plan, start, sums is not...  5.81 us
    pallas_call x1, Pallas kernels, make_local(): pl.pallas_call(functools.partial(local_kernel, width), in_specs=[SMEM, SM...  4.54 us
    pallas_call x1, Pallas kernels, make_state(): pl.pallas_call(functools.partial(state_kernel, slices), in_specs=[SMEM, H...  3.63 us
  transfers between devices with their start and end apart: 20, of which 7 were waited for; matrix products, arithmetic and copies ran while one was open for 0% of the time, Pallas kernels for 16%

profile of v6, /device:TPU:0, one launch (start us, length us, event | category | flops | bytes accessed | tf_op | source)
XLA Modules:
  0.0 105.1 jit_solution(13947224313599725156)
XLA Ops:
  0.0 0.1 pad_add_fusion.at_ref
  0.1 3.6 %state.1 = (f32[4,136,128]{2,1,0:T(8,128)S(1)}, bf16[4,144,128]{2,1,0:T(8,128)(2,1)S(1)}, bf16[1024,512]{1,0:T(8,128)(2,1)S(1)}, bf16[1024,512]{1,0:T(8,128)(2,1...) custom-call(s32[2]{0:T(128)S(1)} %pad_add_fusion.at_ref, ...), custom_call_target="tpu_custom_call" | custom-call | flops 10000000000 | bytes 4194304 | tf_op jit(solution)/shard_map/state/pallas_call | solution.py:149
  3.7 3.0 %collective-permute-start.3 = (bf16[4,144,128]{2,1,0:T(8,128)(2,1)S(1)}, bf16[4,144,128]{2,1,0:T(8,128)(2,1)S(1)}, u32[]{:S(2)}, u32[]{:S(2)}) collective-permute-start(bf16[4,144,128]{2,1,0:T(8,128)(2,1)S(1)} %get-tuple-element.32), channel_id=1, source_target_pairs={{0,4},{4,0},{8,12},{12,8},{16,20},{20,16},{24,28},{28,24},{1,5},{5... | collective-permute-start | bytes 442376 | tf_op jit(solution)/shard_map/ppermute | solution.py:414
  6.7 3.9 %collective-permute-done.3.refs_0_ = bf16[4,144,128]{2,1,0:T(8,128)(2,1)S(1)} collective-permute-done((bf16[4,144,128]{2,1,0:T(8,128)(2,1)S(1)}, bf16[4,144,128]{2,1,0:T(8,128)(2,1)S(1)}, u32[]{:S(2)}, u32[]{:S(2)}) %collective-permute-start.3) | collective-permute-done | bytes 147488 | tf_op jit(solution)/shard_map/ppermute | solution.py:414
  10.6 0.6 shard_map.73
  11.3 1.9 %collective-permute-start.4 = (bf16[4,144,128]{2,1,0:T(8,128)(2,1)S(1)}, bf16[4,144,128]{2,1,0:T(8,128)(2,1)S(1)}, u32[]{:S(2)}, u32[]{:S(2)}) collective-permute-start(bf16[4,144,128]{2,1,0:T(8,128)(2,1)S(1)} %get-tuple-element.35), channel_id=1, source_target_pairs={{0,8},{4,12},{8,0},{12,4},{16,24},{20,28},{24,16},{28,20},{1,9},{5... | collective-permute-start | bytes 442376 | tf_op jit(solution)/shard_map/ppermute | solution.py:414
  13.1 3.4 %collective-permute-start = (bf16[128,512]{1,0:T(8,128)(2,1)S(1)}, bf16[128,512]{1,0:T(8,128)(2,1)S(1)}, u32[]{:S(2)}, u32[]{:S(2)}) collective-permute-start(bf16[128,512]{1,0:T(8,128)(2,1)S(1)} %get-tuple-element.29), channel_id=1, source_target_pairs={{0,4},{4,8},{8,12},{12,16},{16,20},{20,24},{24,28},{1,5},{5,9},{9,... | collective-permute-start | bytes 393224 | tf_op jit(solution)/shard_map/ppermute | solution.py:456
  16.5 2.1 %collective-permute-start.1 = (bf16[384,512]{1,0:T(8,128)(2,1)S(1)}, bf16[384,512]{1,0:T(8,128)(2,1)S(1)}, u32[]{:S(2)}, u32[]{:S(2)}) collective-permute-start(bf16[384,512]{1,0:T(8,128)(2,1)S(1)} %get-tuple-element.30), channel_id=1, source_target_pairs={{0,4},{4,8},{8,12},{12,16},{16,20},{20,24},{24,28},{1,5},{5,9},{9,... | collective-permute-start | bytes 1179656 | tf_op jit(solution)/shard_map/ppermute | solution.py:456
  18.6 3.7 %collective-permute-start.2 = (bf16[512,512]{1,0:T(8,128)(2,1)S(1)}, bf16[512,512]{1,0:T(8,128)(2,1)S(1)}, u32[]{:S(2)}, u32[]{:S(2)}) collective-permute-start(bf16[512,512]{1,0:T(8,128)(2,1)S(1)} %get-tuple-element.31), channel_id=1, source_target_pairs={{0,4},{4,8},{8,12},{12,16},{16,20},{20,24},{24,28},{1,5},{5,9},{9,... | collective-permute-start | bytes 1572872 | tf_op jit(solution)/shard_map/ppermute | solution.py:456
  22.4 0.7 shard_map.74
  23.1 2.6 %collective-permute-start.5 = (bf16[4,144,128]{2,1,0:T(8,128)(2,1)S(1)}, bf16[4,144,128]{2,1,0:T(8,128)(2,1)S(1)}, u32[]{:S(2)}, u32[]{:S(2)}) collective-permute-start(bf16[4,144,128]{2,1,0:T(8,128)(2,1)S(1)} %get-tuple-element.38), channel_id=1, source_target_pairs={{0,16},{4,20},{8,24},{12,28},{16,0},{20,4},{24,8},{28,12},{1,17},{... | collective-permute-start | bytes 442376 | tf_op jit(solution)/shard_map/ppermute | solution.py:414
  25.7 4.5 %local.1.local_ref = f32[512,512]{1,0:T(8,128)S(1)} custom-call(s32[1]{0:T(128)} %bitcast.me_ref, s32[2,16]{1,0:T(2,128)S(1)} %bitcast.7, bf16[1024,512]{1,0:T(8,128)(2,1)S(1)} %get-tuple-element.26.q_ref, bf16[1024,512]{1,0:T(8,128)(2,1)S(1)} %get-tuple-element.27.k_ref, bf16[1024,512]{1,0:T(8,128)(2,1)S(1)} %get-tuple-element.28.v_ref), custom_call_target="tpu_custom_call" | custom-call | flops 15000000512 | bytes 3145728 | tf_op jit(solution)/shard_map/local/pallas_call | solution.py:253
  30.2 3.2 %collective-permute-done.5.refs_1_ = bf16[4,144,128]{2,1,0:T(8,128)(2,1)S(1)} collective-permute-done((bf16[4,144,128]{2,1,0:T(8,128)(2,1)S(1)}, bf16[4,144,128]{2,1,0:T(8,128)(2,1)S(1)}, u32[]{:S(2)}, u32[]{:S(2)}) %collective-permute-start.5) | collective-permute-done | bytes 147488 | tf_op jit(solution)/shard_map/ppermute | solution.py:414
  33.4 1.5 %collective-permute-start.10 = (bf16[256,1024]{1,0:T(8,128)(2,1)S(1)}, bf16[256,1024]{1,0:T(8,128)(2,1)S(1)}, u32[]{:S(2)}, u32[]{:S(2)}) collective-permute-start(bf16[256,1024]{1,0:T(8,128)(2,1)S(1)} %get-tuple-element.44), channel_id=1, source_target_pairs={{0,2},{1,3},{2,0},{3,1},{4,6},{5,7},{6,4},{7,5},{8,10},{9,11},{10,... | collective-permute-start | bytes 1572872 | tf_op jit(solution)/shard_map/ppermute | solution.py:414
  34.9 1.4 %readout.1 = (bf16[512,512]{1,0:T(8,128)(2,1)S(1)}, bf16[4,256,256]{2,1,0:T(8,128)(2,1)S(1)}, f32[4,8,128]{2,1,0:T(8,128)S(1)}) custom-call(s32[1]{0:T(128)} %bitcast.me_ref, f32[4,8]{1,0:T(4,128)S(1)} %bitcast.6, f32[4]{0:T(128)S(1)} %copy-done.2, bf16[1024,512]{1,0:T(8,128)(2,1)S(1)} %get-tuple-element.26.q_ref, f32[512,512]{1,0:T(8,128)S(1)} %local.1.local_ref, ...), custom_call_target="tpu_custom_call" | custom-call | flops 2000000000 | bytes 2097152 | tf_op jit(solution)/shard_map/readout/pallas_call | solution.py:289
  36.4 2.7 %shard_map.76.refs_0_ = bf16[256,512]{1,0:T(8,128)(2,1)S(1)} custom-call(s32[1]{0:T(128)} %bitcast.me_ref, s32[2,16]{1,0:T(2,128)S(1)} %bitcast.8, f32[4]{0:T(128)S(1)} %copy-done.2, bf16[1024,512]{1,0:T(8,128)(2,1)S(1)} %get-tuple-element.26.q_ref, bf16[1024,512]{1,0:T(8,128)(2,1)S(1)} %get-tuple-element.27.k_ref, ...), custom_call_target="tpu_custom_call" | custom-call | flops 8000000000 | bytes 3145728 | tf_op jit(solution)/shard_map/pallas_call | solution.py:332
  39.1 1.0 collective-permute-start.15
  40.2 1.1 %collective-permute-start.17 = (bf16[512,512]{1,0:T(8,128)(2,1)S(1)}, bf16[512,512]{1,0:T(8,128)(2,1)S(1)}, u32[]{:S(2)}, u32[]{:S(2)}) collective-permute-start(bf16[512,512]{1,0:T(8,128)(2,1)S(1)} %get-tuple-element.46.refs_0_), channel_id=1, source_target_pairs={{0,2},{1,3},{2,0},{3,1},{4,6},{5,7},{6,4},{7,5},{8,10},{9,11},{10,... | collective-permute-start | bytes 1572872 | tf_op jit(solution)/shard_map/ppermute | solution.py:414
  41.2 3.3 %shard_map.75.refs_0_ = bf16[256,512]{1,0:T(8,128)(2,1)S(1)} custom-call(s32[1]{0:T(128)} %bitcast.me_ref, s32[2,16]{1,0:T(2,128)S(1)} %bitcast.9, f32[4]{0:T(128)S(1)} %copy-done.2, bf16[1024,512]{1,0:T(8,128)(2,1)S(1)} %get-tuple-element.26.q_ref, bf16[1024,512]{1,0:T(8,128)(2,1)S(1)} %get-tuple-element.27.k_ref, ...), custom_call_target="tpu_custom_call" | custom-call | flops 8000000000 | bytes 3145728 | tf_op jit(solution)/shard_map/pallas_call | solution.py:332
  44.6 3.7 %collective-permute-done.10.refs_6_ = bf16[256,1024]{1,0:T(8,128)(2,1)S(1)} collective-permute-done((bf16[256,1024]{1,0:T(8,128)(2,1)S(1)}, bf16[256,1024]{1,0:T(8,128)(2,1)S(1)}, u32[]{:S(2)}, u32[]{:S(2)}) %collective-permute-start.10) | collective-permute-done | bytes 524320 | tf_op jit(solution)/shard_map/ppermute | solution.py:414
  48.2 10.3 %collective-permute-done.12.refs_8_.refs_7_ = bf16[256,1024]{1,0:T(8,128)(2,1)S(1)} collective-permute-done((bf16[256,1024]{1,0:T(8,128)(2,1)S(1)}, bf16[256,1024]{1,0:T(8,128)(2,1)S(1)}, u32[]{:S(2)}, u32[]{:S(2)}) %collective-permute-start.12) | collective-permute-done | bytes 524320 | tf_op jit(solution)/shard_map/ppermute | solution.py:414
  58.5 0.5 collective-permute-start.7
  59.0 6.1 %collective-permute-done.15.refs_2_ = bf16[256,512]{1,0:T(8,128)(2,1)S(1)} collective-permute-done((bf16[256,512]{1,0:T(8,128)(2,1)S(1)}, bf16[256,512]{1,0:T(8,128)(2,1)S(1)}, u32[]{:S(2)}, u32[]{:S(2)}) %collective-permute-start.15) | collective-permute-done | bytes 262176 | tf_op jit(solution)/shard_map/ppermute | solution.py:414
  65.1 15.5 %collective-permute-done.7.refs_2_ = bf16[256,512]{1,0:T(8,128)(2,1)S(1)} collective-permute-done((bf16[256,512]{1,0:T(8,128)(2,1)S(1)}, bf16[256,512]{1,0:T(8,128)(2,1)S(1)}, u32[]{:S(2)}, u32[]{:S(2)}) %collective-permute-start.7) | collective-permute-done | bytes 262176 | tf_op jit(solution)/shard_map/ppermute | solution.py:414
  80.6 8.7 %collective-permute-start.13 = (bf16[256,1024]{1,0:T(8,128)(2,1)S(1)}, bf16[256,1024]{1,0:T(8,128)(2,1)S(1)}, u32[]{:S(2)}, u32[]{:S(2)}) collective-permute-start(bf16[256,1024]{1,0:T(8,128)(2,1)S(1)} %collective-permute-done.12.refs_8_.refs_7_), channel_id=1, source_target_pairs={{0,4},{4,0},{8,12},{12,8},{16,20},{20,16},{24,28},{28,24},{1,5},{5... | collective-permute-start | bytes 1572872 | tf_op jit(solution)/shard_map/ppermute | solution.py:414
  89.3 0.5 collective-permute-start.18
  89.9 0.4 collective-permute-start.8
  90.3 8.9 %collective-permute-done.13.refs_9_.refs_2_ = bf16[256,1024]{1,0:T(8,128)(2,1)S(1)} collective-permute-done((bf16[256,1024]{1,0:T(8,128)(2,1)S(1)}, bf16[256,1024]{1,0:T(8,128)(2,1)S(1)}, u32[]{:S(2)}, u32[]{:S(2)}) %collective-permute-start.13) | collective-permute-done | bytes 524320 | tf_op jit(solution)/shard_map/ppermute | solution.py:414
  99.2 1.3 %shard_map.77.refs_10_ = bf16[256,1024]{1,0:T(8,128)(2,1)S(1)} custom-call(s32[1]{0:T(128)} %bitcast.me_ref, bf16[256,512]{1,0:T(8,128)(2,1)S(1)} %shard_map.76.refs_0_, bf16[256,512]{1,0:T(8,128)(2,1)S(1)} %collective-permute-done.14.refs_1_, bf16[256,512]{1,0:T(8,128)(2,1)S(1)} %collective-permute-done.15.refs_2_, ...), custom_call_target="tpu_custom_call" | custom-call | flops 1073741824 | bytes 4194304 | tf_op jit(solution)/shard_map/pallas_call | solution.py:401
  100.5 1.8 %shard_map.78.refs_4_ = f32[512,1024]{1,0:T(8,128)S(1)} custom-call(s32[1]{0:T(128)} %bitcast.me_ref, bf16[512,512]{1,0:T(8,128)(2,1)S(1)} %get-tuple-element.46.refs_0_, bf16[512,512]{1,0:T(8,128)(2,1)S(1)} %collective-permute-done.19.refs_1_, bf16[512,512]{1,0:T(8,128)(2,1)S(1)} %collective-permute-done.17.refs_2_.refs_1_, ...), custom_call_target="tpu_custom_call" | custom-call | flops 1610612736 | bytes 3145728 | tf_op jit(solution)/shard_map/pallas_call | solution.py:401
  102.3 0.7 shard_map.79.refs_11_
  103.1 2.0 %shard_map.80 = bf16[1024,1024]{1,0:T(8,128)(2,1)} custom-call(s32[1]{0:T(128)} %bitcast.me_ref, bf16[256,512]{1,0:T(8,128)(2,1)S(1)} %shard_map.75.refs_0_, bf16[256,512]{1,0:T(8,128)(2,1)S(1)} %collective-permute-done.6.refs_1_, bf16[256,512]{1,0:T(8,128)(2,1)S(1)} %collective-permute-done.7.refs_2_, bf16[256,512]{1,0:T(8,128)(2,1)S(1)} %collective-permute-done.8.refs_3_, ...), custom_call_target="tpu_custom_call" | custom-call | flops 1073741824 | bytes 4194304 | tf_op jit(solution)/shard_map/pallas_call | solution.py:401
  (26 shorter events, 0.3 us)
Async XLA Ops:
  0.1 10.5 %copy-start = (f32[8,4]{0,1:T(4,128)S(1)}, f32[8,4]{0,1:T(4,128)}, u32[]{:S(2)}) copy-start(f32[8,4]{0,1:T(4,128)} %param.11) | copy-start | bytes 388
  3.7 6.9 %collective-permute-start.3 = (bf16[4,144,128]{2,1,0:T(8,128)(2,1)S(1)}, bf16[4,144,128]{2,1,0:T(8,128)(2,1)S(1)}, u32[]{:S(2)}, u32[]{:S(2)}) collective-permute-start(bf16[4,144,128]{2,1,0:T(8,128)(2,1)S(1)} %get-tuple-element.32), channel_id=1, source_target_pairs={{0,4},{4,0},{8,12},{12,8},{16,20},{20,16},{24,28},{28,24},{1,5},{5... | collective-permute-start | bytes 442376 | tf_op jit(solution)/shard_map/ppermute | solution.py:414
  11.2 14.4 %copy-start.1 = (s32[16,2]{0,1:T(2,128)S(1)}, s32[16,2]{0,1:T(2,128)}, u32[]{:S(2)}) copy-start(s32[16,2]{0,1:T(2,128)} %param.10) | copy-start | bytes 388
  11.3 11.1 %collective-permute-start.4 = (bf16[4,144,128]{2,1,0:T(8,128)(2,1)S(1)}, bf16[4,144,128]{2,1,0:T(8,128)(2,1)S(1)}, u32[]{:S(2)}, u32[]{:S(2)}) collective-permute-start(bf16[4,144,128]{2,1,0:T(8,128)(2,1)S(1)} %get-tuple-element.35), channel_id=1, source_target_pairs={{0,8},{4,12},{8,0},{12,4},{16,24},{20,28},{24,16},{28,20},{1,9},{5... | collective-permute-start | bytes 442376 | tf_op jit(solution)/shard_map/ppermute | solution.py:414
  13.1 23.2 %collective-permute-start = (bf16[128,512]{1,0:T(8,128)(2,1)S(1)}, bf16[128,512]{1,0:T(8,128)(2,1)S(1)}, u32[]{:S(2)}, u32[]{:S(2)}) collective-permute-start(bf16[128,512]{1,0:T(8,128)(2,1)S(1)} %get-tuple-element.29), channel_id=1, source_target_pairs={{0,4},{4,8},{8,12},{12,16},{16,20},{20,24},{24,28},{1,5},{5,9},{9,... | collective-permute-start | bytes 393224 | tf_op jit(solution)/shard_map/ppermute | solution.py:456
  16.5 19.9 %collective-permute-start.1 = (bf16[384,512]{1,0:T(8,128)(2,1)S(1)}, bf16[384,512]{1,0:T(8,128)(2,1)S(1)}, u32[]{:S(2)}, u32[]{:S(2)}) collective-permute-start(bf16[384,512]{1,0:T(8,128)(2,1)S(1)} %get-tuple-element.30), channel_id=1, source_target_pairs={{0,4},{4,8},{8,12},{12,16},{16,20},{20,24},{24,28},{1,5},{5,9},{9,... | collective-permute-start | bytes 1179656 | tf_op jit(solution)/shard_map/ppermute | solution.py:456
  18.6 21.5 %collective-permute-start.2 = (bf16[512,512]{1,0:T(8,128)(2,1)S(1)}, bf16[512,512]{1,0:T(8,128)(2,1)S(1)}, u32[]{:S(2)}, u32[]{:S(2)}) collective-permute-start(bf16[512,512]{1,0:T(8,128)(2,1)S(1)} %get-tuple-element.31), channel_id=1, source_target_pairs={{0,4},{4,8},{8,12},{12,16},{16,20},{20,24},{24,28},{1,5},{5,9},{9,... | collective-permute-start | bytes 1572872 | tf_op jit(solution)/shard_map/ppermute | solution.py:456
  22.3 67.5 %collective-permute-start.9 = (bf16[512,1024]{1,0:T(8,128)(2,1)S(1)}, bf16[512,1024]{1,0:T(8,128)(2,1)S(1)}, u32[]{:S(2)}, u32[]{:S(2)}) collective-permute-start(bf16[512,1024]{1,0:T(8,128)(2,1)S(1)} %get-tuple-element.43), channel_id=1, source_target_pairs={{0,1},{1,0},{2,3},{3,2},{4,5},{5,4},{6,7},{7,6},{8,9},{9,8},{10,11... | collective-permute-start | bytes 3145736 | tf_op jit(solution)/shard_map/ppermute | solution.py:414
  23.1 10.4 %collective-permute-start.5 = (bf16[4,144,128]{2,1,0:T(8,128)(2,1)S(1)}, bf16[4,144,128]{2,1,0:T(8,128)(2,1)S(1)}, u32[]{:S(2)}, u32[]{:S(2)}) collective-permute-start(bf16[4,144,128]{2,1,0:T(8,128)(2,1)S(1)} %get-tuple-element.38), channel_id=1, source_target_pairs={{0,16},{4,20},{8,24},{12,28},{16,0},{20,4},{24,8},{28,12},{1,17},{... | collective-permute-start | bytes 442376 | tf_op jit(solution)/shard_map/ppermute | solution.py:414
  25.7 9.3 %copy-start.2 = (f32[4]{0:T(128)S(1)}, f32[4]{0:T(128)}, u32[]{:S(2)}) copy-start(f32[4]{0:T(128)} %gate_ref.5) | copy-start | bytes 52
  33.4 14.8 %collective-permute-start.10 = (bf16[256,1024]{1,0:T(8,128)(2,1)S(1)}, bf16[256,1024]{1,0:T(8,128)(2,1)S(1)}, u32[]{:S(2)}, u32[]{:S(2)}) collective-permute-start(bf16[256,1024]{1,0:T(8,128)(2,1)S(1)} %get-tuple-element.44), channel_id=1, source_target_pairs={{0,2},{1,3},{2,0},{3,1},{4,6},{5,7},{6,4},{7,5},{8,10},{9,11},{10,... | collective-permute-start | bytes 1572872 | tf_op jit(solution)/shard_map/ppermute | solution.py:414
  36.3 22.2 %collective-permute-start.12 = (bf16[256,1024]{1,0:T(8,128)(2,1)S(1)}, bf16[256,1024]{1,0:T(8,128)(2,1)S(1)}, u32[]{:S(2)}, u32[]{:S(2)}) collective-permute-start(bf16[256,1024]{1,0:T(8,128)(2,1)S(1)} %get-tuple-element.45), channel_id=1, source_target_pairs={{0,3},{1,2},{2,1},{3,0},{4,7},{5,6},{6,5},{7,4},{8,11},{9,10},{10,... | collective-permute-start | bytes 1572872 | tf_op jit(solution)/shard_map/ppermute | solution.py:414
  39.1 25.9 %collective-permute-start.15 = (bf16[256,512]{1,0:T(8,128)(2,1)S(1)}, bf16[256,512]{1,0:T(8,128)(2,1)S(1)}, u32[]{:S(2)}, u32[]{:S(2)}) collective-permute-start(bf16[256,512]{1,0:T(8,128)(2,1)S(1)} %shard_map.76.refs_0_), channel_id=1, source_target_pairs={{0,2},{1,3},{2,0},{3,1},{4,6},{5,7},{6,4},{7,5},{8,10},{9,11},{10,... | collective-permute-start | bytes 786440 | tf_op jit(solution)/shard_map/ppermute | solution.py:414
  40.2 49.1 %collective-permute-start.17 = (bf16[512,512]{1,0:T(8,128)(2,1)S(1)}, bf16[512,512]{1,0:T(8,128)(2,1)S(1)}, u32[]{:S(2)}, u32[]{:S(2)}) collective-permute-start(bf16[512,512]{1,0:T(8,128)(2,1)S(1)} %get-tuple-element.46.refs_0_), channel_id=1, source_target_pairs={{0,2},{1,3},{2,0},{3,1},{4,6},{5,7},{6,4},{7,5},{8,10},{9,11},{10,... | collective-permute-start | bytes 1572872 | tf_op jit(solution)/shard_map/ppermute | solution.py:414
  48.2 16.9 %collective-permute-start.14 = (bf16[256,512]{1,0:T(8,128)(2,1)S(1)}, bf16[256,512]{1,0:T(8,128)(2,1)S(1)}, u32[]{:S(2)}, u32[]{:S(2)}) collective-permute-start(bf16[256,512]{1,0:T(8,128)(2,1)S(1)} %shard_map.76.refs_0_), channel_id=1, source_target_pairs={{0,1},{1,0},{2,3},{3,2},{4,5},{5,4},{6,7},{7,6},{8,9},{9,8},{10,11... | collective-permute-start | bytes 786440 | tf_op jit(solution)/shard_map/ppermute | solution.py:414
  58.5 22.1 %collective-permute-start.7 = (bf16[256,512]{1,0:T(8,128)(2,1)S(1)}, bf16[256,512]{1,0:T(8,128)(2,1)S(1)}, u32[]{:S(2)}, u32[]{:S(2)}) collective-permute-start(bf16[256,512]{1,0:T(8,128)(2,1)S(1)} %shard_map.75.refs_0_), channel_id=1, source_target_pairs={{0,2},{1,3},{2,0},{3,1},{4,6},{5,7},{6,4},{7,5},{8,10},{9,11},{10,... | collective-permute-start | bytes 786440 | tf_op jit(solution)/shard_map/ppermute | solution.py:414
  65.1 24.2 %collective-permute-start.16 = (bf16[256,512]{1,0:T(8,128)(2,1)S(1)}, bf16[256,512]{1,0:T(8,128)(2,1)S(1)}, u32[]{:S(2)}, u32[]{:S(2)}) collective-permute-start(bf16[256,512]{1,0:T(8,128)(2,1)S(1)} %collective-permute-done.15.refs_2_), channel_id=1, source_target_pairs={{0,1},{1,0},{2,3},{3,2},{4,5},{5,4},{6,7},{7,6},{8,9},{9,8},{10,11... | collective-permute-start | bytes 786440 | tf_op jit(solution)/shard_map/ppermute | solution.py:414
  65.1 24.8 %collective-permute-start.11 = (bf16[256,1024]{1,0:T(8,128)(2,1)S(1)}, bf16[256,1024]{1,0:T(8,128)(2,1)S(1)}, u32[]{:S(2)}, u32[]{:S(2)}) collective-permute-start(bf16[256,1024]{1,0:T(8,128)(2,1)S(1)} %collective-permute-done.10.refs_6_), channel_id=1, source_target_pairs={{0,8},{4,12},{8,0},{12,4},{16,24},{20,28},{24,16},{28,20},{1,9},{5... | collective-permute-start | bytes 1572872 | tf_op jit(solution)/shard_map/ppermute | solution.py:414
  80.6 18.6 %collective-permute-start.13 = (bf16[256,1024]{1,0:T(8,128)(2,1)S(1)}, bf16[256,1024]{1,0:T(8,128)(2,1)S(1)}, u32[]{:S(2)}, u32[]{:S(2)}) collective-permute-start(bf16[256,1024]{1,0:T(8,128)(2,1)S(1)} %collective-permute-done.12.refs_8_.refs_7_), channel_id=1, source_target_pairs={{0,4},{4,0},{8,12},{12,8},{16,20},{20,16},{24,28},{28,24},{1,5},{5... | collective-permute-start | bytes 1572872 | tf_op jit(solution)/shard_map/ppermute | solution.py:414
  89.3 11.2 %collective-permute-start.19 = (bf16[512,512]{1,0:T(8,128)(2,1)S(1)}, bf16[512,512]{1,0:T(8,128)(2,1)S(1)}, u32[]{:S(2)}, u32[]{:S(2)}) collective-permute-start(bf16[512,512]{1,0:T(8,128)(2,1)S(1)} %get-tuple-element.46.refs_0_), channel_id=1, source_target_pairs={{0,1},{1,0},{2,3},{3,2},{4,5},{5,4},{6,7},{7,6},{8,9},{9,8},{10,11... | collective-permute-start | bytes 1572872 | tf_op jit(solution)/shard_map/ppermute | solution.py:414
  89.3 11.2 %collective-permute-start.18 = (bf16[512,512]{1,0:T(8,128)(2,1)S(1)}, bf16[512,512]{1,0:T(8,128)(2,1)S(1)}, u32[]{:S(2)}, u32[]{:S(2)}) collective-permute-start(bf16[512,512]{1,0:T(8,128)(2,1)S(1)} %collective-permute-done.17.refs_2_.refs_1_), channel_id=1, source_target_pairs={{0,1},{1,0},{2,3},{3,2},{4,5},{5,4},{6,7},{7,6},{8,9},{9,8},{10,11... | collective-permute-start | bytes 1572872 | tf_op jit(solution)/shard_map/ppermute | solution.py:414
  89.8 13.3 %collective-permute-start.6 = (bf16[256,512]{1,0:T(8,128)(2,1)S(1)}, bf16[256,512]{1,0:T(8,128)(2,1)S(1)}, u32[]{:S(2)}, u32[]{:S(2)}) collective-permute-start(bf16[256,512]{1,0:T(8,128)(2,1)S(1)} %shard_map.75.refs_0_), channel_id=1, source_target_pairs={{0,1},{1,0},{2,3},{3,2},{4,5},{5,4},{6,7},{7,6},{8,9},{9,8},{10,11... | collective-permute-start | bytes 786440 | tf_op jit(solution)/shard_map/ppermute | solution.py:414
  89.9 13.2 %collective-permute-start.8 = (bf16[256,512]{1,0:T(8,128)(2,1)S(1)}, bf16[256,512]{1,0:T(8,128)(2,1)S(1)}, u32[]{:S(2)}, u32[]{:S(2)}) collective-permute-start(bf16[256,512]{1,0:T(8,128)(2,1)S(1)} %collective-permute-done.7.refs_2_), channel_id=1, source_target_pairs={{0,1},{1,0},{2,3},{3,2},{4,5},{5,4},{6,7},{7,6},{8,9},{9,8},{10,11... | collective-permute-start | bytes 786440 | tf_op jit(solution)/shard_map/ppermute | solution.py:414

commit v7 on v6

--- a/solution.py
+++ b/solution.py
@@ -15,6 +15,7 @@
 MASKED = -1e30
 BLOCK = 256
 TILE = 256
+EARLY = 320
 LATE = 384
 
 
@@ -129,12 +130,12 @@
             if step == steps - 1:
                 pack(send_ref, head, memory, total)
     base = rows - BAND
-    middle = LATE - BLOCK
+    middle = LATE - EARLY
     tails[0][...] = k_buf[base + LATE :, :]
-    tails[1][:middle, :] = k_buf[base + BLOCK : base + LATE, :]
-    tails[1][middle:, :] = v_buf[base + BLOCK :, :]
-    tails[2][:BLOCK, :] = k_buf[base : base + BLOCK, :]
-    tails[2][BLOCK:, :] = v_buf[base : base + BLOCK, :]
+    tails[1][:middle, :] = k_buf[base + EARLY : base + LATE, :]
+    tails[1][middle:, :] = v_buf[base + EARLY :, :]
+    tails[2][:EARLY, :] = k_buf[base : base + EARLY, :]
+    tails[2][EARLY:, :] = v_buf[base : base + EARLY, :]
     for copy in moves:
         copy.wait()
 
@@ -145,7 +146,7 @@
     split_in = [sum(other[0] == mask for other in slices) for mask, _, _ in slices]
     sizes = [depth // (2 * n if by else n) for n, (_, by, _) in zip(split_in, slices)]
     steps = rows // BLOCK
-    tails = (BAND - LATE, LATE - BLOCK + BAND - BLOCK, 2 * BLOCK)
+    tails = (BAND - LATE, LATE - EARLY + BAND - EARLY, 2 * EARLY)
     return pl.pallas_call(
         functools.partial(state_kernel, slices),
         in_specs=[SMEM, HBM, HBM, HBM, HBM],
@@ -200,7 +201,7 @@
         pack(send_ref, head, *both)
 
 
-def local_block(half, start, me_ref, spans_ref, query, keys_before, values_before, keys, values):
+def local_block(half, start, base, me_ref, spans_ref, query, keys_before, values_before, keys, values):
     me = me_ref[0]
     rows, width = keys.shape
     factor = math.log2(math.e) / math.sqrt(width)
@@ -213,7 +214,7 @@
     own = lax.dot_general(query, keys, dims, preferred_element_type=F32)
     row = start + lax.broadcasted_iota(jnp.int32, (query.shape[0], 1), 0)
     limit = jnp.where((row >= first) & (row < end), end - 1, row)
-    col = lax.broadcasted_iota(jnp.int32, prev.shape, 1) + start
+    col = lax.broadcasted_iota(jnp.int32, prev.shape, 1) + base
     prev = jnp.where(col > row + shift, prev, MASKED)
     col = lax.broadcasted_iota(jnp.int32, own.shape, 1)
     own = jnp.where(col <= limit, own, MASKED)
@@ -243,7 +244,7 @@
         at = slice(head * width, (head + 1) * width)
         for start in range(0, rows, BLOCK):
             out_ref[start : start + BLOCK, at] = local_block(
-                1, start, me_ref, spans_ref, q_ref[rows + start : rows + start + BLOCK, at],
+                1, start, start, me_ref, spans_ref, q_ref[rows + start : rows + start + BLOCK, at],
                 k_ref[start:rows, at], v_ref[start:rows, at], k_ref[rows:, at], v_ref[rows:, at],
             )
 
@@ -301,22 +302,25 @@
     )(me, decay, gate, *map(in_vmem, (queries, local)), *memory)
 
 
-def attend_kernel(start, me_ref, spans_ref, gate_ref, q_ref, k_ref, v_ref, *refs):
+def attend_kernel(start, base, me_ref, spans_ref, gate_ref, q_ref, k_ref, v_ref, *refs):
     *halo, memory_ref, norm_ref, out_ref, keys_ref, values_ref = refs
     heads, width = norm_ref.shape[0], norm_ref.shape[2]
     rows = q_ref.shape[0] // SPAN_DEV
-    middle = LATE - BLOCK
+    middle = LATE - EARLY
     if start == 0:
-        keys_ref[:BLOCK, :] = halo[2][:BLOCK, :]
-        values_ref[:BLOCK, :] = halo[2][BLOCK:, :]
-    keys_ref[BLOCK - start : LATE - start, :] = halo[1][:middle, :]
-    keys_ref[LATE - start :, :] = halo[0][...]
-    values_ref[BLOCK - start :, :] = halo[1][middle:, :]
+        keys_ref[:EARLY, :] = halo[2][:EARLY, :]
+        values_ref[:EARLY, :] = halo[2][EARLY:, :]
+    elif base < EARLY:
+        for ref in (keys_ref, values_ref):
+            ref[: EARLY - base, :] = jnp.zeros((EARLY - base, ref.shape[1]), ref.dtype)
+    keys_ref[EARLY - base : LATE - base, :] = halo[1][:middle, :]
+    keys_ref[LATE - base :, :] = halo[0][...]
+    values_ref[EARLY - base :, :] = halo[1][middle:, :]
     for head in range(heads):
         at = slice(head * width, (head + 1) * width)
-        query = q_ref[start : start + BLOCK, at]
+        query = q_ref[start : start + out_ref.shape[0], at]
         local = local_block(
-            0, start, me_ref, spans_ref, query, keys_ref[:, at], values_ref[:, at],
+            0, start, base, me_ref, spans_ref, query, keys_ref[:, at], values_ref[:, at],
             k_ref[:rows, at], v_ref[:rows, at],
         )
         out_ref[:, at] = read_block(
@@ -324,16 +328,17 @@
         )
 
 
-def make_attend(start, queries, keys, values, halo, memory, norm, spans, me, gate):
+def make_attend(start, size, queries, keys, values, halo, memory, norm, spans, me, gate):
     rows, cols = queries.shape[0] // SPAN_DEV, queries.shape[1]
-    before = pltpu.VMEM((BAND - start, cols), BF16)
+    base = start // BLOCK * BLOCK
+    before = pltpu.VMEM((BAND - base, cols), BF16)
     halo = halo if start == 0 else halo[:2]
     operands = [*map(in_vmem, (queries, keys, values, *halo)), memory, norm]
     return pl.pallas_call(
-        functools.partial(attend_kernel, start),
+        functools.partial(attend_kernel, start, base),
         in_specs=[SMEM] * 3 + [VMEM] * len(operands),
         out_specs=VMEM,
-        out_shape=pltpu.VMEM((BLOCK, cols), BF16),
+        out_shape=pltpu.VMEM((size, cols), BF16),
         scratch_shapes=[before, before],
         compiler_params=params(24),
         cost_estimate=cost(8e9, 6 * rows * cols * 2),
@@ -476,10 +481,10 @@
     local = make_local(queries, keys, values, span_bounds, me, width)
     own, total, norm = make_readout(distance, queries, local, memory, me, mem_decay, mem_gate)
     chunks = [(BAND, own)]
-    for start in (BLOCK, 0):
+    for start, size in ((EARLY, BAND - EARLY), (0, EARLY)):
         own = make_attend(
-            start, queries, keys,
-            values, halo, total, norm, span_bounds, me, mem_gate,
+            start, size, queries, keys, values,
+            halo, total, norm, span_bounds, me, mem_gate,
         )
         chunks.append((start, own))
 

time: 107 us -> 97 us (0.907); the launches traced: 105 us -> 96.6 us
  waiting for transfers between devices: 51.5 us -> 36.8 us
  starting transfers between devices: 30.6 us -> 36.6 us
    ppermute x17, waiting for transfers between devices: 51.5 us -> 36.8 us  [swap(): return lax.ppermute(x, axis, [(i, i ^ mask) for i in range(size)])]
    ppermute x17, starting transfers between devices: 21.5 us -> 27.4 us  [swap(): return lax.ppermute(x, axis, [(i, i ^ mask) for i in range(size)])]
  transfers between devices with their start and end apart: 20 -> 20, of which waited for: 7 -> 8; matrix products, arithmetic and copies ran while one was open for 0% -> 0% of each run, Pallas kernels for 16% -> 17%
where the time goes in v7:
time: 97 us; the launch traced here: 96.6 us
  waiting for transfers between devices  36.8 us (38%)
  starting transfers between devices  36.6 us (38%)
  Pallas kernels  22.9 us (24%)
    ppermute x17, waiting for transfers between devices, swap(): return lax.ppermute(x, axis, [(i, i ^ mask) for i in range(size)])  36.8 us
    ppermute x17, starting transfers between devices, swap(): return lax.ppermute(x, axis, [(i, i ^ mask) for i in range(size)])  27.4 us
    ppermute x3, starting transfers between devices, body(): lax.ppermute(tail, 'seq', [(i, i + 1) for i in range(seq_size - 1)])  9.15 us
    pallas_call x2, Pallas kernels, make_attend(): pl.pallas_call(functools.partial(attend_kernel, start, base), in_specs=[S...  6.19 us
    pallas_call x4, Pallas kernels, project(): pl.pallas_call(functools.partial(project_kernel, plan, start, sums is not...  5.85 us
    pallas_call x1, Pallas kernels, make_local(): pl.pallas_call(functools.partial(local_kernel, width), in_specs=[SMEM, SM...  4.59 us
    pallas_call x1, Pallas kernels, make_state(): pl.pallas_call(functools.partial(state_kernel, slices), in_specs=[SMEM, H...  3.64 us
  transfers between devices with their start and end apart: 20, of which 8 were waited for; matrix products, arithmetic and copies ran while one was open for 0% of the time, Pallas kernels for 17%

profile of v7, /device:TPU:0, one launch (start us, length us, event | category | flops | bytes accessed | tf_op | source)
XLA Modules:
  0.0 96.6 jit_solution(11251992045650701211)
XLA Ops:
  0.1 3.6 %state.1 = (f32[4,136,128]{2,1,0:T(8,128)S(1)}, bf16[4,144,128]{2,1,0:T(8,128)(2,1)S(1)}, bf16[1024,512]{1,0:T(8,128)(2,1)S(1)}, bf16[1024,512]{1,0:T(8,128)(2,1...) custom-call(s32[2]{0:T(128)S(1)} %pad_add_fusion.at_ref, ...), custom_call_target="tpu_custom_call" | custom-call | flops 10000000000 | bytes 4194304 | tf_op jit(solution)/shard_map/state/pallas_call | solution.py:150
  3.7 3.0 %collective-permute-start.3 = (bf16[4,144,128]{2,1,0:T(8,128)(2,1)S(1)}, bf16[4,144,128]{2,1,0:T(8,128)(2,1)S(1)}, u32[]{:S(2)}, u32[]{:S(2)}) collective-permute-start(bf16[4,144,128]{2,1,0:T(8,128)(2,1)S(1)} %get-tuple-element.32), channel_id=1, source_target_pairs={{0,4},{4,0},{8,12},{12,8},{16,20},{20,16},{24,28},{28,24},{1,5},{5... | collective-permute-start | bytes 442376 | tf_op jit(solution)/shard_map/ppermute | solution.py:419
  6.7 3.8 %collective-permute-done.3.refs_0_ = bf16[4,144,128]{2,1,0:T(8,128)(2,1)S(1)} collective-permute-done((bf16[4,144,128]{2,1,0:T(8,128)(2,1)S(1)}, bf16[4,144,128]{2,1,0:T(8,128)(2,1)S(1)}, u32[]{:S(2)}, u32[]{:S(2)}) %collective-permute-start.3) | collective-permute-done | bytes 147488 | tf_op jit(solution)/shard_map/ppermute | solution.py:419
  10.6 0.6 shard_map.73
  11.2 1.9 %collective-permute-start.4 = (bf16[4,144,128]{2,1,0:T(8,128)(2,1)S(1)}, bf16[4,144,128]{2,1,0:T(8,128)(2,1)S(1)}, u32[]{:S(2)}, u32[]{:S(2)}) collective-permute-start(bf16[4,144,128]{2,1,0:T(8,128)(2,1)S(1)} %get-tuple-element.35), channel_id=1, source_target_pairs={{0,8},{4,12},{8,0},{12,4},{16,24},{20,28},{24,16},{28,20},{1,9},{5... | collective-permute-start | bytes 442376 | tf_op jit(solution)/shard_map/ppermute | solution.py:419
  13.1 3.4 %collective-permute-start = (bf16[128,512]{1,0:T(8,128)(2,1)S(1)}, bf16[128,512]{1,0:T(8,128)(2,1)S(1)}, u32[]{:S(2)}, u32[]{:S(2)}) collective-permute-start(bf16[128,512]{1,0:T(8,128)(2,1)S(1)} %get-tuple-element.29), channel_id=1, source_target_pairs={{0,4},{4,8},{8,12},{12,16},{16,20},{20,24},{24,28},{1,5},{5,9},{9,... | collective-permute-start | bytes 393224 | tf_op jit(solution)/shard_map/ppermute | solution.py:461
  16.5 2.1 %collective-permute-start.1 = (bf16[256,512]{1,0:T(8,128)(2,1)S(1)}, bf16[256,512]{1,0:T(8,128)(2,1)S(1)}, u32[]{:S(2)}, u32[]{:S(2)}) collective-permute-start(bf16[256,512]{1,0:T(8,128)(2,1)S(1)} %get-tuple-element.30), channel_id=1, source_target_pairs={{0,4},{4,8},{8,12},{12,16},{16,20},{20,24},{24,28},{1,5},{5,9},{9,... | collective-permute-start | bytes 786440 | tf_op jit(solution)/shard_map/ppermute | solution.py:461
  18.6 3.7 %collective-permute-start.2 = (bf16[640,512]{1,0:T(8,128)(2,1)S(1)}, bf16[640,512]{1,0:T(8,128)(2,1)S(1)}, u32[]{:S(2)}, u32[]{:S(2)}) collective-permute-start(bf16[640,512]{1,0:T(8,128)(2,1)S(1)} %get-tuple-element.31), channel_id=1, source_target_pairs={{0,4},{4,8},{8,12},{12,16},{16,20},{20,24},{24,28},{1,5},{5,9},{9,... | collective-permute-start | bytes 1966088 | tf_op jit(solution)/shard_map/ppermute | solution.py:461
  22.4 0.7 shard_map.74
  23.1 2.6 %collective-permute-start.5 = (bf16[4,144,128]{2,1,0:T(8,128)(2,1)S(1)}, bf16[4,144,128]{2,1,0:T(8,128)(2,1)S(1)}, u32[]{:S(2)}, u32[]{:S(2)}) collective-permute-start(bf16[4,144,128]{2,1,0:T(8,128)(2,1)S(1)} %get-tuple-element.38), channel_id=1, source_target_pairs={{0,16},{4,20},{8,24},{12,28},{16,0},{20,4},{24,8},{28,12},{1,17},{... | collective-permute-start | bytes 442376 | tf_op jit(solution)/shard_map/ppermute | solution.py:419
  25.7 4.6 %local.1.local_ref = f32[512,512]{1,0:T(8,128)S(1)} custom-call(s32[1]{0:T(128)} %bitcast.me_ref, s32[2,16]{1,0:T(2,128)S(1)} %bitcast.7, bf16[1024,512]{1,0:T(8,128)(2,1)S(1)} %get-tuple-element.26.q_ref, bf16[1024,512]{1,0:T(8,128)(2,1)S(1)} %get-tuple-element.27.k_ref, bf16[1024,512]{1,0:T(8,128)(2,1)S(1)} %get-tuple-element.28.v_ref), custom_call_target="tpu_custom_call" | custom-call | flops 15000000512 | bytes 3145728 | tf_op jit(solution)/shard_map/local/pallas_call | solution.py:254
  30.3 3.1 %collective-permute-done.5.refs_1_ = bf16[4,144,128]{2,1,0:T(8,128)(2,1)S(1)} collective-permute-done((bf16[4,144,128]{2,1,0:T(8,128)(2,1)S(1)}, bf16[4,144,128]{2,1,0:T(8,128)(2,1)S(1)}, u32[]{:S(2)}, u32[]{:S(2)}) %collective-permute-start.5) | collective-permute-done | bytes 147488 | tf_op jit(solution)/shard_map/ppermute | solution.py:419
  33.4 1.5 %collective-permute-start.10 = (bf16[256,1024]{1,0:T(8,128)(2,1)S(1)}, bf16[256,1024]{1,0:T(8,128)(2,1)S(1)}, u32[]{:S(2)}, u32[]{:S(2)}) collective-permute-start(bf16[256,1024]{1,0:T(8,128)(2,1)S(1)} %get-tuple-element.44), channel_id=1, source_target_pairs={{0,2},{1,3},{2,0},{3,1},{4,6},{5,7},{6,4},{7,5},{8,10},{9,11},{10,... | collective-permute-start | bytes 1572872 | tf_op jit(solution)/shard_map/ppermute | solution.py:419
  35.0 1.4 %readout.1 = (bf16[512,512]{1,0:T(8,128)(2,1)S(1)}, bf16[4,256,256]{2,1,0:T(8,128)(2,1)S(1)}, f32[4,8,128]{2,1,0:T(8,128)S(1)}) custom-call(s32[1]{0:T(128)} %bitcast.me_ref, f32[4,8]{1,0:T(4,128)S(1)} %bitcast.6, f32[4]{0:T(128)S(1)} %copy-done.2, bf16[1024,512]{1,0:T(8,128)(2,1)S(1)} %get-tuple-element.26.q_ref, f32[512,512]{1,0:T(8,128)S(1)} %local.1.local_ref, ...), custom_call_target="tpu_custom_call" | custom-call | flops 2000000000 | bytes 2097152 | tf_op jit(solution)/shard_map/readout/pallas_call | solution.py:290
  36.4 2.4 %shard_map.76.refs_0_ = bf16[192,512]{1,0:T(8,128)(2,1)S(1)} custom-call(s32[1]{0:T(128)} %bitcast.me_ref, s32[2,16]{1,0:T(2,128)S(1)} %bitcast.8, f32[4]{0:T(128)S(1)} %copy-done.2, bf16[1024,512]{1,0:T(8,128)(2,1)S(1)} %get-tuple-element.26.q_ref, bf16[1024,512]{1,0:T(8,128)(2,1)S(1)} %get-tuple-element.27.k_ref, ...), custom_call_target="tpu_custom_call" | custom-call | flops 8000000000 | bytes 3145728 | tf_op jit(solution)/shard_map/pallas_call | solution.py:337
  38.9 1.0 %collective-permute-start.15 = (bf16[192,512]{1,0:T(8,128)(2,1)S(1)}, bf16[192,512]{1,0:T(8,128)(2,1)S(1)}, u32[]{:S(2)}, u32[]{:S(2)}) collective-permute-start(bf16[192,512]{1,0:T(8,128)(2,1)S(1)} %shard_map.76.refs_0_), channel_id=1, source_target_pairs={{0,2},{1,3},{2,0},{3,1},{4,6},{5,7},{6,4},{7,5},{8,10},{9,11},{10,... | collective-permute-start | bytes 589832 | tf_op jit(solution)/shard_map/ppermute | solution.py:419
  39.9 1.1 %collective-permute-start.17 = (bf16[512,512]{1,0:T(8,128)(2,1)S(1)}, bf16[512,512]{1,0:T(8,128)(2,1)S(1)}, u32[]{:S(2)}, u32[]{:S(2)}) collective-permute-start(bf16[512,512]{1,0:T(8,128)(2,1)S(1)} %get-tuple-element.46.refs_0_), channel_id=1, source_target_pairs={{0,2},{1,3},{2,0},{3,1},{4,6},{5,7},{6,4},{7,5},{8,10},{9,11},{10,... | collective-permute-start | bytes 1572872 | tf_op jit(solution)/shard_map/ppermute | solution.py:419
  41.0 3.8 %shard_map.75.refs_0_ = bf16[320,512]{1,0:T(8,128)(2,1)S(1)} custom-call(s32[1]{0:T(128)} %bitcast.me_ref, s32[2,16]{1,0:T(2,128)S(1)} %bitcast.9, f32[4]{0:T(128)S(1)} %copy-done.2, bf16[1024,512]{1,0:T(8,128)(2,1)S(1)} %get-tuple-element.26.q_ref, bf16[1024,512]{1,0:T(8,128)(2,1)S(1)} %get-tuple-element.27.k_ref, ...), custom_call_target="tpu_custom_call" | custom-call | flops 8000000000 | bytes 3145728 | tf_op jit(solution)/shard_map/pallas_call | solution.py:337
  44.7 3.5 %collective-permute-done.10.refs_6_ = bf16[256,1024]{1,0:T(8,128)(2,1)S(1)} collective-permute-done((bf16[256,1024]{1,0:T(8,128)(2,1)S(1)}, bf16[256,1024]{1,0:T(8,128)(2,1)S(1)}, u32[]{:S(2)}, u32[]{:S(2)}) %collective-permute-start.10) | collective-permute-done | bytes 524320 | tf_op jit(solution)/shard_map/ppermute | solution.py:419
  48.2 1.5 %collective-permute-start.7 = (bf16[320,512]{1,0:T(8,128)(2,1)S(1)}, bf16[320,512]{1,0:T(8,128)(2,1)S(1)}, u32[]{:S(2)}, u32[]{:S(2)}) collective-permute-start(bf16[320,512]{1,0:T(8,128)(2,1)S(1)} %shard_map.75.refs_0_), channel_id=1, source_target_pairs={{0,2},{1,3},{2,0},{3,1},{4,6},{5,7},{6,4},{7,5},{8,10},{9,11},{10,... | collective-permute-start | bytes 983048 | tf_op jit(solution)/shard_map/ppermute | solution.py:419
  49.7 8.8 %collective-permute-done.12.refs_8_.refs_7_ = bf16[256,1024]{1,0:T(8,128)(2,1)S(1)} collective-permute-done((bf16[256,1024]{1,0:T(8,128)(2,1)S(1)}, bf16[256,1024]{1,0:T(8,128)(2,1)S(1)}, u32[]{:S(2)}, u32[]{:S(2)}) %collective-permute-start.12) | collective-permute-done | bytes 524320 | tf_op jit(solution)/shard_map/ppermute | solution.py:419
  58.5 0.8 collective-permute-start.14
  59.3 4.4 %collective-permute-done.15.refs_2_ = bf16[192,512]{1,0:T(8,128)(2,1)S(1)} collective-permute-done((bf16[192,512]{1,0:T(8,128)(2,1)S(1)}, bf16[192,512]{1,0:T(8,128)(2,1)S(1)}, u32[]{:S(2)}, u32[]{:S(2)}) %collective-permute-start.15) | collective-permute-done | bytes 196640 | tf_op jit(solution)/shard_map/ppermute | solution.py:419
  63.7 1.4 %collective-permute-done.16.refs_3_ = bf16[192,512]{1,0:T(8,128)(2,1)S(1)} collective-permute-done((bf16[192,512]{1,0:T(8,128)(2,1)S(1)}, bf16[192,512]{1,0:T(8,128)(2,1)S(1)}, u32[]{:S(2)}, u32[]{:S(2)}) %collective-permute-start.16) | collective-permute-done | bytes 196640 | tf_op jit(solution)/shard_map/ppermute | solution.py:419
  65.1 13.3 %collective-permute-start.13 = (bf16[256,1024]{1,0:T(8,128)(2,1)S(1)}, bf16[256,1024]{1,0:T(8,128)(2,1)S(1)}, u32[]{:S(2)}, u32[]{:S(2)}) collective-permute-start(bf16[256,1024]{1,0:T(8,128)(2,1)S(1)} %collective-permute-done.12.refs_8_.refs_7_), channel_id=1, source_target_pairs={{0,4},{4,0},{8,12},{12,8},{16,20},{20,16},{24,28},{28,24},{1,5},{5... | collective-permute-start | bytes 1572872 | tf_op jit(solution)/shard_map/ppermute | solution.py:419
  78.4 2.2 %collective-permute-done.7.refs_2_ = bf16[320,512]{1,0:T(8,128)(2,1)S(1)} collective-permute-done((bf16[320,512]{1,0:T(8,128)(2,1)S(1)}, bf16[320,512]{1,0:T(8,128)(2,1)S(1)}, u32[]{:S(2)}, u32[]{:S(2)}) %collective-permute-start.7) | collective-permute-done | bytes 327712 | tf_op jit(solution)/shard_map/ppermute | solution.py:419
  80.6 0.5 collective-permute-start.6
  81.2 9.5 %collective-permute-done.13.refs_9_.refs_2_ = bf16[256,1024]{1,0:T(8,128)(2,1)S(1)} collective-permute-done((bf16[256,1024]{1,0:T(8,128)(2,1)S(1)}, bf16[256,1024]{1,0:T(8,128)(2,1)S(1)}, u32[]{:S(2)}, u32[]{:S(2)}) %collective-permute-start.13) | collective-permute-done | bytes 524320 | tf_op jit(solution)/shard_map/ppermute | solution.py:419
  90.7 1.0 %shard_map.77.refs_10_ = bf16[192,1024]{1,0:T(8,128)(2,1)S(1)} custom-call(s32[1]{0:T(128)} %bitcast.me_ref, bf16[192,512]{1,0:T(8,128)(2,1)S(1)} %shard_map.76.refs_0_, bf16[192,512]{1,0:T(8,128)(2,1)S(1)} %collective-permute-done.14.refs_1_, bf16[192,512]{1,0:T(8,128)(2,1)S(1)} %collective-permute-done.15.refs_2_, ...), custom_call_target="tpu_custom_call" | custom-call | flops 805306368 | bytes 4194304 | tf_op jit(solution)/shard_map/pallas_call | solution.py:406
  91.7 1.8 %shard_map.78.refs_4_ = f32[512,1024]{1,0:T(8,128)S(1)} custom-call(s32[1]{0:T(128)} %bitcast.me_ref, bf16[512,512]{1,0:T(8,128)(2,1)S(1)} %get-tuple-element.46.refs_0_, bf16[512,512]{1,0:T(8,128)(2,1)S(1)} %collective-permute-done.19.refs_1_, bf16[512,512]{1,0:T(8,128)(2,1)S(1)} %collective-permute-done.17.refs_2_.refs_1_, ...), custom_call_target="tpu_custom_call" | custom-call | flops 1610612736 | bytes 3145728 | tf_op jit(solution)/shard_map/pallas_call | solution.py:406
  93.5 0.7 shard_map.79.refs_11_
  94.3 2.3 %shard_map.80 = bf16[1024,1024]{1,0:T(8,128)(2,1)} custom-call(s32[1]{0:T(128)} %bitcast.me_ref, bf16[320,512]{1,0:T(8,128)(2,1)S(1)} %shard_map.75.refs_0_, bf16[320,512]{1,0:T(8,128)(2,1)S(1)} %collective-permute-done.6.refs_1_, bf16[320,512]{1,0:T(8,128)(2,1)S(1)} %collective-permute-done.7.refs_2_, bf16[320,512]{1,0:T(8,128)(2,1)S(1)} %collective-permute-done.8.refs_3_, ...), custom_call_target="tpu_custom_call" | custom-call | flops 1342177280 | bytes 4194304 | tf_op jit(solution)/shard_map/pallas_call | solution.py:406
  (26 shorter events, 0.3 us)
Async XLA Ops:
  0.1 10.5 %copy-start = (f32[8,4]{0,1:T(4,128)S(1)}, f32[8,4]{0,1:T(4,128)}, u32[]{:S(2)}) copy-start(f32[8,4]{0,1:T(4,128)} %param.11) | copy-start | bytes 388
  3.7 6.9 %collective-permute-start.3 = (bf16[4,144,128]{2,1,0:T(8,128)(2,1)S(1)}, bf16[4,144,128]{2,1,0:T(8,128)(2,1)S(1)}, u32[]{:S(2)}, u32[]{:S(2)}) collective-permute-start(bf16[4,144,128]{2,1,0:T(8,128)(2,1)S(1)} %get-tuple-element.32), channel_id=1, source_target_pairs={{0,4},{4,0},{8,12},{12,8},{16,20},{20,16},{24,28},{28,24},{1,5},{5... | collective-permute-start | bytes 442376 | tf_op jit(solution)/shard_map/ppermute | solution.py:419
  11.2 14.4 %copy-start.1 = (s32[16,2]{0,1:T(2,128)S(1)}, s32[16,2]{0,1:T(2,128)}, u32[]{:S(2)}) copy-start(s32[16,2]{0,1:T(2,128)} %param.10) | copy-start | bytes 388
  11.2 11.1 %collective-permute-start.4 = (bf16[4,144,128]{2,1,0:T(8,128)(2,1)S(1)}, bf16[4,144,128]{2,1,0:T(8,128)(2,1)S(1)}, u32[]{:S(2)}, u32[]{:S(2)}) collective-permute-start(bf16[4,144,128]{2,1,0:T(8,128)(2,1)S(1)} %get-tuple-element.35), channel_id=1, source_target_pairs={{0,8},{4,12},{8,0},{12,4},{16,24},{20,28},{24,16},{28,20},{1,9},{5... | collective-permute-start | bytes 442376 | tf_op jit(solution)/shard_map/ppermute | solution.py:419
  13.1 23.2 %collective-permute-start = (bf16[128,512]{1,0:T(8,128)(2,1)S(1)}, bf16[128,512]{1,0:T(8,128)(2,1)S(1)}, u32[]{:S(2)}, u32[]{:S(2)}) collective-permute-start(bf16[128,512]{1,0:T(8,128)(2,1)S(1)} %get-tuple-element.29), channel_id=1, source_target_pairs={{0,4},{4,8},{8,12},{12,16},{16,20},{20,24},{24,28},{1,5},{5,9},{9,... | collective-permute-start | bytes 393224 | tf_op jit(solution)/shard_map/ppermute | solution.py:461
  16.5 19.9 %collective-permute-start.1 = (bf16[256,512]{1,0:T(8,128)(2,1)S(1)}, bf16[256,512]{1,0:T(8,128)(2,1)S(1)}, u32[]{:S(2)}, u32[]{:S(2)}) collective-permute-start(bf16[256,512]{1,0:T(8,128)(2,1)S(1)} %get-tuple-element.30), channel_id=1, source_target_pairs={{0,4},{4,8},{8,12},{12,16},{16,20},{20,24},{24,28},{1,5},{5,9},{9,... | collective-permute-start | bytes 786440 | tf_op jit(solution)/shard_map/ppermute | solution.py:461
  18.6 21.2 %collective-permute-start.2 = (bf16[640,512]{1,0:T(8,128)(2,1)S(1)}, bf16[640,512]{1,0:T(8,128)(2,1)S(1)}, u32[]{:S(2)}, u32[]{:S(2)}) collective-permute-start(bf16[640,512]{1,0:T(8,128)(2,1)S(1)} %get-tuple-element.31), channel_id=1, source_target_pairs={{0,4},{4,8},{8,12},{12,16},{16,20},{20,24},{24,28},{1,5},{5,9},{9,... | collective-permute-start | bytes 1966088 | tf_op jit(solution)/shard_map/ppermute | solution.py:461
  22.3 58.3 %collective-permute-start.9 = (bf16[512,1024]{1,0:T(8,128)(2,1)S(1)}, bf16[512,1024]{1,0:T(8,128)(2,1)S(1)}, u32[]{:S(2)}, u32[]{:S(2)}) collective-permute-start(bf16[512,1024]{1,0:T(8,128)(2,1)S(1)} %get-tuple-element.43), channel_id=1, source_target_pairs={{0,1},{1,0},{2,3},{3,2},{4,5},{5,4},{6,7},{7,6},{8,9},{9,8},{10,11... | collective-permute-start | bytes 3145736 | tf_op jit(solution)/shard_map/ppermute | solution.py:419
  23.1 10.4 %collective-permute-start.5 = (bf16[4,144,128]{2,1,0:T(8,128)(2,1)S(1)}, bf16[4,144,128]{2,1,0:T(8,128)(2,1)S(1)}, u32[]{:S(2)}, u32[]{:S(2)}) collective-permute-start(bf16[4,144,128]{2,1,0:T(8,128)(2,1)S(1)} %get-tuple-element.38), channel_id=1, source_target_pairs={{0,16},{4,20},{8,24},{12,28},{16,0},{20,4},{24,8},{28,12},{1,17},{... | collective-permute-start | bytes 442376 | tf_op jit(solution)/shard_map/ppermute | solution.py:419
  25.7 9.3 %copy-start.2 = (f32[4]{0:T(128)S(1)}, f32[4]{0:T(128)}, u32[]{:S(2)}) copy-start(f32[4]{0:T(128)} %gate_ref.5) | copy-start | bytes 52
  33.4 14.8 %collective-permute-start.10 = (bf16[256,1024]{1,0:T(8,128)(2,1)S(1)}, bf16[256,1024]{1,0:T(8,128)(2,1)S(1)}, u32[]{:S(2)}, u32[]{:S(2)}) collective-permute-start(bf16[256,1024]{1,0:T(8,128)(2,1)S(1)} %get-tuple-element.44), channel_id=1, source_target_pairs={{0,2},{1,3},{2,0},{3,1},{4,6},{5,7},{6,4},{7,5},{8,10},{9,11},{10,... | collective-permute-start | bytes 1572872 | tf_op jit(solution)/shard_map/ppermute | solution.py:419
  36.3 22.2 %collective-permute-start.12 = (bf16[256,1024]{1,0:T(8,128)(2,1)S(1)}, bf16[256,1024]{1,0:T(8,128)(2,1)S(1)}, u32[]{:S(2)}, u32[]{:S(2)}) collective-permute-start(bf16[256,1024]{1,0:T(8,128)(2,1)S(1)} %get-tuple-element.45), channel_id=1, source_target_pairs={{0,3},{1,2},{2,1},{3,0},{4,7},{5,6},{6,5},{7,4},{8,11},{9,10},{10,... | collective-permute-start | bytes 1572872 | tf_op jit(solution)/shard_map/ppermute | solution.py:419
  38.9 24.8 %collective-permute-start.15 = (bf16[192,512]{1,0:T(8,128)(2,1)S(1)}, bf16[192,512]{1,0:T(8,128)(2,1)S(1)}, u32[]{:S(2)}, u32[]{:S(2)}) collective-permute-start(bf16[192,512]{1,0:T(8,128)(2,1)S(1)} %shard_map.76.refs_0_), channel_id=1, source_target_pairs={{0,2},{1,3},{2,0},{3,1},{4,6},{5,7},{6,4},{7,5},{8,10},{9,11},{10,... | collective-permute-start | bytes 589832 | tf_op jit(solution)/shard_map/ppermute | solution.py:419
  39.9 38.5 %collective-permute-start.17 = (bf16[512,512]{1,0:T(8,128)(2,1)S(1)}, bf16[512,512]{1,0:T(8,128)(2,1)S(1)}, u32[]{:S(2)}, u32[]{:S(2)}) collective-permute-start(bf16[512,512]{1,0:T(8,128)(2,1)S(1)} %get-tuple-element.46.refs_0_), channel_id=1, source_target_pairs={{0,2},{1,3},{2,0},{3,1},{4,6},{5,7},{6,4},{7,5},{8,10},{9,11},{10,... | collective-permute-start | bytes 1572872 | tf_op jit(solution)/shard_map/ppermute | solution.py:419
  48.2 32.4 %collective-permute-start.7 = (bf16[320,512]{1,0:T(8,128)(2,1)S(1)}, bf16[320,512]{1,0:T(8,128)(2,1)S(1)}, u32[]{:S(2)}, u32[]{:S(2)}) collective-permute-start(bf16[320,512]{1,0:T(8,128)(2,1)S(1)} %shard_map.75.refs_0_), channel_id=1, source_target_pairs={{0,2},{1,3},{2,0},{3,1},{4,6},{5,7},{6,4},{7,5},{8,10},{9,11},{10,... | collective-permute-start | bytes 983048 | tf_op jit(solution)/shard_map/ppermute | solution.py:419
  58.5 5.2 %collective-permute-start.14 = (bf16[192,512]{1,0:T(8,128)(2,1)S(1)}, bf16[192,512]{1,0:T(8,128)(2,1)S(1)}, u32[]{:S(2)}, u32[]{:S(2)}) collective-permute-start(bf16[192,512]{1,0:T(8,128)(2,1)S(1)} %shard_map.76.refs_0_), channel_id=1, source_target_pairs={{0,1},{1,0},{2,3},{3,2},{4,5},{5,4},{6,7},{7,6},{8,9},{9,8},{10,11... | collective-permute-start | bytes 589832 | tf_op jit(solution)/shard_map/ppermute | solution.py:419
  63.7 1.4 %collective-permute-start.16 = (bf16[192,512]{1,0:T(8,128)(2,1)S(1)}, bf16[192,512]{1,0:T(8,128)(2,1)S(1)}, u32[]{:S(2)}, u32[]{:S(2)}) collective-permute-start(bf16[192,512]{1,0:T(8,128)(2,1)S(1)} %collective-permute-done.15.refs_2_), channel_id=1, source_target_pairs={{0,1},{1,0},{2,3},{3,2},{4,5},{5,4},{6,7},{7,6},{8,9},{9,8},{10,11... | collective-permute-start | bytes 589832 | tf_op jit(solution)/shard_map/ppermute | solution.py:419
  63.7 17.4 %collective-permute-start.11 = (bf16[256,1024]{1,0:T(8,128)(2,1)S(1)}, bf16[256,1024]{1,0:T(8,128)(2,1)S(1)}, u32[]{:S(2)}, u32[]{:S(2)}) collective-permute-start(bf16[256,1024]{1,0:T(8,128)(2,1)S(1)} %collective-permute-done.10.refs_6_), channel_id=1, source_target_pairs={{0,8},{4,12},{8,0},{12,4},{16,24},{20,28},{24,16},{28,20},{1,9},{5... | collective-permute-start | bytes 1572872 | tf_op jit(solution)/shard_map/ppermute | solution.py:419
  65.1 25.6 %collective-permute-start.13 = (bf16[256,1024]{1,0:T(8,128)(2,1)S(1)}, bf16[256,1024]{1,0:T(8,128)(2,1)S(1)}, u32[]{:S(2)}, u32[]{:S(2)}) collective-permute-start(bf16[256,1024]{1,0:T(8,128)(2,1)S(1)} %collective-permute-done.12.refs_8_.refs_7_), channel_id=1, source_target_pairs={{0,4},{4,0},{8,12},{12,8},{16,20},{20,16},{24,28},{28,24},{1,5},{5... | collective-permute-start | bytes 1572872 | tf_op jit(solution)/shard_map/ppermute | solution.py:419
  78.4 13.3 %collective-permute-start.19 = (bf16[512,512]{1,0:T(8,128)(2,1)S(1)}, bf16[512,512]{1,0:T(8,128)(2,1)S(1)}, u32[]{:S(2)}, u32[]{:S(2)}) collective-permute-start(bf16[512,512]{1,0:T(8,128)(2,1)S(1)} %get-tuple-element.46.refs_0_), channel_id=1, source_target_pairs={{0,1},{1,0},{2,3},{3,2},{4,5},{5,4},{6,7},{7,6},{8,9},{9,8},{10,11... | collective-permute-start | bytes 1572872 | tf_op jit(solution)/shard_map/ppermute | solution.py:419
  80.6 11.1 %collective-permute-start.18 = (bf16[512,512]{1,0:T(8,128)(2,1)S(1)}, bf16[512,512]{1,0:T(8,128)(2,1)S(1)}, u32[]{:S(2)}, u32[]{:S(2)}) collective-permute-start(bf16[512,512]{1,0:T(8,128)(2,1)S(1)} %collective-permute-done.17.refs_2_.refs_1_), channel_id=1, source_target_pairs={{0,1},{1,0},{2,3},{3,2},{4,5},{5,4},{6,7},{7,6},{8,9},{9,8},{10,11... | collective-permute-start | bytes 1572872 | tf_op jit(solution)/shard_map/ppermute | solution.py:419
  80.6 13.6 %collective-permute-start.6 = (bf16[320,512]{1,0:T(8,128)(2,1)S(1)}, bf16[320,512]{1,0:T(8,128)(2,1)S(1)}, u32[]{:S(2)}, u32[]{:S(2)}) collective-permute-start(bf16[320,512]{1,0:T(8,128)(2,1)S(1)} %shard_map.75.refs_0_), channel_id=1, source_target_pairs={{0,1},{1,0},{2,3},{3,2},{4,5},{5,4},{6,7},{7,6},{8,9},{9,8},{10,11... | collective-permute-start | bytes 983048 | tf_op jit(solution)/shard_map/ppermute | solution.py:419
  81.1 13.1 %collective-permute-start.8 = (bf16[320,512]{1,0:T(8,128)(2,1)S(1)}, bf16[320,512]{1,0:T(8,128)(2,1)S(1)}, u32[]{:S(2)}, u32[]{:S(2)}) collective-permute-start(bf16[320,512]{1,0:T(8,128)(2,1)S(1)} %collective-permute-done.7.refs_2_), channel_id=1, source_target_pairs={{0,1},{1,0},{2,3},{3,2},{4,5},{5,4},{6,7},{7,6},{8,9},{9,8},{10,11... | collective-permute-start | bytes 983048 | tf_op jit(solution)/shard_map/ppermute | solution.py:419

commit v8 on v7

--- a/solution.py
+++ b/solution.py
@@ -107,7 +107,17 @@
             copy.start()
         copies.append(pair)
     moves = slice_copies(slices, at_ref, w_hbm, blocks, w_sems)
-    moves.append(pltpu.make_async_copy(q_hbm, q_buf, w_sems.at[len(slices)]))
+    base, middle = rows - BAND, LATE - EARLY
+    pieces = [
+        (q_hbm, q_buf),
+        (k_hbm.at[base + LATE : rows], tails[0]),
+        (k_hbm.at[base + EARLY : base + LATE], tails[1].at[:middle]),
+        (v_hbm.at[base + EARLY : rows], tails[1].at[middle:]),
+        (k_hbm.at[base : base + EARLY], tails[2].at[:EARLY]),
+        (v_hbm.at[base : base + EARLY], tails[2].at[EARLY:]),
+    ]
+    for number, (source, target) in enumerate(pieces, len(slices)):
+        moves.append(pltpu.make_async_copy(source, target, w_sems.at[number]))
     for copy in moves:
         copy.start()
     for step in range(steps):
@@ -129,13 +139,6 @@
             store(state_ref, head, memory, total)
             if step == steps - 1:
                 pack(send_ref, head, memory, total)
-    base = rows - BAND
-    middle = LATE - EARLY
-    tails[0][...] = k_buf[base + LATE :, :]
-    tails[1][:middle, :] = k_buf[base + EARLY : base + LATE, :]
-    tails[1][middle:, :] = v_buf[base + EARLY :, :]
-    tails[2][:EARLY, :] = k_buf[base : base + EARLY, :]
-    tails[2][EARLY:, :] = v_buf[base : base + EARLY, :]
     for copy in moves:
         copy.wait()
 
@@ -160,7 +163,7 @@
         ],
         scratch_shapes=[
             pltpu.SemaphoreType.DMA((2, steps)),
-            pltpu.SemaphoreType.DMA((len(slices) + 1,)),
+            pltpu.SemaphoreType.DMA((len(slices) + 6,)),
         ],
         compiler_params=params(24),
         cost_estimate=cost(1e10, 4 * keys.size * 2),
@@ -214,10 +217,19 @@
     own = lax.dot_general(query, keys, dims, preferred_element_type=F32)
     row = start + lax.broadcasted_iota(jnp.int32, (query.shape[0], 1), 0)
     limit = jnp.where((row >= first) & (row < end), end - 1, row)
-    col = lax.broadcasted_iota(jnp.int32, prev.shape, 1) + base
-    prev = jnp.where(col > row + shift, prev, MASKED)
-    col = lax.broadcasted_iota(jnp.int32, own.shape, 1)
-    own = jnp.where(col <= limit, own, MASKED)
+    mixed_to = start + query.shape[0] - base if half else prev.shape[1]
+    near = prev[:, :mixed_to]
+    col = lax.broadcasted_iota(jnp.int32, near.shape, 1) + base
+    near = jnp.where(col > row + shift, near, MASKED)
+    if mixed_to < prev.shape[1]:
+        prev = jnp.concatenate([near, prev[:, mixed_to:]], axis=1)
+    else:
+        prev = near
+    seen = start // BLOCK * BLOCK
+    ahead = own[:, seen:]
+    col = lax.broadcasted_iota(jnp.int32, ahead.shape, 1) + seen
+    ahead = jnp.where(col <= limit, ahead, MASKED)
+    own = jnp.concatenate([own[:, :seen], ahead], axis=1) if seen else ahead
     top = jnp.maximum(jnp.max(prev, axis=1, keepdims=True), jnp.max(own, axis=1, keepdims=True))
     prev = jnp.exp2((prev - top) * factor)
     own = jnp.exp2((own - top) * factor)

time: 97 us -> 97.6 us (level)
  no operation moved by 1% of the time
where the time goes in v8:
time: 97.6 us; the launch traced here: 97.2 us
  waiting for transfers between devices  36.9 us (38%)
  starting transfers between devices  36.6 us (38%)
  Pallas kernels  23.5 us (24%)
    ppermute x17, waiting for transfers between devices, swap(): return lax.ppermute(x, axis, [(i, i ^ mask) for i in range(size)])  36.9 us
    ppermute x17, starting transfers between devices, swap(): return lax.ppermute(x, axis, [(i, i ^ mask) for i in range(size)])  27.4 us
    ppermute x3, starting transfers between devices, body(): lax.ppermute(tail, 'seq', [(i, i + 1) for i in range(seq_size - 1)])  9.15 us
    pallas_call x2, Pallas kernels, make_attend(): pl.pallas_call(functools.partial(attend_kernel, start, base), in_specs=[S...  6.15 us
    pallas_call x4, Pallas kernels, project(): pl.pallas_call(functools.partial(project_kernel, plan, start, sums is not...  5.85 us
    pallas_call x1, Pallas kernels, make_local(): pl.pallas_call(functools.partial(local_kernel, width), in_specs=[SMEM, SM...  4.56 us
    pallas_call x1, Pallas kernels, make_state(): pl.pallas_call(functools.partial(state_kernel, slices), in_specs=[SMEM, H...  4.25 us
  transfers between devices with their start and end apart: 20, of which 8 were waited for; matrix products, arithmetic and copies ran while one was open for 0% of the time, Pallas kernels for 17%

profile of v8, /device:TPU:0, one launch (start us, length us, event | category | flops | bytes accessed | tf_op | source)
XLA Modules:
  0.0 97.2 jit_solution(4445615488860143451)
XLA Ops:
  0.1 4.2 %state.1 = (f32[4,136,128]{2,1,0:T(8,128)S(1)}, bf16[4,144,128]{2,1,0:T(8,128)(2,1)S(1)}, bf16[1024,512]{1,0:T(8,128)(2,1)S(1)}, bf16[1024,512]{1,0:T(8,128)(2,1...) custom-call(s32[2]{0:T(128)S(1)} %pad_add_fusion.at_ref, ...), custom_call_target="tpu_custom_call" | custom-call | flops 10000000000 | bytes 4194304 | tf_op jit(solution)/shard_map/state/pallas_call | solution.py:153
  4.3 3.0 %collective-permute-start.3 = (bf16[4,144,128]{2,1,0:T(8,128)(2,1)S(1)}, bf16[4,144,128]{2,1,0:T(8,128)(2,1)S(1)}, u32[]{:S(2)}, u32[]{:S(2)}) collective-permute-start(bf16[4,144,128]{2,1,0:T(8,128)(2,1)S(1)} %get-tuple-element.32), channel_id=1, source_target_pairs={{0,4},{4,0},{8,12},{12,8},{16,20},{20,16},{24,28},{28,24},{1,5},{5... | collective-permute-start | bytes 442376 | tf_op jit(solution)/shard_map/ppermute | solution.py:431
  7.4 3.8 %collective-permute-done.3.refs_0_ = bf16[4,144,128]{2,1,0:T(8,128)(2,1)S(1)} collective-permute-done((bf16[4,144,128]{2,1,0:T(8,128)(2,1)S(1)}, bf16[4,144,128]{2,1,0:T(8,128)(2,1)S(1)}, u32[]{:S(2)}, u32[]{:S(2)}) %collective-permute-start.3) | collective-permute-done | bytes 147488 | tf_op jit(solution)/shard_map/ppermute | solution.py:431
  11.2 0.6 shard_map.73
  11.9 1.9 %collective-permute-start.4 = (bf16[4,144,128]{2,1,0:T(8,128)(2,1)S(1)}, bf16[4,144,128]{2,1,0:T(8,128)(2,1)S(1)}, u32[]{:S(2)}, u32[]{:S(2)}) collective-permute-start(bf16[4,144,128]{2,1,0:T(8,128)(2,1)S(1)} %get-tuple-element.35), channel_id=1, source_target_pairs={{0,8},{4,12},{8,0},{12,4},{16,24},{20,28},{24,16},{28,20},{1,9},{5... | collective-permute-start | bytes 442376 | tf_op jit(solution)/shard_map/ppermute | solution.py:431
  13.8 3.4 %collective-permute-start = (bf16[128,512]{1,0:T(8,128)(2,1)S(1)}, bf16[128,512]{1,0:T(8,128)(2,1)S(1)}, u32[]{:S(2)}, u32[]{:S(2)}) collective-permute-start(bf16[128,512]{1,0:T(8,128)(2,1)S(1)} %get-tuple-element.29), channel_id=1, source_target_pairs={{0,4},{4,8},{8,12},{12,16},{16,20},{20,24},{24,28},{1,5},{5,9},{9,... | collective-permute-start | bytes 393224 | tf_op jit(solution)/shard_map/ppermute | solution.py:473
  17.2 2.1 %collective-permute-start.1 = (bf16[256,512]{1,0:T(8,128)(2,1)S(1)}, bf16[256,512]{1,0:T(8,128)(2,1)S(1)}, u32[]{:S(2)}, u32[]{:S(2)}) collective-permute-start(bf16[256,512]{1,0:T(8,128)(2,1)S(1)} %get-tuple-element.30), channel_id=1, source_target_pairs={{0,4},{4,8},{8,12},{12,16},{16,20},{20,24},{24,28},{1,5},{5,9},{9,... | collective-permute-start | bytes 786440 | tf_op jit(solution)/shard_map/ppermute | solution.py:473
  19.3 3.7 %collective-permute-start.2 = (bf16[640,512]{1,0:T(8,128)(2,1)S(1)}, bf16[640,512]{1,0:T(8,128)(2,1)S(1)}, u32[]{:S(2)}, u32[]{:S(2)}) collective-permute-start(bf16[640,512]{1,0:T(8,128)(2,1)S(1)} %get-tuple-element.31), channel_id=1, source_target_pairs={{0,4},{4,8},{8,12},{12,16},{16,20},{20,24},{24,28},{1,5},{5,9},{9,... | collective-permute-start | bytes 1966088 | tf_op jit(solution)/shard_map/ppermute | solution.py:473
  23.0 0.7 shard_map.74
  23.7 2.6 %collective-permute-start.5 = (bf16[4,144,128]{2,1,0:T(8,128)(2,1)S(1)}, bf16[4,144,128]{2,1,0:T(8,128)(2,1)S(1)}, u32[]{:S(2)}, u32[]{:S(2)}) collective-permute-start(bf16[4,144,128]{2,1,0:T(8,128)(2,1)S(1)} %get-tuple-element.38), channel_id=1, source_target_pairs={{0,16},{4,20},{8,24},{12,28},{16,0},{20,4},{24,8},{28,12},{1,17},{... | collective-permute-start | bytes 442376 | tf_op jit(solution)/shard_map/ppermute | solution.py:431
  26.3 4.6 %local.1.local_ref = f32[512,512]{1,0:T(8,128)S(1)} custom-call(s32[1]{0:T(128)} %bitcast.me_ref, s32[2,16]{1,0:T(2,128)S(1)} %bitcast.7, bf16[1024,512]{1,0:T(8,128)(2,1)S(1)} %get-tuple-element.26.q_ref, bf16[1024,512]{1,0:T(8,128)(2,1)S(1)} %get-tuple-element.27.k_ref, bf16[1024,512]{1,0:T(8,128)(2,1)S(1)} %get-tuple-element.28.v_ref), custom_call_target="tpu_custom_call" | custom-call | flops 15000000512 | bytes 3145728 | tf_op jit(solution)/shard_map/local/pallas_call | solution.py:266
  30.9 3.2 %collective-permute-done.5.refs_1_ = bf16[4,144,128]{2,1,0:T(8,128)(2,1)S(1)} collective-permute-done((bf16[4,144,128]{2,1,0:T(8,128)(2,1)S(1)}, bf16[4,144,128]{2,1,0:T(8,128)(2,1)S(1)}, u32[]{:S(2)}, u32[]{:S(2)}) %collective-permute-start.5) | collective-permute-done | bytes 147488 | tf_op jit(solution)/shard_map/ppermute | solution.py:431
  34.0 1.5 %collective-permute-start.10 = (bf16[256,1024]{1,0:T(8,128)(2,1)S(1)}, bf16[256,1024]{1,0:T(8,128)(2,1)S(1)}, u32[]{:S(2)}, u32[]{:S(2)}) collective-permute-start(bf16[256,1024]{1,0:T(8,128)(2,1)S(1)} %get-tuple-element.44), channel_id=1, source_target_pairs={{0,2},{1,3},{2,0},{3,1},{4,6},{5,7},{6,4},{7,5},{8,10},{9,11},{10,... | collective-permute-start | bytes 1572872 | tf_op jit(solution)/shard_map/ppermute | solution.py:431
  35.6 1.4 %readout.1 = (bf16[512,512]{1,0:T(8,128)(2,1)S(1)}, bf16[4,256,256]{2,1,0:T(8,128)(2,1)S(1)}, f32[4,8,128]{2,1,0:T(8,128)S(1)}) custom-call(s32[1]{0:T(128)} %bitcast.me_ref, f32[4,8]{1,0:T(4,128)S(1)} %bitcast.6, f32[4]{0:T(128)S(1)} %copy-done.2, bf16[1024,512]{1,0:T(8,128)(2,1)S(1)} %get-tuple-element.26.q_ref, f32[512,512]{1,0:T(8,128)S(1)} %local.1.local_ref, ...), custom_call_target="tpu_custom_call" | custom-call | flops 2000000000 | bytes 2097152 | tf_op jit(solution)/shard_map/readout/pallas_call | solution.py:302
  37.0 2.4 %shard_map.76.refs_0_ = bf16[192,512]{1,0:T(8,128)(2,1)S(1)} custom-call(s32[1]{0:T(128)} %bitcast.me_ref, s32[2,16]{1,0:T(2,128)S(1)} %bitcast.8, f32[4]{0:T(128)S(1)} %copy-done.2, bf16[1024,512]{1,0:T(8,128)(2,1)S(1)} %get-tuple-element.26.q_ref, bf16[1024,512]{1,0:T(8,128)(2,1)S(1)} %get-tuple-element.27.k_ref, ...), custom_call_target="tpu_custom_call" | custom-call | flops 8000000000 | bytes 3145728 | tf_op jit(solution)/shard_map/pallas_call | solution.py:349
  39.4 1.0 %collective-permute-start.15 = (bf16[192,512]{1,0:T(8,128)(2,1)S(1)}, bf16[192,512]{1,0:T(8,128)(2,1)S(1)}, u32[]{:S(2)}, u32[]{:S(2)}) collective-permute-start(bf16[192,512]{1,0:T(8,128)(2,1)S(1)} %shard_map.76.refs_0_), channel_id=1, source_target_pairs={{0,2},{1,3},{2,0},{3,1},{4,6},{5,7},{6,4},{7,5},{8,10},{9,11},{10,... | collective-permute-start | bytes 589832 | tf_op jit(solution)/shard_map/ppermute | solution.py:431
  40.5 1.1 %collective-permute-start.17 = (bf16[512,512]{1,0:T(8,128)(2,1)S(1)}, bf16[512,512]{1,0:T(8,128)(2,1)S(1)}, u32[]{:S(2)}, u32[]{:S(2)}) collective-permute-start(bf16[512,512]{1,0:T(8,128)(2,1)S(1)} %get-tuple-element.46.refs_0_), channel_id=1, source_target_pairs={{0,2},{1,3},{2,0},{3,1},{4,6},{5,7},{6,4},{7,5},{8,10},{9,11},{10,... | collective-permute-start | bytes 1572872 | tf_op jit(solution)/shard_map/ppermute | solution.py:431
  41.5 3.8 %shard_map.75.refs_0_ = bf16[320,512]{1,0:T(8,128)(2,1)S(1)} custom-call(s32[1]{0:T(128)} %bitcast.me_ref, s32[2,16]{1,0:T(2,128)S(1)} %bitcast.9, f32[4]{0:T(128)S(1)} %copy-done.2, bf16[1024,512]{1,0:T(8,128)(2,1)S(1)} %get-tuple-element.26.q_ref, bf16[1024,512]{1,0:T(8,128)(2,1)S(1)} %get-tuple-element.27.k_ref, ...), custom_call_target="tpu_custom_call" | custom-call | flops 8000000000 | bytes 3145728 | tf_op jit(solution)/shard_map/pallas_call | solution.py:349
  45.3 3.5 %collective-permute-done.10.refs_6_ = bf16[256,1024]{1,0:T(8,128)(2,1)S(1)} collective-permute-done((bf16[256,1024]{1,0:T(8,128)(2,1)S(1)}, bf16[256,1024]{1,0:T(8,128)(2,1)S(1)}, u32[]{:S(2)}, u32[]{:S(2)}) %collective-permute-start.10) | collective-permute-done | bytes 524320 | tf_op jit(solution)/shard_map/ppermute | solution.py:431
  48.8 1.5 %collective-permute-start.7 = (bf16[320,512]{1,0:T(8,128)(2,1)S(1)}, bf16[320,512]{1,0:T(8,128)(2,1)S(1)}, u32[]{:S(2)}, u32[]{:S(2)}) collective-permute-start(bf16[320,512]{1,0:T(8,128)(2,1)S(1)} %shard_map.75.refs_0_), channel_id=1, source_target_pairs={{0,2},{1,3},{2,0},{3,1},{4,6},{5,7},{6,4},{7,5},{8,10},{9,11},{10,... | collective-permute-start | bytes 983048 | tf_op jit(solution)/shard_map/ppermute | solution.py:431
  50.4 8.8 %collective-permute-done.12.refs_8_.refs_7_ = bf16[256,1024]{1,0:T(8,128)(2,1)S(1)} collective-permute-done((bf16[256,1024]{1,0:T(8,128)(2,1)S(1)}, bf16[256,1024]{1,0:T(8,128)(2,1)S(1)}, u32[]{:S(2)}, u32[]{:S(2)}) %collective-permute-start.12) | collective-permute-done | bytes 524320 | tf_op jit(solution)/shard_map/ppermute | solution.py:431
  59.1 0.8 collective-permute-start.14
  59.9 4.4 %collective-permute-done.15.refs_2_ = bf16[192,512]{1,0:T(8,128)(2,1)S(1)} collective-permute-done((bf16[192,512]{1,0:T(8,128)(2,1)S(1)}, bf16[192,512]{1,0:T(8,128)(2,1)S(1)}, u32[]{:S(2)}, u32[]{:S(2)}) %collective-permute-start.15) | collective-permute-done | bytes 196640 | tf_op jit(solution)/shard_map/ppermute | solution.py:431
  64.3 1.4 %collective-permute-done.16.refs_3_ = bf16[192,512]{1,0:T(8,128)(2,1)S(1)} collective-permute-done((bf16[192,512]{1,0:T(8,128)(2,1)S(1)}, bf16[192,512]{1,0:T(8,128)(2,1)S(1)}, u32[]{:S(2)}, u32[]{:S(2)}) %collective-permute-start.16) | collective-permute-done | bytes 196640 | tf_op jit(solution)/shard_map/ppermute | solution.py:431
  65.7 13.3 %collective-permute-start.13 = (bf16[256,1024]{1,0:T(8,128)(2,1)S(1)}, bf16[256,1024]{1,0:T(8,128)(2,1)S(1)}, u32[]{:S(2)}, u32[]{:S(2)}) collective-permute-start(bf16[256,1024]{1,0:T(8,128)(2,1)S(1)} %collective-permute-done.12.refs_8_.refs_7_), channel_id=1, source_target_pairs={{0,4},{4,0},{8,12},{12,8},{16,20},{20,16},{24,28},{28,24},{1,5},{5... | collective-permute-start | bytes 1572872 | tf_op jit(solution)/shard_map/ppermute | solution.py:431
  79.0 2.2 %collective-permute-done.7.refs_2_ = bf16[320,512]{1,0:T(8,128)(2,1)S(1)} collective-permute-done((bf16[320,512]{1,0:T(8,128)(2,1)S(1)}, bf16[320,512]{1,0:T(8,128)(2,1)S(1)}, u32[]{:S(2)}, u32[]{:S(2)}) %collective-permute-start.7) | collective-permute-done | bytes 327712 | tf_op jit(solution)/shard_map/ppermute | solution.py:431
  81.2 0.5 collective-permute-start.6
  81.8 9.5 %collective-permute-done.13.refs_9_.refs_2_ = bf16[256,1024]{1,0:T(8,128)(2,1)S(1)} collective-permute-done((bf16[256,1024]{1,0:T(8,128)(2,1)S(1)}, bf16[256,1024]{1,0:T(8,128)(2,1)S(1)}, u32[]{:S(2)}, u32[]{:S(2)}) %collective-permute-start.13) | collective-permute-done | bytes 524320 | tf_op jit(solution)/shard_map/ppermute | solution.py:431
  91.3 1.0 %shard_map.77.refs_10_ = bf16[192,1024]{1,0:T(8,128)(2,1)S(1)} custom-call(s32[1]{0:T(128)} %bitcast.me_ref, bf16[192,512]{1,0:T(8,128)(2,1)S(1)} %shard_map.76.refs_0_, bf16[192,512]{1,0:T(8,128)(2,1)S(1)} %collective-permute-done.14.refs_1_, bf16[192,512]{1,0:T(8,128)(2,1)S(1)} %collective-permute-done.15.refs_2_, ...), custom_call_target="tpu_custom_call" | custom-call | flops 805306368 | bytes 4194304 | tf_op jit(solution)/shard_map/pallas_call | solution.py:418
  92.3 1.8 %shard_map.78.refs_4_ = f32[512,1024]{1,0:T(8,128)S(1)} custom-call(s32[1]{0:T(128)} %bitcast.me_ref, bf16[512,512]{1,0:T(8,128)(2,1)S(1)} %get-tuple-element.46.refs_0_, bf16[512,512]{1,0:T(8,128)(2,1)S(1)} %collective-permute-done.19.refs_1_, bf16[512,512]{1,0:T(8,128)(2,1)S(1)} %collective-permute-done.17.refs_2_.refs_1_, ...), custom_call_target="tpu_custom_call" | custom-call | flops 1610612736 | bytes 3145728 | tf_op jit(solution)/shard_map/pallas_call | solution.py:418
  94.1 0.7 shard_map.79.refs_11_
  94.9 2.3 %shard_map.80 = bf16[1024,1024]{1,0:T(8,128)(2,1)} custom-call(s32[1]{0:T(128)} %bitcast.me_ref, bf16[320,512]{1,0:T(8,128)(2,1)S(1)} %shard_map.75.refs_0_, bf16[320,512]{1,0:T(8,128)(2,1)S(1)} %collective-permute-done.6.refs_1_, bf16[320,512]{1,0:T(8,128)(2,1)S(1)} %collective-permute-done.7.refs_2_, bf16[320,512]{1,0:T(8,128)(2,1)S(1)} %collective-permute-done.8.refs_3_, ...), custom_call_target="tpu_custom_call" | custom-call | flops 1342177280 | bytes 4194304 | tf_op jit(solution)/shard_map/pallas_call | solution.py:418
  (26 shorter events, 0.3 us)
Async XLA Ops:
  0.1 11.1 %copy-start = (f32[8,4]{0,1:T(4,128)S(1)}, f32[8,4]{0,1:T(4,128)}, u32[]{:S(2)}) copy-start(f32[8,4]{0,1:T(4,128)} %param.11) | copy-start | bytes 388
  4.3 6.9 %collective-permute-start.3 = (bf16[4,144,128]{2,1,0:T(8,128)(2,1)S(1)}, bf16[4,144,128]{2,1,0:T(8,128)(2,1)S(1)}, u32[]{:S(2)}, u32[]{:S(2)}) collective-permute-start(bf16[4,144,128]{2,1,0:T(8,128)(2,1)S(1)} %get-tuple-element.32), channel_id=1, source_target_pairs={{0,4},{4,0},{8,12},{12,8},{16,20},{20,16},{24,28},{28,24},{1,5},{5... | collective-permute-start | bytes 442376 | tf_op jit(solution)/shard_map/ppermute | solution.py:431
  11.9 14.4 %copy-start.1 = (s32[16,2]{0,1:T(2,128)S(1)}, s32[16,2]{0,1:T(2,128)}, u32[]{:S(2)}) copy-start(s32[16,2]{0,1:T(2,128)} %param.10) | copy-start | bytes 388
  11.9 11.1 %collective-permute-start.4 = (bf16[4,144,128]{2,1,0:T(8,128)(2,1)S(1)}, bf16[4,144,128]{2,1,0:T(8,128)(2,1)S(1)}, u32[]{:S(2)}, u32[]{:S(2)}) collective-permute-start(bf16[4,144,128]{2,1,0:T(8,128)(2,1)S(1)} %get-tuple-element.35), channel_id=1, source_target_pairs={{0,8},{4,12},{8,0},{12,4},{16,24},{20,28},{24,16},{28,20},{1,9},{5... | collective-permute-start | bytes 442376 | tf_op jit(solution)/shard_map/ppermute | solution.py:431
  13.8 23.2 %collective-permute-start = (bf16[128,512]{1,0:T(8,128)(2,1)S(1)}, bf16[128,512]{1,0:T(8,128)(2,1)S(1)}, u32[]{:S(2)}, u32[]{:S(2)}) collective-permute-start(bf16[128,512]{1,0:T(8,128)(2,1)S(1)} %get-tuple-element.29), channel_id=1, source_target_pairs={{0,4},{4,8},{8,12},{12,16},{16,20},{20,24},{24,28},{1,5},{5,9},{9,... | collective-permute-start | bytes 393224 | tf_op jit(solution)/shard_map/ppermute | solution.py:473
  17.2 19.9 %collective-permute-start.1 = (bf16[256,512]{1,0:T(8,128)(2,1)S(1)}, bf16[256,512]{1,0:T(8,128)(2,1)S(1)}, u32[]{:S(2)}, u32[]{:S(2)}) collective-permute-start(bf16[256,512]{1,0:T(8,128)(2,1)S(1)} %get-tuple-element.30), channel_id=1, source_target_pairs={{0,4},{4,8},{8,12},{12,16},{16,20},{20,24},{24,28},{1,5},{5,9},{9,... | collective-permute-start | bytes 786440 | tf_op jit(solution)/shard_map/ppermute | solution.py:473
  19.3 21.2 %collective-permute-start.2 = (bf16[640,512]{1,0:T(8,128)(2,1)S(1)}, bf16[640,512]{1,0:T(8,128)(2,1)S(1)}, u32[]{:S(2)}, u32[]{:S(2)}) collective-permute-start(bf16[640,512]{1,0:T(8,128)(2,1)S(1)} %get-tuple-element.31), channel_id=1, source_target_pairs={{0,4},{4,8},{8,12},{12,16},{16,20},{20,24},{24,28},{1,5},{5,9},{9,... | collective-permute-start | bytes 1966088 | tf_op jit(solution)/shard_map/ppermute | solution.py:473
  22.9 58.3 %collective-permute-start.9 = (bf16[512,1024]{1,0:T(8,128)(2,1)S(1)}, bf16[512,1024]{1,0:T(8,128)(2,1)S(1)}, u32[]{:S(2)}, u32[]{:S(2)}) collective-permute-start(bf16[512,1024]{1,0:T(8,128)(2,1)S(1)} %get-tuple-element.43), channel_id=1, source_target_pairs={{0,1},{1,0},{2,3},{3,2},{4,5},{5,4},{6,7},{7,6},{8,9},{9,8},{10,11... | collective-permute-start | bytes 3145736 | tf_op jit(solution)/shard_map/ppermute | solution.py:431
  23.7 10.4 %collective-permute-start.5 = (bf16[4,144,128]{2,1,0:T(8,128)(2,1)S(1)}, bf16[4,144,128]{2,1,0:T(8,128)(2,1)S(1)}, u32[]{:S(2)}, u32[]{:S(2)}) collective-permute-start(bf16[4,144,128]{2,1,0:T(8,128)(2,1)S(1)} %get-tuple-element.38), channel_id=1, source_target_pairs={{0,16},{4,20},{8,24},{12,28},{16,0},{20,4},{24,8},{28,12},{1,17},{... | collective-permute-start | bytes 442376 | tf_op jit(solution)/shard_map/ppermute | solution.py:431
  26.3 9.3 %copy-start.2 = (f32[4]{0:T(128)S(1)}, f32[4]{0:T(128)}, u32[]{:S(2)}) copy-start(f32[4]{0:T(128)} %gate_ref.5) | copy-start | bytes 52
  34.0 14.8 %collective-permute-start.10 = (bf16[256,1024]{1,0:T(8,128)(2,1)S(1)}, bf16[256,1024]{1,0:T(8,128)(2,1)S(1)}, u32[]{:S(2)}, u32[]{:S(2)}) collective-permute-start(bf16[256,1024]{1,0:T(8,128)(2,1)S(1)} %get-tuple-element.44), channel_id=1, source_target_pairs={{0,2},{1,3},{2,0},{3,1},{4,6},{5,7},{6,4},{7,5},{8,10},{9,11},{10,... | collective-permute-start | bytes 1572872 | tf_op jit(solution)/shard_map/ppermute | solution.py:431
  37.0 22.2 %collective-permute-start.12 = (bf16[256,1024]{1,0:T(8,128)(2,1)S(1)}, bf16[256,1024]{1,0:T(8,128)(2,1)S(1)}, u32[]{:S(2)}, u32[]{:S(2)}) collective-permute-start(bf16[256,1024]{1,0:T(8,128)(2,1)S(1)} %get-tuple-element.45), channel_id=1, source_target_pairs={{0,3},{1,2},{2,1},{3,0},{4,7},{5,6},{6,5},{7,4},{8,11},{9,10},{10,... | collective-permute-start | bytes 1572872 | tf_op jit(solution)/shard_map/ppermute | solution.py:431
  39.4 24.9 %collective-permute-start.15 = (bf16[192,512]{1,0:T(8,128)(2,1)S(1)}, bf16[192,512]{1,0:T(8,128)(2,1)S(1)}, u32[]{:S(2)}, u32[]{:S(2)}) collective-permute-start(bf16[192,512]{1,0:T(8,128)(2,1)S(1)} %shard_map.76.refs_0_), channel_id=1, source_target_pairs={{0,2},{1,3},{2,0},{3,1},{4,6},{5,7},{6,4},{7,5},{8,10},{9,11},{10,... | collective-permute-start | bytes 589832 | tf_op jit(solution)/shard_map/ppermute | solution.py:431
  40.5 38.5 %collective-permute-start.17 = (bf16[512,512]{1,0:T(8,128)(2,1)S(1)}, bf16[512,512]{1,0:T(8,128)(2,1)S(1)}, u32[]{:S(2)}, u32[]{:S(2)}) collective-permute-start(bf16[512,512]{1,0:T(8,128)(2,1)S(1)} %get-tuple-element.46.refs_0_), channel_id=1, source_target_pairs={{0,2},{1,3},{2,0},{3,1},{4,6},{5,7},{6,4},{7,5},{8,10},{9,11},{10,... | collective-permute-start | bytes 1572872 | tf_op jit(solution)/shard_map/ppermute | solution.py:431
  48.8 32.4 %collective-permute-start.7 = (bf16[320,512]{1,0:T(8,128)(2,1)S(1)}, bf16[320,512]{1,0:T(8,128)(2,1)S(1)}, u32[]{:S(2)}, u32[]{:S(2)}) collective-permute-start(bf16[320,512]{1,0:T(8,128)(2,1)S(1)} %shard_map.75.refs_0_), channel_id=1, source_target_pairs={{0,2},{1,3},{2,0},{3,1},{4,6},{5,7},{6,4},{7,5},{8,10},{9,11},{10,... | collective-permute-start | bytes 983048 | tf_op jit(solution)/shard_map/ppermute | solution.py:431
  59.1 5.2 %collective-permute-start.14 = (bf16[192,512]{1,0:T(8,128)(2,1)S(1)}, bf16[192,512]{1,0:T(8,128)(2,1)S(1)}, u32[]{:S(2)}, u32[]{:S(2)}) collective-permute-start(bf16[192,512]{1,0:T(8,128)(2,1)S(1)} %shard_map.76.refs_0_), channel_id=1, source_target_pairs={{0,1},{1,0},{2,3},{3,2},{4,5},{5,4},{6,7},{7,6},{8,9},{9,8},{10,11... | collective-permute-start | bytes 589832 | tf_op jit(solution)/shard_map/ppermute | solution.py:431
  64.3 1.4 %collective-permute-start.16 = (bf16[192,512]{1,0:T(8,128)(2,1)S(1)}, bf16[192,512]{1,0:T(8,128)(2,1)S(1)}, u32[]{:S(2)}, u32[]{:S(2)}) collective-permute-start(bf16[192,512]{1,0:T(8,128)(2,1)S(1)} %collective-permute-done.15.refs_2_), channel_id=1, source_target_pairs={{0,1},{1,0},{2,3},{3,2},{4,5},{5,4},{6,7},{7,6},{8,9},{9,8},{10,11... | collective-permute-start | bytes 589832 | tf_op jit(solution)/shard_map/ppermute | solution.py:431
  64.3 17.4 %collective-permute-start.11 = (bf16[256,1024]{1,0:T(8,128)(2,1)S(1)}, bf16[256,1024]{1,0:T(8,128)(2,1)S(1)}, u32[]{:S(2)}, u32[]{:S(2)}) collective-permute-start(bf16[256,1024]{1,0:T(8,128)(2,1)S(1)} %collective-permute-done.10.refs_6_), channel_id=1, source_target_pairs={{0,8},{4,12},{8,0},{12,4},{16,24},{20,28},{24,16},{28,20},{1,9},{5... | collective-permute-start | bytes 1572872 | tf_op jit(solution)/shard_map/ppermute | solution.py:431
  65.7 25.6 %collective-permute-start.13 = (bf16[256,1024]{1,0:T(8,128)(2,1)S(1)}, bf16[256,1024]{1,0:T(8,128)(2,1)S(1)}, u32[]{:S(2)}, u32[]{:S(2)}) collective-permute-start(bf16[256,1024]{1,0:T(8,128)(2,1)S(1)} %collective-permute-done.12.refs_8_.refs_7_), channel_id=1, source_target_pairs={{0,4},{4,0},{8,12},{12,8},{16,20},{20,16},{24,28},{28,24},{1,5},{5... | collective-permute-start | bytes 1572872 | tf_op jit(solution)/shard_map/ppermute | solution.py:431
  79.0 13.3 %collective-permute-start.19 = (bf16[512,512]{1,0:T(8,128)(2,1)S(1)}, bf16[512,512]{1,0:T(8,128)(2,1)S(1)}, u32[]{:S(2)}, u32[]{:S(2)}) collective-permute-start(bf16[512,512]{1,0:T(8,128)(2,1)S(1)} %get-tuple-element.46.refs_0_), channel_id=1, source_target_pairs={{0,1},{1,0},{2,3},{3,2},{4,5},{5,4},{6,7},{7,6},{8,9},{9,8},{10,11... | collective-permute-start | bytes 1572872 | tf_op jit(solution)/shard_map/ppermute | solution.py:431
  81.2 11.1 %collective-permute-start.18 = (bf16[512,512]{1,0:T(8,128)(2,1)S(1)}, bf16[512,512]{1,0:T(8,128)(2,1)S(1)}, u32[]{:S(2)}, u32[]{:S(2)}) collective-permute-start(bf16[512,512]{1,0:T(8,128)(2,1)S(1)} %collective-permute-done.17.refs_2_.refs_1_), channel_id=1, source_target_pairs={{0,1},{1,0},{2,3},{3,2},{4,5},{5,4},{6,7},{7,6},{8,9},{9,8},{10,11... | collective-permute-start | bytes 1572872 | tf_op jit(solution)/shard_map/ppermute | solution.py:431
  81.2 13.6 %collective-permute-start.6 = (bf16[320,512]{1,0:T(8,128)(2,1)S(1)}, bf16[320,512]{1,0:T(8,128)(2,1)S(1)}, u32[]{:S(2)}, u32[]{:S(2)}) collective-permute-start(bf16[320,512]{1,0:T(8,128)(2,1)S(1)} %shard_map.75.refs_0_), channel_id=1, source_target_pairs={{0,1},{1,0},{2,3},{3,2},{4,5},{5,4},{6,7},{7,6},{8,9},{9,8},{10,11... | collective-permute-start | bytes 983048 | tf_op jit(solution)/shard_map/ppermute | solution.py:431
  81.7 13.1 %collective-permute-start.8 = (bf16[320,512]{1,0:T(8,128)(2,1)S(1)}, bf16[320,512]{1,0:T(8,128)(2,1)S(1)}, u32[]{:S(2)}, u32[]{:S(2)}) collective-permute-start(bf16[320,512]{1,0:T(8,128)(2,1)S(1)} %collective-permute-done.7.refs_2_), channel_id=1, source_target_pairs={{0,1},{1,0},{2,3},{3,2},{4,5},{5,4},{6,7},{7,6},{8,9},{9,8},{10,11... | collective-permute-start | bytes 983048 | tf_op jit(solution)/shard_map/ppermute | solution.py:431

commit v9 on v7

--- a/solution.py
+++ b/solution.py
@@ -88,6 +88,29 @@
         source = w_hbm.at[pl.ds(pl.multiple_of(row, rows), rows), pl.ds(col, columns)]
         copies.append(pltpu.make_async_copy(source, blocks[number], sems.at[number]))
     return copies
+
+
+def slice_kernel(slices, at_ref, w_hbm, *refs):
+    *blocks, sems = refs
+    copies = slice_copies(slices, at_ref, w_hbm, blocks, sems)
+    for copy in copies:
+        copy.start()
+    for copy in copies:
+        copy.wait()
+
+
+def make_slices(out_weight, slices, at, columns):
+    block = pltpu.VMEM((out_weight.shape[0], columns), BF16)
+    return pl.pallas_call(
+        functools.partial(slice_kernel, slices),
+        in_specs=[SMEM, HBM],
+        out_specs=[VMEM] * len(slices),
+        out_shape=[block] * len(slices),
+        scratch_shapes=[pltpu.SemaphoreType.DMA((len(slices),))],
+        compiler_params=params(8),
+        cost_estimate=cost(1e9, 4 * out_weight.shape[0] * columns * len(slices)),
+        name="slices",
+    )(at, in_hbm(out_weight))
 
 
 def state_kernel(slices, at_ref, q_hbm, k_hbm, v_hbm, w_hbm, state_ref, send_ref, *refs):
@@ -439,12 +462,15 @@
     for mask in (*masks, 0):
         partner, parts = partners.get(mask, (0, 1))
         slices += [(mask, partner, part) for part in range(parts)]
+    early = len(slices) - 2
     at = jnp.concatenate([me, head_index.astype(jnp.int32).reshape(1)])
     state, send, *more = make_state(
-        queries, keys, values, out_weight, slices, at, heads, width, columns
+        queries, keys, values, out_weight, slices[:early], at, heads, width,
+        columns,
     )
     queries, keys, values = more[:3]
     tails, blocks = more[3:6], more[6:]
+    blocks += make_slices(out_weight, slices[early:], at, columns)
     weights = {mask: [] for mask in (*masks, 0)}
     for (mask, partner, part), block in zip(slices, blocks):
         block = swap(block, "head", mask) if mask else block

time: 97 us -> 96.9 us (level)
  starting transfers between devices: 36.6 us -> 34.5 us
  Pallas kernels: 22.9 us -> 24.9 us
    ppermute x17, starting transfers between devices: 27.4 us -> 25.3 us  [swap(): return lax.ppermute(x, axis, [(i, i ^ mask) for i in range(size)])]
    pallas_call x0 -> x1, Pallas kernels: none -> 2.11 us  [make_slices(): pl.pallas_call(functools.partial(slice_kernel, slices), in_specs=[SMEM, H...]
  transfers between devices with their start and end apart: 20 -> 20, of which waited for: 8 -> 8; matrix products, arithmetic and copies ran while one was open for 0% -> 0% of each run, Pallas kernels for 17% -> 19%
where the time goes in v9:
time: 96.9 us; the launch traced here: 96.4 us
  waiting for transfers between devices  36.8 us (38%)
  starting transfers between devices  34.5 us (36%)
  Pallas kernels  24.9 us (26%)
    ppermute x17, waiting for transfers between devices, swap(): return lax.ppermute(x, axis, [(i, i ^ mask) for i in range(size)])  36.8 us
    ppermute x17, starting transfers between devices, swap(): return lax.ppermute(x, axis, [(i, i ^ mask) for i in range(size)])  25.3 us
    ppermute x3, starting transfers between devices, body(): lax.ppermute(tail, 'seq', [(i, i + 1) for i in range(seq_size - 1)])  9.15 us
    pallas_call x2, Pallas kernels, make_attend(): pl.pallas_call(functools.partial(attend_kernel, start, base), in_specs=[S...  6.2 us
    pallas_call x4, Pallas kernels, project(): pl.pallas_call(functools.partial(project_kernel, plan, start, sums is not...  5.86 us
    pallas_call x1, Pallas kernels, make_local(): pl.pallas_call(functools.partial(local_kernel, width), in_specs=[SMEM, SM...  4.59 us
    pallas_call x1, Pallas kernels, make_state(): pl.pallas_call(functools.partial(state_kernel, slices), in_specs=[SMEM, H...  3.48 us
    pallas_call x1, Pallas kernels, make_slices(): pl.pallas_call(functools.partial(slice_kernel, slices), in_specs=[SMEM, H...  2.11 us
  transfers between devices with their start and end apart: 20, of which 8 were waited for; matrix products, arithmetic and copies ran while one was open for 0% of the time, Pallas kernels for 19%

profile of v9, /device:TPU:0, one launch (start us, length us, event | category | flops | bytes accessed | tf_op | source)
XLA Modules:
  0.0 96.4 jit_solution(16574061079164592937)
XLA Ops:
  0.1 3.5 %state.1 = (f32[4,136,128]{2,1,0:T(8,128)S(1)}, bf16[4,144,128]{2,1,0:T(8,128)(2,1)S(1)}, bf16[1024,512]{1,0:T(8,128)(2,1)S(1)}, bf16[1024,512]{1,0:T(8,128)(2,1...) custom-call(s32[2]{0:T(128)S(1)} %pad_add_fusion.at_ref, ...), custom_call_target="tpu_custom_call" | custom-call | flops 10000000000 | bytes 4194304 | tf_op jit(solution)/shard_map/state/pallas_call | solution.py:173
  3.6 3.0 %collective-permute-start.3 = (bf16[4,144,128]{2,1,0:T(8,128)(2,1)S(1)}, bf16[4,144,128]{2,1,0:T(8,128)(2,1)S(1)}, u32[]{:S(2)}, u32[]{:S(2)}) collective-permute-start(bf16[4,144,128]{2,1,0:T(8,128)(2,1)S(1)} %get-tuple-element.32), channel_id=1, source_target_pairs={{0,4},{4,0},{8,12},{12,8},{16,20},{20,16},{24,28},{28,24},{1,5},{5... | collective-permute-start | bytes 442376 | tf_op jit(solution)/shard_map/ppermute | solution.py:442
  6.6 3.8 %collective-permute-done.3.refs_0_ = bf16[4,144,128]{2,1,0:T(8,128)(2,1)S(1)} collective-permute-done((bf16[4,144,128]{2,1,0:T(8,128)(2,1)S(1)}, bf16[4,144,128]{2,1,0:T(8,128)(2,1)S(1)}, u32[]{:S(2)}, u32[]{:S(2)}) %collective-permute-start.3) | collective-permute-done | bytes 147488 | tf_op jit(solution)/shard_map/ppermute | solution.py:442
  10.4 0.6 shard_map.73
  11.1 1.9 %collective-permute-start.4 = (bf16[4,144,128]{2,1,0:T(8,128)(2,1)S(1)}, bf16[4,144,128]{2,1,0:T(8,128)(2,1)S(1)}, u32[]{:S(2)}, u32[]{:S(2)}) collective-permute-start(bf16[4,144,128]{2,1,0:T(8,128)(2,1)S(1)} %get-tuple-element.35), channel_id=1, source_target_pairs={{0,8},{4,12},{8,0},{12,4},{16,24},{20,28},{24,16},{28,20},{1,9},{5... | collective-permute-start | bytes 442376 | tf_op jit(solution)/shard_map/ppermute | solution.py:442
  13.0 3.4 %collective-permute-start = (bf16[128,512]{1,0:T(8,128)(2,1)S(1)}, bf16[128,512]{1,0:T(8,128)(2,1)S(1)}, u32[]{:S(2)}, u32[]{:S(2)}) collective-permute-start(bf16[128,512]{1,0:T(8,128)(2,1)S(1)} %get-tuple-element.29), channel_id=1, source_target_pairs={{0,4},{4,8},{8,12},{12,16},{16,20},{20,24},{24,28},{1,5},{5,9},{9,... | collective-permute-start | bytes 393224 | tf_op jit(solution)/shard_map/ppermute | solution.py:487
  16.4 2.1 %collective-permute-start.1 = (bf16[256,512]{1,0:T(8,128)(2,1)S(1)}, bf16[256,512]{1,0:T(8,128)(2,1)S(1)}, u32[]{:S(2)}, u32[]{:S(2)}) collective-permute-start(bf16[256,512]{1,0:T(8,128)(2,1)S(1)} %get-tuple-element.30), channel_id=1, source_target_pairs={{0,4},{4,8},{8,12},{12,16},{16,20},{20,24},{24,28},{1,5},{5,9},{9,... | collective-permute-start | bytes 786440 | tf_op jit(solution)/shard_map/ppermute | solution.py:487
  18.5 3.7 %collective-permute-start.2 = (bf16[640,512]{1,0:T(8,128)(2,1)S(1)}, bf16[640,512]{1,0:T(8,128)(2,1)S(1)}, u32[]{:S(2)}, u32[]{:S(2)}) collective-permute-start(bf16[640,512]{1,0:T(8,128)(2,1)S(1)} %get-tuple-element.31), channel_id=1, source_target_pairs={{0,4},{4,8},{8,12},{12,16},{16,20},{20,24},{24,28},{1,5},{5,9},{9,... | collective-permute-start | bytes 1966088 | tf_op jit(solution)/shard_map/ppermute | solution.py:487
  22.2 2.1 %slices.1 = (bf16[512,1024]{1,0:T(8,128)(2,1)S(1)}, bf16[512,1024]{1,0:T(8,128)(2,1)S(1)}) custom-call(s32[2]{0:T(128)S(1)} %pad_add_fusion.at_ref, bf16[512,4096]{1,0:T(8,128)(2,1)} %w_hbm.3), custom_call_target="tpu_custom_call" | custom-call | flops 1000000000 | bytes 4194304 | tf_op jit(solution)/shard_map/slices/pallas_call | solution.py:104
  24.4 0.7 shard_map.74
  25.0 2.6 %collective-permute-start.5 = (bf16[4,144,128]{2,1,0:T(8,128)(2,1)S(1)}, bf16[4,144,128]{2,1,0:T(8,128)(2,1)S(1)}, u32[]{:S(2)}, u32[]{:S(2)}) collective-permute-start(bf16[4,144,128]{2,1,0:T(8,128)(2,1)S(1)} %get-tuple-element.38), channel_id=1, source_target_pairs={{0,16},{4,20},{8,24},{12,28},{16,0},{20,4},{24,8},{28,12},{1,17},{... | collective-permute-start | bytes 442376 | tf_op jit(solution)/shard_map/ppermute | solution.py:442
  27.7 4.6 %local.1.local_ref = f32[512,512]{1,0:T(8,128)S(1)} custom-call(s32[1]{0:T(128)} %bitcast.me_ref, s32[2,16]{1,0:T(2,128)S(1)} %bitcast.7, bf16[1024,512]{1,0:T(8,128)(2,1)S(1)} %get-tuple-element.26.q_ref, bf16[1024,512]{1,0:T(8,128)(2,1)S(1)} %get-tuple-element.27.k_ref, bf16[1024,512]{1,0:T(8,128)(2,1)S(1)} %get-tuple-element.28.v_ref), custom_call_target="tpu_custom_call" | custom-call | flops 15000000512 | bytes 3145728 | tf_op jit(solution)/shard_map/local/pallas_call | solution.py:277
  32.3 3.1 %collective-permute-done.5.refs_1_ = bf16[4,144,128]{2,1,0:T(8,128)(2,1)S(1)} collective-permute-done((bf16[4,144,128]{2,1,0:T(8,128)(2,1)S(1)}, bf16[4,144,128]{2,1,0:T(8,128)(2,1)S(1)}, u32[]{:S(2)}, u32[]{:S(2)}) %collective-permute-start.5) | collective-permute-done | bytes 147488 | tf_op jit(solution)/shard_map/ppermute | solution.py:442
  35.4 1.5 %collective-permute-start.10 = (bf16[256,1024]{1,0:T(8,128)(2,1)S(1)}, bf16[256,1024]{1,0:T(8,128)(2,1)S(1)}, u32[]{:S(2)}, u32[]{:S(2)}) collective-permute-start(bf16[256,1024]{1,0:T(8,128)(2,1)S(1)} %get-tuple-element.44), channel_id=1, source_target_pairs={{0,2},{1,3},{2,0},{3,1},{4,6},{5,7},{6,4},{7,5},{8,10},{9,11},{10,... | collective-permute-start | bytes 1572872 | tf_op jit(solution)/shard_map/ppermute | solution.py:442
  36.9 1.4 %readout.1 = (bf16[512,512]{1,0:T(8,128)(2,1)S(1)}, bf16[4,256,256]{2,1,0:T(8,128)(2,1)S(1)}, f32[4,8,128]{2,1,0:T(8,128)S(1)}) custom-call(s32[1]{0:T(128)} %bitcast.me_ref, f32[4,8]{1,0:T(4,128)S(1)} %bitcast.6, f32[4]{0:T(128)S(1)} %copy-done.2, bf16[1024,512]{1,0:T(8,128)(2,1)S(1)} %get-tuple-element.26.q_ref, f32[512,512]{1,0:T(8,128)S(1)} %local.1.local_ref, ...), custom_call_target="tpu_custom_call" | custom-call | flops 2000000000 | bytes 2097152 | tf_op jit(solution)/shard_map/readout/pallas_call | solution.py:313
  38.4 2.4 %shard_map.76.refs_0_ = bf16[192,512]{1,0:T(8,128)(2,1)S(1)} custom-call(s32[1]{0:T(128)} %bitcast.me_ref, s32[2,16]{1,0:T(2,128)S(1)} %bitcast.8, f32[4]{0:T(128)S(1)} %copy-done.2, bf16[1024,512]{1,0:T(8,128)(2,1)S(1)} %get-tuple-element.26.q_ref, bf16[1024,512]{1,0:T(8,128)(2,1)S(1)} %get-tuple-element.27.k_ref, ...), custom_call_target="tpu_custom_call" | custom-call | flops 8000000000 | bytes 3145728 | tf_op jit(solution)/shard_map/pallas_call | solution.py:360
  40.8 1.0 %collective-permute-start.15 = (bf16[192,512]{1,0:T(8,128)(2,1)S(1)}, bf16[192,512]{1,0:T(8,128)(2,1)S(1)}, u32[]{:S(2)}, u32[]{:S(2)}) collective-permute-start(bf16[192,512]{1,0:T(8,128)(2,1)S(1)} %shard_map.76.refs_0_), channel_id=1, source_target_pairs={{0,2},{1,3},{2,0},{3,1},{4,6},{5,7},{6,4},{7,5},{8,10},{9,11},{10,... | collective-permute-start | bytes 589832 | tf_op jit(solution)/shard_map/ppermute | solution.py:442
  41.8 1.1 %collective-permute-start.17 = (bf16[512,512]{1,0:T(8,128)(2,1)S(1)}, bf16[512,512]{1,0:T(8,128)(2,1)S(1)}, u32[]{:S(2)}, u32[]{:S(2)}) collective-permute-start(bf16[512,512]{1,0:T(8,128)(2,1)S(1)} %get-tuple-element.46.refs_0_), channel_id=1, source_target_pairs={{0,2},{1,3},{2,0},{3,1},{4,6},{5,7},{6,4},{7,5},{8,10},{9,11},{10,... | collective-permute-start | bytes 1572872 | tf_op jit(solution)/shard_map/ppermute | solution.py:442
  42.9 3.8 %shard_map.75.refs_0_ = bf16[320,512]{1,0:T(8,128)(2,1)S(1)} custom-call(s32[1]{0:T(128)} %bitcast.me_ref, s32[2,16]{1,0:T(2,128)S(1)} %bitcast.9, f32[4]{0:T(128)S(1)} %copy-done.2, bf16[1024,512]{1,0:T(8,128)(2,1)S(1)} %get-tuple-element.26.q_ref, bf16[1024,512]{1,0:T(8,128)(2,1)S(1)} %get-tuple-element.27.k_ref, ...), custom_call_target="tpu_custom_call" | custom-call | flops 8000000000 | bytes 3145728 | tf_op jit(solution)/shard_map/pallas_call | solution.py:360
  46.7 3.5 %collective-permute-done.10.refs_6_ = bf16[256,1024]{1,0:T(8,128)(2,1)S(1)} collective-permute-done((bf16[256,1024]{1,0:T(8,128)(2,1)S(1)}, bf16[256,1024]{1,0:T(8,128)(2,1)S(1)}, u32[]{:S(2)}, u32[]{:S(2)}) %collective-permute-start.10) | collective-permute-done | bytes 524320 | tf_op jit(solution)/shard_map/ppermute | solution.py:442
  50.2 1.5 %collective-permute-start.7 = (bf16[320,512]{1,0:T(8,128)(2,1)S(1)}, bf16[320,512]{1,0:T(8,128)(2,1)S(1)}, u32[]{:S(2)}, u32[]{:S(2)}) collective-permute-start(bf16[320,512]{1,0:T(8,128)(2,1)S(1)} %shard_map.75.refs_0_), channel_id=1, source_target_pairs={{0,2},{1,3},{2,0},{3,1},{4,6},{5,7},{6,4},{7,5},{8,10},{9,11},{10,... | collective-permute-start | bytes 983048 | tf_op jit(solution)/shard_map/ppermute | solution.py:442
  51.7 8.8 %collective-permute-done.12.refs_8_.refs_7_ = bf16[256,1024]{1,0:T(8,128)(2,1)S(1)} collective-permute-done((bf16[256,1024]{1,0:T(8,128)(2,1)S(1)}, bf16[256,1024]{1,0:T(8,128)(2,1)S(1)}, u32[]{:S(2)}, u32[]{:S(2)}) %collective-permute-start.12) | collective-permute-done | bytes 524320 | tf_op jit(solution)/shard_map/ppermute | solution.py:442
  60.5 0.8 collective-permute-start.14
  61.2 4.4 %collective-permute-done.15.refs_2_ = bf16[192,512]{1,0:T(8,128)(2,1)S(1)} collective-permute-done((bf16[192,512]{1,0:T(8,128)(2,1)S(1)}, bf16[192,512]{1,0:T(8,128)(2,1)S(1)}, u32[]{:S(2)}, u32[]{:S(2)}) %collective-permute-start.15) | collective-permute-done | bytes 196640 | tf_op jit(solution)/shard_map/ppermute | solution.py:442
  65.7 1.4 %collective-permute-done.16.refs_3_ = bf16[192,512]{1,0:T(8,128)(2,1)S(1)} collective-permute-done((bf16[192,512]{1,0:T(8,128)(2,1)S(1)}, bf16[192,512]{1,0:T(8,128)(2,1)S(1)}, u32[]{:S(2)}, u32[]{:S(2)}) %collective-permute-start.16) | collective-permute-done | bytes 196640 | tf_op jit(solution)/shard_map/ppermute | solution.py:442
  67.1 11.1 %collective-permute-start.13 = (bf16[256,1024]{1,0:T(8,128)(2,1)S(1)}, bf16[256,1024]{1,0:T(8,128)(2,1)S(1)}, u32[]{:S(2)}, u32[]{:S(2)}) collective-permute-start(bf16[256,1024]{1,0:T(8,128)(2,1)S(1)} %collective-permute-done.12.refs_8_.refs_7_), channel_id=1, source_target_pairs={{0,4},{4,0},{8,12},{12,8},{16,20},{20,16},{24,28},{28,24},{1,5},{5... | collective-permute-start | bytes 1572872 | tf_op jit(solution)/shard_map/ppermute | solution.py:442
  78.2 4.3 %collective-permute-done.7.refs_2_ = bf16[320,512]{1,0:T(8,128)(2,1)S(1)} collective-permute-done((bf16[320,512]{1,0:T(8,128)(2,1)S(1)}, bf16[320,512]{1,0:T(8,128)(2,1)S(1)}, u32[]{:S(2)}, u32[]{:S(2)}) %collective-permute-start.7) | collective-permute-done | bytes 327712 | tf_op jit(solution)/shard_map/ppermute | solution.py:442
  83.2 7.4 %collective-permute-done.13.refs_9_.refs_2_ = bf16[256,1024]{1,0:T(8,128)(2,1)S(1)} collective-permute-done((bf16[256,1024]{1,0:T(8,128)(2,1)S(1)}, bf16[256,1024]{1,0:T(8,128)(2,1)S(1)}, u32[]{:S(2)}, u32[]{:S(2)}) %collective-permute-start.13) | collective-permute-done | bytes 524320 | tf_op jit(solution)/shard_map/ppermute | solution.py:442
  90.5 1.0 %shard_map.77.refs_10_ = bf16[192,1024]{1,0:T(8,128)(2,1)S(1)} custom-call(s32[1]{0:T(128)} %bitcast.me_ref, bf16[192,512]{1,0:T(8,128)(2,1)S(1)} %shard_map.76.refs_0_, bf16[192,512]{1,0:T(8,128)(2,1)S(1)} %collective-permute-done.14.refs_1_, bf16[192,512]{1,0:T(8,128)(2,1)S(1)} %collective-permute-done.15.refs_2_, ...), custom_call_target="tpu_custom_call" | custom-call | flops 805306368 | bytes 4194304 | tf_op jit(solution)/shard_map/pallas_call | solution.py:429
  91.5 1.8 %shard_map.78.refs_4_ = f32[512,1024]{1,0:T(8,128)S(1)} custom-call(s32[1]{0:T(128)} %bitcast.me_ref, bf16[512,512]{1,0:T(8,128)(2,1)S(1)} %get-tuple-element.46.refs_0_, bf16[512,512]{1,0:T(8,128)(2,1)S(1)} %collective-permute-done.19.refs_1_, bf16[512,512]{1,0:T(8,128)(2,1)S(1)} %collective-permute-done.17.refs_2_.refs_1_, ...), custom_call_target="tpu_custom_call" | custom-call | flops 1610612736 | bytes 3145728 | tf_op jit(solution)/shard_map/pallas_call | solution.py:429
  93.3 0.7 shard_map.79.refs_11_
  94.1 2.3 %shard_map.80 = bf16[1024,1024]{1,0:T(8,128)(2,1)} custom-call(s32[1]{0:T(128)} %bitcast.me_ref, bf16[320,512]{1,0:T(8,128)(2,1)S(1)} %shard_map.75.refs_0_, bf16[320,512]{1,0:T(8,128)(2,1)S(1)} %collective-permute-done.6.refs_1_, bf16[320,512]{1,0:T(8,128)(2,1)S(1)} %collective-permute-done.7.refs_2_, bf16[320,512]{1,0:T(8,128)(2,1)S(1)} %collective-permute-done.8.refs_3_, ...), custom_call_target="tpu_custom_call" | custom-call | flops 1342177280 | bytes 4194304 | tf_op jit(solution)/shard_map/pallas_call | solution.py:429
  (27 shorter events, 0.9 us)
Async XLA Ops:
  0.1 10.4 %copy-start = (f32[8,4]{0,1:T(4,128)S(1)}, f32[8,4]{0,1:T(4,128)}, u32[]{:S(2)}) copy-start(f32[8,4]{0,1:T(4,128)} %param.11) | copy-start | bytes 388
  3.6 6.9 %collective-permute-start.3 = (bf16[4,144,128]{2,1,0:T(8,128)(2,1)S(1)}, bf16[4,144,128]{2,1,0:T(8,128)(2,1)S(1)}, u32[]{:S(2)}, u32[]{:S(2)}) collective-permute-start(bf16[4,144,128]{2,1,0:T(8,128)(2,1)S(1)} %get-tuple-element.32), channel_id=1, source_target_pairs={{0,4},{4,0},{8,12},{12,8},{16,20},{20,16},{24,28},{28,24},{1,5},{5... | collective-permute-start | bytes 442376 | tf_op jit(solution)/shard_map/ppermute | solution.py:442
  11.1 13.3 %collective-permute-start.4 = (bf16[4,144,128]{2,1,0:T(8,128)(2,1)S(1)}, bf16[4,144,128]{2,1,0:T(8,128)(2,1)S(1)}, u32[]{:S(2)}, u32[]{:S(2)}) collective-permute-start(bf16[4,144,128]{2,1,0:T(8,128)(2,1)S(1)} %get-tuple-element.35), channel_id=1, source_target_pairs={{0,8},{4,12},{8,0},{12,4},{16,24},{20,28},{24,16},{28,20},{1,9},{5... | collective-permute-start | bytes 442376 | tf_op jit(solution)/shard_map/ppermute | solution.py:442
  13.0 25.3 %collective-permute-start = (bf16[128,512]{1,0:T(8,128)(2,1)S(1)}, bf16[128,512]{1,0:T(8,128)(2,1)S(1)}, u32[]{:S(2)}, u32[]{:S(2)}) collective-permute-start(bf16[128,512]{1,0:T(8,128)(2,1)S(1)} %get-tuple-element.29), channel_id=1, source_target_pairs={{0,4},{4,8},{8,12},{12,16},{16,20},{20,24},{24,28},{1,5},{5,9},{9,... | collective-permute-start | bytes 393224 | tf_op jit(solution)/shard_map/ppermute | solution.py:487
  16.4 22.0 %collective-permute-start.1 = (bf16[256,512]{1,0:T(8,128)(2,1)S(1)}, bf16[256,512]{1,0:T(8,128)(2,1)S(1)}, u32[]{:S(2)}, u32[]{:S(2)}) collective-permute-start(bf16[256,512]{1,0:T(8,128)(2,1)S(1)} %get-tuple-element.30), channel_id=1, source_target_pairs={{0,4},{4,8},{8,12},{12,16},{16,20},{20,24},{24,28},{1,5},{5,9},{9,... | collective-permute-start | bytes 786440 | tf_op jit(solution)/shard_map/ppermute | solution.py:487
  18.5 23.4 %collective-permute-start.2 = (bf16[640,512]{1,0:T(8,128)(2,1)S(1)}, bf16[640,512]{1,0:T(8,128)(2,1)S(1)}, u32[]{:S(2)}, u32[]{:S(2)}) collective-permute-start(bf16[640,512]{1,0:T(8,128)(2,1)S(1)} %get-tuple-element.31), channel_id=1, source_target_pairs={{0,4},{4,8},{8,12},{12,16},{16,20},{20,24},{24,28},{1,5},{5,9},{9,... | collective-permute-start | bytes 1966088 | tf_op jit(solution)/shard_map/ppermute | solution.py:487
  24.3 3.4 %copy-start.1 = (s32[16,2]{0,1:T(2,128)S(1)}, s32[16,2]{0,1:T(2,128)}, u32[]{:S(2)}) copy-start(s32[16,2]{0,1:T(2,128)} %param.10) | copy-start | bytes 388
  24.3 58.3 %collective-permute-start.9 = (bf16[512,1024]{1,0:T(8,128)(2,1)S(1)}, bf16[512,1024]{1,0:T(8,128)(2,1)S(1)}, u32[]{:S(2)}, u32[]{:S(2)}) collective-permute-start(bf16[512,1024]{1,0:T(8,128)(2,1)S(1)} %get-tuple-element.43), channel_id=1, source_target_pairs={{0,1},{1,0},{2,3},{3,2},{4,5},{5,4},{6,7},{7,6},{8,9},{9,8},{10,11... | collective-permute-start | bytes 3145736 | tf_op jit(solution)/shard_map/ppermute | solution.py:442
  25.0 10.4 %collective-permute-start.5 = (bf16[4,144,128]{2,1,0:T(8,128)(2,1)S(1)}, bf16[4,144,128]{2,1,0:T(8,128)(2,1)S(1)}, u32[]{:S(2)}, u32[]{:S(2)}) collective-permute-start(bf16[4,144,128]{2,1,0:T(8,128)(2,1)S(1)} %get-tuple-element.38), channel_id=1, source_target_pairs={{0,16},{4,20},{8,24},{12,28},{16,0},{20,4},{24,8},{28,12},{1,17},{... | collective-permute-start | bytes 442376 | tf_op jit(solution)/shard_map/ppermute | solution.py:442
  27.7 9.3 %copy-start.2 = (f32[4]{0:T(128)S(1)}, f32[4]{0:T(128)}, u32[]{:S(2)}) copy-start(f32[4]{0:T(128)} %gate_ref.5) | copy-start | bytes 52
  35.4 14.8 %collective-permute-start.10 = (bf16[256,1024]{1,0:T(8,128)(2,1)S(1)}, bf16[256,1024]{1,0:T(8,128)(2,1)S(1)}, u32[]{:S(2)}, u32[]{:S(2)}) collective-permute-start(bf16[256,1024]{1,0:T(8,128)(2,1)S(1)} %get-tuple-element.44), channel_id=1, source_target_pairs={{0,2},{1,3},{2,0},{3,1},{4,6},{5,7},{6,4},{7,5},{8,10},{9,11},{10,... | collective-permute-start | bytes 1572872 | tf_op jit(solution)/shard_map/ppermute | solution.py:442
  38.3 22.2 %collective-permute-start.12 = (bf16[256,1024]{1,0:T(8,128)(2,1)S(1)}, bf16[256,1024]{1,0:T(8,128)(2,1)S(1)}, u32[]{:S(2)}, u32[]{:S(2)}) collective-permute-start(bf16[256,1024]{1,0:T(8,128)(2,1)S(1)} %get-tuple-element.45), channel_id=1, source_target_pairs={{0,3},{1,2},{2,1},{3,0},{4,7},{5,6},{6,5},{7,4},{8,11},{9,10},{10,... | collective-permute-start | bytes 1572872 | tf_op jit(solution)/shard_map/ppermute | solution.py:442
  40.8 24.8 %collective-permute-start.15 = (bf16[192,512]{1,0:T(8,128)(2,1)S(1)}, bf16[192,512]{1,0:T(8,128)(2,1)S(1)}, u32[]{:S(2)}, u32[]{:S(2)}) collective-permute-start(bf16[192,512]{1,0:T(8,128)(2,1)S(1)} %shard_map.76.refs_0_), channel_id=1, source_target_pairs={{0,2},{1,3},{2,0},{3,1},{4,6},{5,7},{6,4},{7,5},{8,10},{9,11},{10,... | collective-permute-start | bytes 589832 | tf_op jit(solution)/shard_map/ppermute | solution.py:442
  41.8 36.4 %collective-permute-start.17 = (bf16[512,512]{1,0:T(8,128)(2,1)S(1)}, bf16[512,512]{1,0:T(8,128)(2,1)S(1)}, u32[]{:S(2)}, u32[]{:S(2)}) collective-permute-start(bf16[512,512]{1,0:T(8,128)(2,1)S(1)} %get-tuple-element.46.refs_0_), channel_id=1, source_target_pairs={{0,2},{1,3},{2,0},{3,1},{4,6},{5,7},{6,4},{7,5},{8,10},{9,11},{10,... | collective-permute-start | bytes 1572872 | tf_op jit(solution)/shard_map/ppermute | solution.py:442
  50.2 32.4 %collective-permute-start.7 = (bf16[320,512]{1,0:T(8,128)(2,1)S(1)}, bf16[320,512]{1,0:T(8,128)(2,1)S(1)}, u32[]{:S(2)}, u32[]{:S(2)}) collective-permute-start(bf16[320,512]{1,0:T(8,128)(2,1)S(1)} %shard_map.75.refs_0_), channel_id=1, source_target_pairs={{0,2},{1,3},{2,0},{3,1},{4,6},{5,7},{6,4},{7,5},{8,10},{9,11},{10,... | collective-permute-start | bytes 983048 | tf_op jit(solution)/shard_map/ppermute | solution.py:442
  60.5 5.2 %collective-permute-start.14 = (bf16[192,512]{1,0:T(8,128)(2,1)S(1)}, bf16[192,512]{1,0:T(8,128)(2,1)S(1)}, u32[]{:S(2)}, u32[]{:S(2)}) collective-permute-start(bf16[192,512]{1,0:T(8,128)(2,1)S(1)} %shard_map.76.refs_0_), channel_id=1, source_target_pairs={{0,1},{1,0},{2,3},{3,2},{4,5},{5,4},{6,7},{7,6},{8,9},{9,8},{10,11... | collective-permute-start | bytes 589832 | tf_op jit(solution)/shard_map/ppermute | solution.py:442
  65.6 1.4 %collective-permute-start.16 = (bf16[192,512]{1,0:T(8,128)(2,1)S(1)}, bf16[192,512]{1,0:T(8,128)(2,1)S(1)}, u32[]{:S(2)}, u32[]{:S(2)}) collective-permute-start(bf16[192,512]{1,0:T(8,128)(2,1)S(1)} %collective-permute-done.15.refs_2_), channel_id=1, source_target_pairs={{0,1},{1,0},{2,3},{3,2},{4,5},{5,4},{6,7},{7,6},{8,9},{9,8},{10,11... | collective-permute-start | bytes 589832 | tf_op jit(solution)/shard_map/ppermute | solution.py:442
  65.6 17.4 %collective-permute-start.11 = (bf16[256,1024]{1,0:T(8,128)(2,1)S(1)}, bf16[256,1024]{1,0:T(8,128)(2,1)S(1)}, u32[]{:S(2)}, u32[]{:S(2)}) collective-permute-start(bf16[256,1024]{1,0:T(8,128)(2,1)S(1)} %collective-permute-done.10.refs_6_), channel_id=1, source_target_pairs={{0,8},{4,12},{8,0},{12,4},{16,24},{20,28},{24,16},{28,20},{1,9},{5... | collective-permute-start | bytes 1572872 | tf_op jit(solution)/shard_map/ppermute | solution.py:442
  67.1 23.4 %collective-permute-start.13 = (bf16[256,1024]{1,0:T(8,128)(2,1)S(1)}, bf16[256,1024]{1,0:T(8,128)(2,1)S(1)}, u32[]{:S(2)}, u32[]{:S(2)}) collective-permute-start(bf16[256,1024]{1,0:T(8,128)(2,1)S(1)} %collective-permute-done.12.refs_8_.refs_7_), channel_id=1, source_target_pairs={{0,4},{4,0},{8,12},{12,8},{16,20},{20,16},{24,28},{28,24},{1,5},{5... | collective-permute-start | bytes 1572872 | tf_op jit(solution)/shard_map/ppermute | solution.py:442
  78.2 13.3 %collective-permute-start.19 = (bf16[512,512]{1,0:T(8,128)(2,1)S(1)}, bf16[512,512]{1,0:T(8,128)(2,1)S(1)}, u32[]{:S(2)}, u32[]{:S(2)}) collective-permute-start(bf16[512,512]{1,0:T(8,128)(2,1)S(1)} %get-tuple-element.46.refs_0_), channel_id=1, source_target_pairs={{0,1},{1,0},{2,3},{3,2},{4,5},{5,4},{6,7},{7,6},{8,9},{9,8},{10,11... | collective-permute-start | bytes 1572872 | tf_op jit(solution)/shard_map/ppermute | solution.py:442
  82.6 9.0 %collective-permute-start.18 = (bf16[512,512]{1,0:T(8,128)(2,1)S(1)}, bf16[512,512]{1,0:T(8,128)(2,1)S(1)}, u32[]{:S(2)}, u32[]{:S(2)}) collective-permute-start(bf16[512,512]{1,0:T(8,128)(2,1)S(1)} %collective-permute-done.17.refs_2_.refs_1_), channel_id=1, source_target_pairs={{0,1},{1,0},{2,3},{3,2},{4,5},{5,4},{6,7},{7,6},{8,9},{9,8},{10,11... | collective-permute-start | bytes 1572872 | tf_op jit(solution)/shard_map/ppermute | solution.py:442
  82.6 11.5 %collective-permute-start.6 = (bf16[320,512]{1,0:T(8,128)(2,1)S(1)}, bf16[320,512]{1,0:T(8,128)(2,1)S(1)}, u32[]{:S(2)}, u32[]{:S(2)}) collective-permute-start(bf16[320,512]{1,0:T(8,128)(2,1)S(1)} %shard_map.75.refs_0_), channel_id=1, source_target_pairs={{0,1},{1,0},{2,3},{3,2},{4,5},{5,4},{6,7},{7,6},{8,9},{9,8},{10,11... | collective-permute-start | bytes 983048 | tf_op jit(solution)/shard_map/ppermute | solution.py:442
  83.1 11.0 %collective-permute-start.8 = (bf16[320,512]{1,0:T(8,128)(2,1)S(1)}, bf16[320,512]{1,0:T(8,128)(2,1)S(1)}, u32[]{:S(2)}, u32[]{:S(2)}) collective-permute-start(bf16[320,512]{1,0:T(8,128)(2,1)S(1)} %collective-permute-done.7.refs_2_), channel_id=1, source_target_pairs={{0,1},{1,0},{2,3},{3,2},{4,5},{5,4},{6,7},{7,6},{8,9},{9,8},{10,11... | collective-permute-start | bytes 983048 | tf_op jit(solution)/shard_map/ppermute | solution.py:442
